TPU v7x, 32 devices: a whole 2x2x4 slice. The times are simulated.
32 devices in a mesh: shard: 4 (over y, x), ctx: 2 (over core), tp: 4 (over z).
Axes of the slice: x: 2, y: 2, z: 4, core: 2. Of those that a mesh axis runs over, the one named last changes fastest.
Arguments:
- tokens: bfloat16 [4, 2048, 2048], P('shard', 'ctx'), may hold values from -6 to 6
- lengths: int32 [4], P('shard'), may hold values from 512 to 2048, as said below
- cotangent: bfloat16 [4, 2048, 2048], P('shard', 'ctx'), may hold values from -6 to 6
- w_query: float32 [2048, 2048], P(('shard', 'ctx'), 'tp'), may hold values from -0.1875 to 0.1875
- w_key: float32 [2048, 2048], P(('shard', 'ctx'), 'tp'), may hold values from -0.1875 to 0.1875
- w_value: float32 [2048, 2048], P(('shard', 'ctx'), 'tp'), may hold values from -0.125 to 0.125
- w_output: float32 [2048, 2048], P('tp', ('shard', 'ctx')), may hold values from -1 to 1
- w_gate: float32 [2048, 8192], P(('shard', 'ctx'), 'tp'), may hold values from -0.125 to 0.125
- w_up: float32 [2048, 8192], P(('shard', 'ctx'), 'tp'), may hold values from -0.125 to 0.125
- w_down: float32 [8192, 2048], P('tp', ('shard', 'ctx')), may hold values from -0.0625 to 0.0625
Outputs:
- output: bfloat16 [4, 2048, 2048], P('shard', 'ctx')
- grad_tokens: float32 [4, 2048, 2048], P('shard', 'ctx')
- grad_query: float32 [2048, 2048], P(('shard', 'ctx'), 'tp')
- grad_key: float32 [2048, 2048], P(('shard', 'ctx'), 'tp')
- grad_value: float32 [2048, 2048], P(('shard', 'ctx'), 'tp')
- grad_output: float32 [2048, 2048], P('tp', ('shard', 'ctx'))
- grad_gate: float32 [2048, 8192], P(('shard', 'ctx'), 'tp')
- grad_up: float32 [2048, 8192], P(('shard', 'ctx'), 'tp')
- grad_down: float32 [8192, 2048], P('tp', ('shard', 'ctx'))
Inputs may be any that keep to these rules, and one draw needn't show every extreme that they name: Slots 0 to lengths[b] - 1 of sequence b are valid, the rest padding; some sequence is full and some has 512 valid slots.
All inputs are finite; a program needn't handle non-finite values.
Results may differ from a plain program's by a relative error of at most 0.014.
The roundings to bfloat16 on the way count: a program that leaves them out, or rounds other values in their place, can miss the bound.
Values may be sent and summed in bfloat16 or wider, within the bound.
A program may use at most 256 MiB of HBM per device.

v0:
```python
import jax
import jax.numpy as jnp
from jax import lax
from jax.sharding import PartitionSpec as P

HEAD_DIM = 128


EPSILON = 1e-05


def normalize(values):
    center = values - jnp.mean(values, axis=-1, keepdims=True)
    inv_scale = lax.rsqrt(jnp.mean(center * center, axis=-1, keepdims=True) + EPSILON)
    return (center * inv_scale, inv_scale)


def norm_back(normed, inv_scale, upstream):
    first_mean = jnp.mean(upstream, axis=-1, keepdims=True)
    second_mean = jnp.mean(upstream * normed, axis=-1, keepdims=True)
    return inv_scale * (upstream - first_mean - normed * second_mean)


def rope_tables(row_count, head_size, offset):
    positions = (jnp.arange(row_count) + offset).astype(jnp.float32)
    inverse = 10000.0 ** (-(jnp.arange(head_size // 2).astype(jnp.float32) * 2.0) / head_size)
    angles = positions[:, None] * inverse[None, :]
    angles = jnp.concatenate([angles, angles], axis=-1)
    return (jnp.cos(angles)[:, None, :], jnp.sin(angles)[:, None, :])


def turn_half(values):
    half_dim = values.shape[-1] // 2
    return jnp.concatenate([-values[..., half_dim:], values[..., :half_dim]], axis=-1)


def rotate(values, cosine, sine_table):
    return values * cosine + turn_half(values) * sine_table


def rotate_back(values, cosine, sine_table):
    return values * cosine - turn_half(values) * sine_table


def score_block(query_rows, keys_seq, length, row_start):
    block_rows = query_rows.shape[0]
    key_pos = jnp.arange(keys_seq.shape[0])
    row_pos = row_start + jnp.arange(block_rows)
    scores = jnp.einsum(
        "qhd,khd->hqk", query_rows, keys_seq, preferred_element_type=jnp.float32
    ) * HEAD_DIM ** (-0.5)
    allowed = (key_pos[None, :] <= row_pos[:, None]) & (key_pos[None, :] < length)
    return jnp.where(allowed[None], scores, -1e30)


def attend_forward(queries_seq, keys_seq, values_seq, length, offset):
    half_len, head_count, head_size = queries_seq.shape
    block_rows = min(512, half_len)
    block_count = half_len // block_rows
    grouped = queries_seq.reshape(block_count, block_rows, head_count, head_size)

    def one_block(paired):
        query_rows, block_index = paired
        scores = score_block(query_rows, keys_seq, length, offset + block_index * block_rows)
        row_peak = jnp.max(scores, axis=-1, keepdims=True)
        log_total = jnp.log(jnp.sum(jnp.exp(scores - row_peak), axis=-1, keepdims=True)) + row_peak
        probability = jnp.exp(scores - log_total).astype(jnp.bfloat16)
        attended = jnp.einsum(
            "hqk,khd->qhd", probability, values_seq, preferred_element_type=jnp.float32
        )
        return (attended.astype(jnp.bfloat16), log_total[..., 0])

    attended, log_totals = lax.map(one_block, (grouped, jnp.arange(block_count)))
    return (attended.reshape(half_len, head_count, head_size), log_totals)


def attend_backward(queries_seq, keys_seq, values_seq, length, offset, log_totals, grad_seq):
    half_len, head_count, head_size = queries_seq.shape
    block_rows = min(512, half_len)
    block_count = half_len // block_rows
    score_scale = HEAD_DIM ** (-0.5)
    grouped = queries_seq.reshape(block_count, block_rows, head_count, head_size)
    grad_grouped = grad_seq.reshape(block_count, block_rows, head_count, head_size)

    def one_block(carried, paired):
        query_rows, grad_rows, log_rows, block_index = paired
        scores = score_block(query_rows, keys_seq, length, offset + block_index * block_rows)
        probability = jnp.exp(scores - log_rows[..., None])
        prob_low = probability.astype(jnp.bfloat16)
        grad_prob = jnp.einsum(
            "qhd,khd->hqk", grad_rows, values_seq, preferred_element_type=jnp.float32
        )
        inner_sum = jnp.sum(probability * grad_prob, axis=-1, keepdims=True)
        grad_scores = (probability * (grad_prob - inner_sum)).astype(jnp.bfloat16)
        grad_query_rows = (
            jnp.einsum("hqk,khd->qhd", grad_scores, keys_seq, preferred_element_type=jnp.float32)
            * score_scale
        )
        key_part = (
            jnp.einsum("hqk,qhd->khd", grad_scores, query_rows, preferred_element_type=jnp.float32)
            * score_scale
        )
        value_part = jnp.einsum(
            "hqk,qhd->khd", prob_low, grad_rows, preferred_element_type=jnp.float32
        )
        return ((carried[0] + key_part, carried[1] + value_part), grad_query_rows)

    empty = jnp.zeros(keys_seq.shape, jnp.float32)
    sums, grad_queries = lax.scan(
        one_block, (empty, empty), (grouped, grad_grouped, log_totals, jnp.arange(block_count))
    )
    return (grad_queries.reshape(half_len, head_count, head_size), sums[0], sums[1])


def matmul_low(left, right):
    return jnp.dot(left, right, preferred_element_type=jnp.float32)


def body(tokens, lengths, cotangent, w_query, w_key, w_value, w_output, w_gate, w_up, w_down):
    seq_count, half_len, model_width = tokens.shape
    head_cols = w_query.shape[1]
    head_count = head_cols // HEAD_DIM
    row_total = seq_count * half_len
    offset = lax.axis_index("ctx") * half_len
    positions = offset + jnp.arange(half_len)
    valid_mask = (positions[None, :] < lengths[:, None]).astype(jnp.float32)
    bf_type = jnp.bfloat16
    attn_low = (
        w_query.astype(bf_type),
        w_key.astype(bf_type),
        w_value.astype(bf_type),
        w_output.astype(bf_type),
    )
    mlp_low = (w_gate.astype(bf_type), w_up.astype(bf_type), w_down.astype(bf_type))
    query_full, key_full, value_full, output_full = (
        lax.all_gather(attn_low[0], ("shard", "ctx"), axis=0, tiled=True),
        lax.all_gather(attn_low[1], ("shard", "ctx"), axis=0, tiled=True),
        lax.all_gather(attn_low[2], ("shard", "ctx"), axis=0, tiled=True),
        lax.all_gather(attn_low[3], ("shard", "ctx"), axis=1, tiled=True),
    )
    gate_full, up_full, down_full = (
        lax.all_gather(mlp_low[0], ("shard", "ctx"), axis=0, tiled=True),
        lax.all_gather(mlp_low[1], ("shard", "ctx"), axis=0, tiled=True),
        lax.all_gather(mlp_low[2], ("shard", "ctx"), axis=1, tiled=True),
    )
    tokens_wide = tokens.astype(jnp.float32).reshape(row_total, model_width)
    normed_one, scale_one = normalize(tokens_wide)
    input_one = normed_one.astype(bf_type)
    split_heads = (seq_count, half_len, head_count, HEAD_DIM)
    query_pre = matmul_low(input_one, query_full).reshape(split_heads)
    key_pre = matmul_low(input_one, key_full).reshape(split_heads)
    value_pre = matmul_low(input_one, value_full).reshape(split_heads)
    cosine, sine_table = rope_tables(half_len, HEAD_DIM, offset)
    queries = rotate(query_pre, cosine, sine_table).astype(bf_type)
    keys_rot = rotate(key_pre, cosine, sine_table).astype(bf_type)
    values_low = value_pre.astype(bf_type)
    keys_all, values_all = (
        lax.all_gather(keys_rot, "ctx", axis=1, tiled=True),
        lax.all_gather(values_low, "ctx", axis=1, tiled=True),
    )
    seq_index = 0
    attended, log_totals = attend_forward(
        queries[seq_index], keys_all[seq_index], values_all[seq_index], lengths[seq_index], offset
    )
    attended_list = [attended]
    log_list = [log_totals]
    attn_out = jnp.stack(attended_list).reshape(row_total, head_cols)
    branch_part = matmul_low(attn_out, output_full)
    resid = tokens_wide + lax.psum(branch_part, "tp")
    normed_two, scale_two = normalize(resid)
    input_two = normed_two.astype(bf_type)
    gate_proj = matmul_low(input_two, gate_full)
    up_proj = matmul_low(input_two, up_full)
    gate_sigmoid = jax.nn.sigmoid(gate_proj)
    hidden = (gate_proj * gate_sigmoid * up_proj).astype(bf_type)
    branch_two_part = matmul_low(hidden, down_full)
    final_sum = resid + lax.psum(branch_two_part.astype(jnp.bfloat16), "tp").astype(jnp.float32)
    grad_final = cotangent.astype(jnp.float32).reshape(row_total, model_width) * valid_mask.reshape(
        row_total, 1
    )
    grad_branch = grad_final.astype(bf_type)
    grad_down = jnp.einsum("rf,rd->fd", hidden, grad_branch, preferred_element_type=jnp.float32)
    grad_hidden = jnp.einsum(
        "rd,fd->rf", grad_branch, down_full, preferred_element_type=jnp.float32
    )
    grad_gate_act = (
        grad_hidden * up_proj * gate_sigmoid * (1.0 + gate_proj * (1.0 - gate_sigmoid))
    ).astype(bf_type)
    grad_up_act = (grad_hidden * gate_proj * gate_sigmoid).astype(bf_type)
    grad_gate = jnp.einsum(
        "rd,rf->df", input_two, grad_gate_act, preferred_element_type=jnp.float32
    )
    grad_up = jnp.einsum("rd,rf->df", input_two, grad_up_act, preferred_element_type=jnp.float32)
    grad_input_two = jnp.einsum(
        "rf,df->rd", grad_gate_act, gate_full, preferred_element_type=jnp.float32
    ) + jnp.einsum("rf,df->rd", grad_up_act, up_full, preferred_element_type=jnp.float32)
    mlp_grads = (
        lax.psum_scatter(grad_gate, ("shard", "ctx"), scatter_dimension=0, tiled=True),
        lax.psum_scatter(grad_up, ("shard", "ctx"), scatter_dimension=0, tiled=True),
        lax.psum_scatter(grad_down, ("shard", "ctx"), scatter_dimension=1, tiled=True),
    )
    grad_input_two = lax.psum(grad_input_two, "tp")
    grad_resid = grad_final + norm_back(normed_two, scale_two, grad_input_two)
    grad_resid_low = grad_resid.astype(bf_type)
    grad_wout = jnp.einsum(
        "rc,rd->cd", attn_out, grad_resid_low, preferred_element_type=jnp.float32
    )
    grad_attn = jnp.einsum(
        "rd,cd->rc", grad_resid_low, output_full, preferred_element_type=jnp.float32
    )
    grad_attn = grad_attn.astype(bf_type).reshape(split_heads)
    seq_index = 0
    grad_queries, grad_keys_seq, grad_values_seq = attend_backward(
        queries[seq_index],
        keys_all[seq_index],
        values_all[seq_index],
        lengths[seq_index],
        offset,
        log_list[seq_index],
        grad_attn[seq_index],
    )
    query_grads = [grad_queries]
    key_grads = [grad_keys_seq]
    value_grads = [grad_values_seq]
    grad_keys, grad_values = (
        lax.psum_scatter(jnp.stack(key_grads), "ctx", scatter_dimension=1, tiled=True),
        lax.psum_scatter(jnp.stack(value_grads), "ctx", scatter_dimension=1, tiled=True),
    )
    grad_q_pre = (
        rotate_back(jnp.stack(query_grads), cosine, sine_table)
        .astype(bf_type)
        .reshape(row_total, head_cols)
    )
    grad_k_pre = (
        rotate_back(grad_keys, cosine, sine_table).astype(bf_type).reshape(row_total, head_cols)
    )
    grad_v_pre = grad_values.astype(bf_type).reshape(row_total, head_cols)
    grad_wq = jnp.einsum("rd,rc->dc", input_one, grad_q_pre, preferred_element_type=jnp.float32)
    grad_wk = jnp.einsum("rd,rc->dc", input_one, grad_k_pre, preferred_element_type=jnp.float32)
    grad_wv = jnp.einsum("rd,rc->dc", input_one, grad_v_pre, preferred_element_type=jnp.float32)
    grad_input_one = (
        jnp.einsum("rc,dc->rd", grad_q_pre, query_full, preferred_element_type=jnp.float32)
        + jnp.einsum("rc,dc->rd", grad_k_pre, key_full, preferred_element_type=jnp.float32)
        + jnp.einsum("rc,dc->rd", grad_v_pre, value_full, preferred_element_type=jnp.float32)
    )
    attn_grads = (
        lax.psum_scatter(grad_wq, ("shard", "ctx"), scatter_dimension=0, tiled=True),
        lax.psum_scatter(grad_wk, ("shard", "ctx"), scatter_dimension=0, tiled=True),
        lax.psum_scatter(grad_wv, ("shard", "ctx"), scatter_dimension=0, tiled=True),
        lax.psum_scatter(grad_wout, ("shard", "ctx"), scatter_dimension=1, tiled=True),
    )
    grad_input_one = lax.psum(grad_input_one, "tp")
    grad_tokens = grad_resid + norm_back(normed_one, scale_one, grad_input_one)
    output = final_sum.astype(bf_type).reshape(seq_count, half_len, model_width)
    grad_tokens = grad_tokens.reshape(seq_count, half_len, model_width)
    return (
        output,
        grad_tokens,
        attn_grads[0],
        attn_grads[1],
        attn_grads[2],
        attn_grads[3],
        mlp_grads[0],
        mlp_grads[1],
        mlp_grads[2],
    )


def solution(mesh):
    return jax.shard_map(
        body,
        mesh=mesh,
        in_specs=(
            P("shard", "ctx", None),
            P("shard"),
            P("shard", "ctx", None),
            P(("shard", "ctx"), "tp"),
            P(("shard", "ctx"), "tp"),
            P(("shard", "ctx"), "tp"),
            P("tp", ("shard", "ctx")),
            P(("shard", "ctx"), "tp"),
            P(("shard", "ctx"), "tp"),
            P("tp", ("shard", "ctx")),
        ),
        out_specs=(
            P("shard", "ctx", None),
            P("shard", "ctx", None),
            P(("shard", "ctx"), "tp"),
            P(("shard", "ctx"), "tp"),
            P(("shard", "ctx"), "tp"),
            P("tp", ("shard", "ctx")),
            P(("shard", "ctx"), "tp"),
            P(("shard", "ctx"), "tp"),
            P("tp", ("shard", "ctx")),
        ),
        check_vma=False,
    )
```

profile of v0, /device:TPU:0, one launch (start us, length us, event | category | flops | bytes accessed | tf_op | source)
XLA Modules:
  0.0 2208.8 jit_solution(8768566741574588461)
XLA Ops:
  21.9 19.1 all-gather.13.cloned.1.call-done
  48.2 23.1 %all-gather.17.cloned.1.call-done = bf16[2048,512]{1,0:T(8,128)(2,1)} async-done(((bf16[256,512]{1,0:T(8,128)(2,1)}), bf16[2048,512]{1,0:T(8,128)(2,1)}) %all-gather.17.cloned.1.call-update) | async-done | bytes 2097168 | tf_op jit(solution)/shard_map/all_gather | solution.py:138
  83.4 18.1 all-gather.11.cloned.1.call-done
  136.1 35.1 %while.27 = (s32[]{:T(128)}, bf16[2,512,4,128]{3,2,1,0:T(4,128)(2,1)S(1)}, f32[2,4,512]{2,1,0:T(4,128)S(1)}, s32[2]{0:T(128)S(1)}, s32[]{:T(128)}, /*index=5*/s3...) while((s32[]{:T(128)}, ...), condition=%wide.region_5.6_spmd, body=%wide.region_2.5_spmd.sunk | while | flops 2195980800 | bytes 69280448 | solution.py:73
  187.3 283.6 %all-reduce.5.cloned.1.call-done = f32[1024,2048]{1,0:T(8,128)} async-done(((f32[1024,2048]{1,0:T(8,128)}), f32[1024,2048]{1,0:T(8,128)}) %all-reduce.5.cloned.1.call-update) | async-done | bytes 8388624 | tf_op jit(solution)/shard_map/psum | solution.py:169
  482.5 44.2 %all-gather.21.cloned.1.call-done = bf16[2048,2048]{1,0:T(8,128)(2,1)} async-done(((bf16[256,2048]{1,0:T(8,128)(2,1)}), bf16[2048,2048]{1,0:T(8,128)(2,1)}) %all-gather.21.cloned.1.call-update) | async-done | bytes 8388624 | tf_op jit(solution)/shard_map/all_gather | solution.py:142
  526.6 14.5 fusion.108
  541.1 42.3 %all-gather.23.cloned.1.call-done = bf16[2048,2048]{1,0:T(8,128)(2,1)} async-done(((bf16[256,2048]{1,0:T(8,128)(2,1)}), bf16[2048,2048]{1,0:T(8,128)(2,1)}) %all-gather.23.cloned.1.call-update) | async-done | bytes 8388624 | tf_op jit(solution)/shard_map/all_gather | solution.py:143
  583.4 14.4 fusion.109
  597.8 43.8 %all-gather.25.cloned.1.call-done = bf16[2048,2048]{1,0:T(8,128)(2,1)} async-done(((bf16[2048,256]{1,0:T(8,128)(2,1)}), bf16[2048,2048]{1,0:T(8,128)(2,1)}) %all-gather.25.cloned.1.call-update) | async-done | bytes 8388624 | tf_op jit(solution)/shard_map/all_gather | solution.py:144
  641.6 22.0 multiply_convert_fusion.1
  663.6 15.1 fusion.110
  678.8 13.0 convolution_add_fusion
  691.8 13.8 convolution_convert_fusion
  705.7 277.0 %all-reduce.9.cloned.1.call-done = f32[1024,2048]{1,0:T(8,128)} async-done(((f32[1024,2048]{1,0:T(8,128)}), f32[1024,2048]{1,0:T(8,128)}) %all-reduce.9.cloned.1.call-update) | async-done | bytes 8388624 | tf_op jit(solution)/shard_map/psum | solution.py:202
  989.6 149.9 %all-reduce.7.cloned.1.call-done = bf16[1024,2048]{1,0:T(8,128)(2,1)} async-done(((bf16[1024,2048]{1,0:T(8,128)(2,1)}), bf16[1024,2048]{1,0:T(8,128)(2,1)}) %all-reduce.7.cloned.1.call-update) | async-done | bytes 4194320 | tf_op jit(solution)/shard_map/psum | solution.py:177
  1158.7 129.7 %while.28 = (s32[]{:T(128)}, f32[2048,4,128]{0,2,1:T(8,128)}, f32[2048,4,128]{0,2,1:T(8,128)}, f32[2,512,4,128]{3,1,2,0:T(8,128)}, bf16[2,512,4,128]{3,1,2,0:T(8...) while((s32[]{:T(128)}, f32[2048,4,128]{0,2,1:T(8,128)}, ...), condition=%wide.region_15.16_spmd.clone, body=%wide.region_13.15_spmd.clone.sunk | while | flops 5439226368 | bytes 211879280 | solution.py:109
  1172.0 13.1 multiply_reduce_fusion.4
  1185.2 14.9 multiply_convert_fusion.5
  1235.4 13.1 multiply_reduce_fusion.4
  1248.6 14.9 multiply_convert_fusion.5
  1364.4 15.3 fusion.112
  1379.8 15.2 fusion.113
  1395.6 15.6 fusion.72
  1411.3 210.5 %all-reduce.11.cloned.1.call-done = f32[1024,2048]{1,0:T(8,128)} async-done(((f32[1024,2048]{1,0:T(8,128)}), f32[1024,2048]{1,0:T(8,128)}) %all-reduce.11.cloned.1.call-update) | async-done | bytes 8388624 | tf_op jit(solution)/shard_map/psum | solution.py:252
  1637.7 38.1 %reduce-scatter.14.cloned.1.call-done = f32[256,512]{1,0:T(8,128)} async-done(((f32[2048,512]{1,0:T(8,128)}), f32[256,512]{1,0:T(8,128)}) %reduce-scatter.14.cloned.1.call-update) | async-done | bytes 524304 | tf_op jit(solution)/shard_map/reduce_scatter | solution.py:247
  1675.8 54.9 %reduce-scatter.20.cloned.1.call-done = f32[512,256]{1,0:T(8,128)} async-done(((f32[512,2048]{1,0:T(8,128)}), f32[512,256]{1,0:T(8,128)}) %reduce-scatter.20.cloned.1.call-update) | async-done | bytes 524304 | tf_op jit(solution)/shard_map/reduce_scatter | solution.py:250
  1730.7 55.0 %reduce-scatter.16.cloned.1.call-done = f32[256,512]{1,0:T(8,128)} async-done(((f32[2048,512]{1,0:T(8,128)}), f32[256,512]{1,0:T(8,128)}) %reduce-scatter.16.cloned.1.call-update) | async-done | bytes 524304 | tf_op jit(solution)/shard_map/reduce_scatter | solution.py:248
  1785.7 55.1 %reduce-scatter.18.cloned.1.call-done = f32[256,512]{1,0:T(8,128)} async-done(((f32[2048,512]{1,0:T(8,128)}), f32[256,512]{1,0:T(8,128)}) %reduce-scatter.18.cloned.1.call-update) | async-done | bytes 524304 | tf_op jit(solution)/shard_map/reduce_scatter | solution.py:249
  1840.8 120.2 %reduce-scatter.22.cloned.1.call-done = f32[256,2048]{1,0:T(8,128)} async-done(((f32[2048,2048]{1,0:T(8,128)}), f32[256,2048]{1,0:T(8,128)}) %reduce-scatter.22.cloned.1.call-update) | async-done | bytes 2097168 | tf_op jit(solution)/shard_map/reduce_scatter | solution.py:198
  1961.0 120.4 %reduce-scatter.24.cloned.1.call-done = f32[256,2048]{1,0:T(8,128)} async-done(((f32[2048,2048]{1,0:T(8,128)}), f32[256,2048]{1,0:T(8,128)}) %reduce-scatter.24.cloned.1.call-update) | async-done | bytes 2097168 | tf_op jit(solution)/shard_map/reduce_scatter | solution.py:199
  2081.4 120.2 %reduce-scatter.26.cloned.1.call-done = f32[2048,256]{1,0:T(8,128)} async-done(((f32[2048,2048]{1,0:T(8,128)}), f32[2048,256]{1,0:T(8,128)}) %reduce-scatter.26.cloned.1.call-update) | async-done | bytes 2097168 | tf_op jit(solution)/shard_map/reduce_scatter | solution.py:200
  (277 shorter events, 318.4 us)
Async XLA Ops:
  7.2 33.8 %all-gather.13.cloned.1.call-start = ((), (), s32[]{:S(2)}) async-start(), calls=%async_computation.10 | async-start | bytes 2359296 | tf_op jit(solution)/shard_map/all_gather | solution.py:137
  9.0 62.2 %all-gather.17.cloned.1.call-start = ((), (), s32[]{:S(2)}) async-start(), calls=%async_computation.12 | async-start | bytes 2359296 | tf_op jit(solution)/shard_map/all_gather | solution.py:138
  10.9 90.7 %all-gather.11.cloned.1.call-start = ((), (), s32[]{:S(2)}) async-start(), calls=%async_computation.9 | async-start | bytes 2359296 | tf_op jit(solution)/shard_map/all_gather | solution.py:136
  12.7 120.2 %all-gather.15.cloned.1.call-start = ((), (), s32[]{:S(2)}) async-start(), calls=%async_computation.11 | async-start | bytes 3145728 | tf_op jit(solution)/shard_map/all_gather | solution.py:158
  14.8 31.7 %copy-start.17 = (f32[1024,128]{0,1:T(8,128)}, f32[1024,128]{0,1:T(8,128)S(1)}, u32[]{:S(2)}) copy-start(f32[1024,128]{0,1:T(8,128)S(1)} %get-tuple-element.318) | copy-start | bytes 1572868
  14.8 31.7 %copy-start.19 = (f32[1024,128]{0,1:T(8,128)}, f32[1024,128]{0,1:T(8,128)S(1)}, u32[]{:S(2)}) copy-start(f32[1024,128]{0,1:T(8,128)S(1)} %get-tuple-element.319) | copy-start | bytes 1572868
  18.0 56.2 %copy-start.38 = (f32[1024]{0:T(1024)}, f32[1024]{0:T(1024)S(1)}, u32[]{:S(2)}) copy-start(f32[1024]{0:T(1024)S(1)} %broadcast_multiply_fusion.7) | copy-start | bytes 12292
  19.3 54.9 %copy-start.42 = (f32[1024]{0:T(1024)}, f32[1024]{0:T(1024)S(1)}, u32[]{:S(2)}) copy-start(f32[1024]{0:T(1024)S(1)} %add_rsqrt_fusion.1) | copy-start | bytes 12292
  48.1 87.9 %all-gather.27.cloned.1.call-start = ((), (), s32[]{:S(2)}) async-start(), calls=%async_computation.30 | async-start | bytes 3145728 | tf_op jit(solution)/shard_map/all_gather | solution.py:159
  79.9 91.4 %all-gather.19.cloned.1.call-start = ((), (), s32[]{:S(2)}) async-start(), calls=%async_computation.13 | async-start | bytes 2359296 | tf_op jit(solution)/shard_map/all_gather | solution.py:139
  80.7 390.2 %all-reduce.5.cloned.1.call-start = ((), (), s32[]{:S(2)}) async-start(), calls=%async_computation.14 | async-start | bytes 16777216 | tf_op jit(solution)/shard_map/psum | solution.py:169
  83.4 45.1 %copy-start.21 = (f32[2,512,128]{2,1,0:T(8,128)}, f32[2,512,128]{2,1,0:T(8,128)S(1)}, u32[]{:S(2)}) copy-start(f32[2,512,128]{2,1,0:T(8,128)S(1)} %get-tuple-element.316) | copy-start | bytes 1572868
  83.4 45.0 %copy-start.23 = (f32[2,512,128]{2,1,0:T(8,128)}, f32[2,512,128]{2,1,0:T(8,128)S(1)}, u32[]{:S(2)}) copy-start(f32[2,512,128]{2,1,0:T(8,128)S(1)} %get-tuple-element.317) | copy-start | bytes 1572868
  179.8 346.9 %all-gather.21.cloned.1.call-start = ((), (), s32[]{:S(2)}) async-start(), calls=%async_computation.15 | async-start | bytes 9437184 | tf_op jit(solution)/shard_map/all_gather | solution.py:142
  182.5 400.9 %all-gather.23.cloned.1.call-start = ((), (), s32[]{:S(2)}) async-start(), calls=%async_computation.16 | async-start | bytes 9437184 | tf_op jit(solution)/shard_map/all_gather | solution.py:143
  185.4 456.2 %all-gather.25.cloned.1.call-start = ((), (), s32[]{:S(2)}) async-start(), calls=%async_computation.17 | async-start | bytes 9437184 | tf_op jit(solution)/shard_map/all_gather | solution.py:144
  186.6 796.2 %all-reduce.9.cloned.1.call-start = ((), (), s32[]{:S(2)}) async-start(), calls=%async_computation.19 | async-start | bytes 16777216 | tf_op jit(solution)/shard_map/psum | solution.py:202
  187.3 952.3 %copy-start.44 = (f32[1024]{0:T(1024)}, f32[1024]{0:T(1024)S(1)}, u32[]{:S(2)}) copy-start(f32[1024]{0:T(1024)S(1)} %fusion.97) | copy-start | bytes 12292
  663.6 15.1 copy-start.46
  663.6 15.1 copy-start.49
  691.8 447.8 %all-reduce.7.cloned.1.call-start = ((), (), s32[]{:S(2)}) async-start(), calls=%async_computation.18 | async-start | bytes 8388608 | tf_op jit(solution)/shard_map/psum | solution.py:177
  705.6 596.5 %reduce-scatter.10.cloned.1.call-start = ((), (), s32[]{:S(2)}) async-start(), calls=%async_computation.20 | async-start | bytes 6291456 | tf_op jit(solution)/shard_map/reduce_scatter | solution.py:226
  1139.5 15.7 copy-start.48
  1288.6 26.4 %reduce-scatter.12.cloned.1.call-start = ((), (), s32[]{:S(2)}) async-start(), calls=%async_computation.21 | async-start | bytes 6291456 | tf_op jit(solution)/shard_map/reduce_scatter | solution.py:227
  1289.1 332.7 %all-reduce.11.cloned.1.call-start = ((), (), s32[]{:S(2)}) async-start(), calls=%async_computation.22 | async-start | bytes 16777216 | tf_op jit(solution)/shard_map/psum | solution.py:252
  1329.6 346.2 %reduce-scatter.14.cloned.1.call-start = ((), (), s32[]{:S(2)}) async-start(), calls=%async_computation.23 | async-start | bytes 4718592 | tf_op jit(solution)/shard_map/reduce_scatter | solution.py:247
  1338.8 391.9 %reduce-scatter.20.cloned.1.call-start = ((), (), s32[]{:S(2)}) async-start(), calls=%async_computation.26 | async-start | bytes 4718592 | tf_op jit(solution)/shard_map/reduce_scatter | solution.py:250
  1347.8 437.9 %reduce-scatter.16.cloned.1.call-start = ((), (), s32[]{:S(2)}) async-start(), calls=%async_computation.24 | async-start | bytes 4718592 | tf_op jit(solution)/shard_map/reduce_scatter | solution.py:248
  1356.0 484.8 %reduce-scatter.18.cloned.1.call-start = ((), (), s32[]{:S(2)}) async-start(), calls=%async_computation.25 | async-start | bytes 4718592 | tf_op jit(solution)/shard_map/reduce_scatter | solution.py:249
  1364.3 596.7 %reduce-scatter.22.cloned.1.call-start = ((), (), s32[]{:S(2)}) async-start(), calls=%async_computation.27 | async-start | bytes 18874368 | tf_op jit(solution)/shard_map/reduce_scatter | solution.py:198
  1379.7 701.7 %reduce-scatter.24.cloned.1.call-start = ((), (), s32[]{:S(2)}) async-start(), calls=%async_computation.28 | async-start | bytes 18874368 | tf_op jit(solution)/shard_map/reduce_scatter | solution.py:199
  1395.0 806.6 %reduce-scatter.26.cloned.1.call-start = ((), (), s32[]{:S(2)}) async-start(), calls=%async_computation.29 | async-start | bytes 18874368 | tf_op jit(solution)/shard_map/reduce_scatter | solution.py:200
  (46 other events, 186.7 us)
Sparse Core Ops, SparseCore 0:
  10.4 30.4 all-gather.12
  43.4 27.7 all-gather.16
  73.7 27.7 all-gather.10
  102.9 10.5 all-gather.14
  114.9 11.7 all-gather.26
  128.4 29.3 all-gather.18
  179.9 290.9 all-reduce.4
  473.4 53.2 all-gather.20
  529.1 54.2 all-gather.22
  585.7 55.8 all-gather.24
  691.9 290.8 all-reduce.8
  985.5 153.9 all-reduce.6
  1288.7 10.8 reduce-scatter.9
  1301.7 13.1 reduce-scatter.11
  1329.7 292.0 all-reduce.10
  1625.6 50.1 reduce-scatter.13
  1679.6 51.0 reduce-scatter.19
  1734.5 51.1 reduce-scatter.15
  1789.6 51.1 reduce-scatter.17
  1844.8 116.1 reduce-scatter.21
  1965.1 116.1 reduce-scatter.23
  2085.5 115.9 reduce-scatter.25
where the time goes:
time: 2220 us; the launch traced here: 2210 us
  waiting for transfers between devices  1680 us (76%)
  matrix products  326 us (15%)
  other arithmetic  127 us (6%)
  local copies, waits for them, and re-layouts  55.2 us (2%)
    psum x1, waiting for transfers between devices, body(): resid = tokens_wide + lax.psum(branch_part, 'tp')  284 us
    psum x1, waiting for transfers between devices, body(): grad_input_two = lax.psum(grad_input_two, 'tp')  277 us
    psum x1, waiting for transfers between devices, body(): grad_input_one = lax.psum(grad_input_one, 'tp')  211 us
    psum x1, waiting for transfers between devices, body(): lax.psum(branch_two_part.astype(jnp.bfloat16), 'tp').astype(jnp.float32)  150 us
    reduce_scatter x1, waiting for transfers between devices, body(): lax.psum_scatter(grad_up, ('shard', 'ctx'), scatter_dimension=0, tiled=True)  120 us
    reduce_scatter x1, waiting for transfers between devices, body(): lax.psum_scatter(grad_gate, ('shard', 'ctx'), scatter_dimension=0, tiled=...  120 us
    reduce_scatter x1, waiting for transfers between devices, body(): lax.psum_scatter(grad_down, ('shard', 'ctx'), scatter_dimension=1, tiled=...  120 us
    dot_general x7, matrix products, matmul_low(): return jnp.dot(left, right, preferred_element_type=jnp.float32)  68.5 us
  transfers between devices with their start and end apart: 22, of which 18 were waited for; matrix products, arithmetic and copies ran while one was open for 12% of the time, Pallas kernels for 0%

commit v1 on v0

--- a/solution.py
+++ b/solution.py
@@ -110,6 +110,13 @@
         one_block, (empty, empty), (grouped, grad_grouped, log_totals, jnp.arange(block_count))
     )
     return (grad_queries.reshape(half_len, head_count, head_size), sums[0], sums[1])
+
+
+def scatter_low(grad, dim):
+    summed = lax.psum_scatter(
+        grad.astype(jnp.bfloat16), ("shard", "ctx"), scatter_dimension=dim, tiled=True
+    )
+    return summed.astype(jnp.float32)
 
 
 def matmul_low(left, right):
@@ -166,7 +173,7 @@
     log_list = [log_totals]
     attn_out = jnp.stack(attended_list).reshape(row_total, head_cols)
     branch_part = matmul_low(attn_out, output_full)
-    resid = tokens_wide + lax.psum(branch_part, "tp")
+    resid = tokens_wide + lax.psum(branch_part.astype(bf_type), "tp").astype(jnp.float32)
     normed_two, scale_two = normalize(resid)
     input_two = normed_two.astype(bf_type)
     gate_proj = matmul_low(input_two, gate_full)
@@ -195,11 +202,11 @@
         "rf,df->rd", grad_gate_act, gate_full, preferred_element_type=jnp.float32
     ) + jnp.einsum("rf,df->rd", grad_up_act, up_full, preferred_element_type=jnp.float32)
     mlp_grads = (
-        lax.psum_scatter(grad_gate, ("shard", "ctx"), scatter_dimension=0, tiled=True),
-        lax.psum_scatter(grad_up, ("shard", "ctx"), scatter_dimension=0, tiled=True),
-        lax.psum_scatter(grad_down, ("shard", "ctx"), scatter_dimension=1, tiled=True),
-    )
-    grad_input_two = lax.psum(grad_input_two, "tp")
+        scatter_low(grad_gate, 0),
+        scatter_low(grad_up, 0),
+        scatter_low(grad_down, 1),
+    )
+    grad_input_two = lax.psum(grad_input_two.astype(bf_type), "tp").astype(jnp.float32)
     grad_resid = grad_final + norm_back(normed_two, scale_two, grad_input_two)
     grad_resid_low = grad_resid.astype(bf_type)
     grad_wout = jnp.einsum(
@@ -244,12 +251,12 @@
         + jnp.einsum("rc,dc->rd", grad_v_pre, value_full, preferred_element_type=jnp.float32)
     )
     attn_grads = (
-        lax.psum_scatter(grad_wq, ("shard", "ctx"), scatter_dimension=0, tiled=True),
-        lax.psum_scatter(grad_wk, ("shard", "ctx"), scatter_dimension=0, tiled=True),
-        lax.psum_scatter(grad_wv, ("shard", "ctx"), scatter_dimension=0, tiled=True),
-        lax.psum_scatter(grad_wout, ("shard", "ctx"), scatter_dimension=1, tiled=True),
-    )
-    grad_input_one = lax.psum(grad_input_one, "tp")
+        scatter_low(grad_wq, 0),
+        scatter_low(grad_wk, 0),
+        scatter_low(grad_wv, 0),
+        scatter_low(grad_wout, 1),
+    )
+    grad_input_one = lax.psum(grad_input_one.astype(bf_type), "tp").astype(jnp.float32)
     grad_tokens = grad_resid + norm_back(normed_one, scale_one, grad_input_one)
     output = final_sum.astype(bf_type).reshape(seq_count, half_len, model_width)
     grad_tokens = grad_tokens.reshape(seq_count, half_len, model_width)

time: 2220 us -> 1610 us (0.73)
  waiting for transfers between devices: 1680 us -> 1090 us
  matrix products: 326 us -> 300 us
    psum x3 -> x2, waiting for transfers between devices: 771 us -> 301 us  [the longest x1 155 us: body(): lax.psum(grad_input_two.astype(bf_type), 'tp').astype(jnp.float32)]
    reduce_scatter x7, waiting for transfers between devices: 564 us -> 305 us  [scatter_low(): lax.psum_scatter(grad.astype(jnp.bfloat16), ('shard', 'ctx'), scatter_dim...]
    psum x1, waiting for transfers between devices: 150 us -> 292 us  [body(): lax.psum(branch_two_part.astype(jnp.bfloat16), 'tp').astype(jnp.float32)]
  transfers between devices with their start and end apart: 22 -> 21, of which waited for: 18 -> 15; matrix products, arithmetic and copies ran while one was open for 12% -> 16% of each run, Pallas kernels for 0% -> 0%
where the time goes in v1:
time: 1610 us; the launch traced here: 1600 us
  waiting for transfers between devices  1090 us (68%)
  matrix products  300 us (19%)
  other arithmetic  144 us (9%)
  local copies, waits for them, and re-layouts  49.2 us (3%)
    reduce_scatter x7, waiting for transfers between devices, scatter_low(): lax.psum_scatter(grad.astype(jnp.bfloat16), ('shard', 'ctx'), scatter_dim...  305 us
    psum x1, waiting for transfers between devices, body(): lax.psum(branch_two_part.astype(jnp.bfloat16), 'tp').astype(jnp.float32)  292 us
    psum x1, waiting for transfers between devices, body(): lax.psum(grad_input_two.astype(bf_type), 'tp').astype(jnp.float32)  155 us
    psum x1, waiting for transfers between devices, body(): lax.psum(branch_part.astype(bf_type), 'tp').astype(jnp.float32)  146 us
    dot_general x7, matrix products, matmul_low(): return jnp.dot(left, right, preferred_element_type=jnp.float32)  67.1 us
    all_gather x1, waiting for transfers between devices, body(): lax.all_gather(mlp_low[0], ('shard', 'ctx'), axis=0, tiled=True)  44 us
    all_gather x1, waiting for transfers between devices, body(): lax.all_gather(mlp_low[2], ('shard', 'ctx'), axis=1, tiled=True)  43.6 us
    all_gather x1, waiting for transfers between devices, body(): lax.all_gather(mlp_low[1], ('shard', 'ctx'), axis=0, tiled=True)  42.3 us
  transfers between devices with their start and end apart: 21, of which 15 were waited for; matrix products, arithmetic and copies ran while one was open for 16% of the time, Pallas kernels for 0%

profile of v1, /device:TPU:0, one launch (start us, length us, event | category | flops | bytes accessed | tf_op | source)
XLA Modules:
  0.0 1603.6 jit_solution(9619642317359347338)
XLA Ops:
  21.9 19.1 %all-gather.13.cloned.1.call-done = bf16[2048,512]{1,0:T(8,128)(2,1)} async-done(((bf16[256,512]{1,0:T(8,128)(2,1)}), bf16[2048,512]{1,0:T(8,128)(2,1)}) %all-gather.13.cloned.1.call-update) | async-done | bytes 2097168 | tf_op jit(solution)/shard_map/all_gather | solution.py:144
  48.2 23.1 %all-gather.17.cloned.1.call-done = bf16[2048,512]{1,0:T(8,128)(2,1)} async-done(((bf16[256,512]{1,0:T(8,128)(2,1)}), bf16[2048,512]{1,0:T(8,128)(2,1)}) %all-gather.17.cloned.1.call-update) | async-done | bytes 2097168 | tf_op jit(solution)/shard_map/all_gather | solution.py:145
  84.0 17.6 %all-gather.11.cloned.1.call-done = bf16[2048,512]{1,0:T(8,128)(2,1)} async-done(((bf16[256,512]{1,0:T(8,128)(2,1)}), bf16[2048,512]{1,0:T(8,128)(2,1)}) %all-gather.11.cloned.1.call-update) | async-done | bytes 2097168 | tf_op jit(solution)/shard_map/all_gather | solution.py:143
  131.7 35.0 %while.27 = (s32[]{:T(128)}, bf16[2,512,4,128]{3,2,1,0:T(4,128)(2,1)}, f32[2,4,512]{2,1,0:T(4,128)S(1)}, s32[2]{0:T(128)S(1)}, s32[]{:T(128)}, /*index=5*/s32[]{...) while((s32[]{:T(128)}, ...), condition=%wide.region_5.6_spmd, body=%wide.region_2.5_spmd.sunk | while | flops 2195980800 | bytes 77668600 | solution.py:73
  182.4 146.1 %all-reduce.5.cloned.1.call-done = bf16[1024,2048]{1,0:T(8,128)(2,1)} async-done(((bf16[1024,2048]{1,0:T(8,128)(2,1)}), bf16[1024,2048]{1,0:T(8,128)(2,1)}) %all-reduce.5.cloned.1.call-update) | async-done | bytes 4194320 | tf_op jit(solution)/shard_map/psum | solution.py:176
  340.2 44.0 %all-gather.21.cloned.1.call-done = bf16[2048,2048]{1,0:T(8,128)(2,1)} async-done(((bf16[256,2048]{1,0:T(8,128)(2,1)}), bf16[2048,2048]{1,0:T(8,128)(2,1)}) %all-gather.21.cloned.1.call-update) | async-done | bytes 8388624 | tf_op jit(solution)/shard_map/all_gather | solution.py:149
  384.2 14.5 fusion.113
  398.7 42.3 %all-gather.23.cloned.1.call-done = bf16[2048,2048]{1,0:T(8,128)(2,1)} async-done(((bf16[256,2048]{1,0:T(8,128)(2,1)}), bf16[2048,2048]{1,0:T(8,128)(2,1)}) %all-gather.23.cloned.1.call-update) | async-done | bytes 8388624 | tf_op jit(solution)/shard_map/all_gather | solution.py:150
  440.9 14.6 fusion.114
  455.5 43.6 %all-gather.25.cloned.1.call-done = bf16[2048,2048]{1,0:T(8,128)(2,1)} async-done(((bf16[2048,256]{1,0:T(8,128)(2,1)}), bf16[2048,2048]{1,0:T(8,128)(2,1)}) %all-gather.25.cloned.1.call-update) | async-done | bytes 8388624 | tf_op jit(solution)/shard_map/all_gather | solution.py:151
  499.1 22.0 %multiply_convert_fusion.1 = (bf16[1024,2048]{1,0:T(8,128)(2,1)}, bf16[1024,2048]{1,0:T(8,128)(2,1)}, bf16[1024,2048]{1,0:T(8,128)(2,1)}) fusion(f32[1024,2048]{1,0:T(8,128)} %fusion.113, f32[1024,2048]{1,0:T(8,128)} %fusion.114, bf16[2048,2048]{1,0:T(8,128)(2,1)} %all-gather.25.cloned.1.call-done, bf16[1,1024,2048]{2,1,0:T(8,128)(2,1)} %param.16, ...), kind=kOutput, calls=%fused_computation.80 | convolution fusion | flops 8629780480 | bytes 41947136 | tf_op jit(solution)/shard_map/rd,fd->rf/dot_general | solution.py:190
  521.1 14.7 fusion.115
  535.8 12.2 add_convert_fusion.1
  548.1 155.1 %all-reduce.7.cloned.1.call-done = bf16[1024,2048]{1,0:T(8,128)(2,1)} async-done(((bf16[1024,2048]{1,0:T(8,128)(2,1)}), bf16[1024,2048]{1,0:T(8,128)(2,1)}) %all-reduce.7.cloned.1.call-update) | async-done | bytes 4194320 | tf_op jit(solution)/shard_map/psum | solution.py:209
  726.5 128.1 %while.28 = (s32[]{:T(128)}, f32[2048,4,128]{0,2,1:T(8,128)}, f32[2048,4,128]{0,2,1:T(8,128)}, f32[2,512,4,128]{3,1,2,0:T(8,128)}, bf16[2,512,4,128]{3,1,2,0:T(8...) while((s32[]{:T(128)}, f32[2048,4,128]{0,2,1:T(8,128)}, ...), condition=%wide.region_15.16_spmd.clone, body=%wide.region_13.15_spmd.clone.sunk | while | flops 5439226368 | bytes 211878384 | solution.py:109
  739.1 13.1 multiply_reduce_fusion.3
  752.2 14.9 multiply_convert_fusion.5
  774.5 11.2 bitcast_add_fusion.5
  801.6 13.2 multiply_reduce_fusion.3
  814.8 14.9 multiply_convert_fusion.5
  838.3 12.4 bitcast_add_fusion.5
  873.0 15.0 convolution_convert_fusion.2
  888.1 14.0 convolution_convert_fusion.1
  902.8 14.6 convolution_convert_fusion
  937.5 14.4 convolution_convert_fusion.3
  973.9 73.1 %reduce-scatter.22.cloned.1.call-done = bf16[256,2048]{1,0:T(8,128)(2,1)} async-done(((bf16[2048,2048]{1,0:T(8,128)(2,1)}), bf16[256,2048]{1,0:T(8,128)(2,1)}) %reduce-scatter.22.cloned.1.call-update) | async-done | bytes 1048592 | tf_op jit(solution)/shard_map/reduce_scatter | solution.py:116
  1049.8 72.1 %reduce-scatter.24.cloned.1.call-done = bf16[256,2048]{1,0:T(8,128)(2,1)} async-done(((bf16[2048,2048]{1,0:T(8,128)(2,1)}), bf16[256,2048]{1,0:T(8,128)(2,1)}) %reduce-scatter.24.cloned.1.call-update) | async-done | bytes 1048592 | tf_op jit(solution)/shard_map/reduce_scatter | solution.py:116
  1124.7 71.9 %reduce-scatter.26.cloned.1.call-done = bf16[2048,256]{1,0:T(8,128)(2,1)} async-done(((bf16[2048,2048]{1,0:T(8,128)(2,1)}), bf16[2048,256]{1,0:T(8,128)(2,1)}) %reduce-scatter.26.cloned.1.call-update) | async-done | bytes 1048592 | tf_op jit(solution)/shard_map/reduce_scatter | solution.py:116
  1199.2 41.7 %reduce-scatter.16.cloned.1.call-done = bf16[256,512]{1,0:T(8,128)(2,1)} async-done(((bf16[2048,512]{1,0:T(8,128)(2,1)}), bf16[256,512]{1,0:T(8,128)(2,1)}) %reduce-scatter.16.cloned.1.call-update) | async-done | bytes 262160 | tf_op jit(solution)/shard_map/reduce_scatter | solution.py:116
  1242.8 42.5 %reduce-scatter.18.cloned.1.call-done = bf16[256,512]{1,0:T(8,128)(2,1)} async-done(((bf16[2048,512]{1,0:T(8,128)(2,1)}), bf16[256,512]{1,0:T(8,128)(2,1)}) %reduce-scatter.18.cloned.1.call-update) | async-done | bytes 262160 | tf_op jit(solution)/shard_map/reduce_scatter | solution.py:116
  1287.0 292.3 %all-reduce.9.cloned.1.call-done = (bf16[1024,2048]{1,0:T(8,128)(2,1)}, bf16[1024,2048]{1,0:T(8,128)(2,1)}) async-done(((bf16[1024,2048]{1,0:T(8,128)(2,1)}, bf16[1024,2048]{1,0:T(8,128)(2,1)}), (bf16[1024,2048]{1,0:T(8,128)(2,1)}, bf16[1024,2048]{1,0:T(8,128)(2,1)})) %all-reduce.9.cloned.1.call-update) | async-done | bytes 8388624 | tf_op jit(solution)/shard_map/psum | solution.py:184
  1586.0 10.5 fusion.40
  (297 shorter events, 273.5 us)
Async XLA Ops:
  7.2 33.8 %all-gather.13.cloned.1.call-start = ((), (), s32[]{:S(2)}) async-start(), calls=%async_computation.10 | async-start | bytes 2359296 | tf_op jit(solution)/shard_map/all_gather | solution.py:144
  9.0 62.2 %all-gather.17.cloned.1.call-start = ((), (), s32[]{:S(2)}) async-start(), calls=%async_computation.12 | async-start | bytes 2359296 | tf_op jit(solution)/shard_map/all_gather | solution.py:145
  10.9 90.7 %all-gather.11.cloned.1.call-start = ((), (), s32[]{:S(2)}) async-start(), calls=%async_computation.9 | async-start | bytes 2359296 | tf_op jit(solution)/shard_map/all_gather | solution.py:143
  12.7 115.8 %all-gather.15.cloned.1.call-start = ((), (), s32[]{:S(2)}) async-start(), calls=%async_computation.11 | async-start | bytes 3145728 | tf_op jit(solution)/shard_map/all_gather | solution.py:165
  14.8 31.7 %copy-start.23 = (f32[1024,128]{0,1:T(8,128)}, f32[1024,128]{0,1:T(8,128)S(1)}, u32[]{:S(2)}) copy-start(f32[1024,128]{0,1:T(8,128)S(1)} %get-tuple-element.318) | copy-start | bytes 1572868
  14.8 31.7 %copy-start.25 = (f32[1024,128]{0,1:T(8,128)}, f32[1024,128]{0,1:T(8,128)S(1)}, u32[]{:S(2)}) copy-start(f32[1024,128]{0,1:T(8,128)S(1)} %get-tuple-element.319) | copy-start | bytes 1572868
  18.0 56.2 %copy-start.38 = (f32[1024]{0:T(1024)}, f32[1024]{0:T(1024)S(1)}, u32[]{:S(2)}) copy-start(f32[1024]{0:T(1024)S(1)} %broadcast_multiply_fusion.7) | copy-start | bytes 12292
  19.3 54.9 %copy-start.42 = (f32[1024]{0:T(1024)}, f32[1024]{0:T(1024)S(1)}, u32[]{:S(2)}) copy-start(f32[1024]{0:T(1024)S(1)} %add_rsqrt_fusion.1) | copy-start | bytes 12292
  48.1 83.5 %all-gather.27.cloned.1.call-start = ((), (), s32[]{:S(2)}) async-start(), calls=%async_computation.28 | async-start | bytes 3145728 | tf_op jit(solution)/shard_map/all_gather | solution.py:166
  79.8 86.8 %all-gather.19.cloned.1.call-start = ((), (), s32[]{:S(2)}) async-start(), calls=%async_computation.13 | async-start | bytes 2359296 | tf_op jit(solution)/shard_map/all_gather | solution.py:146
  80.6 247.8 %all-reduce.5.cloned.1.call-start = ((), (), s32[]{:S(2)}) async-start(), calls=%async_computation.14 | async-start | bytes 8388608 | tf_op jit(solution)/shard_map/psum | solution.py:176
  173.0 211.2 %all-gather.21.cloned.1.call-start = ((), (), s32[]{:S(2)}) async-start(), calls=%async_computation.15 | async-start | bytes 9437184 | tf_op jit(solution)/shard_map/all_gather | solution.py:149
  175.8 265.2 %all-gather.23.cloned.1.call-start = ((), (), s32[]{:S(2)}) async-start(), calls=%async_computation.16 | async-start | bytes 9437184 | tf_op jit(solution)/shard_map/all_gather | solution.py:150
  178.6 320.6 %all-gather.25.cloned.1.call-start = ((), (), s32[]{:S(2)}) async-start(), calls=%async_computation.17 | async-start | bytes 9437184 | tf_op jit(solution)/shard_map/all_gather | solution.py:151
  181.7 521.5 %all-reduce.7.cloned.1.call-start = ((), (), s32[]{:S(2)}) async-start(), calls=%async_computation.18 | async-start | bytes 8388608 | tf_op jit(solution)/shard_map/psum | solution.py:209
  182.4 529.1 %copy-start.44 = (f32[1024]{0:T(1024)}, f32[1024]{0:T(1024)S(1)}, u32[]{:S(2)}) copy-start(f32[1024]{0:T(1024)S(1)} %fusion.106) | copy-start | bytes 12292
  521.1 14.7 copy-start.46
  521.1 14.7 copy-start.49
  548.0 369.4 %reduce-scatter.10.cloned.1.call-start = ((), (), s32[]{:S(2)}) async-start(), calls=%async_computation.19 | async-start | bytes 6291456 | tf_op jit(solution)/shard_map/reduce_scatter | solution.py:233
  739.1 13.2 copy-start.12
  767.1 18.7 %slice-start = ((s8[8388608]{0:T(1024)(128)(4,1)}), s8[4194304]{0:T(1024)(128)(4,1)S(1)}, s32[]{:S(2)}) async-start(s8[8388608]{0:T(1024)(128)(4,1)} %bitcast.246), calls=%async_computation.30 | async-start | bytes 8388608 | tf_op jit(solution)/shard_map/while
  801.6 13.2 copy-start.12
  829.7 21.1 %slice-start = ((s8[8388608]{0:T(1024)(128)(4,1)}), s8[4194304]{0:T(1024)(128)(4,1)S(1)}, s32[]{:S(2)}) async-start(s8[8388608]{0:T(1024)(128)(4,1)} %bitcast.246), calls=%async_computation.30 | async-start | bytes 8388608 | tf_op jit(solution)/shard_map/while
  854.6 73.5 %reduce-scatter.12.cloned.1.call-start = ((), (), s32[]{:S(2)}) async-start(), calls=%async_computation.20 | async-start | bytes 6291456 | tf_op jit(solution)/shard_map/reduce_scatter | solution.py:234
  855.4 111.0 %reduce-scatter.14.cloned.1.call-start = ((), (), s32[]{:S(2)}) async-start(), calls=%async_computation.21 | async-start | bytes 2359296 | tf_op jit(solution)/shard_map/reduce_scatter | solution.py:116
  865.8 106.3 %reduce-scatter.20.cloned.1.call-start = ((), (), s32[]{:S(2)}) async-start(), calls=%async_computation.24 | async-start | bytes 2359296 | tf_op jit(solution)/shard_map/reduce_scatter | solution.py:116
  873.0 174.0 %reduce-scatter.22.cloned.1.call-start = ((), (), s32[]{:S(2)}) async-start(), calls=%async_computation.25 | async-start | bytes 9437184 | tf_op jit(solution)/shard_map/reduce_scatter | solution.py:116
  888.0 233.9 %reduce-scatter.24.cloned.1.call-start = ((), (), s32[]{:S(2)}) async-start(), calls=%async_computation.26 | async-start | bytes 9437184 | tf_op jit(solution)/shard_map/reduce_scatter | solution.py:116
  902.1 294.4 %reduce-scatter.26.cloned.1.call-start = ((), (), s32[]{:S(2)}) async-start(), calls=%async_computation.27 | async-start | bytes 9437184 | tf_op jit(solution)/shard_map/reduce_scatter | solution.py:116
  917.4 323.6 %reduce-scatter.16.cloned.1.call-start = ((), (), s32[]{:S(2)}) async-start(), calls=%async_computation.22 | async-start | bytes 2359296 | tf_op jit(solution)/shard_map/reduce_scatter | solution.py:116
  926.4 358.8 %reduce-scatter.18.cloned.1.call-start = ((), (), s32[]{:S(2)}) async-start(), calls=%async_computation.23 | async-start | bytes 2359296 | tf_op jit(solution)/shard_map/reduce_scatter | solution.py:116
  937.5 641.8 %all-reduce.9.cloned.1.call-start = ((), (), s32[]{:S(2)}) async-start(), calls=%async_computation.29 | async-start | bytes 16777216 | tf_op jit(solution)/shard_map/psum | solution.py:184
  (52 other events, 241.2 us)
Sparse Core Ops, SparseCore 0:
  10.4 30.4 all-gather.12
  43.4 27.7 all-gather.16
  73.7 27.7 all-gather.10
  103.5 10.5 all-gather.14
  115.5 11.7 all-gather.26
  129.0 29.2 all-gather.18
  173.1 155.3 all-reduce.4
  330.9 53.2 all-gather.20
  386.7 54.2 all-gather.22
  443.2 55.8 all-gather.24
  548.2 154.9 all-reduce.6
  854.7 10.8 reduce-scatter.9
  867.9 13.1 reduce-scatter.11
  884.9 42.3 reduce-scatter.13
  931.0 41.0 reduce-scatter.19
  975.4 71.5 reduce-scatter.21
  1050.3 71.5 reduce-scatter.23
  1125.2 71.2 reduce-scatter.25
  1199.8 41.1 reduce-scatter.15
  1244.1 41.1 reduce-scatter.17
  1288.4 290.8 all-reduce.8

commit v2 on v1

--- a/solution.py
+++ b/solution.py
@@ -1,3 +1,5 @@
+import functools
+
 import jax
 import jax.numpy as jnp
 from jax import lax
@@ -112,6 +114,28 @@
     return (grad_queries.reshape(half_len, head_count, head_size), sums[0], sums[1])
 
 
+def tp_psum(part, count):
+    me = lax.axis_index("tp")
+    low_part = part.astype(jnp.bfloat16)
+    rows = part.shape[0] // count
+    chunks = low_part.reshape((count, rows) + part.shape[1:])
+    total = lax.dynamic_index_in_dim(chunks, me, 0, keepdims=False).astype(jnp.float32)
+    for shift in range(1, count):
+        pairs = [(i, (i + shift) % count) for i in range(count)]
+        piece = lax.dynamic_index_in_dim(chunks, (me + shift) % count, 0, keepdims=False)
+        total = total + lax.ppermute(piece, "tp", pairs).astype(jnp.float32)
+    reduced = total.astype(jnp.bfloat16)
+    gathered = jnp.zeros(low_part.shape, jnp.bfloat16)
+    gathered = lax.dynamic_update_slice_in_dim(gathered, reduced, me * rows, 0)
+    for shift in range(1, count):
+        pairs = [(i, (i + shift) % count) for i in range(count)]
+        got = lax.ppermute(reduced, "tp", pairs)
+        gathered = lax.dynamic_update_slice_in_dim(
+            gathered, got, ((me + count - shift) % count) * rows, 0
+        )
+    return gathered
+
+
 def scatter_low(grad, dim):
     summed = lax.psum_scatter(
         grad.astype(jnp.bfloat16), ("shard", "ctx"), scatter_dimension=dim, tiled=True
@@ -123,7 +147,7 @@
     return jnp.dot(left, right, preferred_element_type=jnp.float32)
 
 
-def body(tokens, lengths, cotangent, w_query, w_key, w_value, w_output, w_gate, w_up, w_down):
+def body(tp_count, tokens, lengths, cotangent, w_query, w_key, w_value, w_output, w_gate, w_up, w_down):
     seq_count, half_len, model_width = tokens.shape
     head_cols = w_query.shape[1]
     head_count = head_cols // HEAD_DIM
@@ -173,7 +197,7 @@
     log_list = [log_totals]
     attn_out = jnp.stack(attended_list).reshape(row_total, head_cols)
     branch_part = matmul_low(attn_out, output_full)
-    resid = tokens_wide + lax.psum(branch_part.astype(bf_type), "tp").astype(jnp.float32)
+    resid = tokens_wide + tp_psum(branch_part, tp_count).astype(jnp.float32)
     normed_two, scale_two = normalize(resid)
     input_two = normed_two.astype(bf_type)
     gate_proj = matmul_low(input_two, gate_full)
@@ -181,7 +205,7 @@
     gate_sigmoid = jax.nn.sigmoid(gate_proj)
     hidden = (gate_proj * gate_sigmoid * up_proj).astype(bf_type)
     branch_two_part = matmul_low(hidden, down_full)
-    final_sum = resid + lax.psum(branch_two_part.astype(jnp.bfloat16), "tp").astype(jnp.float32)
+    final_sum = resid + tp_psum(branch_two_part, tp_count).astype(jnp.float32)
     grad_final = cotangent.astype(jnp.float32).reshape(row_total, model_width) * valid_mask.reshape(
         row_total, 1
     )
@@ -206,7 +230,7 @@
         scatter_low(grad_up, 0),
         scatter_low(grad_down, 1),
     )
-    grad_input_two = lax.psum(grad_input_two.astype(bf_type), "tp").astype(jnp.float32)
+    grad_input_two = tp_psum(grad_input_two, tp_count).astype(jnp.float32)
     grad_resid = grad_final + norm_back(normed_two, scale_two, grad_input_two)
     grad_resid_low = grad_resid.astype(bf_type)
     grad_wout = jnp.einsum(
@@ -256,7 +280,7 @@
         scatter_low(grad_wv, 0),
         scatter_low(grad_wout, 1),
     )
-    grad_input_one = lax.psum(grad_input_one.astype(bf_type), "tp").astype(jnp.float32)
+    grad_input_one = tp_psum(grad_input_one, tp_count).astype(jnp.float32)
     grad_tokens = grad_resid + norm_back(normed_one, scale_one, grad_input_one)
     output = final_sum.astype(bf_type).reshape(seq_count, half_len, model_width)
     grad_tokens = grad_tokens.reshape(seq_count, half_len, model_width)
@@ -275,7 +299,7 @@
 
 def solution(mesh):
     return jax.shard_map(
-        body,
+        functools.partial(body, mesh.shape["tp"]),
         mesh=mesh,
         in_specs=(
             P("shard", "ctx", None),

time: 1610 us -> 1420 us (0.88)
  waiting for transfers between devices: 1090 us -> 653 us
  starting transfers between devices: 1.55 us -> 211 us
  local copies, waits for them, and re-layouts: 49.2 us -> 74 us
    psum x3 -> x0, waiting for transfers between devices: 593 us -> none  [the longest x1 292 us: body(): lax.psum(branch_two_part.astype(jnp.bfloat16), 'tp').astype(jnp.float32)]
    ppermute x0 -> x24, waiting for transfers between devices: none -> 405 us  [the longest x12 244 us: tp_psum(): total = total + lax.ppermute(piece, 'tp', pairs).astype(jnp.float32)]
    ppermute x0 -> x24, starting transfers between devices: none -> 209 us  [the longest x12 148 us: tp_psum(): got = lax.ppermute(reduced, 'tp', pairs)]
    reduce_scatter x7, waiting for transfers between devices: 305 us -> 194 us  [scatter_low(): lax.psum_scatter(grad.astype(jnp.bfloat16), ('shard', 'ctx'), scatter_dim...]
    all_gather x1, waiting for transfers between devices: 44 us -> 0.01 us  [body(): lax.all_gather(mlp_low[0], ('shard', 'ctx'), axis=0, tiled=True)]
    all_gather x1, waiting for transfers between devices: 43.6 us -> 0.01 us  [body(): lax.all_gather(mlp_low[2], ('shard', 'ctx'), axis=1, tiled=True)]
    all_gather x1, waiting for transfers between devices: 42.3 us -> 0.01 us  [body(): lax.all_gather(mlp_low[1], ('shard', 'ctx'), axis=0, tiled=True)]
  transfers between devices with their start and end apart: 21 -> 42, of which waited for: 15 -> 19; matrix products, arithmetic and copies ran while one was open for 16% -> 23% of each run, Pallas kernels for 0% -> 0%
where the time goes in v2:
time: 1420 us; the launch traced here: 1410 us
  waiting for transfers between devices  653 us (46%)
  matrix products  307 us (22%)
  starting transfers between devices  211 us (15%)
  other arithmetic  150 us (11%)
  local copies, waits for them, and re-layouts  74 us (5%)
  between operations  16.1 us (1%)
    ppermute x12, waiting for transfers between devices, tp_psum(): total = total + lax.ppermute(piece, 'tp', pairs).astype(jnp.float32)  244 us
    reduce_scatter x7, waiting for transfers between devices, scatter_low(): lax.psum_scatter(grad.astype(jnp.bfloat16), ('shard', 'ctx'), scatter_dim...  194 us
    ppermute x12, waiting for transfers between devices, tp_psum(): got = lax.ppermute(reduced, 'tp', pairs)  161 us
    ppermute x12, starting transfers between devices, tp_psum(): got = lax.ppermute(reduced, 'tp', pairs)  148 us
    dot_general x7, matrix products, matmul_low(): return jnp.dot(left, right, preferred_element_type=jnp.float32)  68.9 us
    ppermute x12, starting transfers between devices, tp_psum(): total = total + lax.ppermute(piece, 'tp', pairs).astype(jnp.float32)  61.9 us
    convert_element_type x2, other arithmetic, one_block(): grad_scores = (probability * (grad_prob - inner_sum)).astype(jnp.bfloat16)  29.7 us
  transfers between devices with their start and end apart: 42, of which 19 were waited for; matrix products, arithmetic and copies ran while one was open for 23% of the time, Pallas kernels for 0%

profile of v2, /device:TPU:0, one launch (start us, length us, event | category | flops | bytes accessed | tf_op | source)
XLA Modules:
  0.0 1414.6 jit_solution(14012262534603150184)
XLA Ops:
  21.9 19.1 %all-gather.13.cloned.1.call-done = bf16[2048,512]{1,0:T(8,128)(2,1)} async-done(((bf16[256,512]{1,0:T(8,128)(2,1)}), bf16[2048,512]{1,0:T(8,128)(2,1)}) %all-gather.13.cloned.1.call-update) | async-done | bytes 2097168 | tf_op jit(solution)/shard_map/all_gather | solution.py:168
  48.2 23.0 %all-gather.17.cloned.1.call-done = bf16[2048,512]{1,0:T(8,128)(2,1)} async-done(((bf16[256,512]{1,0:T(8,128)(2,1)}), bf16[2048,512]{1,0:T(8,128)(2,1)}) %all-gather.17.cloned.1.call-update) | async-done | bytes 2097168 | tf_op jit(solution)/shard_map/all_gather | solution.py:169
  136.1 34.9 %while.27 = (s32[]{:T(128)}, bf16[2,512,4,128]{3,2,1,0:T(4,128)(2,1)S(1)}, f32[2,4,512]{2,1,0:T(4,128)S(1)}, s32[2]{0:T(128)S(1)}, s32[]{:T(128)}, /*index=5*/s3...) while((s32[]{:T(128)}, ...), condition=%wide.region_5.6_spmd, body=%wide.region_2.5_spmd.sunk | while | flops 2195980800 | bytes 69280448 | solution.py:75
  185.3 22.7 %collective-permute-done = bf16[256,2048]{1,0:T(8,128)(2,1)S(1)} collective-permute-done((bf16[256,2048]{1,0:T(8,128)(2,1)}, bf16[256,2048]{1,0:T(8,128)(2,1)S(1)}, u32[]{:S(2)}, u32[]{:S(2)}) %collective-permute-start) | collective-permute-done | bytes 1048608 | tf_op jit(solution)/shard_map/ppermute | solution.py:126
  208.0 44.3 %collective-permute-done.1 = bf16[256,2048]{1,0:T(8,128)(2,1)S(1)} collective-permute-done((bf16[256,2048]{1,0:T(8,128)(2,1)}, bf16[256,2048]{1,0:T(8,128)(2,1)S(1)}, u32[]{:S(2)}, u32[]{:S(2)}) %collective-permute-start.1) | collective-permute-done | bytes 1048608 | tf_op jit(solution)/shard_map/ppermute | solution.py:126
  258.4 23.0 %collective-permute-start.3 = (bf16[256,2048]{1,0:T(8,128)(2,1)}, bf16[256,2048]{1,0:T(8,128)(2,1)S(1)}, u32[]{:S(2)}, u32[]{:S(2)}) collective-permute-start(bf16[256,2048]{1,0:T(8,128)(2,1)} %get-tuple-element.304), channel_id=1, source_target_pairs={{0,1},{1,2},{2,3},{3,0},{4,5},{5,6},{6,7},{7,4},{8,9},{9,10},{10,1... | collective-permute-start | bytes 3145736 | tf_op jit(solution)/shard_map/ppermute | solution.py:132
  284.5 22.2 %collective-permute-done.3 = bf16[256,2048]{1,0:T(8,128)(2,1)S(1)} collective-permute-done((bf16[256,2048]{1,0:T(8,128)(2,1)}, bf16[256,2048]{1,0:T(8,128)(2,1)S(1)}, u32[]{:S(2)}, u32[]{:S(2)}) %collective-permute-start.3) | collective-permute-done | bytes 1048608 | tf_op jit(solution)/shard_map/ppermute | solution.py:132
  307.8 42.5 %collective-permute-done.4 = bf16[256,2048]{1,0:T(8,128)(2,1)S(1)} collective-permute-done((bf16[256,2048]{1,0:T(8,128)(2,1)}, bf16[256,2048]{1,0:T(8,128)(2,1)S(1)}, u32[]{:S(2)}, u32[]{:S(2)}) %collective-permute-start.4) | collective-permute-done | bytes 1048608 | tf_op jit(solution)/shard_map/ppermute | solution.py:132
  364.7 14.4 %fusion.129 = f32[1024,2048]{1,0:T(8,128)} fusion(bf16[1024,2048]{1,0:T(8,128)(2,1)} %fusion.51, bf16[2048,2048]{1,0:T(8,128)(2,1)} %all-gather.23.cloned.1.call-done), kind=kOutput, calls=%fused_computation.209 | convolution fusion | flops 8589934592 | bytes 20971520 | tf_op jit(solution)/shard_map/dot_general | solution.py:147
  379.1 14.6 %fusion.96 = f32[1024,2048]{1,0:T(8,128)} fusion(bf16[2048,2048]{1,0:T(8,128)(2,1)} %all-gather.25.cloned.1.call-done, bf16[1,1024,2048]{2,1,0:T(8,128)(2,1)} %param.16, f32[1024]{0:T(1024)S(1)} %fusion.118), kind=kOutput, calls=%fused_computation.144 | convolution fusion | flops 8596226048 | bytes 20975616 | tf_op jit(solution)/shard_map/rd,fd->rf/dot_general | solution.py:214
  393.6 22.3 %multiply_convert_fusion.1 = (bf16[1024,2048]{1,0:T(8,128)(2,1)}, bf16[1024,2048]{1,0:T(8,128)(2,1)}, bf16[1024,2048]{1,0:T(8,128)(2,1)}) fusion(f32[1024,2048]{1,0:T(8,128)} %fusion.96, f32[1024,2048]{1,0:T(8,128)} %fusion.129, bf16[1024,2048]{1,0:T(8,128)(2,1)} %fusion.51, bf16[2048,2048]{1,0:T(8,128)(2,1)} %all-gather.21.cloned.1.call-done), kind=kOutput, calls=%fused_computation.80 | convolution fusion | flops 8623489024 | bytes 41943040 | tf_op jit(solution)/shard_map/dot_general | solution.py:147
  415.9 14.7 %fusion.130 = f32[1024,2048]{1,0:T(8,128)} fusion(bf16[1024,2048]{1,0:T(8,128)(2,1)} %get-tuple-element.310, bf16[2048,2048]{1,0:T(8,128)(2,1)} %all-gather.21.cloned.1.call-done), kind=kOutput, calls=%fused_computation.210 | convolution fusion | flops 8589934592 | bytes 20971520 | tf_op jit(solution)/shard_map/rf,df->rd/dot_general | solution.py:225
  430.6 14.2 %add_convert_fusion.1 = bf16[1024,2048]{1,0:T(8,128)(2,1)S(1)} fusion(f32[1024,2048]{1,0:T(8,128)} %fusion.130, bf16[1024,2048]{1,0:T(8,128)(2,1)} %get-tuple-element.309, bf16[2048,2048]{1,0:T(8,128)(2,1)} %all-gather.23.cloned.1.call-done), kind=kOutput, calls=%fused_computation.79 | convolution fusion | flops 8594128896 | bytes 25165824 | tf_op jit(solution)/shard_map/rf,df->rd/dot_general | solution.py:227
  445.0 22.0 %collective-permute-start.12 = (bf16[256,2048]{1,0:T(8,128)(2,1)S(1)}, bf16[256,2048]{1,0:T(8,128)(2,1)S(1)}, u32[]{:S(2)}, u32[]{:S(2)}) collective-permute-start(bf16[256,2048]{1,0:T(8,128)(2,1)S(1)} %get-tuple-element.317), channel_id=1, source_target_pairs={{0,1},{1,2},{2,3},{3,0},{4,5},{5,6},{6,7},{7,4},{8,9},{9,10},{10,1... | collective-permute-start | bytes 3145736 | tf_op jit(solution)/shard_map/ppermute | solution.py:126
  496.9 41.8 %collective-permute-done.13 = bf16[256,2048]{1,0:T(8,128)(2,1)S(1)} collective-permute-done((bf16[256,2048]{1,0:T(8,128)(2,1)S(1)}, bf16[256,2048]{1,0:T(8,128)(2,1)S(1)}, u32[]{:S(2)}, u32[]{:S(2)}) %collective-permute-start.13) | collective-permute-done | bytes 1048608 | tf_op jit(solution)/shard_map/ppermute | solution.py:126
  543.0 68.0 %collective-permute-start.15 = (bf16[256,2048]{1,0:T(8,128)(2,1)S(1)}, bf16[256,2048]{1,0:T(8,128)(2,1)S(1)}, u32[]{:S(2)}, u32[]{:S(2)}) collective-permute-start(bf16[256,2048]{1,0:T(8,128)(2,1)S(1)} %get-tuple-element.300), channel_id=1, source_target_pairs={{0,1},{1,2},{2,3},{3,0},{4,5},{5,6},{6,7},{7,4},{8,9},{9,10},{10,1... | collective-permute-start | bytes 3145736 | tf_op jit(solution)/shard_map/ppermute | solution.py:132
  613.3 59.1 %collective-permute-done.7 = bf16[256,2048]{1,0:T(8,128)(2,1)} collective-permute-done((bf16[256,2048]{1,0:T(8,128)(2,1)}, bf16[256,2048]{1,0:T(8,128)(2,1)}, u32[]{:S(2)}, u32[]{:S(2)}) %collective-permute-start.7) | collective-permute-done | bytes 1048608 | tf_op jit(solution)/shard_map/ppermute | solution.py:126
  675.9 23.1 %collective-permute-start.9 = (bf16[256,2048]{1,0:T(8,128)(2,1)S(1)}, bf16[256,2048]{1,0:T(8,128)(2,1)S(1)}, u32[]{:S(2)}, u32[]{:S(2)}) collective-permute-start(bf16[256,2048]{1,0:T(8,128)(2,1)S(1)} %get-tuple-element.302), channel_id=1, source_target_pairs={{0,1},{1,2},{2,3},{3,0},{4,5},{5,6},{6,7},{7,4},{8,9},{9,10},{10,1... | collective-permute-start | bytes 3145736 | tf_op jit(solution)/shard_map/ppermute | solution.py:132
  702.4 59.8 %collective-permute-done.16 = bf16[256,2048]{1,0:T(8,128)(2,1)S(1)} collective-permute-done((bf16[256,2048]{1,0:T(8,128)(2,1)S(1)}, bf16[256,2048]{1,0:T(8,128)(2,1)S(1)}, u32[]{:S(2)}, u32[]{:S(2)}) %collective-permute-start.16) | collective-permute-done | bytes 1048608 | tf_op jit(solution)/shard_map/ppermute | solution.py:132
  770.8 36.3 %collective-permute-done.10 = bf16[256,2048]{1,0:T(8,128)(2,1)S(1)} collective-permute-done((bf16[256,2048]{1,0:T(8,128)(2,1)S(1)}, bf16[256,2048]{1,0:T(8,128)(2,1)S(1)}, u32[]{:S(2)}, u32[]{:S(2)}) %collective-permute-start.10) | collective-permute-done | bytes 1048608 | tf_op jit(solution)/shard_map/ppermute | solution.py:132
  824.7 129.8 %while.28 = (s32[]{:T(128)}, f32[2048,4,128]{0,2,1:T(8,128)}, f32[2048,4,128]{0,2,1:T(8,128)}, f32[2,512,4,128]{3,1,2,0:T(8,128)}, bf16[2,512,4,128]{3,1,2,0:T(8...) while((s32[]{:T(128)}, f32[2048,4,128]{0,2,1:T(8,128)}, ...), condition=%wide.region_12.13_spmd.clone, body=%wide.region_10.12_spmd.clone.sunk | while | flops 5439226368 | bytes 211879280 | solution.py:111
  851.2 14.9 %multiply_convert_fusion.5 = bf16[4,512,2048]{2,1,0:T(8,128)(2,1)} fusion(f32[4,512,2048]{2,1,0:T(8,128)} %get-tuple-element.478, f32[4,512,2048]{2,1,0:T(8,128)} %fusion.198, f32[4,512]{1,0:T(4,128)S(1)} %get-tuple-element.479, f32[4,512]{1,0:T(4,128)S(1)} %dynamic-slice_bitcast_fusion.14, pred[512,2048]{1,0:T(8,128)(4,1)S(1)} %fusion.199), kind=kLoop, calls=%fused_computation.21.clone.1 | loop fusion | flops 25165824 | bytes 43008000 | tf_op jit(solution)/shard_map/while/body/eval_jaxpr/convert_element_type | solution.py:96
  914.6 14.9 %multiply_convert_fusion.5 = bf16[4,512,2048]{2,1,0:T(8,128)(2,1)} fusion(f32[4,512,2048]{2,1,0:T(8,128)} %get-tuple-element.478, f32[4,512,2048]{2,1,0:T(8,128)} %fusion.198, f32[4,512]{1,0:T(4,128)S(1)} %get-tuple-element.479, f32[4,512]{1,0:T(4,128)S(1)} %dynamic-slice_bitcast_fusion.14, pred[512,2048]{1,0:T(8,128)(4,1)S(1)} %fusion.199), kind=kLoop, calls=%fused_computation.21.clone.1 | loop fusion | flops 25165824 | bytes 43008000 | tf_op jit(solution)/shard_map/while/body/eval_jaxpr/convert_element_type | solution.py:96
  1001.2 14.4 %convolution_convert_fusion = bf16[2048,2048]{1,0:T(8,128)(2,1)} fusion(bf16[1024,2048]{1,0:T(8,128)(2,1)} %get-tuple-element.311, bf16[1,1024,2048]{2,1,0:T(8,128)(2,1)} %param.16, f32[1024]{0:T(1024)S(1)} %copy-done.48), kind=kOutput, calls=%fused_computation.87 | convolution fusion | flops 8600420352 | bytes 16781312 | tf_op jit(solution)/shard_map/rf,rd->fd/dot_general | solution.py:213
  1053.4 23.7 %collective-permute-start.18 = (bf16[256,2048]{1,0:T(8,128)(2,1)S(1)}, bf16[256,2048]{1,0:T(8,128)(2,1)S(1)}, u32[]{:S(2)}, u32[]{:S(2)}) collective-permute-start(bf16[256,2048]{1,0:T(8,128)(2,1)S(1)} %get-tuple-element.314), channel_id=1, source_target_pairs={{0,1},{1,2},{2,3},{3,0},{4,5},{5,6},{6,7},{7,4},{8,9},{9,10},{10,1... | collective-permute-start | bytes 3145736 | tf_op jit(solution)/shard_map/ppermute | solution.py:126
  1079.6 21.1 %collective-permute-done.18 = bf16[256,2048]{1,0:T(8,128)(2,1)S(1)} collective-permute-done((bf16[256,2048]{1,0:T(8,128)(2,1)S(1)}, bf16[256,2048]{1,0:T(8,128)(2,1)S(1)}, u32[]{:S(2)}, u32[]{:S(2)}) %collective-permute-start.18) | collective-permute-done | bytes 1048608 | tf_op jit(solution)/shard_map/ppermute | solution.py:126
  1100.7 44.0 %collective-permute-done.19 = bf16[256,2048]{1,0:T(8,128)(2,1)S(1)} collective-permute-done((bf16[256,2048]{1,0:T(8,128)(2,1)S(1)}, bf16[256,2048]{1,0:T(8,128)(2,1)S(1)}, u32[]{:S(2)}, u32[]{:S(2)}) %collective-permute-start.19) | collective-permute-done | bytes 1048608 | tf_op jit(solution)/shard_map/ppermute | solution.py:126
  1149.6 22.7 %collective-permute-start.21 = (bf16[256,2048]{1,0:T(8,128)(2,1)}, bf16[256,2048]{1,0:T(8,128)(2,1)S(1)}, u32[]{:S(2)}, u32[]{:S(2)}) collective-permute-start(bf16[256,2048]{1,0:T(8,128)(2,1)} %get-tuple-element.298), channel_id=1, source_target_pairs={{0,1},{1,2},{2,3},{3,0},{4,5},{5,6},{6,7},{7,4},{8,9},{9,10},{10,1... | collective-permute-start | bytes 3145736 | tf_op jit(solution)/shard_map/ppermute | solution.py:132
  1187.1 55.4 %reduce-scatter.24.cloned.1.call-done = bf16[256,2048]{1,0:T(8,128)(2,1)} async-done(((bf16[2048,2048]{1,0:T(8,128)(2,1)}), bf16[256,2048]{1,0:T(8,128)(2,1)}) %reduce-scatter.24.cloned.1.call-update) | async-done | bytes 1048592 | tf_op jit(solution)/shard_map/reduce_scatter | solution.py:140
  1245.2 71.8 %reduce-scatter.26.cloned.1.call-done = bf16[2048,256]{1,0:T(8,128)(2,1)} async-done(((bf16[2048,2048]{1,0:T(8,128)(2,1)}), bf16[2048,256]{1,0:T(8,128)(2,1)}) %reduce-scatter.26.cloned.1.call-update) | async-done | bytes 1048592 | tf_op jit(solution)/shard_map/reduce_scatter | solution.py:140
  1336.9 24.4 %reduce-scatter.16.cloned.1.call-done = bf16[256,512]{1,0:T(8,128)(2,1)} async-done(((bf16[2048,512]{1,0:T(8,128)(2,1)}), bf16[256,512]{1,0:T(8,128)(2,1)}) %reduce-scatter.16.cloned.1.call-update) | async-done | bytes 262160 | tf_op jit(solution)/shard_map/reduce_scatter | solution.py:140
  1363.2 42.5 %reduce-scatter.18.cloned.1.call-done = bf16[256,512]{1,0:T(8,128)(2,1)} async-done(((bf16[2048,512]{1,0:T(8,128)(2,1)}), bf16[256,512]{1,0:T(8,128)(2,1)}) %reduce-scatter.18.cloned.1.call-update) | async-done | bytes 262160 | tf_op jit(solution)/shard_map/reduce_scatter | solution.py:140
  (351 shorter events, 458.2 us)
Async XLA Ops:
  10.9 90.7 %all-gather.11.cloned.1.call-start = ((), (), s32[]{:S(2)}) async-start(), calls=%async_computation.9 | async-start | bytes 2359296 | tf_op jit(solution)/shard_map/all_gather | solution.py:167
  12.7 120.2 %all-gather.15.cloned.1.call-start = ((), (), s32[]{:S(2)}) async-start(), calls=%async_computation.11 | async-start | bytes 3145728 | tf_op jit(solution)/shard_map/all_gather | solution.py:189
  48.2 87.9 %all-gather.27.cloned.1.call-start = ((), (), s32[]{:S(2)}) async-start(), calls=%async_computation.26 | async-start | bytes 3145728 | tf_op jit(solution)/shard_map/all_gather | solution.py:190
  81.6 89.5 %all-gather.19.cloned.1.call-start = ((), (), s32[]{:S(2)}) async-start(), calls=%async_computation.13 | async-start | bytes 2359296 | tf_op jit(solution)/shard_map/all_gather | solution.py:170
  82.4 282.3 %all-gather.23.cloned.1.call-start = ((), (), s32[]{:S(2)}) async-start(), calls=%async_computation.15 | async-start | bytes 9437184 | tf_op jit(solution)/shard_map/all_gather | solution.py:174
  83.7 295.4 %all-gather.25.cloned.1.call-start = ((), (), s32[]{:S(2)}) async-start(), calls=%async_computation.16 | async-start | bytes 9437184 | tf_op jit(solution)/shard_map/all_gather | solution.py:175
  86.6 307.1 %all-gather.21.cloned.1.call-start = ((), (), s32[]{:S(2)}) async-start(), calls=%async_computation.14 | async-start | bytes 9437184 | tf_op jit(solution)/shard_map/all_gather | solution.py:173
  87.8 940.3 %reduce-scatter.10.cloned.1.call-start = ((), (), s32[]{:S(2)}) async-start(), calls=%async_computation.17 | async-start | bytes 6291456 | tf_op jit(solution)/shard_map/reduce_scatter | solution.py:257
  181.4 70.8 %collective-permute-start.1 = (bf16[256,2048]{1,0:T(8,128)(2,1)}, bf16[256,2048]{1,0:T(8,128)(2,1)S(1)}, u32[]{:S(2)}, u32[]{:S(2)}) collective-permute-start(bf16[256,2048]{1,0:T(8,128)(2,1)} %get-tuple-element.325), channel_id=1, source_target_pairs={{0,2},{1,3},{2,0},{3,1},{4,6},{5,7},{6,4},{7,5},{8,10},{9,11},{10,... | collective-permute-start | bytes 3145736 | tf_op jit(solution)/shard_map/ppermute | solution.py:126
  281.5 68.9 %collective-permute-start.4 = (bf16[256,2048]{1,0:T(8,128)(2,1)}, bf16[256,2048]{1,0:T(8,128)(2,1)S(1)}, u32[]{:S(2)}, u32[]{:S(2)}) collective-permute-start(bf16[256,2048]{1,0:T(8,128)(2,1)} %get-tuple-element.304), channel_id=1, source_target_pairs={{0,2},{1,3},{2,0},{3,1},{4,6},{5,7},{6,4},{7,5},{8,10},{9,11},{10,... | collective-permute-start | bytes 3145736 | tf_op jit(solution)/shard_map/ppermute | solution.py:132
  467.0 71.7 %collective-permute-start.13 = (bf16[256,2048]{1,0:T(8,128)(2,1)S(1)}, bf16[256,2048]{1,0:T(8,128)(2,1)S(1)}, u32[]{:S(2)}, u32[]{:S(2)}) collective-permute-start(bf16[256,2048]{1,0:T(8,128)(2,1)S(1)} %get-tuple-element.319), channel_id=1, source_target_pairs={{0,2},{1,3},{2,0},{3,1},{4,6},{5,7},{6,4},{7,5},{8,10},{9,11},{10,... | collective-permute-start | bytes 3145736 | tf_op jit(solution)/shard_map/ppermute | solution.py:126
  470.1 68.6 %collective-permute-start.14 = (bf16[256,2048]{1,0:T(8,128)(2,1)S(1)}, bf16[256,2048]{1,0:T(8,128)(2,1)S(1)}, u32[]{:S(2)}, u32[]{:S(2)}) collective-permute-start(bf16[256,2048]{1,0:T(8,128)(2,1)S(1)} %get-tuple-element.318), channel_id=1, source_target_pairs={{0,3},{1,0},{2,1},{3,2},{4,7},{5,4},{6,5},{7,6},{8,11},{9,8},{10,9... | collective-permute-start | bytes 3145736 | tf_op jit(solution)/shard_map/ppermute | solution.py:126
  481.1 129.9 %collective-permute-start.6 = (bf16[256,2048]{1,0:T(8,128)(2,1)}, bf16[256,2048]{1,0:T(8,128)(2,1)}, u32[]{:S(2)}, u32[]{:S(2)}) collective-permute-start(bf16[256,2048]{1,0:T(8,128)(2,1)} %get-tuple-element.320), channel_id=1, source_target_pairs={{0,1},{1,2},{2,3},{3,0},{4,5},{5,6},{6,7},{7,4},{8,9},{9,10},{10,1... | collective-permute-start | bytes 3145736 | tf_op jit(solution)/shard_map/ppermute | solution.py:126
  483.1 189.3 %collective-permute-start.7 = (bf16[256,2048]{1,0:T(8,128)(2,1)}, bf16[256,2048]{1,0:T(8,128)(2,1)}, u32[]{:S(2)}, u32[]{:S(2)}) collective-permute-start(bf16[256,2048]{1,0:T(8,128)(2,1)} %get-tuple-element.322), channel_id=1, source_target_pairs={{0,2},{1,3},{2,0},{3,1},{4,6},{5,7},{6,4},{7,5},{8,10},{9,11},{10,... | collective-permute-start | bytes 3145736 | tf_op jit(solution)/shard_map/ppermute | solution.py:126
  493.7 178.7 %collective-permute-start.8 = (bf16[256,2048]{1,0:T(8,128)(2,1)}, bf16[256,2048]{1,0:T(8,128)(2,1)}, u32[]{:S(2)}, u32[]{:S(2)}) collective-permute-start(bf16[256,2048]{1,0:T(8,128)(2,1)} %get-tuple-element.321), channel_id=1, source_target_pairs={{0,3},{1,0},{2,1},{3,2},{4,7},{5,4},{6,5},{7,6},{8,11},{9,8},{10,9... | collective-permute-start | bytes 3145736 | tf_op jit(solution)/shard_map/ppermute | solution.py:126
  543.0 156.9 %collective-permute-start.15 = (bf16[256,2048]{1,0:T(8,128)(2,1)S(1)}, bf16[256,2048]{1,0:T(8,128)(2,1)S(1)}, u32[]{:S(2)}, u32[]{:S(2)}) collective-permute-start(bf16[256,2048]{1,0:T(8,128)(2,1)S(1)} %get-tuple-element.300), channel_id=1, source_target_pairs={{0,1},{1,2},{2,3},{3,0},{4,5},{5,6},{6,7},{7,4},{8,9},{9,10},{10,1... | collective-permute-start | bytes 3145736 | tf_op jit(solution)/shard_map/ppermute | solution.py:132
  610.9 151.3 %collective-permute-start.16 = (bf16[256,2048]{1,0:T(8,128)(2,1)S(1)}, bf16[256,2048]{1,0:T(8,128)(2,1)S(1)}, u32[]{:S(2)}, u32[]{:S(2)}) collective-permute-start(bf16[256,2048]{1,0:T(8,128)(2,1)S(1)} %get-tuple-element.300), channel_id=1, source_target_pairs={{0,2},{1,3},{2,0},{3,1},{4,6},{5,7},{6,4},{7,5},{8,10},{9,11},{10,... | collective-permute-start | bytes 3145736 | tf_op jit(solution)/shard_map/ppermute | solution.py:132
  610.9 152.3 %collective-permute-start.17 = (bf16[256,2048]{1,0:T(8,128)(2,1)S(1)}, bf16[256,2048]{1,0:T(8,128)(2,1)S(1)}, u32[]{:S(2)}, u32[]{:S(2)}) collective-permute-start(bf16[256,2048]{1,0:T(8,128)(2,1)S(1)} %get-tuple-element.300), channel_id=1, source_target_pairs={{0,3},{1,0},{2,1},{3,2},{4,7},{5,4},{6,5},{7,6},{8,11},{9,8},{10,9... | collective-permute-start | bytes 3145736 | tf_op jit(solution)/shard_map/ppermute | solution.py:132
  675.9 94.8 %collective-permute-start.9 = (bf16[256,2048]{1,0:T(8,128)(2,1)S(1)}, bf16[256,2048]{1,0:T(8,128)(2,1)S(1)}, u32[]{:S(2)}, u32[]{:S(2)}) collective-permute-start(bf16[256,2048]{1,0:T(8,128)(2,1)S(1)} %get-tuple-element.302), channel_id=1, source_target_pairs={{0,1},{1,2},{2,3},{3,0},{4,5},{5,6},{6,7},{7,4},{8,9},{9,10},{10,1... | collective-permute-start | bytes 3145736 | tf_op jit(solution)/shard_map/ppermute | solution.py:132
  698.9 108.2 %collective-permute-start.10 = (bf16[256,2048]{1,0:T(8,128)(2,1)S(1)}, bf16[256,2048]{1,0:T(8,128)(2,1)S(1)}, u32[]{:S(2)}, u32[]{:S(2)}) collective-permute-start(bf16[256,2048]{1,0:T(8,128)(2,1)S(1)} %get-tuple-element.302), channel_id=1, source_target_pairs={{0,2},{1,3},{2,0},{3,1},{4,6},{5,7},{6,4},{7,5},{8,10},{9,11},{10,... | collective-permute-start | bytes 3145736 | tf_op jit(solution)/shard_map/ppermute | solution.py:132
  699.9 107.3 %collective-permute-start.11 = (bf16[256,2048]{1,0:T(8,128)(2,1)S(1)}, bf16[256,2048]{1,0:T(8,128)(2,1)S(1)}, u32[]{:S(2)}, u32[]{:S(2)}) collective-permute-start(bf16[256,2048]{1,0:T(8,128)(2,1)S(1)} %get-tuple-element.302), channel_id=1, source_target_pairs={{0,3},{1,0},{2,1},{3,2},{4,7},{5,4},{6,5},{7,6},{8,11},{9,8},{10,9... | collective-permute-start | bytes 3145736 | tf_op jit(solution)/shard_map/ppermute | solution.py:132
  954.5 88.1 %reduce-scatter.12.cloned.1.call-start = ((), (), s32[]{:S(2)}) async-start(), calls=%async_computation.18 | async-start | bytes 6291456 | tf_op jit(solution)/shard_map/reduce_scatter | solution.py:258
  955.2 225.3 %reduce-scatter.14.cloned.1.call-start = ((), (), s32[]{:S(2)}) async-start(), calls=%async_computation.19 | async-start | bytes 2359296 | tf_op jit(solution)/shard_map/reduce_scatter | solution.py:140
  965.1 217.3 %reduce-scatter.20.cloned.1.call-start = ((), (), s32[]{:S(2)}) async-start(), calls=%async_computation.22 | async-start | bytes 2359296 | tf_op jit(solution)/shard_map/reduce_scatter | solution.py:140
  972.2 211.9 %reduce-scatter.22.cloned.1.call-start = ((), (), s32[]{:S(2)}) async-start(), calls=%async_computation.23 | async-start | bytes 9437184 | tf_op jit(solution)/shard_map/reduce_scatter | solution.py:140
  986.5 256.0 %reduce-scatter.24.cloned.1.call-start = ((), (), s32[]{:S(2)}) async-start(), calls=%async_computation.24 | async-start | bytes 9437184 | tf_op jit(solution)/shard_map/reduce_scatter | solution.py:140
  1000.5 316.5 %reduce-scatter.26.cloned.1.call-start = ((), (), s32[]{:S(2)}) async-start(), calls=%async_computation.25 | async-start | bytes 9437184 | tf_op jit(solution)/shard_map/reduce_scatter | solution.py:140
  1015.7 345.7 %reduce-scatter.16.cloned.1.call-start = ((), (), s32[]{:S(2)}) async-start(), calls=%async_computation.20 | async-start | bytes 2359296 | tf_op jit(solution)/shard_map/reduce_scatter | solution.py:140
  1036.7 369.0 %reduce-scatter.18.cloned.1.call-start = ((), (), s32[]{:S(2)}) async-start(), calls=%async_computation.21 | async-start | bytes 2359296 | tf_op jit(solution)/shard_map/reduce_scatter | solution.py:140
  1149.6 170.3 %collective-permute-start.21 = (bf16[256,2048]{1,0:T(8,128)(2,1)}, bf16[256,2048]{1,0:T(8,128)(2,1)S(1)}, u32[]{:S(2)}, u32[]{:S(2)}) collective-permute-start(bf16[256,2048]{1,0:T(8,128)(2,1)} %get-tuple-element.298), channel_id=1, source_target_pairs={{0,1},{1,2},{2,3},{3,0},{4,5},{5,6},{6,7},{7,4},{8,9},{9,10},{10,1... | collective-permute-start | bytes 3145736 | tf_op jit(solution)/shard_map/ppermute | solution.py:132
  1172.3 148.7 %collective-permute-start.22 = (bf16[256,2048]{1,0:T(8,128)(2,1)}, bf16[256,2048]{1,0:T(8,128)(2,1)S(1)}, u32[]{:S(2)}, u32[]{:S(2)}) collective-permute-start(bf16[256,2048]{1,0:T(8,128)(2,1)} %get-tuple-element.298), channel_id=1, source_target_pairs={{0,2},{1,3},{2,0},{3,1},{4,6},{5,7},{6,4},{7,5},{8,10},{9,11},{10,... | collective-permute-start | bytes 3145736 | tf_op jit(solution)/shard_map/ppermute | solution.py:132
  1175.7 146.3 %collective-permute-start.23 = (bf16[256,2048]{1,0:T(8,128)(2,1)}, bf16[256,2048]{1,0:T(8,128)(2,1)S(1)}, u32[]{:S(2)}, u32[]{:S(2)}) collective-permute-start(bf16[256,2048]{1,0:T(8,128)(2,1)} %get-tuple-element.298), channel_id=1, source_target_pairs={{0,3},{1,0},{2,1},{3,2},{4,7},{5,4},{6,5},{7,6},{8,11},{9,8},{10,9... | collective-permute-start | bytes 3145736 | tf_op jit(solution)/shard_map/ppermute | solution.py:132
  (69 other events, 1936.5 us)
Sparse Core Ops, SparseCore 0:
  10.4 30.4 all-gather.12
  43.4 27.7 all-gather.16
  73.7 27.7 all-gather.10
  102.9 10.5 all-gather.14
  114.9 11.7 all-gather.26
  128.4 29.2 all-gather.18
  159.6 54.2 all-gather.22
  216.4 55.8 all-gather.24
  274.2 54.2 all-gather.20
  954.6 31.4 reduce-scatter.9
  988.4 13.1 reduce-scatter.11
  1005.3 42.3 reduce-scatter.13
  1051.6 41.0 reduce-scatter.19
  1096.0 71.5 reduce-scatter.21
  1170.9 71.5 reduce-scatter.23
  1245.8 71.2 reduce-scatter.25
  1320.2 41.1 reduce-scatter.15
  1364.5 41.1 reduce-scatter.17

commit v3 on v2

--- a/solution.py
+++ b/solution.py
@@ -4,6 +4,8 @@
 import jax.numpy as jnp
 from jax import lax
 from jax.sharding import PartitionSpec as P
+
+SHARD, CTX, TP = "shard", "ctx", "tp"
 
 HEAD_DIM = 128
 
@@ -115,7 +117,7 @@
 
 
 def tp_psum(part, count):
-    me = lax.axis_index("tp")
+    me = lax.axis_index(TP)
     low_part = part.astype(jnp.bfloat16)
     rows = part.shape[0] // count
     chunks = low_part.reshape((count, rows) + part.shape[1:])
@@ -123,22 +125,43 @@
     for shift in range(1, count):
         pairs = [(i, (i + shift) % count) for i in range(count)]
         piece = lax.dynamic_index_in_dim(chunks, (me + shift) % count, 0, keepdims=False)
-        total = total + lax.ppermute(piece, "tp", pairs).astype(jnp.float32)
+        total = total + lax.ppermute(piece, TP, pairs).astype(jnp.float32)
     reduced = total.astype(jnp.bfloat16)
     gathered = jnp.zeros(low_part.shape, jnp.bfloat16)
     gathered = lax.dynamic_update_slice_in_dim(gathered, reduced, me * rows, 0)
     for shift in range(1, count):
         pairs = [(i, (i + shift) % count) for i in range(count)]
-        got = lax.ppermute(reduced, "tp", pairs)
+        got = lax.ppermute(reduced, TP, pairs)
         gathered = lax.dynamic_update_slice_in_dim(
             gathered, got, ((me + count - shift) % count) * rows, 0
         )
     return gathered
 
 
+def exchange_gather(piece, axis, count):
+    me = lax.axis_index(axis)
+    gathered = jnp.zeros((count,) + piece.shape, piece.dtype)
+    gathered = lax.dynamic_update_index_in_dim(gathered, piece, me, 0)
+    for shift in range(1, count):
+        pairs = [(i, (i + shift) % count) for i in range(count)]
+        got = lax.ppermute(piece, axis, pairs)
+        gathered = lax.dynamic_update_index_in_dim(gathered, got, (me + count - shift) % count, 0)
+    return gathered
+
+
+def exchange_scatter(blocks, axis, count):
+    me = lax.axis_index(axis)
+    total = lax.dynamic_index_in_dim(blocks, me, 0, keepdims=False)
+    for shift in range(1, count):
+        pairs = [(i, (i + shift) % count) for i in range(count)]
+        piece = lax.dynamic_index_in_dim(blocks, (me + shift) % count, 0, keepdims=False)
+        total = total + lax.ppermute(piece, axis, pairs)
+    return total
+
+
 def scatter_low(grad, dim):
     summed = lax.psum_scatter(
-        grad.astype(jnp.bfloat16), ("shard", "ctx"), scatter_dimension=dim, tiled=True
+        grad.astype(jnp.bfloat16), (SHARD, CTX), scatter_dimension=dim, tiled=True
     )
     return summed.astype(jnp.float32)
 
@@ -147,12 +170,52 @@
     return jnp.dot(left, right, preferred_element_type=jnp.float32)
 
 
-def body(tp_count, tokens, lengths, cotangent, w_query, w_key, w_value, w_output, w_gate, w_up, w_down):
+MID_SPLIT = (3, 5)
+
+
+def middle_rows(attn_rows, tokens_rows, grad_final, output_full, gate_full, up_full, down_full, tp_count):
+    bf_type = jnp.bfloat16
+    resid = tokens_rows + tp_psum(matmul_low(attn_rows, output_full), tp_count).astype(jnp.float32)
+    normed_two, scale_two = normalize(resid)
+    input_two = normed_two.astype(bf_type)
+    gate_proj = matmul_low(input_two, gate_full)
+    up_proj = matmul_low(input_two, up_full)
+    gate_sigmoid = jax.nn.sigmoid(gate_proj)
+    hidden = (gate_proj * gate_sigmoid * up_proj).astype(bf_type)
+    grad_branch = grad_final.astype(bf_type)
+    grad_hidden = jnp.einsum(
+        "rd,fd->rf", grad_branch, down_full, preferred_element_type=jnp.float32
+    )
+    grad_gate_act = (
+        grad_hidden * up_proj * gate_sigmoid * (1.0 + gate_proj * (1.0 - gate_sigmoid))
+    ).astype(bf_type)
+    grad_up_act = (grad_hidden * gate_proj * gate_sigmoid).astype(bf_type)
+    grad_input_two = jnp.einsum(
+        "rf,df->rd", grad_gate_act, gate_full, preferred_element_type=jnp.float32
+    ) + jnp.einsum("rf,df->rd", grad_up_act, up_full, preferred_element_type=jnp.float32)
+    branch_two = matmul_low(hidden, down_full)
+    grad_down = jnp.einsum("rf,rd->fd", hidden, grad_branch, preferred_element_type=jnp.float32)
+    grad_gate = jnp.einsum(
+        "rd,rf->df", input_two, grad_gate_act, preferred_element_type=jnp.float32
+    )
+    grad_up = jnp.einsum("rd,rf->df", input_two, grad_up_act, preferred_element_type=jnp.float32)
+    grad_input_two = tp_psum(grad_input_two, tp_count)
+    return [
+        resid, branch_two, normed_two, scale_two, grad_final, grad_input_two,
+        grad_gate, grad_up, grad_down,
+    ]
+
+
+def body(tp_count, ctx_count, *args):
+    return block(tp_count, ctx_count, *args)
+
+
+def block(tp_count, ctx_count, tokens, lengths, cotangent, w_query, w_key, w_value, w_output, w_gate, w_up, w_down):
     seq_count, half_len, model_width = tokens.shape
     head_cols = w_query.shape[1]
     head_count = head_cols // HEAD_DIM
     row_total = seq_count * half_len
-    offset = lax.axis_index("ctx") * half_len
+    offset = lax.axis_index(CTX) * half_len
     positions = offset + jnp.arange(half_len)
     valid_mask = (positions[None, :] < lengths[:, None]).astype(jnp.float32)
     bf_type = jnp.bfloat16
@@ -163,16 +226,18 @@
         w_output.astype(bf_type),
     )
     mlp_low = (w_gate.astype(bf_type), w_up.astype(bf_type), w_down.astype(bf_type))
-    query_full, key_full, value_full, output_full = (
-        lax.all_gather(attn_low[0], ("shard", "ctx"), axis=0, tiled=True),
-        lax.all_gather(attn_low[1], ("shard", "ctx"), axis=0, tiled=True),
-        lax.all_gather(attn_low[2], ("shard", "ctx"), axis=0, tiled=True),
-        lax.all_gather(attn_low[3], ("shard", "ctx"), axis=1, tiled=True),
-    )
+    attn_joined = lax.all_gather(
+        jnp.concatenate([attn_low[0], attn_low[1], attn_low[2], attn_low[3].T], axis=1),
+        (SHARD, CTX),
+        axis=0,
+        tiled=True,
+    )
+    query_full, key_full, value_full, output_t = jnp.split(attn_joined, 4, axis=1)
+    output_full = output_t.T
     gate_full, up_full, down_full = (
-        lax.all_gather(mlp_low[0], ("shard", "ctx"), axis=0, tiled=True),
-        lax.all_gather(mlp_low[1], ("shard", "ctx"), axis=0, tiled=True),
-        lax.all_gather(mlp_low[2], ("shard", "ctx"), axis=1, tiled=True),
+        lax.all_gather(mlp_low[0], (SHARD, CTX), axis=0, tiled=True),
+        lax.all_gather(mlp_low[1], (SHARD, CTX), axis=0, tiled=True),
+        lax.all_gather(mlp_low[2], (SHARD, CTX), axis=1, tiled=True),
     )
     tokens_wide = tokens.astype(jnp.float32).reshape(row_total, model_width)
     normed_one, scale_one = normalize(tokens_wide)
@@ -186,8 +251,12 @@
     keys_rot = rotate(key_pre, cosine, sine_table).astype(bf_type)
     values_low = value_pre.astype(bf_type)
     keys_all, values_all = (
-        lax.all_gather(keys_rot, "ctx", axis=1, tiled=True),
-        lax.all_gather(values_low, "ctx", axis=1, tiled=True),
+        jnp.swapaxes(exchange_gather(keys_rot, CTX, ctx_count), 0, 1).reshape(
+            (seq_count, ctx_count * half_len, head_count, HEAD_DIM)
+        ),
+        jnp.swapaxes(exchange_gather(values_low, CTX, ctx_count), 0, 1).reshape(
+            (seq_count, ctx_count * half_len, head_count, HEAD_DIM)
+        ),
     )
     seq_index = 0
     attended, log_totals = attend_forward(
@@ -196,42 +265,43 @@
     attended_list = [attended]
     log_list = [log_totals]
     attn_out = jnp.stack(attended_list).reshape(row_total, head_cols)
-    branch_part = matmul_low(attn_out, output_full)
-    resid = tokens_wide + tp_psum(branch_part, tp_count).astype(jnp.float32)
-    normed_two, scale_two = normalize(resid)
-    input_two = normed_two.astype(bf_type)
-    gate_proj = matmul_low(input_two, gate_full)
-    up_proj = matmul_low(input_two, up_full)
-    gate_sigmoid = jax.nn.sigmoid(gate_proj)
-    hidden = (gate_proj * gate_sigmoid * up_proj).astype(bf_type)
-    branch_two_part = matmul_low(hidden, down_full)
-    final_sum = resid + tp_psum(branch_two_part, tp_count).astype(jnp.float32)
     grad_final = cotangent.astype(jnp.float32).reshape(row_total, model_width) * valid_mask.reshape(
         row_total, 1
     )
-    grad_branch = grad_final.astype(bf_type)
-    grad_down = jnp.einsum("rf,rd->fd", hidden, grad_branch, preferred_element_type=jnp.float32)
-    grad_hidden = jnp.einsum(
-        "rd,fd->rf", grad_branch, down_full, preferred_element_type=jnp.float32
-    )
-    grad_gate_act = (
-        grad_hidden * up_proj * gate_sigmoid * (1.0 + gate_proj * (1.0 - gate_sigmoid))
-    ).astype(bf_type)
-    grad_up_act = (grad_hidden * gate_proj * gate_sigmoid).astype(bf_type)
-    grad_gate = jnp.einsum(
-        "rd,rf->df", input_two, grad_gate_act, preferred_element_type=jnp.float32
-    )
-    grad_up = jnp.einsum("rd,rf->df", input_two, grad_up_act, preferred_element_type=jnp.float32)
-    grad_input_two = jnp.einsum(
-        "rf,df->rd", grad_gate_act, gate_full, preferred_element_type=jnp.float32
-    ) + jnp.einsum("rf,df->rd", grad_up_act, up_full, preferred_element_type=jnp.float32)
+    unit = row_total // sum(MID_SPLIT)
+    bounds = [0]
+    for share in MID_SPLIT:
+        bounds.append(bounds[-1] + share * unit)
+    pieces = []
+    for index in range(len(MID_SPLIT)):
+        rows = slice(bounds[index], bounds[index + 1])
+        pieces.append(
+            middle_rows(
+                attn_out[rows], tokens_wide[rows], grad_final[rows],
+                output_full, gate_full, up_full, down_full, tp_count,
+            )
+        )
+    grad_gate = sum(piece[6] for piece in pieces)
+    grad_up = sum(piece[7] for piece in pieces)
+    grad_down = sum(piece[8] for piece in pieces)
+    last_sum = pieces[-1][5]
+    (grad_gate, grad_up, grad_down), last_sum = lax.optimization_barrier(
+        ((grad_gate, grad_up, grad_down), last_sum)
+    )
+    pieces[-1][5] = last_sum
     mlp_grads = (
         scatter_low(grad_gate, 0),
         scatter_low(grad_up, 0),
         scatter_low(grad_down, 1),
     )
-    grad_input_two = tp_psum(grad_input_two, tp_count).astype(jnp.float32)
-    grad_resid = grad_final + norm_back(normed_two, scale_two, grad_input_two)
+    resid = jnp.concatenate([piece[0] for piece in pieces], axis=0)
+    branch_two_part = jnp.concatenate([piece[1] for piece in pieces], axis=0)
+    grad_resid_parts = [
+        piece[4]
+        + norm_back(piece[2], piece[3], piece[5].astype(jnp.float32))
+        for piece in pieces
+    ]
+    grad_resid = jnp.concatenate(grad_resid_parts, axis=0)
     grad_resid_low = grad_resid.astype(bf_type)
     grad_wout = jnp.einsum(
         "rc,rd->cd", attn_out, grad_resid_low, preferred_element_type=jnp.float32
@@ -240,6 +310,8 @@
         "rd,cd->rc", grad_resid_low, output_full, preferred_element_type=jnp.float32
     )
     grad_attn = grad_attn.astype(bf_type).reshape(split_heads)
+    branch_two_part, grad_attn = lax.optimization_barrier((branch_two_part, grad_attn))
+    final_sum = resid + tp_psum(branch_two_part, tp_count).astype(jnp.float32)
     seq_index = 0
     grad_queries, grad_keys_seq, grad_values_seq = attend_backward(
         queries[seq_index],
@@ -254,8 +326,12 @@
     key_grads = [grad_keys_seq]
     value_grads = [grad_values_seq]
     grad_keys, grad_values = (
-        lax.psum_scatter(jnp.stack(key_grads), "ctx", scatter_dimension=1, tiled=True),
-        lax.psum_scatter(jnp.stack(value_grads), "ctx", scatter_dimension=1, tiled=True),
+        exchange_scatter(
+            jnp.stack(key_grads).reshape((ctx_count, half_len, head_count, HEAD_DIM)), CTX, ctx_count
+        ).reshape(split_heads),
+        exchange_scatter(
+            jnp.stack(value_grads).reshape((ctx_count, half_len, head_count, HEAD_DIM)), CTX, ctx_count
+        ).reshape(split_heads),
     )
     grad_q_pre = (
         rotate_back(jnp.stack(query_grads), cosine, sine_table)
@@ -274,12 +350,10 @@
         + jnp.einsum("rc,dc->rd", grad_k_pre, key_full, preferred_element_type=jnp.float32)
         + jnp.einsum("rc,dc->rd", grad_v_pre, value_full, preferred_element_type=jnp.float32)
     )
-    attn_grads = (
-        scatter_low(grad_wq, 0),
-        scatter_low(grad_wk, 0),
-        scatter_low(grad_wv, 0),
-        scatter_low(grad_wout, 1),
-    )
+    qkv_grads = jnp.split(
+        scatter_low(jnp.concatenate([grad_wq, grad_wk, grad_wv], axis=1), 0), 3, axis=1
+    )
+    attn_grads = (qkv_grads[0], qkv_grads[1], qkv_grads[2], scatter_low(grad_wout, 1))
     grad_input_one = tp_psum(grad_input_one, tp_count).astype(jnp.float32)
     grad_tokens = grad_resid + norm_back(normed_one, scale_one, grad_input_one)
     output = final_sum.astype(bf_type).reshape(seq_count, half_len, model_width)
@@ -299,30 +373,30 @@
 
 def solution(mesh):
     return jax.shard_map(
-        functools.partial(body, mesh.shape["tp"]),
+        functools.partial(body, mesh.shape[TP], mesh.shape[CTX]),
         mesh=mesh,
         in_specs=(
-            P("shard", "ctx", None),
-            P("shard"),
-            P("shard", "ctx", None),
-            P(("shard", "ctx"), "tp"),
-            P(("shard", "ctx"), "tp"),
-            P(("shard", "ctx"), "tp"),
-            P("tp", ("shard", "ctx")),
-            P(("shard", "ctx"), "tp"),
-            P(("shard", "ctx"), "tp"),
-            P("tp", ("shard", "ctx")),
+            P(SHARD, CTX, None),
+            P(SHARD),
+            P(SHARD, CTX, None),
+            P((SHARD, CTX), TP),
+            P((SHARD, CTX), TP),
+            P((SHARD, CTX), TP),
+            P(TP, (SHARD, CTX)),
+            P((SHARD, CTX), TP),
+            P((SHARD, CTX), TP),
+            P(TP, (SHARD, CTX)),
         ),
         out_specs=(
-            P("shard", "ctx", None),
-            P("shard", "ctx", None),
-            P(("shard", "ctx"), "tp"),
-            P(("shard", "ctx"), "tp"),
-            P(("shard", "ctx"), "tp"),
-            P("tp", ("shard", "ctx")),
-            P(("shard", "ctx"), "tp"),
-            P(("shard", "ctx"), "tp"),
-            P("tp", ("shard", "ctx")),
+            P(SHARD, CTX, None),
+            P(SHARD, CTX, None),
+            P((SHARD, CTX), TP),
+            P((SHARD, CTX), TP),
+            P((SHARD, CTX), TP),
+            P(TP, (SHARD, CTX)),
+            P((SHARD, CTX), TP),
+            P((SHARD, CTX), TP),
+            P(TP, (SHARD, CTX)),
         ),
         check_vma=False,
     )

time: 1420 us -> 1360 us (0.958)
  waiting for transfers between devices: 653 us -> 541 us
  local copies, waits for them, and re-layouts: 74 us -> 143 us
  starting transfers between devices: 211 us -> 153 us
  matrix products: 307 us -> 335 us
    reduce_scatter x9 -> x5, waiting for transfers between devices: 194 us -> 0.01 us  [scatter_low(): lax.psum_scatter(grad.astype(jnp.bfloat16), (SHARD, CTX), scatter_dimensi...]
    ppermute x24 -> x40, waiting for transfers between devices: 405 us -> 477 us  [the longest x18 307 us: tp_psum(): total = total + lax.ppermute(piece, TP, pairs).astype(jnp.float32)]
    ppermute x24 -> x40, starting transfers between devices: 209 us -> 152 us  [the longest x18 82.3 us: tp_psum(): total = total + lax.ppermute(piece, TP, pairs).astype(jnp.float32)]
    dynamic_slice x0 -> x3, local copies, waits for them, and re-layouts: none -> 25.8 us  [the longest x2 19.8 us: exchange_scatter(): total = lax.dynamic_index_in_dim(blocks, me, 0, keepdims=False)]
    dot_general x14 -> x20, matrix products: 130 us -> 150 us  [the longest x2 24.1 us: middle_rows(): jnp.einsum('rf,rd->fd', hidden, grad_branch, preferred_element_type=jnp.f...]
    concatenate x0 -> x3, other arithmetic: none -> 14.7 us  [the longest x1 11.2 us: block(): jnp.concatenate([grad_wq, grad_wk, grad_wv], axis=1)]
    all_gather x9 -> x4, waiting for transfers between devices: 53.1 us -> 61.7 us  [the longest x1 37.1 us: block(): lax.all_gather(mlp_low[2], (SHARD, CTX), axis=1, tiled=True)]
    dot_general x7 -> x11, matrix products: 68.9 us -> 75.9 us  [matmul_low(): return jnp.dot(left, right, preferred_element_type=jnp.float32)]
  transfers between devices with their start and end apart: 42 -> 49, of which waited for: 19 -> 18; matrix products, arithmetic and copies ran while one was open for 23% -> 32% of each run, Pallas kernels for 0% -> 0%
where the time goes in v3:
time: 1360 us; the launch traced here: 1350 us
  waiting for transfers between devices  541 us (40%)
  matrix products  335 us (25%)
  other arithmetic  160 us (12%)
  starting transfers between devices  153 us (11%)
  local copies, waits for them, and re-layouts  143 us (11%)
  between operations  16.5 us (1%)
    ppermute x18, waiting for transfers between devices, tp_psum(): total = total + lax.ppermute(piece, TP, pairs).astype(jnp.float32)  307 us
    ppermute x18, waiting for transfers between devices, tp_psum(): got = lax.ppermute(reduced, TP, pairs)  170 us
    ppermute x18, starting transfers between devices, tp_psum(): total = total + lax.ppermute(piece, TP, pairs).astype(jnp.float32)  82.3 us
    dot_general x11, matrix products, matmul_low(): return jnp.dot(left, right, preferred_element_type=jnp.float32)  75.9 us
    ppermute x18, starting transfers between devices, tp_psum(): got = lax.ppermute(reduced, TP, pairs)  68.9 us
    all_gather x1, waiting for transfers between devices, block(): lax.all_gather(mlp_low[2], (SHARD, CTX), axis=1, tiled=True)  37.1 us
    convert_element_type x2, other arithmetic, one_block(): grad_scores = (probability * (grad_prob - inner_sum)).astype(jnp.bfloat16)  29.7 us
  transfers between devices with their start and end apart: 49, of which 18 were waited for; matrix products, arithmetic and copies ran while one was open for 32% of the time, Pallas kernels for 0%

profile of v3, /device:TPU:0, one launch (start us, length us, event | category | flops | bytes accessed | tf_op | source)
XLA Modules:
  0.0 1352.5 jit_solution(1291228818926174938)
XLA Ops:
  47.2 24.6 %all-gather.5.cloned.1.call-done = bf16[2048,2048]{0,1:T(8,128)(2,1)} async-done(((bf16[256,2048]{0,1:T(8,128)(2,1)}), bf16[2048,2048]{0,1:T(8,128)(2,1)}) %all-gather.5.cloned.1.call-update) | async-done | bytes 8388624 | tf_op jit(solution)/shard_map/all_gather | solution.py:229
  93.1 37.1 %all-gather.11.cloned.1.call-done = bf16[2048,2048]{1,0:T(8,128)(2,1)} async-done(((bf16[2048,256]{1,0:T(8,128)(2,1)}), bf16[2048,2048]{1,0:T(8,128)(2,1)}) %all-gather.11.cloned.1.call-update) | async-done | bytes 8388624 | tf_op jit(solution)/shard_map/all_gather | solution.py:240
  130.1 11.4 fusion.126
  181.2 35.0 %while.27 = (s32[]{:T(128)}, bf16[2,512,4,128]{3,2,1,0:T(4,128)(2,1)}, f32[2,4,512]{2,1,0:T(4,128)S(1)}, s32[2]{0:T(128)S(1)}, s32[]{:T(128)}, /*index=5*/s32[]{...) while((s32[]{:T(128)}, ...), condition=%wide.region_5.6_spmd, body=%wide.region_2.5_spmd.sunk | while | flops 2195980800 | bytes 77668600 | solution.py:77
  242.2 73.0 %collective-permute-done.3 = bf16[96,2048]{1,0:T(8,128)(2,1)S(1)} collective-permute-done((bf16[96,2048]{1,0:T(8,128)(2,1)S(1)}, bf16[96,2048]{1,0:T(8,128)(2,1)S(1)}, u32[]{:S(2)}, u32[]{:S(2)}) %collective-permute-start.3) | collective-permute-done | bytes 393248 | tf_op jit(solution)/shard_map/ppermute | solution.py:128
  329.7 16.8 %collective-permute-done.6 = bf16[96,2048]{1,0:T(8,128)(2,1)S(1)} collective-permute-done((bf16[96,2048]{1,0:T(8,128)(2,1)S(1)}, bf16[96,2048]{1,0:T(8,128)(2,1)S(1)}, u32[]{:S(2)}, u32[]{:S(2)}) %collective-permute-start.6) | collective-permute-done | bytes 393248 | tf_op jit(solution)/shard_map/ppermute | solution.py:134
  393.7 26.1 %collective-permute-start.15 = (bf16[96,2048]{1,0:T(8,128)(2,1)S(1)}, bf16[96,2048]{1,0:T(8,128)(2,1)S(1)}, u32[]{:S(2)}, u32[]{:S(2)}) collective-permute-start(bf16[96,2048]{1,0:T(8,128)(2,1)S(1)} %get-tuple-element.362), channel_id=1, source_target_pairs={{0,2},{1,3},{2,0},{3,1},{4,6},{5,7},{6,4},{7,5},{8,10},{9,11},{10,... | collective-permute-start | bytes 1179656 | tf_op jit(solution)/shard_map/ppermute | solution.py:128
  431.9 23.3 %collective-permute-done.15 = bf16[96,2048]{1,0:T(8,128)(2,1)S(1)} collective-permute-done((bf16[96,2048]{1,0:T(8,128)(2,1)S(1)}, bf16[96,2048]{1,0:T(8,128)(2,1)S(1)}, u32[]{:S(2)}, u32[]{:S(2)}) %collective-permute-start.15) | collective-permute-done | bytes 393248 | tf_op jit(solution)/shard_map/ppermute | solution.py:128
  486.2 12.0 multiply_convert_fusion.2
  519.1 13.1 fusion.169
  542.4 13.1 fusion.125
  584.3 16.1 %collective-permute-start.21 = (bf16[160,2048]{1,0:T(8,128)(2,1)S(1)}, bf16[160,2048]{1,0:T(8,128)(2,1)S(1)}, u32[]{:S(2)}, u32[]{:S(2)}) collective-permute-start(bf16[160,2048]{1,0:T(8,128)(2,1)S(1)} %get-tuple-element.346), channel_id=1, source_target_pairs={{0,2},{1,3},{2,0},{3,1},{4,6},{5,7},{6,4},{7,5},{8,10},{9,11},{10,... | collective-permute-start | bytes 1966088 | tf_op jit(solution)/shard_map/ppermute | solution.py:128
  616.0 39.1 %collective-permute-done.21 = bf16[160,2048]{1,0:T(8,128)(2,1)S(1)} collective-permute-done((bf16[160,2048]{1,0:T(8,128)(2,1)S(1)}, bf16[160,2048]{1,0:T(8,128)(2,1)S(1)}, u32[]{:S(2)}, u32[]{:S(2)}) %collective-permute-start.21) | collective-permute-done | bytes 655392 | tf_op jit(solution)/shard_map/ppermute | solution.py:128
  661.0 14.5 %collective-permute-done.23 = bf16[160,2048]{1,0:T(8,128)(2,1)S(1)} collective-permute-done((bf16[160,2048]{1,0:T(8,128)(2,1)S(1)}, bf16[160,2048]{1,0:T(8,128)(2,1)S(1)}, u32[]{:S(2)}, u32[]{:S(2)}) %collective-permute-start.23) | collective-permute-done | bytes 655392 | tf_op jit(solution)/shard_map/ppermute | solution.py:134
  675.6 24.3 %collective-permute-done.24 = bf16[160,2048]{1,0:T(8,128)(2,1)S(1)} collective-permute-done((bf16[160,2048]{1,0:T(8,128)(2,1)S(1)}, bf16[160,2048]{1,0:T(8,128)(2,1)S(1)}, u32[]{:S(2)}, u32[]{:S(2)}) %collective-permute-start.24) | collective-permute-done | bytes 655392 | tf_op jit(solution)/shard_map/ppermute | solution.py:134
  711.2 130.1 %while.28 = (s32[]{:T(128)}, f32[2048,4,128]{0,2,1:T(8,128)}, f32[2048,4,128]{0,2,1:T(8,128)}, f32[2,512,4,128]{3,1,2,0:T(8,128)}, bf16[2,512,4,128]{3,1,2,0:T(8...) while((s32[]{:T(128)}, f32[2048,4,128]{0,2,1:T(8,128)}, ...), condition=%wide.region_16.17_spmd.clone, body=%wide.region_14.16_spmd.clone.sunk | while | flops 5439226368 | bytes 198246768 | solution.py:113
  723.5 12.9 multiply_reduce_fusion.5
  736.4 14.8 %multiply_convert_fusion.13 = bf16[4,512,2048]{2,1,0:T(8,128)(2,1)} fusion(f32[4,512,2048]{2,1,0:T(8,128)} %get-tuple-element.515, f32[4,512,2048]{2,1,0:T(8,128)} %fusion.246, f32[4,512]{1,0:T(4,128)S(1)} %get-tuple-element.516, f32[4,512]{1,0:T(4,128)S(1)} %dynamic-slice_bitcast_fusion.20, pred[512,2048]{1,0:T(8,128)(4,1)S(1)} %fusion.247), kind=kLoop, calls=%fused_computation.21.clone.1 | loop fusion | flops 25165824 | bytes 43008000 | tf_op jit(solution)/shard_map/while/body/eval_jaxpr/convert_element_type | solution.py:98
  758.6 12.9 bitcast_add_fusion.7
  787.1 12.9 multiply_reduce_fusion.5
  800.0 14.8 %multiply_convert_fusion.13 = bf16[4,512,2048]{2,1,0:T(8,128)(2,1)} fusion(f32[4,512,2048]{2,1,0:T(8,128)} %get-tuple-element.515, f32[4,512,2048]{2,1,0:T(8,128)} %fusion.246, f32[4,512]{1,0:T(4,128)S(1)} %get-tuple-element.516, f32[4,512]{1,0:T(4,128)S(1)} %dynamic-slice_bitcast_fusion.20, pred[512,2048]{1,0:T(8,128)(4,1)S(1)} %fusion.247), kind=kLoop, calls=%fused_computation.21.clone.1 | loop fusion | flops 25165824 | bytes 43008000 | tf_op jit(solution)/shard_map/while/body/eval_jaxpr/convert_element_type | solution.py:98
  823.4 14.1 %bitcast_add_fusion.7 = f32[2048,4,128]{0,2,1:T(8,128)} fusion(f32[2048,4,128]{0,2,1:T(8,128)} %get-tuple-element.567, f32[4,512,2048]{2,1,0:T(8,128)} %fusion.246, f32[4,512]{1,0:T(4,128)S(1)} %dynamic-slice_bitcast_fusion.20, pred[512,2048]{1,0:T(8,128)(4,1)S(1)} %fusion.247, pred[]{:T(512)S(6)} %compare.11, ...), kind=kOutput, calls=%fused_computation.27.clone.1 | convolution fusion | flops 1092616192 | bytes 26746884 | tf_op jit(solution)/shard_map/while/body/eval_jaxpr/hqk,qhd->khd/dot_general | solution.py:107
  856.2 13.8 %constant_dynamic-slice_fusion.1 = (f32[1,1024,4,128]{1,0,3,2:T(1,128)}, f32[1,1024,4,128]{1,0,3,2:T(1,128)}, f32[1,1024,4,128]{1,0,3,2:T(1,128)}, f32[1,1024,4,128]{1,0,3,2:T(1,128)}) fusion(f32[2,1024,4,128]{1,0,3,2:T(2,128)} %reshape_stack.7, s32[]{:T(128)S(6)} %select_n.195, s32[]{:T(128)S(6)} %select_n.197, f32[2,1024,4,128]{1,0,3,2:T(2,128)} %reshape_stack.6), kind=kLoop, calls=%fused_computation.245 | loop fusion | bytes 16777224 | tf_op jit(solution)/shard_map/jit(dynamic_index_in_dim)/dynamic_slice | solution.py:154
  932.1 12.9 collective-permute-start.28
  955.3 14.4 %collective-permute-done.28 = bf16[256,2048]{1,0:T(8,128)(2,1)} collective-permute-done((bf16[256,2048]{1,0:T(8,128)(2,1)}, bf16[256,2048]{1,0:T(8,128)(2,1)}, u32[]{:S(2)}, u32[]{:S(2)}) %collective-permute-start.28) | collective-permute-done | bytes 1048608 | tf_op jit(solution)/shard_map/ppermute | solution.py:128
  969.7 68.6 %collective-permute-done.27 = bf16[256,2048]{1,0:T(8,128)(2,1)} collective-permute-done((bf16[256,2048]{1,0:T(8,128)(2,1)}, bf16[256,2048]{1,0:T(8,128)(2,1)}, u32[]{:S(2)}, u32[]{:S(2)}) %collective-permute-start.27) | collective-permute-done | bytes 1048608 | tf_op jit(solution)/shard_map/ppermute | solution.py:128
  1073.6 20.6 %collective-permute-start.31 = (bf16[256,2048]{1,0:T(8,128)(2,1)}, bf16[256,2048]{1,0:T(8,128)(2,1)S(1)}, u32[]{:S(2)}, u32[]{:S(2)}) collective-permute-start(bf16[256,2048]{1,0:T(8,128)(2,1)} %get-tuple-element.311), channel_id=1, source_target_pairs={{0,3},{1,0},{2,1},{3,2},{4,7},{5,4},{6,5},{7,6},{8,11},{9,8},{10,9... | collective-permute-start | bytes 3145736 | tf_op jit(solution)/shard_map/ppermute | solution.py:134
  1096.8 87.6 %collective-permute-done.35 = bf16[256,2048]{1,0:T(8,128)(2,1)S(1)} collective-permute-done((bf16[256,2048]{1,0:T(8,128)(2,1)}, bf16[256,2048]{1,0:T(8,128)(2,1)S(1)}, u32[]{:S(2)}, u32[]{:S(2)}) %collective-permute-start.35) | collective-permute-done | bytes 1048608 | tf_op jit(solution)/shard_map/ppermute | solution.py:128
  1190.9 21.3 %collective-permute-start.37 = (bf16[256,2048]{1,0:T(8,128)(2,1)}, bf16[256,2048]{1,0:T(8,128)(2,1)S(1)}, u32[]{:S(2)}, u32[]{:S(2)}) collective-permute-start(bf16[256,2048]{1,0:T(8,128)(2,1)} %get-tuple-element.309), channel_id=1, source_target_pairs={{0,1},{1,2},{2,3},{3,0},{4,5},{5,6},{6,7},{7,4},{8,9},{9,10},{10,1... | collective-permute-start | bytes 3145736 | tf_op jit(solution)/shard_map/ppermute | solution.py:134
  1212.2 17.2 %collective-permute-done.30 = bf16[256,2048]{1,0:T(8,128)(2,1)S(1)} collective-permute-done((bf16[256,2048]{1,0:T(8,128)(2,1)}, bf16[256,2048]{1,0:T(8,128)(2,1)S(1)}, u32[]{:S(2)}, u32[]{:S(2)}) %collective-permute-start.30) | collective-permute-done | bytes 1048608 | tf_op jit(solution)/shard_map/ppermute | solution.py:134
  1240.5 56.3 %collective-permute-done.38 = bf16[256,2048]{1,0:T(8,128)(2,1)S(1)} collective-permute-done((bf16[256,2048]{1,0:T(8,128)(2,1)}, bf16[256,2048]{1,0:T(8,128)(2,1)S(1)}, u32[]{:S(2)}, u32[]{:S(2)}) %collective-permute-start.38) | collective-permute-done | bytes 1048608 | tf_op jit(solution)/shard_map/ppermute | solution.py:134
  1297.9 21.3 %collective-permute-done.39 = bf16[256,2048]{1,0:T(8,128)(2,1)S(1)} collective-permute-done((bf16[256,2048]{1,0:T(8,128)(2,1)}, bf16[256,2048]{1,0:T(8,128)(2,1)S(1)}, u32[]{:S(2)}, u32[]{:S(2)}) %collective-permute-start.39) | collective-permute-done | bytes 1048608 | tf_op jit(solution)/shard_map/ppermute | solution.py:134
  (503 shorter events, 571.3 us)
Async XLA Ops:
  7.2 64.6 %all-gather.5.cloned.1.call-start = ((), (), s32[]{:S(2)}) async-start(), calls=%async_computation.5 | async-start | bytes 9437184 | tf_op jit(solution)/shard_map/all_gather | solution.py:229
  13.1 117.1 %all-gather.11.cloned.1.call-start = ((), (), s32[]{:S(2)}) async-start(), calls=%async_computation.8 | async-start | bytes 9437184 | tf_op jit(solution)/shard_map/all_gather | solution.py:240
  14.2 337.4 %all-gather.9.cloned.1.call-start = ((), (), s32[]{:S(2)}) async-start(), calls=%async_computation.7 | async-start | bytes 9437184 | tf_op jit(solution)/shard_map/all_gather | solution.py:239
  17.1 342.9 %all-gather.7.cloned.1.call-start = ((), (), s32[]{:S(2)}) async-start(), calls=%async_computation.6 | async-start | bytes 9437184 | tf_op jit(solution)/shard_map/all_gather | solution.py:238
  18.3 1219.3 %reduce-scatter.8.cloned.1.call-start = ((), (), s32[]{:S(2)}) async-start(), calls=%async_computation.10 | async-start | bytes 2359296 | tf_op jit(solution)/shard_map/reduce_scatter | solution.py:163
  80.5 93.4 %collective-permute-start = (bf16[1,1024,4,128]{1,3,2,0:T(8,128)(2,1)}, bf16[1,1024,4,128]{1,3,2,0:T(8,128)(2,1)}, u32[]{:S(2)}, u32[]{:S(2)}) collective-permute-start(bf16[1,1024,4,128]{1,3,2,0:T(8,128)(2,1)} %fusion.84), channel_id=1, source_target_pairs={{0,4},{4,0},{1,5},{5,1},{2,6},{6,2},{3,7},{7,3},{8,12},{12,8},{9,1... | collective-permute-start | bytes 3145736 | tf_op jit(solution)/shard_map/ppermute | solution.py:147
  89.1 89.4 %collective-permute-start.1 = (bf16[1,1024,4,128]{3,1,2,0:T(8,128)(2,1)}, bf16[1,1024,4,128]{3,1,2,0:T(8,128)(2,1)}, u32[]{:S(2)}, u32[]{:S(2)}) collective-permute-start(bf16[1,1024,4,128]{3,1,2,0:T(8,128)(2,1)} %bitcast.21), channel_id=1, source_target_pairs={{0,4},{4,0},{1,5},{5,1},{2,6},{6,2},{3,7},{7,3},{8,12},{12,8},{9,1... | collective-permute-start | bytes 3145736 | tf_op jit(solution)/shard_map/ppermute | solution.py:147
  228.3 91.0 %collective-permute-start.10 = (bf16[160,2048]{1,0:T(8,128)(2,1)S(1)}, bf16[160,2048]{1,0:T(8,128)(2,1)S(1)}, u32[]{:S(2)}, u32[]{:S(2)}) collective-permute-start(bf16[160,2048]{1,0:T(8,128)(2,1)S(1)} %get-tuple-element.348), channel_id=1, source_target_pairs={{0,3},{1,0},{2,1},{3,2},{4,7},{5,4},{6,5},{7,6},{8,11},{9,8},{10,9... | collective-permute-start | bytes 1966088 | tf_op jit(solution)/shard_map/ppermute | solution.py:128
  229.2 93.3 %collective-permute-start.9 = (bf16[160,2048]{1,0:T(8,128)(2,1)S(1)}, bf16[160,2048]{1,0:T(8,128)(2,1)S(1)}, u32[]{:S(2)}, u32[]{:S(2)}) collective-permute-start(bf16[160,2048]{1,0:T(8,128)(2,1)S(1)} %get-tuple-element.349), channel_id=1, source_target_pairs={{0,2},{1,3},{2,0},{3,1},{4,6},{5,7},{6,4},{7,5},{8,10},{9,11},{10,... | collective-permute-start | bytes 1966088 | tf_op jit(solution)/shard_map/ppermute | solution.py:128
  229.2 93.3 %collective-permute-start.8 = (bf16[160,2048]{1,0:T(8,128)(2,1)S(1)}, bf16[160,2048]{1,0:T(8,128)(2,1)S(1)}, u32[]{:S(2)}, u32[]{:S(2)}) collective-permute-start(bf16[160,2048]{1,0:T(8,128)(2,1)S(1)} %get-tuple-element.347), channel_id=1, source_target_pairs={{0,1},{1,2},{2,3},{3,0},{4,5},{5,6},{6,7},{7,4},{8,9},{9,10},{10,1... | collective-permute-start | bytes 1966088 | tf_op jit(solution)/shard_map/ppermute | solution.py:128
  230.3 84.9 %collective-permute-start.3 = (bf16[96,2048]{1,0:T(8,128)(2,1)S(1)}, bf16[96,2048]{1,0:T(8,128)(2,1)S(1)}, u32[]{:S(2)}, u32[]{:S(2)}) collective-permute-start(bf16[96,2048]{1,0:T(8,128)(2,1)S(1)} %get-tuple-element.365), channel_id=1, source_target_pairs={{0,2},{1,3},{2,0},{3,1},{4,6},{5,7},{6,4},{7,5},{8,10},{9,11},{10,... | collective-permute-start | bytes 1179656 | tf_op jit(solution)/shard_map/ppermute | solution.py:128
  234.5 80.8 %collective-permute-start.2 = (bf16[96,2048]{1,0:T(8,128)(2,1)S(1)}, bf16[96,2048]{1,0:T(8,128)(2,1)S(1)}, u32[]{:S(2)}, u32[]{:S(2)}) collective-permute-start(bf16[96,2048]{1,0:T(8,128)(2,1)S(1)} %get-tuple-element.363), channel_id=1, source_target_pairs={{0,1},{1,2},{2,3},{3,0},{4,5},{5,6},{6,7},{7,4},{8,9},{9,10},{10,1... | collective-permute-start | bytes 1179656 | tf_op jit(solution)/shard_map/ppermute | solution.py:128
  324.3 137.4 %collective-permute-start.11 = (bf16[160,2048]{1,0:T(8,128)(2,1)}, bf16[160,2048]{1,0:T(8,128)(2,1)}, u32[]{:S(2)}, u32[]{:S(2)}) collective-permute-start(bf16[160,2048]{1,0:T(8,128)(2,1)} %get-tuple-element.323), channel_id=1, source_target_pairs={{0,1},{1,2},{2,3},{3,0},{4,5},{5,6},{6,7},{7,4},{8,9},{9,10},{10,1... | collective-permute-start | bytes 1966088 | tf_op jit(solution)/shard_map/ppermute | solution.py:134
  324.3 141.4 %collective-permute-start.12 = (bf16[160,2048]{1,0:T(8,128)(2,1)}, bf16[160,2048]{1,0:T(8,128)(2,1)}, u32[]{:S(2)}, u32[]{:S(2)}) collective-permute-start(bf16[160,2048]{1,0:T(8,128)(2,1)} %get-tuple-element.323), channel_id=1, source_target_pairs={{0,2},{1,3},{2,0},{3,1},{4,6},{5,7},{6,4},{7,5},{8,10},{9,11},{10,... | collective-permute-start | bytes 1966088 | tf_op jit(solution)/shard_map/ppermute | solution.py:134
  393.7 61.4 %collective-permute-start.15 = (bf16[96,2048]{1,0:T(8,128)(2,1)S(1)}, bf16[96,2048]{1,0:T(8,128)(2,1)S(1)}, u32[]{:S(2)}, u32[]{:S(2)}) collective-permute-start(bf16[96,2048]{1,0:T(8,128)(2,1)S(1)} %get-tuple-element.362), channel_id=1, source_target_pairs={{0,2},{1,3},{2,0},{3,1},{4,6},{5,7},{6,4},{7,5},{8,10},{9,11},{10,... | collective-permute-start | bytes 1179656 | tf_op jit(solution)/shard_map/ppermute | solution.py:128
  456.4 154.6 %collective-permute-start.17 = (bf16[96,2048]{1,0:T(8,128)(2,1)}, bf16[96,2048]{1,0:T(8,128)(2,1)}, u32[]{:S(2)}, u32[]{:S(2)}) collective-permute-start(bf16[96,2048]{1,0:T(8,128)(2,1)} %get-tuple-element.313), channel_id=1, source_target_pairs={{0,1},{1,2},{2,3},{3,0},{4,5},{5,6},{6,7},{7,4},{8,9},{9,10},{10,1... | collective-permute-start | bytes 1179656 | tf_op jit(solution)/shard_map/ppermute | solution.py:134
  459.7 153.1 %collective-permute-start.18 = (bf16[96,2048]{1,0:T(8,128)(2,1)}, bf16[96,2048]{1,0:T(8,128)(2,1)}, u32[]{:S(2)}, u32[]{:S(2)}) collective-permute-start(bf16[96,2048]{1,0:T(8,128)(2,1)} %get-tuple-element.313), channel_id=1, source_target_pairs={{0,2},{1,3},{2,0},{3,1},{4,6},{5,7},{6,4},{7,5},{8,10},{9,11},{10,... | collective-permute-start | bytes 1179656 | tf_op jit(solution)/shard_map/ppermute | solution.py:134
  461.6 152.2 %collective-permute-start.19 = (bf16[96,2048]{1,0:T(8,128)(2,1)}, bf16[96,2048]{1,0:T(8,128)(2,1)}, u32[]{:S(2)}, u32[]{:S(2)}) collective-permute-start(bf16[96,2048]{1,0:T(8,128)(2,1)} %get-tuple-element.313), channel_id=1, source_target_pairs={{0,3},{1,0},{2,1},{3,2},{4,7},{5,4},{6,5},{7,6},{8,11},{9,8},{10,9... | collective-permute-start | bytes 1179656 | tf_op jit(solution)/shard_map/ppermute | solution.py:134
  584.3 70.9 %collective-permute-start.21 = (bf16[160,2048]{1,0:T(8,128)(2,1)S(1)}, bf16[160,2048]{1,0:T(8,128)(2,1)S(1)}, u32[]{:S(2)}, u32[]{:S(2)}) collective-permute-start(bf16[160,2048]{1,0:T(8,128)(2,1)S(1)} %get-tuple-element.346), channel_id=1, source_target_pairs={{0,2},{1,3},{2,0},{3,1},{4,6},{5,7},{6,4},{7,5},{8,10},{9,11},{10,... | collective-permute-start | bytes 1966088 | tf_op jit(solution)/shard_map/ppermute | solution.py:128
  894.9 438.3 %reduce-scatter.6.cloned.1.call-start = ((), (), s32[]{:S(2)}) async-start(), calls=%async_computation.9 | async-start | bytes 7077888 | tf_op jit(solution)/shard_map/reduce_scatter | solution.py:163
  926.2 411.2 %reduce-scatter.10.cloned.1.call-start = ((), (), s32[]{:S(2)}) async-start(), calls=%async_computation.11 | async-start | bytes 9437184 | tf_op jit(solution)/shard_map/reduce_scatter | solution.py:163
  927.0 413.2 %reduce-scatter.12.cloned.1.call-start = ((), (), s32[]{:S(2)}) async-start(), calls=%async_computation.12 | async-start | bytes 9437184 | tf_op jit(solution)/shard_map/reduce_scatter | solution.py:163
  927.7 415.3 %reduce-scatter.14.cloned.1.call-start = ((), (), s32[]{:S(2)}) async-start(), calls=%async_computation.13 | async-start | bytes 9437184 | tf_op jit(solution)/shard_map/reduce_scatter | solution.py:163
  945.0 93.3 %collective-permute-start.27 = (bf16[256,2048]{1,0:T(8,128)(2,1)}, bf16[256,2048]{1,0:T(8,128)(2,1)}, u32[]{:S(2)}, u32[]{:S(2)}) collective-permute-start(bf16[256,2048]{1,0:T(8,128)(2,1)} %get-tuple-element.343), channel_id=1, source_target_pairs={{0,2},{1,3},{2,0},{3,1},{4,6},{5,7},{6,4},{7,5},{8,10},{9,11},{10,... | collective-permute-start | bytes 3145736 | tf_op jit(solution)/shard_map/ppermute | solution.py:128
  947.5 90.8 %collective-permute-start.26 = (bf16[256,2048]{1,0:T(8,128)(2,1)}, bf16[256,2048]{1,0:T(8,128)(2,1)}, u32[]{:S(2)}, u32[]{:S(2)}) collective-permute-start(bf16[256,2048]{1,0:T(8,128)(2,1)} %get-tuple-element.341), channel_id=1, source_target_pairs={{0,1},{1,2},{2,3},{3,0},{4,5},{5,6},{6,7},{7,4},{8,9},{9,10},{10,1... | collective-permute-start | bytes 3145736 | tf_op jit(solution)/shard_map/ppermute | solution.py:128
  1061.0 123.5 %collective-permute-start.35 = (bf16[256,2048]{1,0:T(8,128)(2,1)}, bf16[256,2048]{1,0:T(8,128)(2,1)S(1)}, u32[]{:S(2)}, u32[]{:S(2)}) collective-permute-start(bf16[256,2048]{1,0:T(8,128)(2,1)} %get-tuple-element.336), channel_id=1, source_target_pairs={{0,2},{1,3},{2,0},{3,1},{4,6},{5,7},{6,4},{7,5},{8,10},{9,11},{10,... | collective-permute-start | bytes 3145736 | tf_op jit(solution)/shard_map/ppermute | solution.py:128
  1061.0 123.5 %collective-permute-start.34 = (bf16[256,2048]{1,0:T(8,128)(2,1)}, bf16[256,2048]{1,0:T(8,128)(2,1)}, u32[]{:S(2)}, u32[]{:S(2)}) collective-permute-start(bf16[256,2048]{1,0:T(8,128)(2,1)} %get-tuple-element.334), channel_id=1, source_target_pairs={{0,1},{1,2},{2,3},{3,0},{4,5},{5,6},{6,7},{7,4},{8,9},{9,10},{10,1... | collective-permute-start | bytes 3145736 | tf_op jit(solution)/shard_map/ppermute | solution.py:128
  1061.5 167.8 %collective-permute-start.30 = (bf16[256,2048]{1,0:T(8,128)(2,1)}, bf16[256,2048]{1,0:T(8,128)(2,1)S(1)}, u32[]{:S(2)}, u32[]{:S(2)}) collective-permute-start(bf16[256,2048]{1,0:T(8,128)(2,1)} %get-tuple-element.311), channel_id=1, source_target_pairs={{0,2},{1,3},{2,0},{3,1},{4,6},{5,7},{6,4},{7,5},{8,10},{9,11},{10,... | collective-permute-start | bytes 3145736 | tf_op jit(solution)/shard_map/ppermute | solution.py:134
  1073.6 156.8 %collective-permute-start.31 = (bf16[256,2048]{1,0:T(8,128)(2,1)}, bf16[256,2048]{1,0:T(8,128)(2,1)S(1)}, u32[]{:S(2)}, u32[]{:S(2)}) collective-permute-start(bf16[256,2048]{1,0:T(8,128)(2,1)} %get-tuple-element.311), channel_id=1, source_target_pairs={{0,3},{1,0},{2,1},{3,2},{4,7},{5,4},{6,5},{7,6},{8,11},{9,8},{10,9... | collective-permute-start | bytes 3145736 | tf_op jit(solution)/shard_map/ppermute | solution.py:134
  1190.9 48.5 %collective-permute-start.37 = (bf16[256,2048]{1,0:T(8,128)(2,1)}, bf16[256,2048]{1,0:T(8,128)(2,1)S(1)}, u32[]{:S(2)}, u32[]{:S(2)}) collective-permute-start(bf16[256,2048]{1,0:T(8,128)(2,1)} %get-tuple-element.309), channel_id=1, source_target_pairs={{0,1},{1,2},{2,3},{3,0},{4,5},{5,6},{6,7},{7,4},{8,9},{9,10},{10,1... | collective-permute-start | bytes 3145736 | tf_op jit(solution)/shard_map/ppermute | solution.py:134
  1230.4 66.4 %collective-permute-start.38 = (bf16[256,2048]{1,0:T(8,128)(2,1)}, bf16[256,2048]{1,0:T(8,128)(2,1)S(1)}, u32[]{:S(2)}, u32[]{:S(2)}) collective-permute-start(bf16[256,2048]{1,0:T(8,128)(2,1)} %get-tuple-element.309), channel_id=1, source_target_pairs={{0,2},{1,3},{2,0},{3,1},{4,6},{5,7},{6,4},{7,5},{8,10},{9,11},{10,... | collective-permute-start | bytes 3145736 | tf_op jit(solution)/shard_map/ppermute | solution.py:134
  1231.5 87.7 %collective-permute-start.39 = (bf16[256,2048]{1,0:T(8,128)(2,1)}, bf16[256,2048]{1,0:T(8,128)(2,1)S(1)}, u32[]{:S(2)}, u32[]{:S(2)}) collective-permute-start(bf16[256,2048]{1,0:T(8,128)(2,1)} %get-tuple-element.309), channel_id=1, source_target_pairs={{0,3},{1,0},{2,1},{3,2},{4,7},{5,4},{6,5},{7,6},{8,11},{9,8},{10,9... | collective-permute-start | bytes 3145736 | tf_op jit(solution)/shard_map/ppermute | solution.py:134
  (118 other events, 1853.2 us)
Sparse Core Ops, SparseCore 0:
  13.2 58.5 all-gather.4
  74.2 55.8 all-gather.10
  132.0 54.2 all-gather.8
  188.1 54.2 all-gather.6
  895.0 51.3 reduce-scatter.7
  949.7 61.5 reduce-scatter.5
  1014.7 71.5 reduce-scatter.9
  1089.7 71.4 reduce-scatter.11
  1164.7 71.2 reduce-scatter.13

commit v4 on v3

--- a/solution.py
+++ b/solution.py
@@ -296,20 +296,20 @@
     )
     resid = jnp.concatenate([piece[0] for piece in pieces], axis=0)
     branch_two_part = jnp.concatenate([piece[1] for piece in pieces], axis=0)
-    grad_resid_parts = [
-        piece[4]
-        + norm_back(piece[2], piece[3], piece[5].astype(jnp.float32))
-        for piece in pieces
-    ]
+    grad_resid_parts, grad_attn_parts, grad_wout = [], [], 0.0
+    for index, piece in enumerate(pieces):
+        grad_resid_part = piece[4] + norm_back(piece[2], piece[3], piece[5].astype(jnp.float32))
+        resid_low = grad_resid_part.astype(bf_type)
+        grad_wout = grad_wout + jnp.einsum(
+            "rc,rd->cd", attn_out[bounds[index]:bounds[index + 1]], resid_low,
+            preferred_element_type=jnp.float32,
+        )
+        grad_attn_parts.append(
+            jnp.einsum("rd,cd->rc", resid_low, output_full, preferred_element_type=jnp.float32)
+        )
+        grad_resid_parts.append(grad_resid_part)
     grad_resid = jnp.concatenate(grad_resid_parts, axis=0)
-    grad_resid_low = grad_resid.astype(bf_type)
-    grad_wout = jnp.einsum(
-        "rc,rd->cd", attn_out, grad_resid_low, preferred_element_type=jnp.float32
-    )
-    grad_attn = jnp.einsum(
-        "rd,cd->rc", grad_resid_low, output_full, preferred_element_type=jnp.float32
-    )
-    grad_attn = grad_attn.astype(bf_type).reshape(split_heads)
+    grad_attn = jnp.concatenate(grad_attn_parts, axis=0).astype(bf_type).reshape(split_heads)
     branch_two_part, grad_attn = lax.optimization_barrier((branch_two_part, grad_attn))
     final_sum = resid + tp_psum(branch_two_part, tp_count).astype(jnp.float32)
     seq_index = 0

time: 1360 us -> 1370 us (level)
  transfers between devices with their start and end apart: 49 -> 49, of which waited for: 18 -> 18; matrix products, arithmetic and copies ran while one was open for 32% -> 33% of each run, Pallas kernels for 0% -> 0%
where the time goes in v4:
time: 1370 us; the launch traced here: 1360 us
  waiting for transfers between devices  529 us (39%)
  matrix products  342 us (25%)
  other arithmetic  169 us (12%)
  starting transfers between devices  152 us (11%)
  local copies, waits for them, and re-layouts  148 us (11%)
  between operations  16.6 us (1%)
    ppermute x18, waiting for transfers between devices, tp_psum(): total = total + lax.ppermute(piece, TP, pairs).astype(jnp.float32)  306 us
    ppermute x18, waiting for transfers between devices, tp_psum(): got = lax.ppermute(reduced, TP, pairs)  160 us
    ppermute x18, starting transfers between devices, tp_psum(): total = total + lax.ppermute(piece, TP, pairs).astype(jnp.float32)  80.4 us
    dot_general x11, matrix products, matmul_low(): return jnp.dot(left, right, preferred_element_type=jnp.float32)  75.9 us
    ppermute x18, starting transfers between devices, tp_psum(): got = lax.ppermute(reduced, TP, pairs)  69.5 us
    all_gather x1, waiting for transfers between devices, block(): lax.all_gather(mlp_low[2], (SHARD, CTX), axis=1, tiled=True)  37.1 us
    convert_element_type x2, other arithmetic, one_block(): grad_scores = (probability * (grad_prob - inner_sum)).astype(jnp.bfloat16)  29.7 us
  transfers between devices with their start and end apart: 49, of which 18 were waited for; matrix products, arithmetic and copies ran while one was open for 33% of the time, Pallas kernels for 0%

profile of v4, /device:TPU:0, one launch (start us, length us, event | category | flops | bytes accessed | tf_op | source)
XLA Modules:
  0.0 1360.5 jit_solution(11768932381036728288)
XLA Ops:
  47.3 24.5 %all-gather.5.cloned.1.call-done = bf16[2048,2048]{0,1:T(8,128)(2,1)} async-done(((bf16[256,2048]{0,1:T(8,128)(2,1)}), bf16[2048,2048]{0,1:T(8,128)(2,1)}) %all-gather.5.cloned.1.call-update) | async-done | bytes 8388624 | tf_op jit(solution)/shard_map/all_gather | solution.py:229
  93.1 37.1 %all-gather.11.cloned.1.call-done = bf16[2048,2048]{1,0:T(8,128)(2,1)} async-done(((bf16[2048,256]{1,0:T(8,128)(2,1)}), bf16[2048,2048]{1,0:T(8,128)(2,1)}) %all-gather.11.cloned.1.call-update) | async-done | bytes 8388624 | tf_op jit(solution)/shard_map/all_gather | solution.py:240
  130.1 11.3 fusion.133
  181.2 34.9 %while.27 = (s32[]{:T(128)}, bf16[2,512,4,128]{3,2,1,0:T(4,128)(2,1)}, f32[2,4,512]{2,1,0:T(4,128)S(1)}, s32[2]{0:T(128)S(1)}, s32[]{:T(128)}, /*index=5*/s32[]{...) while((s32[]{:T(128)}, ...), condition=%wide.region_5.6_spmd, body=%wide.region_2.5_spmd.sunk | while | flops 2195980800 | bytes 77668600 | solution.py:77
  242.3 73.0 %collective-permute-done.3 = bf16[96,2048]{1,0:T(8,128)(2,1)S(1)} collective-permute-done((bf16[96,2048]{1,0:T(8,128)(2,1)S(1)}, bf16[96,2048]{1,0:T(8,128)(2,1)S(1)}, u32[]{:S(2)}, u32[]{:S(2)}) %collective-permute-start.3) | collective-permute-done | bytes 393248 | tf_op jit(solution)/shard_map/ppermute | solution.py:128
  329.8 16.8 %collective-permute-done.6 = bf16[96,2048]{1,0:T(8,128)(2,1)S(1)} collective-permute-done((bf16[96,2048]{1,0:T(8,128)(2,1)S(1)}, bf16[96,2048]{1,0:T(8,128)(2,1)S(1)}, u32[]{:S(2)}, u32[]{:S(2)}) %collective-permute-start.6) | collective-permute-done | bytes 393248 | tf_op jit(solution)/shard_map/ppermute | solution.py:134
  393.7 26.1 %collective-permute-start.15 = (bf16[96,2048]{1,0:T(8,128)(2,1)S(1)}, bf16[96,2048]{1,0:T(8,128)(2,1)S(1)}, u32[]{:S(2)}, u32[]{:S(2)}) collective-permute-start(bf16[96,2048]{1,0:T(8,128)(2,1)S(1)} %get-tuple-element.362), channel_id=1, source_target_pairs={{0,2},{1,3},{2,0},{3,1},{4,6},{5,7},{6,4},{7,5},{8,10},{9,11},{10,... | collective-permute-start | bytes 1179656 | tf_op jit(solution)/shard_map/ppermute | solution.py:128
  431.9 23.3 %collective-permute-done.15 = bf16[96,2048]{1,0:T(8,128)(2,1)S(1)} collective-permute-done((bf16[96,2048]{1,0:T(8,128)(2,1)S(1)}, bf16[96,2048]{1,0:T(8,128)(2,1)S(1)}, u32[]{:S(2)}, u32[]{:S(2)}) %collective-permute-start.15) | collective-permute-done | bytes 393248 | tf_op jit(solution)/shard_map/ppermute | solution.py:128
  486.3 12.0 multiply_convert_fusion.2
  518.8 12.8 fusion.179
  541.8 13.2 fusion.132
  583.8 16.0 %collective-permute-start.21 = (bf16[160,2048]{1,0:T(8,128)(2,1)S(1)}, bf16[160,2048]{1,0:T(8,128)(2,1)S(1)}, u32[]{:S(2)}, u32[]{:S(2)}) collective-permute-start(bf16[160,2048]{1,0:T(8,128)(2,1)S(1)} %get-tuple-element.346), channel_id=1, source_target_pairs={{0,2},{1,3},{2,0},{3,1},{4,6},{5,7},{6,4},{7,5},{8,10},{9,11},{10,... | collective-permute-start | bytes 1966088 | tf_op jit(solution)/shard_map/ppermute | solution.py:128
  615.0 39.6 %collective-permute-done.21 = bf16[160,2048]{1,0:T(8,128)(2,1)S(1)} collective-permute-done((bf16[160,2048]{1,0:T(8,128)(2,1)S(1)}, bf16[160,2048]{1,0:T(8,128)(2,1)S(1)}, u32[]{:S(2)}, u32[]{:S(2)}) %collective-permute-start.21) | collective-permute-done | bytes 655392 | tf_op jit(solution)/shard_map/ppermute | solution.py:128
  664.4 11.7 collective-permute-done.23
  677.2 23.2 %collective-permute-done.24 = bf16[160,2048]{1,0:T(8,128)(2,1)} collective-permute-done((bf16[160,2048]{1,0:T(8,128)(2,1)}, bf16[160,2048]{1,0:T(8,128)(2,1)}, u32[]{:S(2)}, u32[]{:S(2)}) %collective-permute-start.24) | collective-permute-done | bytes 655392 | tf_op jit(solution)/shard_map/ppermute | solution.py:134
  717.0 130.0 %while.28 = (s32[]{:T(128)}, f32[2048,4,128]{0,2,1:T(8,128)}, f32[2048,4,128]{0,2,1:T(8,128)}, f32[2,512,4,128]{3,1,2,0:T(8,128)}, bf16[2,512,4,128]{3,1,2,0:T(8...) while((s32[]{:T(128)}, f32[2048,4,128]{0,2,1:T(8,128)}, ...), condition=%wide.region_16.17_spmd.clone, body=%wide.region_14.16_spmd.clone.sunk | while | flops 5439226368 | bytes 198246768 | solution.py:113
  729.2 12.9 multiply_reduce_fusion.5
  742.1 14.8 %multiply_convert_fusion.13 = bf16[4,512,2048]{2,1,0:T(8,128)(2,1)} fusion(f32[4,512,2048]{2,1,0:T(8,128)} %get-tuple-element.515, f32[4,512,2048]{2,1,0:T(8,128)} %fusion.256, f32[4,512]{1,0:T(4,128)S(1)} %get-tuple-element.516, f32[4,512]{1,0:T(4,128)S(1)} %dynamic-slice_bitcast_fusion.20, pred[512,2048]{1,0:T(8,128)(4,1)S(1)} %fusion.257), kind=kLoop, calls=%fused_computation.21.clone.1 | loop fusion | flops 25165824 | bytes 43008000 | tf_op jit(solution)/shard_map/while/body/eval_jaxpr/convert_element_type | solution.py:98
  764.4 12.8 bitcast_add_fusion.7
  792.7 12.9 multiply_reduce_fusion.5
  805.7 14.8 %multiply_convert_fusion.13 = bf16[4,512,2048]{2,1,0:T(8,128)(2,1)} fusion(f32[4,512,2048]{2,1,0:T(8,128)} %get-tuple-element.515, f32[4,512,2048]{2,1,0:T(8,128)} %fusion.256, f32[4,512]{1,0:T(4,128)S(1)} %get-tuple-element.516, f32[4,512]{1,0:T(4,128)S(1)} %dynamic-slice_bitcast_fusion.20, pred[512,2048]{1,0:T(8,128)(4,1)S(1)} %fusion.257), kind=kLoop, calls=%fused_computation.21.clone.1 | loop fusion | flops 25165824 | bytes 43008000 | tf_op jit(solution)/shard_map/while/body/eval_jaxpr/convert_element_type | solution.py:98
  829.1 14.0 %bitcast_add_fusion.7 = f32[2048,4,128]{0,2,1:T(8,128)} fusion(f32[2048,4,128]{0,2,1:T(8,128)} %get-tuple-element.567, f32[4,512,2048]{2,1,0:T(8,128)} %fusion.256, f32[4,512]{1,0:T(4,128)S(1)} %dynamic-slice_bitcast_fusion.20, pred[512,2048]{1,0:T(8,128)(4,1)S(1)} %fusion.257, pred[]{:T(512)S(6)} %compare.11, ...), kind=kOutput, calls=%fused_computation.27.clone.1 | convolution fusion | flops 1092616192 | bytes 26746884 | tf_op jit(solution)/shard_map/while/body/eval_jaxpr/hqk,qhd->khd/dot_general | solution.py:107
  864.5 13.6 %constant_dynamic-slice_fusion.1 = (f32[1,1024,4,128]{1,0,3,2:T(1,128)}, f32[1,1024,4,128]{1,0,3,2:T(1,128)}, f32[1,1024,4,128]{1,0,3,2:T(1,128)}, f32[1,1024,4,128]{1,0,3,2:T(1,128)S(1)}) fusion(f32[2,1024,4,128]{1,0,3,2:T(2,128)} %reshape_stack.7, s32[]{:T(128)S(6)} %select_n.195, s32[]{:T(128)S(6)} %select_n.197, f32[2,1024,4,128]{1,0,3,2:T(2,128)} %reshape_stack.6), kind=kLoop, calls=%fused_computation.255 | loop fusion | bytes 16777224 | tf_op jit(solution)/shard_map/jit(dynamic_index_in_dim)/dynamic_slice | solution.py:154
  943.1 12.9 collective-permute-start.28
  966.8 13.2 collective-permute-done.28
  980.0 67.9 %collective-permute-done.27 = bf16[256,2048]{1,0:T(8,128)(2,1)} collective-permute-done((bf16[256,2048]{1,0:T(8,128)(2,1)}, bf16[256,2048]{1,0:T(8,128)(2,1)}, u32[]{:S(2)}, u32[]{:S(2)}) %collective-permute-start.27) | collective-permute-done | bytes 1048608 | tf_op jit(solution)/shard_map/ppermute | solution.py:128
  1081.4 20.4 %collective-permute-start.31 = (bf16[256,2048]{1,0:T(8,128)(2,1)}, bf16[256,2048]{1,0:T(8,128)(2,1)S(1)}, u32[]{:S(2)}, u32[]{:S(2)}) collective-permute-start(bf16[256,2048]{1,0:T(8,128)(2,1)} %get-tuple-element.311), channel_id=1, source_target_pairs={{0,3},{1,0},{2,1},{3,2},{4,7},{5,4},{6,5},{7,6},{8,11},{9,8},{10,9... | collective-permute-start | bytes 3145736 | tf_op jit(solution)/shard_map/ppermute | solution.py:134
  1104.1 87.4 %collective-permute-done.35 = bf16[256,2048]{1,0:T(8,128)(2,1)} collective-permute-done((bf16[256,2048]{1,0:T(8,128)(2,1)}, bf16[256,2048]{1,0:T(8,128)(2,1)}, u32[]{:S(2)}, u32[]{:S(2)}) %collective-permute-start.35) | collective-permute-done | bytes 1048608 | tf_op jit(solution)/shard_map/ppermute | solution.py:128
  1198.8 21.8 %collective-permute-start.37 = (bf16[256,2048]{1,0:T(8,128)(2,1)}, bf16[256,2048]{1,0:T(8,128)(2,1)}, u32[]{:S(2)}, u32[]{:S(2)}) collective-permute-start(bf16[256,2048]{1,0:T(8,128)(2,1)} %get-tuple-element.309), channel_id=1, source_target_pairs={{0,1},{1,2},{2,3},{3,0},{4,5},{5,6},{6,7},{7,4},{8,9},{9,10},{10,1... | collective-permute-start | bytes 3145736 | tf_op jit(solution)/shard_map/ppermute | solution.py:134
  1220.6 15.8 %collective-permute-done.30 = bf16[256,2048]{1,0:T(8,128)(2,1)} collective-permute-done((bf16[256,2048]{1,0:T(8,128)(2,1)}, bf16[256,2048]{1,0:T(8,128)(2,1)}, u32[]{:S(2)}, u32[]{:S(2)}) %collective-permute-start.30) | collective-permute-done | bytes 1048608 | tf_op jit(solution)/shard_map/ppermute | solution.py:134
  1247.2 56.8 %collective-permute-done.38 = bf16[256,2048]{1,0:T(8,128)(2,1)} collective-permute-done((bf16[256,2048]{1,0:T(8,128)(2,1)}, bf16[256,2048]{1,0:T(8,128)(2,1)}, u32[]{:S(2)}, u32[]{:S(2)}) %collective-permute-start.38) | collective-permute-done | bytes 1048608 | tf_op jit(solution)/shard_map/ppermute | solution.py:134
  1306.3 20.0 %collective-permute-done.39 = bf16[256,2048]{1,0:T(8,128)(2,1)} collective-permute-done((bf16[256,2048]{1,0:T(8,128)(2,1)}, bf16[256,2048]{1,0:T(8,128)(2,1)}, u32[]{:S(2)}, u32[]{:S(2)}) %collective-permute-start.39) | collective-permute-done | bytes 1048608 | tf_op jit(solution)/shard_map/ppermute | solution.py:134
  (525 shorter events, 587.1 us)
Async XLA Ops:
  7.2 64.6 %all-gather.5.cloned.1.call-start = ((), (), s32[]{:S(2)}) async-start(), calls=%async_computation.5 | async-start | bytes 9437184 | tf_op jit(solution)/shard_map/all_gather | solution.py:229
  13.1 117.1 %all-gather.11.cloned.1.call-start = ((), (), s32[]{:S(2)}) async-start(), calls=%async_computation.8 | async-start | bytes 9437184 | tf_op jit(solution)/shard_map/all_gather | solution.py:240
  14.2 337.4 %all-gather.9.cloned.1.call-start = ((), (), s32[]{:S(2)}) async-start(), calls=%async_computation.7 | async-start | bytes 9437184 | tf_op jit(solution)/shard_map/all_gather | solution.py:239
  17.1 343.0 %all-gather.7.cloned.1.call-start = ((), (), s32[]{:S(2)}) async-start(), calls=%async_computation.6 | async-start | bytes 9437184 | tf_op jit(solution)/shard_map/all_gather | solution.py:238
  18.3 1224.5 %reduce-scatter.8.cloned.1.call-start = ((), (), s32[]{:S(2)}) async-start(), calls=%async_computation.10 | async-start | bytes 2359296 | tf_op jit(solution)/shard_map/reduce_scatter | solution.py:163
  80.6 93.3 %collective-permute-start = (bf16[1,1024,4,128]{1,3,2,0:T(8,128)(2,1)}, bf16[1,1024,4,128]{1,3,2,0:T(8,128)(2,1)}, u32[]{:S(2)}, u32[]{:S(2)}) collective-permute-start(bf16[1,1024,4,128]{1,3,2,0:T(8,128)(2,1)} %fusion.83), channel_id=1, source_target_pairs={{0,4},{4,0},{1,5},{5,1},{2,6},{6,2},{3,7},{7,3},{8,12},{12,8},{9,1... | collective-permute-start | bytes 3145736 | tf_op jit(solution)/shard_map/ppermute | solution.py:147
  89.1 89.3 %collective-permute-start.1 = (bf16[1,1024,4,128]{3,1,2,0:T(8,128)(2,1)}, bf16[1,1024,4,128]{3,1,2,0:T(8,128)(2,1)}, u32[]{:S(2)}, u32[]{:S(2)}) collective-permute-start(bf16[1,1024,4,128]{3,1,2,0:T(8,128)(2,1)} %bitcast.21), channel_id=1, source_target_pairs={{0,4},{4,0},{1,5},{5,1},{2,6},{6,2},{3,7},{7,3},{8,12},{12,8},{9,1... | collective-permute-start | bytes 3145736 | tf_op jit(solution)/shard_map/ppermute | solution.py:147
  228.4 90.9 %collective-permute-start.10 = (bf16[160,2048]{1,0:T(8,128)(2,1)S(1)}, bf16[160,2048]{1,0:T(8,128)(2,1)S(1)}, u32[]{:S(2)}, u32[]{:S(2)}) collective-permute-start(bf16[160,2048]{1,0:T(8,128)(2,1)S(1)} %get-tuple-element.348), channel_id=1, source_target_pairs={{0,3},{1,0},{2,1},{3,2},{4,7},{5,4},{6,5},{7,6},{8,11},{9,8},{10,9... | collective-permute-start | bytes 1966088 | tf_op jit(solution)/shard_map/ppermute | solution.py:128
  229.2 93.4 %collective-permute-start.9 = (bf16[160,2048]{1,0:T(8,128)(2,1)S(1)}, bf16[160,2048]{1,0:T(8,128)(2,1)S(1)}, u32[]{:S(2)}, u32[]{:S(2)}) collective-permute-start(bf16[160,2048]{1,0:T(8,128)(2,1)S(1)} %get-tuple-element.349), channel_id=1, source_target_pairs={{0,2},{1,3},{2,0},{3,1},{4,6},{5,7},{6,4},{7,5},{8,10},{9,11},{10,... | collective-permute-start | bytes 1966088 | tf_op jit(solution)/shard_map/ppermute | solution.py:128
  229.2 93.4 %collective-permute-start.8 = (bf16[160,2048]{1,0:T(8,128)(2,1)S(1)}, bf16[160,2048]{1,0:T(8,128)(2,1)S(1)}, u32[]{:S(2)}, u32[]{:S(2)}) collective-permute-start(bf16[160,2048]{1,0:T(8,128)(2,1)S(1)} %get-tuple-element.347), channel_id=1, source_target_pairs={{0,1},{1,2},{2,3},{3,0},{4,5},{5,6},{6,7},{7,4},{8,9},{9,10},{10,1... | collective-permute-start | bytes 1966088 | tf_op jit(solution)/shard_map/ppermute | solution.py:128
  230.4 84.9 %collective-permute-start.3 = (bf16[96,2048]{1,0:T(8,128)(2,1)S(1)}, bf16[96,2048]{1,0:T(8,128)(2,1)S(1)}, u32[]{:S(2)}, u32[]{:S(2)}) collective-permute-start(bf16[96,2048]{1,0:T(8,128)(2,1)S(1)} %get-tuple-element.365), channel_id=1, source_target_pairs={{0,2},{1,3},{2,0},{3,1},{4,6},{5,7},{6,4},{7,5},{8,10},{9,11},{10,... | collective-permute-start | bytes 1179656 | tf_op jit(solution)/shard_map/ppermute | solution.py:128
  234.6 80.8 %collective-permute-start.2 = (bf16[96,2048]{1,0:T(8,128)(2,1)S(1)}, bf16[96,2048]{1,0:T(8,128)(2,1)S(1)}, u32[]{:S(2)}, u32[]{:S(2)}) collective-permute-start(bf16[96,2048]{1,0:T(8,128)(2,1)S(1)} %get-tuple-element.363), channel_id=1, source_target_pairs={{0,1},{1,2},{2,3},{3,0},{4,5},{5,6},{6,7},{7,4},{8,9},{9,10},{10,1... | collective-permute-start | bytes 1179656 | tf_op jit(solution)/shard_map/ppermute | solution.py:128
  324.3 137.3 %collective-permute-start.11 = (bf16[160,2048]{1,0:T(8,128)(2,1)}, bf16[160,2048]{1,0:T(8,128)(2,1)}, u32[]{:S(2)}, u32[]{:S(2)}) collective-permute-start(bf16[160,2048]{1,0:T(8,128)(2,1)} %get-tuple-element.323), channel_id=1, source_target_pairs={{0,1},{1,2},{2,3},{3,0},{4,5},{5,6},{6,7},{7,4},{8,9},{9,10},{10,1... | collective-permute-start | bytes 1966088 | tf_op jit(solution)/shard_map/ppermute | solution.py:134
  324.3 141.4 %collective-permute-start.12 = (bf16[160,2048]{1,0:T(8,128)(2,1)}, bf16[160,2048]{1,0:T(8,128)(2,1)}, u32[]{:S(2)}, u32[]{:S(2)}) collective-permute-start(bf16[160,2048]{1,0:T(8,128)(2,1)} %get-tuple-element.323), channel_id=1, source_target_pairs={{0,2},{1,3},{2,0},{3,1},{4,6},{5,7},{6,4},{7,5},{8,10},{9,11},{10,... | collective-permute-start | bytes 1966088 | tf_op jit(solution)/shard_map/ppermute | solution.py:134
  393.7 61.4 %collective-permute-start.15 = (bf16[96,2048]{1,0:T(8,128)(2,1)S(1)}, bf16[96,2048]{1,0:T(8,128)(2,1)S(1)}, u32[]{:S(2)}, u32[]{:S(2)}) collective-permute-start(bf16[96,2048]{1,0:T(8,128)(2,1)S(1)} %get-tuple-element.362), channel_id=1, source_target_pairs={{0,2},{1,3},{2,0},{3,1},{4,6},{5,7},{6,4},{7,5},{8,10},{9,11},{10,... | collective-permute-start | bytes 1179656 | tf_op jit(solution)/shard_map/ppermute | solution.py:128
  456.3 154.0 %collective-permute-start.17 = (bf16[96,2048]{1,0:T(8,128)(2,1)}, bf16[96,2048]{1,0:T(8,128)(2,1)}, u32[]{:S(2)}, u32[]{:S(2)}) collective-permute-start(bf16[96,2048]{1,0:T(8,128)(2,1)} %get-tuple-element.313), channel_id=1, source_target_pairs={{0,1},{1,2},{2,3},{3,0},{4,5},{5,6},{6,7},{7,4},{8,9},{9,10},{10,1... | collective-permute-start | bytes 1179656 | tf_op jit(solution)/shard_map/ppermute | solution.py:134
  459.7 152.1 %collective-permute-start.18 = (bf16[96,2048]{1,0:T(8,128)(2,1)}, bf16[96,2048]{1,0:T(8,128)(2,1)}, u32[]{:S(2)}, u32[]{:S(2)}) collective-permute-start(bf16[96,2048]{1,0:T(8,128)(2,1)} %get-tuple-element.313), channel_id=1, source_target_pairs={{0,2},{1,3},{2,0},{3,1},{4,6},{5,7},{6,4},{7,5},{8,10},{9,11},{10,... | collective-permute-start | bytes 1179656 | tf_op jit(solution)/shard_map/ppermute | solution.py:134
  461.6 151.2 %collective-permute-start.19 = (bf16[96,2048]{1,0:T(8,128)(2,1)}, bf16[96,2048]{1,0:T(8,128)(2,1)}, u32[]{:S(2)}, u32[]{:S(2)}) collective-permute-start(bf16[96,2048]{1,0:T(8,128)(2,1)} %get-tuple-element.313), channel_id=1, source_target_pairs={{0,3},{1,0},{2,1},{3,2},{4,7},{5,4},{6,5},{7,6},{8,11},{9,8},{10,9... | collective-permute-start | bytes 1179656 | tf_op jit(solution)/shard_map/ppermute | solution.py:134
  583.8 70.8 %collective-permute-start.21 = (bf16[160,2048]{1,0:T(8,128)(2,1)S(1)}, bf16[160,2048]{1,0:T(8,128)(2,1)S(1)}, u32[]{:S(2)}, u32[]{:S(2)}) collective-permute-start(bf16[160,2048]{1,0:T(8,128)(2,1)S(1)} %get-tuple-element.346), channel_id=1, source_target_pairs={{0,2},{1,3},{2,0},{3,1},{4,6},{5,7},{6,4},{7,5},{8,10},{9,11},{10,... | collective-permute-start | bytes 1966088 | tf_op jit(solution)/shard_map/ppermute | solution.py:128
  905.6 435.6 %reduce-scatter.6.cloned.1.call-start = ((), (), s32[]{:S(2)}) async-start(), calls=%async_computation.9 | async-start | bytes 7077888 | tf_op jit(solution)/shard_map/reduce_scatter | solution.py:163
  937.2 408.2 %reduce-scatter.10.cloned.1.call-start = ((), (), s32[]{:S(2)}) async-start(), calls=%async_computation.11 | async-start | bytes 9437184 | tf_op jit(solution)/shard_map/reduce_scatter | solution.py:163
  938.0 410.2 %reduce-scatter.12.cloned.1.call-start = ((), (), s32[]{:S(2)}) async-start(), calls=%async_computation.12 | async-start | bytes 9437184 | tf_op jit(solution)/shard_map/reduce_scatter | solution.py:163
  938.7 412.3 %reduce-scatter.14.cloned.1.call-start = ((), (), s32[]{:S(2)}) async-start(), calls=%async_computation.13 | async-start | bytes 9437184 | tf_op jit(solution)/shard_map/reduce_scatter | solution.py:163
  956.1 91.9 %collective-permute-start.27 = (bf16[256,2048]{1,0:T(8,128)(2,1)}, bf16[256,2048]{1,0:T(8,128)(2,1)}, u32[]{:S(2)}, u32[]{:S(2)}) collective-permute-start(bf16[256,2048]{1,0:T(8,128)(2,1)} %get-tuple-element.343), channel_id=1, source_target_pairs={{0,2},{1,3},{2,0},{3,1},{4,6},{5,7},{6,4},{7,5},{8,10},{9,11},{10,... | collective-permute-start | bytes 3145736 | tf_op jit(solution)/shard_map/ppermute | solution.py:128
  957.0 91.0 %collective-permute-start.26 = (bf16[256,2048]{1,0:T(8,128)(2,1)}, bf16[256,2048]{1,0:T(8,128)(2,1)}, u32[]{:S(2)}, u32[]{:S(2)}) collective-permute-start(bf16[256,2048]{1,0:T(8,128)(2,1)} %get-tuple-element.341), channel_id=1, source_target_pairs={{0,1},{1,2},{2,3},{3,0},{4,5},{5,6},{6,7},{7,4},{8,9},{9,10},{10,1... | collective-permute-start | bytes 3145736 | tf_op jit(solution)/shard_map/ppermute | solution.py:128
  1073.1 118.4 %collective-permute-start.35 = (bf16[256,2048]{1,0:T(8,128)(2,1)}, bf16[256,2048]{1,0:T(8,128)(2,1)}, u32[]{:S(2)}, u32[]{:S(2)}) collective-permute-start(bf16[256,2048]{1,0:T(8,128)(2,1)} %get-tuple-element.336), channel_id=1, source_target_pairs={{0,2},{1,3},{2,0},{3,1},{4,6},{5,7},{6,4},{7,5},{8,10},{9,11},{10,... | collective-permute-start | bytes 3145736 | tf_op jit(solution)/shard_map/ppermute | solution.py:128
  1073.1 118.4 %collective-permute-start.34 = (bf16[256,2048]{1,0:T(8,128)(2,1)}, bf16[256,2048]{1,0:T(8,128)(2,1)}, u32[]{:S(2)}, u32[]{:S(2)}) collective-permute-start(bf16[256,2048]{1,0:T(8,128)(2,1)} %get-tuple-element.334), channel_id=1, source_target_pairs={{0,1},{1,2},{2,3},{3,0},{4,5},{5,6},{6,7},{7,4},{8,9},{9,10},{10,1... | collective-permute-start | bytes 3145736 | tf_op jit(solution)/shard_map/ppermute | solution.py:128
  1073.7 162.8 %collective-permute-start.30 = (bf16[256,2048]{1,0:T(8,128)(2,1)}, bf16[256,2048]{1,0:T(8,128)(2,1)}, u32[]{:S(2)}, u32[]{:S(2)}) collective-permute-start(bf16[256,2048]{1,0:T(8,128)(2,1)} %get-tuple-element.311), channel_id=1, source_target_pairs={{0,2},{1,3},{2,0},{3,1},{4,6},{5,7},{6,4},{7,5},{8,10},{9,11},{10,... | collective-permute-start | bytes 3145736 | tf_op jit(solution)/shard_map/ppermute | solution.py:134
  1081.4 156.5 %collective-permute-start.31 = (bf16[256,2048]{1,0:T(8,128)(2,1)}, bf16[256,2048]{1,0:T(8,128)(2,1)S(1)}, u32[]{:S(2)}, u32[]{:S(2)}) collective-permute-start(bf16[256,2048]{1,0:T(8,128)(2,1)} %get-tuple-element.311), channel_id=1, source_target_pairs={{0,3},{1,0},{2,1},{3,2},{4,7},{5,4},{6,5},{7,6},{8,11},{9,8},{10,9... | collective-permute-start | bytes 3145736 | tf_op jit(solution)/shard_map/ppermute | solution.py:134
  1198.8 45.8 %collective-permute-start.37 = (bf16[256,2048]{1,0:T(8,128)(2,1)}, bf16[256,2048]{1,0:T(8,128)(2,1)}, u32[]{:S(2)}, u32[]{:S(2)}) collective-permute-start(bf16[256,2048]{1,0:T(8,128)(2,1)} %get-tuple-element.309), channel_id=1, source_target_pairs={{0,1},{1,2},{2,3},{3,0},{4,5},{5,6},{6,7},{7,4},{8,9},{9,10},{10,1... | collective-permute-start | bytes 3145736 | tf_op jit(solution)/shard_map/ppermute | solution.py:134
  1237.8 66.1 %collective-permute-start.38 = (bf16[256,2048]{1,0:T(8,128)(2,1)}, bf16[256,2048]{1,0:T(8,128)(2,1)}, u32[]{:S(2)}, u32[]{:S(2)}) collective-permute-start(bf16[256,2048]{1,0:T(8,128)(2,1)} %get-tuple-element.309), channel_id=1, source_target_pairs={{0,2},{1,3},{2,0},{3,1},{4,6},{5,7},{6,4},{7,5},{8,10},{9,11},{10,... | collective-permute-start | bytes 3145736 | tf_op jit(solution)/shard_map/ppermute | solution.py:134
  1238.0 88.3 %collective-permute-start.39 = (bf16[256,2048]{1,0:T(8,128)(2,1)}, bf16[256,2048]{1,0:T(8,128)(2,1)}, u32[]{:S(2)}, u32[]{:S(2)}) collective-permute-start(bf16[256,2048]{1,0:T(8,128)(2,1)} %get-tuple-element.309), channel_id=1, source_target_pairs={{0,3},{1,0},{2,1},{3,2},{4,7},{5,4},{6,5},{7,6},{8,11},{9,8},{10,9... | collective-permute-start | bytes 3145736 | tf_op jit(solution)/shard_map/ppermute | solution.py:134
  (126 other events, 1941.5 us)
Sparse Core Ops, SparseCore 0:
  13.2 58.5 all-gather.4
  74.2 55.8 all-gather.10
  132.0 54.2 all-gather.8
  188.1 54.2 all-gather.6
  905.7 50.3 reduce-scatter.7
  959.3 61.5 reduce-scatter.5
  1024.4 71.5 reduce-scatter.9
  1099.4 71.4 reduce-scatter.11
  1174.4 71.2 reduce-scatter.13

commit v5 on v4

--- a/solution.py
+++ b/solution.py
@@ -138,6 +138,42 @@
     return gathered
 
 
+def tp_psum_line(part, count, axis="tp"):
+    me = lax.axis_index(axis)
+    low_part = part.astype(jnp.bfloat16)
+    rows = part.shape[0] // count
+    chunks = low_part.reshape((count, rows) + part.shape[1:])
+
+    def chunk_at(index):
+        return lax.dynamic_index_in_dim(chunks, jnp.clip(index, 0, count - 1), 0, keepdims=False)
+
+    from_left = jnp.zeros(chunks.shape[1:], jnp.bfloat16)
+    from_right = jnp.zeros(chunks.shape[1:], jnp.bfloat16)
+    for step in range(1, count):
+      right_pairs = [(i, i + 1) for i in range(count - 1) if i <= step - 1]
+      left_pairs = [(i, i - 1) for i in range(1, count) if i >= count - step]
+      send_right = (chunk_at(me + count - step).astype(jnp.float32) + from_left.astype(jnp.float32))
+      send_left = (chunk_at(me + step - count).astype(jnp.float32) + from_right.astype(jnp.float32))
+      from_left = lax.ppermute(send_right.astype(jnp.bfloat16), axis, right_pairs)
+      from_right = lax.ppermute(send_left.astype(jnp.bfloat16), axis, left_pairs)
+    total = chunk_at(me).astype(jnp.float32) + from_left.astype(jnp.float32) + from_right.astype(jnp.float32)
+    reduced = total.astype(jnp.bfloat16)
+    gathered = jnp.zeros(chunks.shape, jnp.bfloat16)
+    gathered = lax.dynamic_update_index_in_dim(gathered, reduced, me, 0)
+    going_right = reduced
+    going_left = reduced
+    for step in range(1, count):
+      right_pairs = [(i, i + 1) for i in range(count - 1) if i >= step - 1]
+      left_pairs = [(i, i - 1) for i in range(1, count) if i <= count - step]
+      going_right = lax.ppermute(going_right, axis, right_pairs)
+      going_left = lax.ppermute(going_left, axis, left_pairs)
+      for got, index in ((going_right, me - step), (going_left, me + step)):
+          spot = jnp.clip(index, 0, count - 1)
+          held = lax.dynamic_index_in_dim(gathered, spot, 0, keepdims=False)
+          gathered = lax.dynamic_update_index_in_dim(gathered, held + got, spot, 0)
+    return gathered.reshape(low_part.shape)
+
+
 def exchange_gather(piece, axis, count):
     me = lax.axis_index(axis)
     gathered = jnp.zeros((count,) + piece.shape, piece.dtype)
@@ -186,9 +222,7 @@
     grad_hidden = jnp.einsum(
         "rd,fd->rf", grad_branch, down_full, preferred_element_type=jnp.float32
     )
-    grad_gate_act = (
-        grad_hidden * up_proj * gate_sigmoid * (1.0 + gate_proj * (1.0 - gate_sigmoid))
-    ).astype(bf_type)
+    grad_gate_act = (grad_hidden * up_proj * gate_sigmoid * (1.0 + gate_proj * (1.0 - gate_sigmoid))).astype(bf_type)
     grad_up_act = (grad_hidden * gate_proj * gate_sigmoid).astype(bf_type)
     grad_input_two = jnp.einsum(
         "rf,df->rd", grad_gate_act, gate_full, preferred_element_type=jnp.float32
@@ -354,7 +388,7 @@
         scatter_low(jnp.concatenate([grad_wq, grad_wk, grad_wv], axis=1), 0), 3, axis=1
     )
     attn_grads = (qkv_grads[0], qkv_grads[1], qkv_grads[2], scatter_low(grad_wout, 1))
-    grad_input_one = tp_psum(grad_input_one, tp_count).astype(jnp.float32)
+    grad_input_one = tp_psum_line(grad_input_one, tp_count).astype(jnp.float32)
     grad_tokens = grad_resid + norm_back(normed_one, scale_one, grad_input_one)
     output = final_sum.astype(bf_type).reshape(seq_count, half_len, model_width)
     grad_tokens = grad_tokens.reshape(seq_count, half_len, model_width)

time: 1370 us -> 1380 us (level)
  waiting for transfers between devices: 529 us -> 442 us
  starting transfers between devices: 152 us -> 212 us
  other arithmetic: 169 us -> 199 us
    ppermute x18 -> x15, waiting for transfers between devices: 306 us -> 203 us  [tp_psum(): total = total + lax.ppermute(piece, TP, pairs).astype(jnp.float32)]
    ppermute x0 -> x12, waiting for transfers between devices: none -> 101 us  [the longest x3 37.6 us: tp_psum_line(): from_left = lax.ppermute(send_right.astype(jnp.bfloat16), axis, right_pairs)]
    ppermute x18 -> x15, waiting for transfers between devices: 160 us -> 75.1 us  [tp_psum(): got = lax.ppermute(reduced, TP, pairs)]
    ppermute x0 -> x12, starting transfers between devices: none -> 64.4 us  [the longest x3 30.1 us: tp_psum_line(): going_right = lax.ppermute(going_right, axis, right_pairs)]
    convert_element_type x0 -> x4, other arithmetic: none -> 17.9 us  [the longest x2 8.16 us: tp_psum_line(): from_left = lax.ppermute(send_right.astype(jnp.bfloat16), axis, right_pairs)]
    ppermute x18 -> x15, starting transfers between devices: 80.4 us -> 64.6 us  [tp_psum(): total = total + lax.ppermute(piece, TP, pairs).astype(jnp.float32)]
    dynamic_update_slice x0 -> x7, other arithmetic: none -> 14.9 us  [the longest x6 10.7 us: tp_psum_line(): gathered = lax.dynamic_update_index_in_dim(gathered, held + got, spot, 0)]
    ppermute x18 -> x15, starting transfers between devices: 69.5 us -> 81.2 us  [tp_psum(): got = lax.ppermute(reduced, TP, pairs)]
  transfers between devices with their start and end apart: 49 -> 55, of which waited for: 18 -> 21; matrix products, arithmetic and copies ran while one was open for 33% -> 36% of each run, Pallas kernels for 0% -> 0%
where the time goes in v5:
time: 1380 us; the launch traced here: 1370 us
  waiting for transfers between devices  442 us (32%)
  matrix products  343 us (25%)
  starting transfers between devices  212 us (15%)
  other arithmetic  199 us (14%)
  local copies, waits for them, and re-layouts  154 us (11%)
  between operations  16.7 us (1%)
    ppermute x15, waiting for transfers between devices, tp_psum(): total = total + lax.ppermute(piece, TP, pairs).astype(jnp.float32)  203 us
    ppermute x15, starting transfers between devices, tp_psum(): got = lax.ppermute(reduced, TP, pairs)  81.2 us
    dot_general x11, matrix products, matmul_low(): return jnp.dot(left, right, preferred_element_type=jnp.float32)  76 us
    ppermute x15, waiting for transfers between devices, tp_psum(): got = lax.ppermute(reduced, TP, pairs)  75.1 us
    ppermute x15, starting transfers between devices, tp_psum(): total = total + lax.ppermute(piece, TP, pairs).astype(jnp.float32)  64.6 us
    ppermute x3, waiting for transfers between devices, tp_psum_line(): from_left = lax.ppermute(send_right.astype(jnp.bfloat16), axis, right_pairs)  37.6 us
    all_gather x1, waiting for transfers between devices, block(): lax.all_gather(mlp_low[2], (SHARD, CTX), axis=1, tiled=True)  37.1 us
    ppermute x3, waiting for transfers between devices, tp_psum_line(): going_left = lax.ppermute(going_left, axis, left_pairs)  35.6 us
  transfers between devices with their start and end apart: 55, of which 21 were waited for; matrix products, arithmetic and copies ran while one was open for 36% of the time, Pallas kernels for 0%

profile of v5, /device:TPU:0, one launch (start us, length us, event | category | flops | bytes accessed | tf_op | source)
XLA Modules:
  0.0 1371.2 jit_solution(16915298182759374377)
XLA Ops:
  46.9 24.9 %all-gather.5.cloned.1.call-done = bf16[2048,2048]{0,1:T(8,128)(2,1)} async-done(((bf16[256,2048]{0,1:T(8,128)(2,1)}), bf16[2048,2048]{0,1:T(8,128)(2,1)}) %all-gather.5.cloned.1.call-update) | async-done | bytes 8388624 | tf_op jit(solution)/shard_map/all_gather | solution.py:263
  93.0 37.1 %all-gather.11.cloned.1.call-done = bf16[2048,2048]{1,0:T(8,128)(2,1)} async-done(((bf16[2048,256]{1,0:T(8,128)(2,1)}), bf16[2048,2048]{1,0:T(8,128)(2,1)}) %all-gather.11.cloned.1.call-update) | async-done | bytes 8388624 | tf_op jit(solution)/shard_map/all_gather | solution.py:274
  181.2 35.1 %while.27 = (s32[]{:T(128)}, bf16[2,512,4,128]{3,2,1,0:T(4,128)(2,1)}, f32[2,4,512]{2,1,0:T(4,128)S(1)}, s32[2]{0:T(128)S(1)}, s32[]{:T(128)}, /*index=5*/s32[]{...) while((s32[]{:T(128)}, ...), condition=%wide.region_5.6_spmd, body=%wide.region_2.5_spmd.sunk | while | flops 2195980800 | bytes 77668600 | solution.py:77
  242.6 73.0 %collective-permute-done.3 = bf16[96,2048]{1,0:T(8,128)(2,1)S(1)} collective-permute-done((bf16[96,2048]{1,0:T(8,128)(2,1)S(1)}, bf16[96,2048]{1,0:T(8,128)(2,1)S(1)}, u32[]{:S(2)}, u32[]{:S(2)}) %collective-permute-start.3) | collective-permute-done | bytes 393248 | tf_op jit(solution)/shard_map/ppermute | solution.py:128
  330.1 16.8 %collective-permute-done.6 = bf16[96,2048]{1,0:T(8,128)(2,1)S(1)} collective-permute-done((bf16[96,2048]{1,0:T(8,128)(2,1)S(1)}, bf16[96,2048]{1,0:T(8,128)(2,1)S(1)}, u32[]{:S(2)}, u32[]{:S(2)}) %collective-permute-start.6) | collective-permute-done | bytes 393248 | tf_op jit(solution)/shard_map/ppermute | solution.py:134
  394.1 26.1 %collective-permute-start.15 = (bf16[96,2048]{1,0:T(8,128)(2,1)S(1)}, bf16[96,2048]{1,0:T(8,128)(2,1)S(1)}, u32[]{:S(2)}, u32[]{:S(2)}) collective-permute-start(bf16[96,2048]{1,0:T(8,128)(2,1)S(1)} %get-tuple-element.363), channel_id=1, source_target_pairs={{0,2},{1,3},{2,0},{3,1},{4,6},{5,7},{6,4},{7,5},{8,10},{9,11},{10,... | collective-permute-start | bytes 1179656 | tf_op jit(solution)/shard_map/ppermute | solution.py:128
  432.4 23.1 %collective-permute-done.15 = bf16[96,2048]{1,0:T(8,128)(2,1)S(1)} collective-permute-done((bf16[96,2048]{1,0:T(8,128)(2,1)S(1)}, bf16[96,2048]{1,0:T(8,128)(2,1)S(1)}, u32[]{:S(2)}, u32[]{:S(2)}) %collective-permute-start.15) | collective-permute-done | bytes 393248 | tf_op jit(solution)/shard_map/ppermute | solution.py:128
  519.2 12.6 fusion.182
  542.2 13.2 fusion.131
  584.5 16.1 %collective-permute-start.21 = (bf16[160,2048]{1,0:T(8,128)(2,1)S(1)}, bf16[160,2048]{1,0:T(8,128)(2,1)S(1)}, u32[]{:S(2)}, u32[]{:S(2)}) collective-permute-start(bf16[160,2048]{1,0:T(8,128)(2,1)S(1)} %get-tuple-element.347), channel_id=1, source_target_pairs={{0,2},{1,3},{2,0},{3,1},{4,6},{5,7},{6,4},{7,5},{8,10},{9,11},{10,... | collective-permute-start | bytes 1966088 | tf_op jit(solution)/shard_map/ppermute | solution.py:128
  615.7 39.6 %collective-permute-done.21 = bf16[160,2048]{1,0:T(8,128)(2,1)S(1)} collective-permute-done((bf16[160,2048]{1,0:T(8,128)(2,1)S(1)}, bf16[160,2048]{1,0:T(8,128)(2,1)S(1)}, u32[]{:S(2)}, u32[]{:S(2)}) %collective-permute-start.21) | collective-permute-done | bytes 655392 | tf_op jit(solution)/shard_map/ppermute | solution.py:128
  677.9 23.2 %collective-permute-done.24 = bf16[160,2048]{1,0:T(8,128)(2,1)} collective-permute-done((bf16[160,2048]{1,0:T(8,128)(2,1)}, bf16[160,2048]{1,0:T(8,128)(2,1)}, u32[]{:S(2)}, u32[]{:S(2)}) %collective-permute-start.24) | collective-permute-done | bytes 655392 | tf_op jit(solution)/shard_map/ppermute | solution.py:134
  717.6 130.1 %while.28 = (s32[]{:T(128)}, f32[2048,4,128]{0,2,1:T(8,128)}, f32[2048,4,128]{0,2,1:T(8,128)}, f32[2,512,4,128]{3,1,2,0:T(8,128)}, bf16[2,512,4,128]{3,1,2,0:T(8...) while((s32[]{:T(128)}, f32[2048,4,128]{0,2,1:T(8,128)}, ...), condition=%wide.region_16.17_spmd.clone, body=%wide.region_14.16_spmd.clone.sunk | while | flops 5439226368 | bytes 198246768 | solution.py:113
  729.6 12.9 multiply_reduce_fusion.6
  742.6 14.8 %multiply_convert_fusion.9 = bf16[4,512,2048]{2,1,0:T(8,128)(2,1)} fusion(f32[4,512,2048]{2,1,0:T(8,128)} %get-tuple-element.516, f32[4,512,2048]{2,1,0:T(8,128)} %fusion.259, f32[4,512]{1,0:T(4,128)S(1)} %get-tuple-element.517, f32[4,512]{1,0:T(4,128)S(1)} %dynamic-slice_bitcast_fusion.19, pred[512,2048]{1,0:T(8,128)(4,1)S(1)} %fusion.260), kind=kLoop, calls=%fused_computation.21.clone.1 | loop fusion | flops 25165824 | bytes 43008000 | tf_op jit(solution)/shard_map/while/body/eval_jaxpr/convert_element_type | solution.py:98
  764.8 12.9 bitcast_add_fusion.13
  793.2 12.9 multiply_reduce_fusion.6
  806.1 14.8 %multiply_convert_fusion.9 = bf16[4,512,2048]{2,1,0:T(8,128)(2,1)} fusion(f32[4,512,2048]{2,1,0:T(8,128)} %get-tuple-element.516, f32[4,512,2048]{2,1,0:T(8,128)} %fusion.259, f32[4,512]{1,0:T(4,128)S(1)} %get-tuple-element.517, f32[4,512]{1,0:T(4,128)S(1)} %dynamic-slice_bitcast_fusion.19, pred[512,2048]{1,0:T(8,128)(4,1)S(1)} %fusion.260), kind=kLoop, calls=%fused_computation.21.clone.1 | loop fusion | flops 25165824 | bytes 43008000 | tf_op jit(solution)/shard_map/while/body/eval_jaxpr/convert_element_type | solution.py:98
  829.5 14.1 %bitcast_add_fusion.13 = f32[2048,4,128]{0,2,1:T(8,128)} fusion(f32[2048,4,128]{0,2,1:T(8,128)} %get-tuple-element.568, f32[4,512,2048]{2,1,0:T(8,128)} %fusion.259, f32[4,512]{1,0:T(4,128)S(1)} %dynamic-slice_bitcast_fusion.19, pred[512,2048]{1,0:T(8,128)(4,1)S(1)} %fusion.260, pred[]{:T(512)S(6)} %compare.11, ...), kind=kOutput, calls=%fused_computation.27.clone.1 | convolution fusion | flops 1092616192 | bytes 26746884 | tf_op jit(solution)/shard_map/while/body/eval_jaxpr/hqk,qhd->khd/dot_general | solution.py:107
  865.2 13.6 constant_dynamic-slice_fusion.7
  965.7 16.5 %collective-permute-start.34 = (bf16[256,2048]{1,0:T(8,128)(2,1)}, bf16[256,2048]{1,0:T(8,128)(2,1)}, u32[]{:S(2)}, u32[]{:S(2)}) collective-permute-start(bf16[256,2048]{1,0:T(8,128)(2,1)} %get-tuple-element.336), channel_id=1, source_target_pairs={{0,1},{4,5},{8,9},{12,13},{16,17},{20,21},{24,25},{28,29}} | collective-permute-start | bytes 3145736 | tf_op jit(solution)/shard_map/ppermute | solution.py:157
  983.8 20.4 %collective-permute-done.34 = bf16[256,2048]{1,0:T(8,128)(2,1)} collective-permute-done((bf16[256,2048]{1,0:T(8,128)(2,1)}, bf16[256,2048]{1,0:T(8,128)(2,1)}, u32[]{:S(2)}, u32[]{:S(2)}) %collective-permute-start.34) | collective-permute-done | bytes 1048608 | tf_op jit(solution)/shard_map/ppermute | solution.py:157
  1018.1 17.2 %collective-permute-done.35 = bf16[256,2048]{1,0:T(8,128)(2,1)} collective-permute-done((bf16[256,2048]{1,0:T(8,128)(2,1)}, bf16[256,2048]{1,0:T(8,128)(2,1)}, u32[]{:S(2)}, u32[]{:S(2)}) %collective-permute-start.35) | collective-permute-done | bytes 1048608 | tf_op jit(solution)/shard_map/ppermute | solution.py:157
  1042.6 15.2 %collective-permute-done.28 = bf16[256,2048]{1,0:T(8,128)(2,1)} collective-permute-done((bf16[256,2048]{1,0:T(8,128)(2,1)}, bf16[256,2048]{1,0:T(8,128)(2,1)}, u32[]{:S(2)}, u32[]{:S(2)}) %collective-permute-start.28) | collective-permute-done | bytes 1048608 | tf_op jit(solution)/shard_map/ppermute | solution.py:128
  1057.8 50.6 %collective-permute-done.27 = bf16[256,2048]{1,0:T(8,128)(2,1)} collective-permute-done((bf16[256,2048]{1,0:T(8,128)(2,1)}, bf16[256,2048]{1,0:T(8,128)(2,1)}, u32[]{:S(2)}, u32[]{:S(2)}) %collective-permute-start.27) | collective-permute-done | bytes 1048608 | tf_op jit(solution)/shard_map/ppermute | solution.py:128
  1116.4 15.0 %collective-permute-start.29 = (bf16[256,2048]{1,0:T(8,128)(2,1)}, bf16[256,2048]{1,0:T(8,128)(2,1)}, u32[]{:S(2)}, u32[]{:S(2)}) collective-permute-start(bf16[256,2048]{1,0:T(8,128)(2,1)} %get-tuple-element.311), channel_id=1, source_target_pairs={{0,1},{1,2},{2,3},{3,0},{4,5},{5,6},{6,7},{7,4},{8,9},{9,10},{10,1... | collective-permute-start | bytes 3145736 | tf_op jit(solution)/shard_map/ppermute | solution.py:134
  1140.4 42.2 %collective-permute-start.31 = (bf16[256,2048]{1,0:T(8,128)(2,1)}, bf16[256,2048]{1,0:T(8,128)(2,1)}, u32[]{:S(2)}, u32[]{:S(2)}) collective-permute-start(bf16[256,2048]{1,0:T(8,128)(2,1)} %get-tuple-element.311), channel_id=1, source_target_pairs={{0,3},{1,0},{2,1},{3,2},{4,7},{5,4},{6,5},{7,6},{8,11},{9,8},{10,9... | collective-permute-start | bytes 3145736 | tf_op jit(solution)/shard_map/ppermute | solution.py:134
  1185.3 13.0 collective-permute-done.30
  1200.6 19.0 %collective-permute-done.39 = bf16[256,2048]{1,0:T(8,128)(2,1)} collective-permute-done((bf16[256,2048]{1,0:T(8,128)(2,1)}, bf16[256,2048]{1,0:T(8,128)(2,1)}, u32[]{:S(2)}, u32[]{:S(2)}) %collective-permute-start.39) | collective-permute-done | bytes 1048608 | tf_op jit(solution)/shard_map/ppermute | solution.py:158
  1226.4 28.6 %collective-permute-start.40 = (bf16[256,2048]{1,0:T(8,128)(2,1)}, bf16[256,2048]{1,0:T(8,128)(2,1)}, u32[]{:S(2)}, u32[]{:S(2)}) collective-permute-start(bf16[256,2048]{1,0:T(8,128)(2,1)} %get-tuple-element.309), channel_id=1, source_target_pairs={{0,1},{1,2},{2,3},{4,5},{5,6},{6,7},{8,9},{9,10},{10,11},{12,13},{... | collective-permute-start | bytes 3145736 | tf_op jit(solution)/shard_map/ppermute | solution.py:168
  1291.5 16.2 %collective-permute-done.43 = bf16[256,2048]{1,0:T(8,128)(2,1)S(1)} collective-permute-done((bf16[256,2048]{1,0:T(8,128)(2,1)}, bf16[256,2048]{1,0:T(8,128)(2,1)S(1)}, u32[]{:S(2)}, u32[]{:S(2)}) %collective-permute-start.43) | collective-permute-done | bytes 1048608 | tf_op jit(solution)/shard_map/ppermute | solution.py:169
  1315.9 15.4 %collective-permute-done.45 = bf16[256,2048]{1,0:T(8,128)(2,1)S(1)} collective-permute-done((bf16[256,2048]{1,0:T(8,128)(2,1)S(1)}, bf16[256,2048]{1,0:T(8,128)(2,1)S(1)}, u32[]{:S(2)}, u32[]{:S(2)}) %collective-permute-start.45) | collective-permute-done | bytes 1048608 | tf_op jit(solution)/shard_map/ppermute | solution.py:169
  (555 shorter events, 679.6 us)
Async XLA Ops:
  7.2 64.6 %all-gather.5.cloned.1.call-start = ((), (), s32[]{:S(2)}) async-start(), calls=%async_computation.5 | async-start | bytes 9437184 | tf_op jit(solution)/shard_map/all_gather | solution.py:263
  13.1 117.1 %all-gather.11.cloned.1.call-start = ((), (), s32[]{:S(2)}) async-start(), calls=%async_computation.8 | async-start | bytes 9437184 | tf_op jit(solution)/shard_map/all_gather | solution.py:274
  14.2 337.7 %all-gather.9.cloned.1.call-start = ((), (), s32[]{:S(2)}) async-start(), calls=%async_computation.7 | async-start | bytes 9437184 | tf_op jit(solution)/shard_map/all_gather | solution.py:273
  17.2 343.2 %all-gather.7.cloned.1.call-start = ((), (), s32[]{:S(2)}) async-start(), calls=%async_computation.6 | async-start | bytes 9437184 | tf_op jit(solution)/shard_map/all_gather | solution.py:272
  18.4 1245.0 %reduce-scatter.8.cloned.1.call-start = ((), (), s32[]{:S(2)}) async-start(), calls=%async_computation.10 | async-start | bytes 2359296 | tf_op jit(solution)/shard_map/reduce_scatter | solution.py:199
  80.5 93.5 %collective-permute-start = (bf16[1,1024,4,128]{1,3,2,0:T(8,128)(2,1)}, bf16[1,1024,4,128]{1,3,2,0:T(8,128)(2,1)}, u32[]{:S(2)}, u32[]{:S(2)}) collective-permute-start(bf16[1,1024,4,128]{1,3,2,0:T(8,128)(2,1)} %fusion.79), channel_id=1, source_target_pairs={{0,4},{4,0},{1,5},{5,1},{2,6},{6,2},{3,7},{7,3},{8,12},{12,8},{9,1... | collective-permute-start | bytes 3145736 | tf_op jit(solution)/shard_map/ppermute | solution.py:183
  89.0 89.4 %collective-permute-start.1 = (bf16[1,1024,4,128]{3,1,2,0:T(8,128)(2,1)}, bf16[1,1024,4,128]{3,1,2,0:T(8,128)(2,1)}, u32[]{:S(2)}, u32[]{:S(2)}) collective-permute-start(bf16[1,1024,4,128]{3,1,2,0:T(8,128)(2,1)} %bitcast.21), channel_id=1, source_target_pairs={{0,4},{4,0},{1,5},{5,1},{2,6},{6,2},{3,7},{7,3},{8,12},{12,8},{9,1... | collective-permute-start | bytes 3145736 | tf_op jit(solution)/shard_map/ppermute | solution.py:183
  228.7 90.9 %collective-permute-start.10 = (bf16[160,2048]{1,0:T(8,128)(2,1)S(1)}, bf16[160,2048]{1,0:T(8,128)(2,1)S(1)}, u32[]{:S(2)}, u32[]{:S(2)}) collective-permute-start(bf16[160,2048]{1,0:T(8,128)(2,1)S(1)} %get-tuple-element.349), channel_id=1, source_target_pairs={{0,3},{1,0},{2,1},{3,2},{4,7},{5,4},{6,5},{7,6},{8,11},{9,8},{10,9... | collective-permute-start | bytes 1966088 | tf_op jit(solution)/shard_map/ppermute | solution.py:128
  229.6 93.1 %collective-permute-start.9 = (bf16[160,2048]{1,0:T(8,128)(2,1)S(1)}, bf16[160,2048]{1,0:T(8,128)(2,1)S(1)}, u32[]{:S(2)}, u32[]{:S(2)}) collective-permute-start(bf16[160,2048]{1,0:T(8,128)(2,1)S(1)} %get-tuple-element.350), channel_id=1, source_target_pairs={{0,2},{1,3},{2,0},{3,1},{4,6},{5,7},{6,4},{7,5},{8,10},{9,11},{10,... | collective-permute-start | bytes 1966088 | tf_op jit(solution)/shard_map/ppermute | solution.py:128
  229.6 93.1 %collective-permute-start.8 = (bf16[160,2048]{1,0:T(8,128)(2,1)S(1)}, bf16[160,2048]{1,0:T(8,128)(2,1)S(1)}, u32[]{:S(2)}, u32[]{:S(2)}) collective-permute-start(bf16[160,2048]{1,0:T(8,128)(2,1)S(1)} %get-tuple-element.348), channel_id=1, source_target_pairs={{0,1},{1,2},{2,3},{3,0},{4,5},{5,6},{6,7},{7,4},{8,9},{9,10},{10,1... | collective-permute-start | bytes 1966088 | tf_op jit(solution)/shard_map/ppermute | solution.py:128
  230.8 84.9 %collective-permute-start.3 = (bf16[96,2048]{1,0:T(8,128)(2,1)S(1)}, bf16[96,2048]{1,0:T(8,128)(2,1)S(1)}, u32[]{:S(2)}, u32[]{:S(2)}) collective-permute-start(bf16[96,2048]{1,0:T(8,128)(2,1)S(1)} %get-tuple-element.366), channel_id=1, source_target_pairs={{0,2},{1,3},{2,0},{3,1},{4,6},{5,7},{6,4},{7,5},{8,10},{9,11},{10,... | collective-permute-start | bytes 1179656 | tf_op jit(solution)/shard_map/ppermute | solution.py:128
  234.9 80.8 %collective-permute-start.2 = (bf16[96,2048]{1,0:T(8,128)(2,1)S(1)}, bf16[96,2048]{1,0:T(8,128)(2,1)S(1)}, u32[]{:S(2)}, u32[]{:S(2)}) collective-permute-start(bf16[96,2048]{1,0:T(8,128)(2,1)S(1)} %get-tuple-element.364), channel_id=1, source_target_pairs={{0,1},{1,2},{2,3},{3,0},{4,5},{5,6},{6,7},{7,4},{8,9},{9,10},{10,1... | collective-permute-start | bytes 1179656 | tf_op jit(solution)/shard_map/ppermute | solution.py:128
  324.4 137.6 %collective-permute-start.11 = (bf16[160,2048]{1,0:T(8,128)(2,1)}, bf16[160,2048]{1,0:T(8,128)(2,1)}, u32[]{:S(2)}, u32[]{:S(2)}) collective-permute-start(bf16[160,2048]{1,0:T(8,128)(2,1)} %get-tuple-element.323), channel_id=1, source_target_pairs={{0,1},{1,2},{2,3},{3,0},{4,5},{5,6},{6,7},{7,4},{8,9},{9,10},{10,1... | collective-permute-start | bytes 1966088 | tf_op jit(solution)/shard_map/ppermute | solution.py:134
  324.4 141.7 %collective-permute-start.12 = (bf16[160,2048]{1,0:T(8,128)(2,1)}, bf16[160,2048]{1,0:T(8,128)(2,1)}, u32[]{:S(2)}, u32[]{:S(2)}) collective-permute-start(bf16[160,2048]{1,0:T(8,128)(2,1)} %get-tuple-element.323), channel_id=1, source_target_pairs={{0,2},{1,3},{2,0},{3,1},{4,6},{5,7},{6,4},{7,5},{8,10},{9,11},{10,... | collective-permute-start | bytes 1966088 | tf_op jit(solution)/shard_map/ppermute | solution.py:134
  394.1 61.4 %collective-permute-start.15 = (bf16[96,2048]{1,0:T(8,128)(2,1)S(1)}, bf16[96,2048]{1,0:T(8,128)(2,1)S(1)}, u32[]{:S(2)}, u32[]{:S(2)}) collective-permute-start(bf16[96,2048]{1,0:T(8,128)(2,1)S(1)} %get-tuple-element.363), channel_id=1, source_target_pairs={{0,2},{1,3},{2,0},{3,1},{4,6},{5,7},{6,4},{7,5},{8,10},{9,11},{10,... | collective-permute-start | bytes 1179656 | tf_op jit(solution)/shard_map/ppermute | solution.py:128
  456.7 154.3 %collective-permute-start.17 = (bf16[96,2048]{1,0:T(8,128)(2,1)}, bf16[96,2048]{1,0:T(8,128)(2,1)}, u32[]{:S(2)}, u32[]{:S(2)}) collective-permute-start(bf16[96,2048]{1,0:T(8,128)(2,1)} %get-tuple-element.313), channel_id=1, source_target_pairs={{0,1},{1,2},{2,3},{3,0},{4,5},{5,6},{6,7},{7,4},{8,9},{9,10},{10,1... | collective-permute-start | bytes 1179656 | tf_op jit(solution)/shard_map/ppermute | solution.py:134
  460.0 152.4 %collective-permute-start.18 = (bf16[96,2048]{1,0:T(8,128)(2,1)}, bf16[96,2048]{1,0:T(8,128)(2,1)}, u32[]{:S(2)}, u32[]{:S(2)}) collective-permute-start(bf16[96,2048]{1,0:T(8,128)(2,1)} %get-tuple-element.313), channel_id=1, source_target_pairs={{0,2},{1,3},{2,0},{3,1},{4,6},{5,7},{6,4},{7,5},{8,10},{9,11},{10,... | collective-permute-start | bytes 1179656 | tf_op jit(solution)/shard_map/ppermute | solution.py:134
  462.0 151.6 %collective-permute-start.19 = (bf16[96,2048]{1,0:T(8,128)(2,1)}, bf16[96,2048]{1,0:T(8,128)(2,1)}, u32[]{:S(2)}, u32[]{:S(2)}) collective-permute-start(bf16[96,2048]{1,0:T(8,128)(2,1)} %get-tuple-element.313), channel_id=1, source_target_pairs={{0,3},{1,0},{2,1},{3,2},{4,7},{5,4},{6,5},{7,6},{8,11},{9,8},{10,9... | collective-permute-start | bytes 1179656 | tf_op jit(solution)/shard_map/ppermute | solution.py:134
  584.5 70.8 %collective-permute-start.21 = (bf16[160,2048]{1,0:T(8,128)(2,1)S(1)}, bf16[160,2048]{1,0:T(8,128)(2,1)S(1)}, u32[]{:S(2)}, u32[]{:S(2)}) collective-permute-start(bf16[160,2048]{1,0:T(8,128)(2,1)S(1)} %get-tuple-element.347), channel_id=1, source_target_pairs={{0,2},{1,3},{2,0},{3,1},{4,6},{5,7},{6,4},{7,5},{8,10},{9,11},{10,... | collective-permute-start | bytes 1966088 | tf_op jit(solution)/shard_map/ppermute | solution.py:128
  906.2 445.7 %reduce-scatter.6.cloned.1.call-start = ((), (), s32[]{:S(2)}) async-start(), calls=%async_computation.9 | async-start | bytes 7077888 | tf_op jit(solution)/shard_map/reduce_scatter | solution.py:199
  937.7 418.5 %reduce-scatter.10.cloned.1.call-start = ((), (), s32[]{:S(2)}) async-start(), calls=%async_computation.11 | async-start | bytes 9437184 | tf_op jit(solution)/shard_map/reduce_scatter | solution.py:199
  938.4 420.5 %reduce-scatter.12.cloned.1.call-start = ((), (), s32[]{:S(2)}) async-start(), calls=%async_computation.12 | async-start | bytes 9437184 | tf_op jit(solution)/shard_map/reduce_scatter | solution.py:199
  939.2 422.6 %reduce-scatter.14.cloned.1.call-start = ((), (), s32[]{:S(2)}) async-start(), calls=%async_computation.13 | async-start | bytes 9437184 | tf_op jit(solution)/shard_map/reduce_scatter | solution.py:199
  1016.1 92.3 %collective-permute-start.27 = (bf16[256,2048]{1,0:T(8,128)(2,1)}, bf16[256,2048]{1,0:T(8,128)(2,1)}, u32[]{:S(2)}, u32[]{:S(2)}) collective-permute-start(bf16[256,2048]{1,0:T(8,128)(2,1)} %get-tuple-element.344), channel_id=1, source_target_pairs={{0,2},{1,3},{2,0},{3,1},{4,6},{5,7},{6,4},{7,5},{8,10},{9,11},{10,... | collective-permute-start | bytes 3145736 | tf_op jit(solution)/shard_map/ppermute | solution.py:128
  1016.7 91.7 %collective-permute-start.26 = (bf16[256,2048]{1,0:T(8,128)(2,1)}, bf16[256,2048]{1,0:T(8,128)(2,1)}, u32[]{:S(2)}, u32[]{:S(2)}) collective-permute-start(bf16[256,2048]{1,0:T(8,128)(2,1)} %get-tuple-element.342), channel_id=1, source_target_pairs={{0,1},{1,2},{2,3},{3,0},{4,5},{5,6},{6,7},{7,4},{8,9},{9,10},{10,1... | collective-permute-start | bytes 3145736 | tf_op jit(solution)/shard_map/ppermute | solution.py:128
  1040.6 95.6 %collective-permute-start.38 = (bf16[256,2048]{1,0:T(8,128)(2,1)}, bf16[256,2048]{1,0:T(8,128)(2,1)}, u32[]{:S(2)}, u32[]{:S(2)}) collective-permute-start(bf16[256,2048]{1,0:T(8,128)(2,1)} %get-tuple-element.335), channel_id=1, source_target_pairs={{2,1},{3,2},{6,5},{7,6},{10,9},{11,10},{14,13},{15,14},{18,17},{19... | collective-permute-start | bytes 3145736 | tf_op jit(solution)/shard_map/ppermute | solution.py:158
  1116.4 66.2 %collective-permute-start.29 = (bf16[256,2048]{1,0:T(8,128)(2,1)}, bf16[256,2048]{1,0:T(8,128)(2,1)}, u32[]{:S(2)}, u32[]{:S(2)}) collective-permute-start(bf16[256,2048]{1,0:T(8,128)(2,1)} %get-tuple-element.311), channel_id=1, source_target_pairs={{0,1},{1,2},{2,3},{3,0},{4,5},{5,6},{6,7},{7,4},{8,9},{9,10},{10,1... | collective-permute-start | bytes 3145736 | tf_op jit(solution)/shard_map/ppermute | solution.py:134
  1131.4 66.9 %collective-permute-start.30 = (bf16[256,2048]{1,0:T(8,128)(2,1)}, bf16[256,2048]{1,0:T(8,128)(2,1)}, u32[]{:S(2)}, u32[]{:S(2)}) collective-permute-start(bf16[256,2048]{1,0:T(8,128)(2,1)} %get-tuple-element.311), channel_id=1, source_target_pairs={{0,2},{1,3},{2,0},{3,1},{4,6},{5,7},{6,4},{7,5},{8,10},{9,11},{10,... | collective-permute-start | bytes 3145736 | tf_op jit(solution)/shard_map/ppermute | solution.py:134
  1132.8 67.9 %collective-permute-start.36 = (bf16[256,2048]{1,0:T(8,128)(2,1)}, bf16[256,2048]{1,0:T(8,128)(2,1)}, u32[]{:S(2)}, u32[]{:S(2)}) collective-permute-start(bf16[256,2048]{1,0:T(8,128)(2,1)} %get-tuple-element.334), channel_id=1, source_target_pairs={{0,1},{1,2},{2,3},{4,5},{5,6},{6,7},{8,9},{9,10},{10,11},{12,13},{... | collective-permute-start | bytes 3145736 | tf_op jit(solution)/shard_map/ppermute | solution.py:157
  1139.1 80.5 %collective-permute-start.39 = (bf16[256,2048]{1,0:T(8,128)(2,1)}, bf16[256,2048]{1,0:T(8,128)(2,1)}, u32[]{:S(2)}, u32[]{:S(2)}) collective-permute-start(bf16[256,2048]{1,0:T(8,128)(2,1)} %fusion.84), channel_id=1, source_target_pairs={{1,0},{2,1},{3,2},{5,4},{6,5},{7,6},{9,8},{10,9},{11,10},{13,12},{... | collective-permute-start | bytes 3145736 | tf_op jit(solution)/shard_map/ppermute | solution.py:158
  1140.4 114.6 %collective-permute-start.31 = (bf16[256,2048]{1,0:T(8,128)(2,1)}, bf16[256,2048]{1,0:T(8,128)(2,1)}, u32[]{:S(2)}, u32[]{:S(2)}) collective-permute-start(bf16[256,2048]{1,0:T(8,128)(2,1)} %get-tuple-element.311), channel_id=1, source_target_pairs={{0,3},{1,0},{2,1},{3,2},{4,7},{5,4},{6,5},{7,6},{8,11},{9,8},{10,9... | collective-permute-start | bytes 3145736 | tf_op jit(solution)/shard_map/ppermute | solution.py:134
  1226.4 49.1 %collective-permute-start.40 = (bf16[256,2048]{1,0:T(8,128)(2,1)}, bf16[256,2048]{1,0:T(8,128)(2,1)}, u32[]{:S(2)}, u32[]{:S(2)}) collective-permute-start(bf16[256,2048]{1,0:T(8,128)(2,1)} %get-tuple-element.309), channel_id=1, source_target_pairs={{0,1},{1,2},{2,3},{4,5},{5,6},{6,7},{8,9},{9,10},{10,11},{12,13},{... | collective-permute-start | bytes 3145736 | tf_op jit(solution)/shard_map/ppermute | solution.py:168
  (132 other events, 1866.8 us)
Sparse Core Ops, SparseCore 0:
  13.2 58.5 all-gather.4
  74.2 55.8 all-gather.10
  132.0 54.2 all-gather.8
  188.1 54.2 all-gather.6
  906.3 50.3 reduce-scatter.7
  960.0 61.5 reduce-scatter.5
  1025.0 71.5 reduce-scatter.9
  1100.0 71.4 reduce-scatter.11
  1175.0 71.2 reduce-scatter.13

commit v6 on v4

--- a/solution.py
+++ b/solution.py
@@ -333,29 +333,41 @@
             jnp.stack(value_grads).reshape((ctx_count, half_len, head_count, HEAD_DIM)), CTX, ctx_count
         ).reshape(split_heads),
     )
-    grad_q_pre = (
-        rotate_back(jnp.stack(query_grads), cosine, sine_table)
-        .astype(bf_type)
-        .reshape(row_total, head_cols)
-    )
-    grad_k_pre = (
-        rotate_back(grad_keys, cosine, sine_table).astype(bf_type).reshape(row_total, head_cols)
-    )
-    grad_v_pre = grad_values.astype(bf_type).reshape(row_total, head_cols)
+    query_grad = jnp.stack(query_grads)
+    q_parts, k_parts, v_parts, token_parts = [], [], [], []
+    for index in range(len(MID_SPLIT)):
+        low_row, high_row = bounds[index], bounds[index + 1]
+        count = high_row - low_row
+        cos_part, sin_part = cosine[low_row:high_row], sine_table[low_row:high_row]
+        q_part = rotate_back(query_grad[:, low_row:high_row], cos_part, sin_part)
+        q_part = q_part.astype(bf_type).reshape(count, head_cols)
+        k_part = rotate_back(grad_keys[:, low_row:high_row], cos_part, sin_part)
+        k_part = k_part.astype(bf_type).reshape(count, head_cols)
+        v_part = grad_values[:, low_row:high_row].astype(bf_type).reshape(count, head_cols)
+        input_part = (
+            jnp.einsum("rc,dc->rd", q_part, query_full, preferred_element_type=jnp.float32)
+            + jnp.einsum("rc,dc->rd", k_part, key_full, preferred_element_type=jnp.float32)
+            + jnp.einsum("rc,dc->rd", v_part, value_full, preferred_element_type=jnp.float32)
+        )
+        input_part = tp_psum(input_part, tp_count).astype(jnp.float32)
+        token_parts.append(
+            grad_resid[low_row:high_row]
+            + norm_back(normed_one[low_row:high_row], scale_one[low_row:high_row], input_part)
+        )
+        q_parts.append(q_part)
+        k_parts.append(k_part)
+        v_parts.append(v_part)
+    grad_q_pre = jnp.concatenate(q_parts, axis=0)
+    grad_k_pre = jnp.concatenate(k_parts, axis=0)
+    grad_v_pre = jnp.concatenate(v_parts, axis=0)
     grad_wq = jnp.einsum("rd,rc->dc", input_one, grad_q_pre, preferred_element_type=jnp.float32)
     grad_wk = jnp.einsum("rd,rc->dc", input_one, grad_k_pre, preferred_element_type=jnp.float32)
     grad_wv = jnp.einsum("rd,rc->dc", input_one, grad_v_pre, preferred_element_type=jnp.float32)
-    grad_input_one = (
-        jnp.einsum("rc,dc->rd", grad_q_pre, query_full, preferred_element_type=jnp.float32)
-        + jnp.einsum("rc,dc->rd", grad_k_pre, key_full, preferred_element_type=jnp.float32)
-        + jnp.einsum("rc,dc->rd", grad_v_pre, value_full, preferred_element_type=jnp.float32)
-    )
     qkv_grads = jnp.split(
         scatter_low(jnp.concatenate([grad_wq, grad_wk, grad_wv], axis=1), 0), 3, axis=1
     )
     attn_grads = (qkv_grads[0], qkv_grads[1], qkv_grads[2], scatter_low(grad_wout, 1))
-    grad_input_one = tp_psum(grad_input_one, tp_count).astype(jnp.float32)
-    grad_tokens = grad_resid + norm_back(normed_one, scale_one, grad_input_one)
+    grad_tokens = jnp.concatenate(token_parts, axis=0)
     output = final_sum.astype(bf_type).reshape(seq_count, half_len, model_width)
     grad_tokens = grad_tokens.reshape(seq_count, half_len, model_width)
     return (

time: 1370 us -> 1370 us (level)
  starting transfers between devices: 152 us -> 251 us
  waiting for transfers between devices: 529 us -> 430 us
  other arithmetic: 169 us -> 186 us
  local copies, waits for them, and re-layouts: 148 us -> 133 us
    ppermute x18 -> x21, starting transfers between devices: 80.4 us -> 215 us  [tp_psum(): total = total + lax.ppermute(piece, TP, pairs).astype(jnp.float32)]
    ppermute x18 -> x21, waiting for transfers between devices: 306 us -> 240 us  [tp_psum(): total = total + lax.ppermute(piece, TP, pairs).astype(jnp.float32)]
    ppermute x18 -> x21, starting transfers between devices: 69.5 us -> 34.1 us  [tp_psum(): got = lax.ppermute(reduced, TP, pairs)]
    ppermute x18 -> x21, waiting for transfers between devices: 160 us -> 135 us  [tp_psum(): got = lax.ppermute(reduced, TP, pairs)]
    unnamed x196 -> x206, local copies, waits for them, and re-layouts: 25.5 us -> 31.9 us
  transfers between devices with their start and end apart: 49 -> 55, of which waited for: 18 -> 20; matrix products, arithmetic and copies ran while one was open for 33% -> 34% of each run, Pallas kernels for 0% -> 0%
where the time goes in v6:
time: 1370 us; the launch traced here: 1350 us
  waiting for transfers between devices  430 us (31%)
  matrix products  334 us (24%)
  starting transfers between devices  251 us (18%)
  other arithmetic  186 us (14%)
  local copies, waits for them, and re-layouts  133 us (10%)
  between operations  16.8 us (1%)
    ppermute x21, waiting for transfers between devices, tp_psum(): total = total + lax.ppermute(piece, TP, pairs).astype(jnp.float32)  240 us
    ppermute x21, starting transfers between devices, tp_psum(): total = total + lax.ppermute(piece, TP, pairs).astype(jnp.float32)  215 us
    ppermute x21, waiting for transfers between devices, tp_psum(): got = lax.ppermute(reduced, TP, pairs)  135 us
    dot_general x11, matrix products, matmul_low(): return jnp.dot(left, right, preferred_element_type=jnp.float32)  75.9 us
    all_gather x1, waiting for transfers between devices, block(): lax.all_gather(mlp_low[2], (SHARD, CTX), axis=1, tiled=True)  37.1 us
    ppermute x21, starting transfers between devices, tp_psum(): got = lax.ppermute(reduced, TP, pairs)  34.1 us
    unnamed x206, local copies, waits for them, and re-layouts  31.9 us
    convert_element_type x2, other arithmetic, one_block(): grad_scores = (probability * (grad_prob - inner_sum)).astype(jnp.bfloat16)  29.7 us
  transfers between devices with their start and end apart: 55, of which 20 were waited for; matrix products, arithmetic and copies ran while one was open for 34% of the time, Pallas kernels for 0%

profile of v6, /device:TPU:0, one launch (start us, length us, event | category | flops | bytes accessed | tf_op | source)
XLA Modules:
  0.0 1354.5 jit_solution(2397396094472087209)
XLA Ops:
  54.9 16.9 %all-gather.5.cloned.1.call-done = bf16[2048,2048]{0,1:T(8,128)(2,1)} async-done(((bf16[256,2048]{0,1:T(8,128)(2,1)}), bf16[2048,2048]{0,1:T(8,128)(2,1)}) %all-gather.5.cloned.1.call-update) | async-done | bytes 8388624 | tf_op jit(solution)/shard_map/all_gather | solution.py:229
  93.0 37.1 %all-gather.11.cloned.1.call-done = bf16[2048,2048]{1,0:T(8,128)(2,1)} async-done(((bf16[2048,256]{1,0:T(8,128)(2,1)}), bf16[2048,2048]{1,0:T(8,128)(2,1)}) %all-gather.11.cloned.1.call-update) | async-done | bytes 8388624 | tf_op jit(solution)/shard_map/all_gather | solution.py:240
  130.1 11.5 fusion.130
  176.7 35.1 %while.27 = (s32[]{:T(128)}, bf16[2,512,4,128]{3,2,1,0:T(4,128)(2,1)}, f32[2,4,512]{2,1,0:T(4,128)S(1)}, s32[2]{0:T(128)S(1)}, s32[]{:T(128)}, /*index=5*/s32[]{...) while((s32[]{:T(128)}, ...), condition=%wide.region_5.6_spmd, body=%wide.region_2.5_spmd.sunk | while | flops 2195980800 | bytes 77668600 | solution.py:77
  237.5 73.1 %collective-permute-done.3 = bf16[96,2048]{1,0:T(8,128)(2,1)S(1)} collective-permute-done((bf16[96,2048]{1,0:T(8,128)(2,1)S(1)}, bf16[96,2048]{1,0:T(8,128)(2,1)S(1)}, u32[]{:S(2)}, u32[]{:S(2)}) %collective-permute-start.3) | collective-permute-done | bytes 393248 | tf_op jit(solution)/shard_map/ppermute | solution.py:128
  325.1 16.8 %collective-permute-done.6 = bf16[96,2048]{1,0:T(8,128)(2,1)S(1)} collective-permute-done((bf16[96,2048]{1,0:T(8,128)(2,1)S(1)}, bf16[96,2048]{1,0:T(8,128)(2,1)S(1)}, u32[]{:S(2)}, u32[]{:S(2)}) %collective-permute-start.6) | collective-permute-done | bytes 393248 | tf_op jit(solution)/shard_map/ppermute | solution.py:134
  389.0 26.0 %collective-permute-start.15 = (bf16[96,2048]{1,0:T(8,128)(2,1)S(1)}, bf16[96,2048]{1,0:T(8,128)(2,1)S(1)}, u32[]{:S(2)}, u32[]{:S(2)}) collective-permute-start(bf16[96,2048]{1,0:T(8,128)(2,1)S(1)} %get-tuple-element.363), channel_id=1, source_target_pairs={{0,2},{1,3},{2,0},{3,1},{4,6},{5,7},{6,4},{7,5},{8,10},{9,11},{10,... | collective-permute-start | bytes 1179656 | tf_op jit(solution)/shard_map/ppermute | solution.py:128
  427.3 23.0 %collective-permute-done.15 = bf16[96,2048]{1,0:T(8,128)(2,1)S(1)} collective-permute-done((bf16[96,2048]{1,0:T(8,128)(2,1)S(1)}, bf16[96,2048]{1,0:T(8,128)(2,1)S(1)}, u32[]{:S(2)}, u32[]{:S(2)}) %collective-permute-start.15) | collective-permute-done | bytes 393248 | tf_op jit(solution)/shard_map/ppermute | solution.py:128
  481.5 12.0 multiply_convert_fusion.2
  514.2 12.6 fusion.186
  537.1 13.1 fusion.129
  579.4 16.0 %collective-permute-start.21 = (bf16[160,2048]{1,0:T(8,128)(2,1)S(1)}, bf16[160,2048]{1,0:T(8,128)(2,1)S(1)}, u32[]{:S(2)}, u32[]{:S(2)}) collective-permute-start(bf16[160,2048]{1,0:T(8,128)(2,1)S(1)} %get-tuple-element.340), channel_id=1, source_target_pairs={{0,2},{1,3},{2,0},{3,1},{4,6},{5,7},{6,4},{7,5},{8,10},{9,11},{10,... | collective-permute-start | bytes 1966088 | tf_op jit(solution)/shard_map/ppermute | solution.py:128
  610.7 39.5 %collective-permute-done.21 = bf16[160,2048]{1,0:T(8,128)(2,1)S(1)} collective-permute-done((bf16[160,2048]{1,0:T(8,128)(2,1)S(1)}, bf16[160,2048]{1,0:T(8,128)(2,1)S(1)}, u32[]{:S(2)}, u32[]{:S(2)}) %collective-permute-start.21) | collective-permute-done | bytes 655392 | tf_op jit(solution)/shard_map/ppermute | solution.py:128
  660.0 11.7 collective-permute-done.23
  672.8 23.2 %collective-permute-done.24 = bf16[160,2048]{1,0:T(8,128)(2,1)} collective-permute-done((bf16[160,2048]{1,0:T(8,128)(2,1)}, bf16[160,2048]{1,0:T(8,128)(2,1)}, u32[]{:S(2)}, u32[]{:S(2)}) %collective-permute-start.24) | collective-permute-done | bytes 655392 | tf_op jit(solution)/shard_map/ppermute | solution.py:134
  712.5 130.1 %while.28 = (s32[]{:T(128)}, f32[2048,4,128]{0,2,1:T(8,128)}, f32[2048,4,128]{0,2,1:T(8,128)}, f32[2,512,4,128]{3,1,0,2:T(8,128)}, bf16[2,512,4,128]{3,1,2,0:T(8...) while((s32[]{:T(128)}, f32[2048,4,128]{0,2,1:T(8,128)}, ...), condition=%wide.region_16.17_spmd.clone, body=%wide.region_14.16_spmd.clone.sunk | while | flops 5439226368 | bytes 198246768 | solution.py:113
  724.5 12.9 multiply_reduce_fusion.5
  737.4 14.8 %multiply_convert_fusion.9 = bf16[4,512,2048]{2,1,0:T(8,128)(2,1)} fusion(f32[4,512,2048]{2,1,0:T(8,128)} %get-tuple-element.520, f32[4,512,2048]{2,1,0:T(8,128)} %fusion.270, f32[4,512]{1,0:T(4,128)S(1)} %get-tuple-element.521, f32[4,512]{1,0:T(4,128)S(1)} %dynamic-slice_bitcast_fusion.23, pred[512,2048]{1,0:T(8,128)(4,1)S(1)} %fusion.271), kind=kLoop, calls=%fused_computation.21.clone.1 | loop fusion | flops 25165824 | bytes 43008000 | tf_op jit(solution)/shard_map/while/body/eval_jaxpr/convert_element_type | solution.py:98
  759.7 13.0 bitcast_add_fusion.7
  788.2 12.9 multiply_reduce_fusion.5
  801.0 14.8 %multiply_convert_fusion.9 = bf16[4,512,2048]{2,1,0:T(8,128)(2,1)} fusion(f32[4,512,2048]{2,1,0:T(8,128)} %get-tuple-element.520, f32[4,512,2048]{2,1,0:T(8,128)} %fusion.270, f32[4,512]{1,0:T(4,128)S(1)} %get-tuple-element.521, f32[4,512]{1,0:T(4,128)S(1)} %dynamic-slice_bitcast_fusion.23, pred[512,2048]{1,0:T(8,128)(4,1)S(1)} %fusion.271), kind=kLoop, calls=%fused_computation.21.clone.1 | loop fusion | flops 25165824 | bytes 43008000 | tf_op jit(solution)/shard_map/while/body/eval_jaxpr/convert_element_type | solution.py:98
  824.5 14.1 %bitcast_add_fusion.7 = f32[2048,4,128]{0,2,1:T(8,128)} fusion(f32[2048,4,128]{0,2,1:T(8,128)} %get-tuple-element.572, f32[4,512,2048]{2,1,0:T(8,128)} %fusion.270, f32[4,512]{1,0:T(4,128)S(1)} %dynamic-slice_bitcast_fusion.23, pred[512,2048]{1,0:T(8,128)(4,1)S(1)} %fusion.271, pred[]{:T(512)S(6)} %compare.11, ...), kind=kOutput, calls=%fused_computation.27.clone.1 | convolution fusion | flops 1092616192 | bytes 26746884 | tf_op jit(solution)/shard_map/while/body/eval_jaxpr/hqk,qhd->khd/dot_general | solution.py:107
  855.7 14.2 %constant_dynamic-slice_fusion.1 = (f32[1,1024,4,128]{1,0,3,2:T(1,128)}, f32[1,1024,4,128]{1,0,3,2:T(1,128)S(1)}, f32[1,1024,4,128]{1,0,3,2:T(1,128)}, f32[1,1024,4,128]{1,0,3,2:T(1,128)S(1)}) fusion(f32[2,1024,4,128]{1,0,3,2:T(2,128)} %reshape_stack.7, s32[]{:T(128)S(6)} %select_n.215, s32[]{:T(128)S(6)} %select_n.217, f32[2,1024,4,128]{1,0,3,2:T(2,128)} %reshape_stack.6), kind=kLoop, calls=%fused_computation.282 | loop fusion | bytes 16777224 | tf_op jit(solution)/shard_map/jit(dynamic_index_in_dim)/dynamic_slice | solution.py:154
  929.5 11.5 pad_maximum_fusion.1
  946.2 12.6 collective-permute-start.28
  960.9 21.9 %collective-permute-done.28 = bf16[256,2048]{1,0:T(8,128)(2,1)} collective-permute-done((bf16[256,2048]{1,0:T(8,128)(2,1)}, bf16[256,2048]{1,0:T(8,128)(2,1)}, u32[]{:S(2)}, u32[]{:S(2)}) %collective-permute-start.28) | collective-permute-done | bytes 1048608 | tf_op jit(solution)/shard_map/ppermute | solution.py:128
  982.7 68.2 %collective-permute-done.27 = bf16[256,2048]{1,0:T(8,128)(2,1)} collective-permute-done((bf16[256,2048]{1,0:T(8,128)(2,1)}, bf16[256,2048]{1,0:T(8,128)(2,1)}, u32[]{:S(2)}, u32[]{:S(2)}) %collective-permute-start.27) | collective-permute-done | bytes 1048608 | tf_op jit(solution)/shard_map/ppermute | solution.py:128
  1084.1 69.2 %collective-permute-start.40 = (bf16[160,2048]{1,0:T(8,128)(2,1)}, bf16[160,2048]{1,0:T(8,128)(2,1)S(1)}, u32[]{:S(2)}, u32[]{:S(2)}) collective-permute-start(bf16[160,2048]{1,0:T(8,128)(2,1)} %get-tuple-element.335), channel_id=1, source_target_pairs={{0,1},{1,2},{2,3},{3,0},{4,5},{5,6},{6,7},{7,4},{8,9},{9,10},{10,1... | collective-permute-start | bytes 1966088 | tf_op jit(solution)/shard_map/ppermute | solution.py:128
  1154.8 24.5 %collective-permute-start.36 = (bf16[96,2048]{1,0:T(8,128)(2,1)S(1)}, bf16[96,2048]{1,0:T(8,128)(2,1)S(1)}, u32[]{:S(2)}, u32[]{:S(2)}) collective-permute-start(bf16[96,2048]{1,0:T(8,128)(2,1)S(1)} %get-tuple-element.359), channel_id=1, source_target_pairs={{0,3},{1,0},{2,1},{3,2},{4,7},{5,4},{6,5},{7,6},{8,11},{9,8},{10,9... | collective-permute-start | bytes 1179656 | tf_op jit(solution)/shard_map/ppermute | solution.py:128
  1188.8 42.8 %collective-permute-start.34 = (bf16[96,2048]{1,0:T(8,128)(2,1)S(1)}, bf16[96,2048]{1,0:T(8,128)(2,1)S(1)}, u32[]{:S(2)}, u32[]{:S(2)}) collective-permute-start(bf16[96,2048]{1,0:T(8,128)(2,1)S(1)} %get-tuple-element.358), channel_id=1, source_target_pairs={{0,1},{1,2},{2,3},{3,0},{4,5},{5,6},{6,7},{7,4},{8,9},{9,10},{10,1... | collective-permute-start | bytes 1179656 | tf_op jit(solution)/shard_map/ppermute | solution.py:128
  1252.9 16.8 %collective-permute-done.38 = bf16[96,2048]{1,0:T(8,128)(2,1)S(1)} collective-permute-done((bf16[96,2048]{1,0:T(8,128)(2,1)S(1)}, bf16[96,2048]{1,0:T(8,128)(2,1)S(1)}, u32[]{:S(2)}, u32[]{:S(2)}) %collective-permute-start.38) | collective-permute-done | bytes 393248 | tf_op jit(solution)/shard_map/ppermute | solution.py:134
  1285.9 32.8 %collective-permute-done.44 = bf16[160,2048]{1,0:T(8,128)(2,1)} collective-permute-done((bf16[160,2048]{1,0:T(8,128)(2,1)}, bf16[160,2048]{1,0:T(8,128)(2,1)}, u32[]{:S(2)}, u32[]{:S(2)}) %collective-permute-start.44) | collective-permute-done | bytes 655392 | tf_op jit(solution)/shard_map/ppermute | solution.py:134
  (566 shorter events, 604.5 us)
Async XLA Ops:
  7.2 64.6 %all-gather.5.cloned.1.call-start = ((), (), s32[]{:S(2)}) async-start(), calls=%async_computation.5 | async-start | bytes 9437184 | tf_op jit(solution)/shard_map/all_gather | solution.py:229
  13.1 117.1 %all-gather.11.cloned.1.call-start = ((), (), s32[]{:S(2)}) async-start(), calls=%async_computation.8 | async-start | bytes 9437184 | tf_op jit(solution)/shard_map/all_gather | solution.py:240
  14.2 332.7 %all-gather.9.cloned.1.call-start = ((), (), s32[]{:S(2)}) async-start(), calls=%async_computation.7 | async-start | bytes 9437184 | tf_op jit(solution)/shard_map/all_gather | solution.py:239
  17.2 338.2 %all-gather.7.cloned.1.call-start = ((), (), s32[]{:S(2)}) async-start(), calls=%async_computation.6 | async-start | bytes 9437184 | tf_op jit(solution)/shard_map/all_gather | solution.py:238
  18.4 1254.7 %reduce-scatter.8.cloned.1.call-start = ((), (), s32[]{:S(2)}) async-start(), calls=%async_computation.10 | async-start | bytes 2359296 | tf_op jit(solution)/shard_map/reduce_scatter | solution.py:163
  80.5 89.1 %collective-permute-start = (bf16[1,1024,4,128]{1,3,2,0:T(8,128)(2,1)}, bf16[1,1024,4,128]{1,3,2,0:T(8,128)(2,1)}, u32[]{:S(2)}, u32[]{:S(2)}) collective-permute-start(bf16[1,1024,4,128]{1,3,2,0:T(8,128)(2,1)} %fusion.70), channel_id=1, source_target_pairs={{0,4},{4,0},{1,5},{5,1},{2,6},{6,2},{3,7},{7,3},{8,12},{12,8},{9,1... | collective-permute-start | bytes 3145736 | tf_op jit(solution)/shard_map/ppermute | solution.py:147
  89.0 85.0 %collective-permute-start.1 = (bf16[1,1024,4,128]{3,1,2,0:T(8,128)(2,1)}, bf16[1,1024,4,128]{3,1,2,0:T(8,128)(2,1)}, u32[]{:S(2)}, u32[]{:S(2)}) collective-permute-start(bf16[1,1024,4,128]{3,1,2,0:T(8,128)(2,1)} %bitcast.21), channel_id=1, source_target_pairs={{0,4},{4,0},{1,5},{5,1},{2,6},{6,2},{3,7},{7,3},{8,12},{12,8},{9,1... | collective-permute-start | bytes 3145736 | tf_op jit(solution)/shard_map/ppermute | solution.py:147
  223.7 90.9 %collective-permute-start.10 = (bf16[160,2048]{1,0:T(8,128)(2,1)S(1)}, bf16[160,2048]{1,0:T(8,128)(2,1)S(1)}, u32[]{:S(2)}, u32[]{:S(2)}) collective-permute-start(bf16[160,2048]{1,0:T(8,128)(2,1)S(1)} %get-tuple-element.342), channel_id=1, source_target_pairs={{0,3},{1,0},{2,1},{3,2},{4,7},{5,4},{6,5},{7,6},{8,11},{9,8},{10,9... | collective-permute-start | bytes 1966088 | tf_op jit(solution)/shard_map/ppermute | solution.py:128
  225.0 92.6 %collective-permute-start.9 = (bf16[160,2048]{1,0:T(8,128)(2,1)S(1)}, bf16[160,2048]{1,0:T(8,128)(2,1)S(1)}, u32[]{:S(2)}, u32[]{:S(2)}) collective-permute-start(bf16[160,2048]{1,0:T(8,128)(2,1)S(1)} %get-tuple-element.343), channel_id=1, source_target_pairs={{0,2},{1,3},{2,0},{3,1},{4,6},{5,7},{6,4},{7,5},{8,10},{9,11},{10,... | collective-permute-start | bytes 1966088 | tf_op jit(solution)/shard_map/ppermute | solution.py:128
  225.0 92.6 %collective-permute-start.8 = (bf16[160,2048]{1,0:T(8,128)(2,1)S(1)}, bf16[160,2048]{1,0:T(8,128)(2,1)S(1)}, u32[]{:S(2)}, u32[]{:S(2)}) collective-permute-start(bf16[160,2048]{1,0:T(8,128)(2,1)S(1)} %get-tuple-element.341), channel_id=1, source_target_pairs={{0,1},{1,2},{2,3},{3,0},{4,5},{5,6},{6,7},{7,4},{8,9},{9,10},{10,1... | collective-permute-start | bytes 1966088 | tf_op jit(solution)/shard_map/ppermute | solution.py:128
  226.1 84.5 %collective-permute-start.3 = (bf16[96,2048]{1,0:T(8,128)(2,1)S(1)}, bf16[96,2048]{1,0:T(8,128)(2,1)S(1)}, u32[]{:S(2)}, u32[]{:S(2)}) collective-permute-start(bf16[96,2048]{1,0:T(8,128)(2,1)S(1)} %get-tuple-element.366), channel_id=1, source_target_pairs={{0,2},{1,3},{2,0},{3,1},{4,6},{5,7},{6,4},{7,5},{8,10},{9,11},{10,... | collective-permute-start | bytes 1179656 | tf_op jit(solution)/shard_map/ppermute | solution.py:128
  229.9 80.7 %collective-permute-start.2 = (bf16[96,2048]{1,0:T(8,128)(2,1)S(1)}, bf16[96,2048]{1,0:T(8,128)(2,1)S(1)}, u32[]{:S(2)}, u32[]{:S(2)}) collective-permute-start(bf16[96,2048]{1,0:T(8,128)(2,1)S(1)} %get-tuple-element.364), channel_id=1, source_target_pairs={{0,1},{1,2},{2,3},{3,0},{4,5},{5,6},{6,7},{7,4},{8,9},{9,10},{10,1... | collective-permute-start | bytes 1179656 | tf_op jit(solution)/shard_map/ppermute | solution.py:128
  319.3 137.5 %collective-permute-start.11 = (bf16[160,2048]{1,0:T(8,128)(2,1)}, bf16[160,2048]{1,0:T(8,128)(2,1)}, u32[]{:S(2)}, u32[]{:S(2)}) collective-permute-start(bf16[160,2048]{1,0:T(8,128)(2,1)} %get-tuple-element.315), channel_id=1, source_target_pairs={{0,1},{1,2},{2,3},{3,0},{4,5},{5,6},{6,7},{7,4},{8,9},{9,10},{10,1... | collective-permute-start | bytes 1966088 | tf_op jit(solution)/shard_map/ppermute | solution.py:134
  319.3 141.6 %collective-permute-start.12 = (bf16[160,2048]{1,0:T(8,128)(2,1)}, bf16[160,2048]{1,0:T(8,128)(2,1)}, u32[]{:S(2)}, u32[]{:S(2)}) collective-permute-start(bf16[160,2048]{1,0:T(8,128)(2,1)} %get-tuple-element.315), channel_id=1, source_target_pairs={{0,2},{1,3},{2,0},{3,1},{4,6},{5,7},{6,4},{7,5},{8,10},{9,11},{10,... | collective-permute-start | bytes 1966088 | tf_op jit(solution)/shard_map/ppermute | solution.py:134
  389.0 61.3 %collective-permute-start.15 = (bf16[96,2048]{1,0:T(8,128)(2,1)S(1)}, bf16[96,2048]{1,0:T(8,128)(2,1)S(1)}, u32[]{:S(2)}, u32[]{:S(2)}) collective-permute-start(bf16[96,2048]{1,0:T(8,128)(2,1)S(1)} %get-tuple-element.363), channel_id=1, source_target_pairs={{0,2},{1,3},{2,0},{3,1},{4,6},{5,7},{6,4},{7,5},{8,10},{9,11},{10,... | collective-permute-start | bytes 1179656 | tf_op jit(solution)/shard_map/ppermute | solution.py:128
  451.5 154.5 %collective-permute-start.17 = (bf16[96,2048]{1,0:T(8,128)(2,1)}, bf16[96,2048]{1,0:T(8,128)(2,1)}, u32[]{:S(2)}, u32[]{:S(2)}) collective-permute-start(bf16[96,2048]{1,0:T(8,128)(2,1)} %get-tuple-element.305), channel_id=1, source_target_pairs={{0,1},{1,2},{2,3},{3,0},{4,5},{5,6},{6,7},{7,4},{8,9},{9,10},{10,1... | collective-permute-start | bytes 1179656 | tf_op jit(solution)/shard_map/ppermute | solution.py:134
  454.9 152.6 %collective-permute-start.18 = (bf16[96,2048]{1,0:T(8,128)(2,1)}, bf16[96,2048]{1,0:T(8,128)(2,1)}, u32[]{:S(2)}, u32[]{:S(2)}) collective-permute-start(bf16[96,2048]{1,0:T(8,128)(2,1)} %get-tuple-element.305), channel_id=1, source_target_pairs={{0,2},{1,3},{2,0},{3,1},{4,6},{5,7},{6,4},{7,5},{8,10},{9,11},{10,... | collective-permute-start | bytes 1179656 | tf_op jit(solution)/shard_map/ppermute | solution.py:134
  456.8 151.7 %collective-permute-start.19 = (bf16[96,2048]{1,0:T(8,128)(2,1)}, bf16[96,2048]{1,0:T(8,128)(2,1)}, u32[]{:S(2)}, u32[]{:S(2)}) collective-permute-start(bf16[96,2048]{1,0:T(8,128)(2,1)} %get-tuple-element.305), channel_id=1, source_target_pairs={{0,3},{1,0},{2,1},{3,2},{4,7},{5,4},{6,5},{7,6},{8,11},{9,8},{10,9... | collective-permute-start | bytes 1179656 | tf_op jit(solution)/shard_map/ppermute | solution.py:134
  579.4 70.8 %collective-permute-start.21 = (bf16[160,2048]{1,0:T(8,128)(2,1)S(1)}, bf16[160,2048]{1,0:T(8,128)(2,1)S(1)}, u32[]{:S(2)}, u32[]{:S(2)}) collective-permute-start(bf16[160,2048]{1,0:T(8,128)(2,1)S(1)} %get-tuple-element.340), channel_id=1, source_target_pairs={{0,2},{1,3},{2,0},{3,1},{4,6},{5,7},{6,4},{7,5},{8,10},{9,11},{10,... | collective-permute-start | bytes 1966088 | tf_op jit(solution)/shard_map/ppermute | solution.py:128
  893.3 442.0 %reduce-scatter.6.cloned.1.call-start = ((), (), s32[]{:S(2)}) async-start(), calls=%async_computation.9 | async-start | bytes 7077888 | tf_op jit(solution)/shard_map/reduce_scatter | solution.py:163
  941.0 398.5 %reduce-scatter.10.cloned.1.call-start = ((), (), s32[]{:S(2)}) async-start(), calls=%async_computation.11 | async-start | bytes 9437184 | tf_op jit(solution)/shard_map/reduce_scatter | solution.py:163
  941.7 400.6 %reduce-scatter.12.cloned.1.call-start = ((), (), s32[]{:S(2)}) async-start(), calls=%async_computation.12 | async-start | bytes 9437184 | tf_op jit(solution)/shard_map/reduce_scatter | solution.py:163
  942.5 402.6 %reduce-scatter.14.cloned.1.call-start = ((), (), s32[]{:S(2)}) async-start(), calls=%async_computation.13 | async-start | bytes 9437184 | tf_op jit(solution)/shard_map/reduce_scatter | solution.py:163
  958.8 92.1 %collective-permute-start.27 = (bf16[256,2048]{1,0:T(8,128)(2,1)}, bf16[256,2048]{1,0:T(8,128)(2,1)}, u32[]{:S(2)}, u32[]{:S(2)}) collective-permute-start(bf16[256,2048]{1,0:T(8,128)(2,1)} %get-tuple-element.334), channel_id=1, source_target_pairs={{0,2},{1,3},{2,0},{3,1},{4,6},{5,7},{6,4},{7,5},{8,10},{9,11},{10,... | collective-permute-start | bytes 3145736 | tf_op jit(solution)/shard_map/ppermute | solution.py:128
  960.2 90.7 %collective-permute-start.26 = (bf16[256,2048]{1,0:T(8,128)(2,1)}, bf16[256,2048]{1,0:T(8,128)(2,1)}, u32[]{:S(2)}, u32[]{:S(2)}) collective-permute-start(bf16[256,2048]{1,0:T(8,128)(2,1)} %get-tuple-element.332), channel_id=1, source_target_pairs={{0,1},{1,2},{2,3},{3,0},{4,5},{5,6},{6,7},{7,4},{8,9},{9,10},{10,1... | collective-permute-start | bytes 3145736 | tf_op jit(solution)/shard_map/ppermute | solution.py:128
  1055.8 99.0 %collective-permute-start.30 = (bf16[256,2048]{1,0:T(8,128)(2,1)}, bf16[256,2048]{1,0:T(8,128)(2,1)S(1)}, u32[]{:S(2)}, u32[]{:S(2)}) collective-permute-start(bf16[256,2048]{1,0:T(8,128)(2,1)} %get-tuple-element.303), channel_id=1, source_target_pairs={{0,2},{1,3},{2,0},{3,1},{4,6},{5,7},{6,4},{7,5},{8,10},{9,11},{10,... | collective-permute-start | bytes 3145736 | tf_op jit(solution)/shard_map/ppermute | solution.py:134
  1056.6 122.8 %collective-permute-start.31 = (bf16[256,2048]{1,0:T(8,128)(2,1)}, bf16[256,2048]{1,0:T(8,128)(2,1)S(1)}, u32[]{:S(2)}, u32[]{:S(2)}) collective-permute-start(bf16[256,2048]{1,0:T(8,128)(2,1)} %get-tuple-element.303), channel_id=1, source_target_pairs={{0,3},{1,0},{2,1},{3,2},{4,7},{5,4},{6,5},{7,6},{8,11},{9,8},{10,9... | collective-permute-start | bytes 3145736 | tf_op jit(solution)/shard_map/ppermute | solution.py:134
  1067.6 173.8 %collective-permute-start.42 = (bf16[160,2048]{1,0:T(8,128)(2,1)}, bf16[160,2048]{1,0:T(8,128)(2,1)}, u32[]{:S(2)}, u32[]{:S(2)}) collective-permute-start(bf16[160,2048]{1,0:T(8,128)(2,1)} %get-tuple-element.336), channel_id=1, source_target_pairs={{0,3},{1,0},{2,1},{3,2},{4,7},{5,4},{6,5},{7,6},{8,11},{9,8},{10,9... | collective-permute-start | bytes 1966088 | tf_op jit(solution)/shard_map/ppermute | solution.py:128
  1068.4 175.7 %collective-permute-start.41 = (bf16[160,2048]{1,0:T(8,128)(2,1)}, bf16[160,2048]{1,0:T(8,128)(2,1)}, u32[]{:S(2)}, u32[]{:S(2)}) collective-permute-start(bf16[160,2048]{1,0:T(8,128)(2,1)} %get-tuple-element.337), channel_id=1, source_target_pairs={{0,2},{1,3},{2,0},{3,1},{4,6},{5,7},{6,4},{7,5},{8,10},{9,11},{10,... | collective-permute-start | bytes 1966088 | tf_op jit(solution)/shard_map/ppermute | solution.py:128
  1084.1 160.0 %collective-permute-start.40 = (bf16[160,2048]{1,0:T(8,128)(2,1)}, bf16[160,2048]{1,0:T(8,128)(2,1)S(1)}, u32[]{:S(2)}, u32[]{:S(2)}) collective-permute-start(bf16[160,2048]{1,0:T(8,128)(2,1)} %get-tuple-element.335), channel_id=1, source_target_pairs={{0,1},{1,2},{2,3},{3,0},{4,5},{5,6},{6,7},{7,4},{8,9},{9,10},{10,1... | collective-permute-start | bytes 1966088 | tf_op jit(solution)/shard_map/ppermute | solution.py:128
  1247.2 71.5 %collective-permute-start.44 = (bf16[160,2048]{1,0:T(8,128)(2,1)}, bf16[160,2048]{1,0:T(8,128)(2,1)}, u32[]{:S(2)}, u32[]{:S(2)}) collective-permute-start(bf16[160,2048]{1,0:T(8,128)(2,1)} %get-tuple-element.301), channel_id=1, source_target_pairs={{0,2},{1,3},{2,0},{3,1},{4,6},{5,7},{6,4},{7,5},{8,10},{9,11},{10,... | collective-permute-start | bytes 1966088 | tf_op jit(solution)/shard_map/ppermute | solution.py:134
  1252.9 68.0 %collective-permute-start.45 = (bf16[160,2048]{1,0:T(8,128)(2,1)}, bf16[160,2048]{1,0:T(8,128)(2,1)}, u32[]{:S(2)}, u32[]{:S(2)}) collective-permute-start(bf16[160,2048]{1,0:T(8,128)(2,1)} %get-tuple-element.301), channel_id=1, source_target_pairs={{0,3},{1,0},{2,1},{3,2},{4,7},{5,4},{6,5},{7,6},{8,11},{9,8},{10,9... | collective-permute-start | bytes 1966088 | tf_op jit(solution)/shard_map/ppermute | solution.py:134
  (137 other events, 2363.3 us)
Sparse Core Ops, SparseCore 0:
  13.2 58.5 all-gather.4
  74.3 55.8 all-gather.10
  132.0 54.2 all-gather.8
  188.1 54.2 all-gather.6
  893.4 50.3 reduce-scatter.7
  947.0 64.9 reduce-scatter.5
  1015.5 71.5 reduce-scatter.9
  1090.5 71.4 reduce-scatter.11
  1165.5 71.2 reduce-scatter.13

commit v7 on v6

--- a/solution.py
+++ b/solution.py
@@ -226,13 +226,14 @@
         w_output.astype(bf_type),
     )
     mlp_low = (w_gate.astype(bf_type), w_up.astype(bf_type), w_down.astype(bf_type))
-    attn_joined = lax.all_gather(
-        jnp.concatenate([attn_low[0], attn_low[1], attn_low[2], attn_low[3].T], axis=1),
-        (SHARD, CTX),
-        axis=0,
-        tiled=True,
-    )
-    query_full, key_full, value_full, output_t = jnp.split(attn_joined, 4, axis=1)
+    key_value = lax.all_gather(
+        jnp.concatenate([attn_low[1], attn_low[2]], axis=1), (SHARD, CTX), axis=0, tiled=True
+    )
+    query_output = lax.all_gather(
+        jnp.concatenate([attn_low[0], attn_low[3].T], axis=1), (SHARD, CTX), axis=0, tiled=True
+    )
+    key_full, value_full = jnp.split(key_value, 2, axis=1)
+    query_full, output_t = jnp.split(query_output, 2, axis=1)
     output_full = output_t.T
     gate_full, up_full, down_full = (
         lax.all_gather(mlp_low[0], (SHARD, CTX), axis=0, tiled=True),

time: 1370 us -> 1320 us (0.964)
  starting transfers between devices: 251 us -> 212 us
  waiting for transfers between devices: 430 us -> 411 us
    ppermute x21, waiting for transfers between devices: 135 us -> 187 us  [tp_psum(): got = lax.ppermute(reduced, TP, pairs)]
    ppermute x21, waiting for transfers between devices: 240 us -> 197 us  [tp_psum(): total = total + lax.ppermute(piece, TP, pairs).astype(jnp.float32)]
    all_gather x1, waiting for transfers between devices: 37.1 us -> 0.01 us  [block(): lax.all_gather(mlp_low[2], (SHARD, CTX), axis=1, tiled=True)]
    ppermute x21, starting transfers between devices: 215 us -> 182 us  [tp_psum(): total = total + lax.ppermute(piece, TP, pairs).astype(jnp.float32)]
    unnamed x206 -> x188, local copies, waits for them, and re-layouts: 31.9 us -> 31.3 us
  transfers between devices with their start and end apart: 55 -> 56, of which waited for: 20 -> 23; matrix products, arithmetic and copies ran while one was open for 34% -> 31% of each run, Pallas kernels for 0% -> 0%
where the time goes in v7:
time: 1320 us; the launch traced here: 1300 us
  waiting for transfers between devices  411 us (31%)
  matrix products  330 us (25%)
  starting transfers between devices  212 us (16%)
  other arithmetic  190 us (14%)
  local copies, waits for them, and re-layouts  140 us (11%)
  between operations  17.2 us (1%)
    ppermute x21, waiting for transfers between devices, tp_psum(): total = total + lax.ppermute(piece, TP, pairs).astype(jnp.float32)  197 us
    ppermute x21, waiting for transfers between devices, tp_psum(): got = lax.ppermute(reduced, TP, pairs)  187 us
    ppermute x21, starting transfers between devices, tp_psum(): total = total + lax.ppermute(piece, TP, pairs).astype(jnp.float32)  182 us
    dot_general x11, matrix products, matmul_low(): return jnp.dot(left, right, preferred_element_type=jnp.float32)  75.4 us
    unnamed x188, local copies, waits for them, and re-layouts  31.3 us
    convert_element_type x2, other arithmetic, one_block(): grad_scores = (probability * (grad_prob - inner_sum)).astype(jnp.bfloat16)  29.7 us
    ppermute x21, starting transfers between devices, tp_psum(): got = lax.ppermute(reduced, TP, pairs)  28.4 us
    dot_general x2, matrix products, one_block(): jnp.einsum('hqk,qhd->khd', prob_low, grad_rows, preferred_element_type=jn...  26.8 us
  transfers between devices with their start and end apart: 56, of which 23 were waited for; matrix products, arithmetic and copies ran while one was open for 31% of the time, Pallas kernels for 0%

profile of v7, /device:TPU:0, one launch (start us, length us, event | category | flops | bytes accessed | tf_op | source)
XLA Modules:
  0.0 1304.0 jit_solution(17820749430945307938)
XLA Ops:
  73.4 16.4 %all-gather.6.cloned.1.call-done = bf16[2048,1024]{0,1:T(8,128)(2,1)} async-done(((bf16[256,1024]{0,1:T(8,128)(2,1)}), bf16[2048,1024]{0,1:T(8,128)(2,1)}) %all-gather.6.cloned.1.call-update) | async-done | bytes 4194320 | tf_op jit(solution)/shard_map/all_gather | solution.py:232
  132.5 34.9 %while.27 = (s32[]{:T(128)}, bf16[2,512,4,128]{3,2,1,0:T(4,128)(2,1)}, f32[2,4,512]{2,1,0:T(4,128)S(1)}, s32[2]{0:T(128)S(1)}, s32[]{:T(128)}, /*index=5*/s32[]{...) while((s32[]{:T(128)}, ...), condition=%wide.region_5.6_spmd, body=%wide.region_2.5_spmd.sunk | while | flops 2195980800 | bytes 77668600 | solution.py:77
  198.8 69.0 %collective-permute-done.3 = bf16[96,2048]{1,0:T(8,128)(2,1)} collective-permute-done((bf16[96,2048]{1,0:T(8,128)(2,1)}, bf16[96,2048]{1,0:T(8,128)(2,1)}, u32[]{:S(2)}, u32[]{:S(2)}) %collective-permute-start.3) | collective-permute-done | bytes 393248 | tf_op jit(solution)/shard_map/ppermute | solution.py:128
  284.6 16.0 %collective-permute-done.6 = bf16[96,2048]{1,0:T(8,128)(2,1)S(1)} collective-permute-done((bf16[96,2048]{1,0:T(8,128)(2,1)S(1)}, bf16[96,2048]{1,0:T(8,128)(2,1)S(1)}, u32[]{:S(2)}, u32[]{:S(2)}) %collective-permute-start.6) | collective-permute-done | bytes 393248 | tf_op jit(solution)/shard_map/ppermute | solution.py:134
  302.7 11.9 collective-permute-done.11
  314.7 34.9 %collective-permute-done.12 = bf16[160,2048]{1,0:T(8,128)(2,1)S(1)} collective-permute-done((bf16[160,2048]{1,0:T(8,128)(2,1)S(1)}, bf16[160,2048]{1,0:T(8,128)(2,1)S(1)}, u32[]{:S(2)}, u32[]{:S(2)}) %collective-permute-start.12) | collective-permute-done | bytes 655392 | tf_op jit(solution)/shard_map/ppermute | solution.py:134
  355.4 11.4 fusion.182
  366.8 11.1 fusion.132
  377.9 14.1 %multiply_convert_fusion.2 = (bf16[640,2048]{1,0:T(8,128)(2,1)S(1)}, bf16[640,2048]{1,0:T(8,128)(2,1)S(1)}, bf16[640,2048]{1,0:T(8,128)(2,1)S(1)}) fusion(f32[640,2048]{1,0:T(8,128)} %fusion.132, f32[640,2048]{1,0:T(8,128)} %fusion.182, bf16[640,2048]{1,0:T(8,128)(2,1)} %fusion.54, bf16[2048,2048]{1,0:T(8,128)(2,1)} %all-gather.10.cloned.1.call-done), kind=kOutput, calls=%fused_computation.85 | convolution fusion | flops 5389680640 | bytes 29360128 | tf_op jit(solution)/shard_map/dot_general | solution.py:170
  444.6 17.2 %collective-permute-start.22 = (bf16[160,2048]{1,0:T(8,128)(2,1)}, bf16[160,2048]{1,0:T(8,128)(2,1)}, u32[]{:S(2)}, u32[]{:S(2)}) collective-permute-start(bf16[160,2048]{1,0:T(8,128)(2,1)} %get-tuple-element.339), channel_id=1, source_target_pairs={{0,3},{1,0},{2,1},{3,2},{4,7},{5,4},{6,5},{7,6},{8,11},{9,8},{10,9... | collective-permute-start | bytes 1966088 | tf_op jit(solution)/shard_map/ppermute | solution.py:128
  491.3 10.6 convolution_add_fusion.1
  521.6 11.0 convolution_add_fusion
  551.4 25.7 %collective-permute-done.15 = bf16[96,2048]{1,0:T(8,128)(2,1)} collective-permute-done((bf16[96,2048]{1,0:T(8,128)(2,1)}, bf16[96,2048]{1,0:T(8,128)(2,1)}, u32[]{:S(2)}, u32[]{:S(2)}) %collective-permute-start.15) | collective-permute-done | bytes 393248 | tf_op jit(solution)/shard_map/ppermute | solution.py:128
  593.5 15.6 %collective-permute-done.18 = bf16[96,2048]{1,0:T(8,128)(2,1)S(1)} collective-permute-done((bf16[96,2048]{1,0:T(8,128)(2,1)S(1)}, bf16[96,2048]{1,0:T(8,128)(2,1)S(1)}, u32[]{:S(2)}, u32[]{:S(2)}) %collective-permute-start.18) | collective-permute-done | bytes 393248 | tf_op jit(solution)/shard_map/ppermute | solution.py:134
  620.3 25.5 %collective-permute-done.24 = bf16[160,2048]{1,0:T(8,128)(2,1)} collective-permute-done((bf16[160,2048]{1,0:T(8,128)(2,1)}, bf16[160,2048]{1,0:T(8,128)(2,1)}, u32[]{:S(2)}, u32[]{:S(2)}) %collective-permute-start.24) | collective-permute-done | bytes 655392 | tf_op jit(solution)/shard_map/ppermute | solution.py:134
  662.2 129.9 %while.28 = (s32[]{:T(128)}, f32[2048,4,128]{0,2,1:T(8,128)}, f32[2048,4,128]{0,2,1:T(8,128)}, f32[2,512,4,128]{3,1,0,2:T(8,128)}, bf16[2,512,4,128]{3,1,2,0:T(8...) while((s32[]{:T(128)}, f32[2048,4,128]{0,2,1:T(8,128)}, ...), condition=%wide.region_16.17_spmd.clone, body=%wide.region_14.16_spmd.clone.sunk | while | flops 5439226368 | bytes 198246768 | solution.py:113
  674.3 12.9 multiply_reduce_fusion.5
  687.2 14.8 %multiply_convert_fusion.9 = bf16[4,512,2048]{2,1,0:T(8,128)(2,1)} fusion(f32[4,512,2048]{2,1,0:T(8,128)} %get-tuple-element.520, f32[4,512,2048]{2,1,0:T(8,128)} %fusion.270, f32[4,512]{1,0:T(4,128)S(1)} %get-tuple-element.521, f32[4,512]{1,0:T(4,128)S(1)} %dynamic-slice_bitcast_fusion.23, pred[512,2048]{1,0:T(8,128)(4,1)S(1)} %fusion.271), kind=kLoop, calls=%fused_computation.21.clone.1 | loop fusion | flops 25165824 | bytes 43008000 | tf_op jit(solution)/shard_map/while/body/eval_jaxpr/convert_element_type | solution.py:98
  709.4 12.8 bitcast_add_fusion.7
  737.8 12.9 multiply_reduce_fusion.5
  750.7 14.8 %multiply_convert_fusion.9 = bf16[4,512,2048]{2,1,0:T(8,128)(2,1)} fusion(f32[4,512,2048]{2,1,0:T(8,128)} %get-tuple-element.520, f32[4,512,2048]{2,1,0:T(8,128)} %fusion.270, f32[4,512]{1,0:T(4,128)S(1)} %get-tuple-element.521, f32[4,512]{1,0:T(4,128)S(1)} %dynamic-slice_bitcast_fusion.23, pred[512,2048]{1,0:T(8,128)(4,1)S(1)} %fusion.271), kind=kLoop, calls=%fused_computation.21.clone.1 | loop fusion | flops 25165824 | bytes 43008000 | tf_op jit(solution)/shard_map/while/body/eval_jaxpr/convert_element_type | solution.py:98
  774.1 14.0 %bitcast_add_fusion.7 = f32[2048,4,128]{0,2,1:T(8,128)} fusion(f32[2048,4,128]{0,2,1:T(8,128)} %get-tuple-element.572, f32[4,512,2048]{2,1,0:T(8,128)} %fusion.270, f32[4,512]{1,0:T(4,128)S(1)} %dynamic-slice_bitcast_fusion.23, pred[512,2048]{1,0:T(8,128)(4,1)S(1)} %fusion.271, pred[]{:T(512)S(6)} %compare.11, ...), kind=kOutput, calls=%fused_computation.27.clone.1 | convolution fusion | flops 1092616192 | bytes 26746884 | tf_op jit(solution)/shard_map/while/body/eval_jaxpr/hqk,qhd->khd/dot_general | solution.py:107
  805.3 14.2 %constant_dynamic-slice_fusion.1 = (f32[1,1024,4,128]{1,0,3,2:T(1,128)}, f32[1,1024,4,128]{1,0,3,2:T(1,128)S(1)}, f32[1,1024,4,128]{1,0,3,2:T(1,128)}, f32[1,1024,4,128]{1,0,3,2:T(1,128)S(1)}) fusion(f32[2,1024,4,128]{1,0,3,2:T(2,128)} %reshape_stack.7, s32[]{:T(128)S(6)} %select_n.215, s32[]{:T(128)S(6)} %select_n.217, f32[2,1024,4,128]{1,0,3,2:T(2,128)} %reshape_stack.6), kind=kLoop, calls=%fused_computation.286 | loop fusion | bytes 16777224 | tf_op jit(solution)/shard_map/jit(dynamic_index_in_dim)/dynamic_slice | solution.py:154
  876.8 11.5 pad_maximum_fusion.1
  893.6 13.0 collective-permute-start.28
  907.3 23.3 %collective-permute-done.28 = bf16[256,2048]{1,0:T(8,128)(2,1)} collective-permute-done((bf16[256,2048]{1,0:T(8,128)(2,1)}, bf16[256,2048]{1,0:T(8,128)(2,1)}, u32[]{:S(2)}, u32[]{:S(2)}) %collective-permute-start.28) | collective-permute-done | bytes 1048608 | tf_op jit(solution)/shard_map/ppermute | solution.py:128
  930.6 65.6 %collective-permute-done.27 = bf16[256,2048]{1,0:T(8,128)(2,1)} collective-permute-done((bf16[256,2048]{1,0:T(8,128)(2,1)}, bf16[256,2048]{1,0:T(8,128)(2,1)}, u32[]{:S(2)}, u32[]{:S(2)}) %collective-permute-start.27) | collective-permute-done | bytes 1048608 | tf_op jit(solution)/shard_map/ppermute | solution.py:128
  1029.4 72.4 %collective-permute-start.40 = (bf16[160,2048]{1,0:T(8,128)(2,1)S(1)}, bf16[160,2048]{1,0:T(8,128)(2,1)}, u32[]{:S(2)}, u32[]{:S(2)}) collective-permute-start(bf16[160,2048]{1,0:T(8,128)(2,1)S(1)} %get-tuple-element.335), channel_id=1, source_target_pairs={{0,1},{1,2},{2,3},{3,0},{4,5},{5,6},{6,7},{7,4},{8,9},{9,10},{10,1... | collective-permute-start | bytes 1966088 | tf_op jit(solution)/shard_map/ppermute | solution.py:128
  1103.3 23.9 %collective-permute-start.36 = (bf16[96,2048]{1,0:T(8,128)(2,1)S(1)}, bf16[96,2048]{1,0:T(8,128)(2,1)S(1)}, u32[]{:S(2)}, u32[]{:S(2)}) collective-permute-start(bf16[96,2048]{1,0:T(8,128)(2,1)S(1)} %get-tuple-element.359), channel_id=1, source_target_pairs={{0,3},{1,0},{2,1},{3,2},{4,7},{5,4},{6,5},{7,6},{8,11},{9,8},{10,9... | collective-permute-start | bytes 1179656 | tf_op jit(solution)/shard_map/ppermute | solution.py:128
  1137.4 40.5 %collective-permute-start.34 = (bf16[96,2048]{1,0:T(8,128)(2,1)S(1)}, bf16[96,2048]{1,0:T(8,128)(2,1)}, u32[]{:S(2)}, u32[]{:S(2)}) collective-permute-start(bf16[96,2048]{1,0:T(8,128)(2,1)S(1)} %get-tuple-element.358), channel_id=1, source_target_pairs={{0,1},{1,2},{2,3},{3,0},{4,5},{5,6},{6,7},{7,4},{8,9},{9,10},{10,1... | collective-permute-start | bytes 1179656 | tf_op jit(solution)/shard_map/ppermute | solution.py:128
  1202.1 16.8 %collective-permute-done.38 = bf16[96,2048]{1,0:T(8,128)(2,1)S(1)} collective-permute-done((bf16[96,2048]{1,0:T(8,128)(2,1)S(1)}, bf16[96,2048]{1,0:T(8,128)(2,1)S(1)}, u32[]{:S(2)}, u32[]{:S(2)}) %collective-permute-start.38) | collective-permute-done | bytes 393248 | tf_op jit(solution)/shard_map/ppermute | solution.py:134
  1235.1 32.7 %collective-permute-done.44 = bf16[160,2048]{1,0:T(8,128)(2,1)} collective-permute-done((bf16[160,2048]{1,0:T(8,128)(2,1)}, bf16[160,2048]{1,0:T(8,128)(2,1)}, u32[]{:S(2)}, u32[]{:S(2)}) %collective-permute-start.44) | collective-permute-done | bytes 655392 | tf_op jit(solution)/shard_map/ppermute | solution.py:134
  (549 shorter events, 596.4 us)
Async XLA Ops:
  10.4 79.3 %all-gather.6.cloned.1.call-start = ((), (), s32[]{:S(2)}) async-start(), calls=%async_computation.5 | async-start | bytes 4718592 | tf_op jit(solution)/shard_map/all_gather | solution.py:232
  11.5 343.8 %all-gather.12.cloned.1.call-start = ((), (), s32[]{:S(2)}) async-start(), calls=%async_computation.8 | async-start | bytes 9437184 | tf_op jit(solution)/shard_map/all_gather | solution.py:240
  12.8 354.0 %all-gather.14.cloned.1.call-start = ((), (), s32[]{:S(2)}) async-start(), calls=%async_computation.9 | async-start | bytes 9437184 | tf_op jit(solution)/shard_map/all_gather | solution.py:241
  15.7 362.2 %all-gather.10.cloned.1.call-start = ((), (), s32[]{:S(2)}) async-start(), calls=%async_computation.7 | async-start | bytes 9437184 | tf_op jit(solution)/shard_map/all_gather | solution.py:239
  16.9 1205.4 %reduce-scatter.8.cloned.1.call-start = ((), (), s32[]{:S(2)}) async-start(), calls=%async_computation.11 | async-start | bytes 2359296 | tf_op jit(solution)/shard_map/reduce_scatter | solution.py:163
  58.7 66.6 %collective-permute-start = (bf16[1,1024,4,128]{1,3,2,0:T(8,128)(2,1)}, bf16[1,1024,4,128]{1,3,2,0:T(8,128)(2,1)}, u32[]{:S(2)}, u32[]{:S(2)}) collective-permute-start(bf16[1,1024,4,128]{1,3,2,0:T(8,128)(2,1)} %fusion.70), channel_id=1, source_target_pairs={{0,4},{4,0},{1,5},{5,1},{2,6},{6,2},{3,7},{7,3},{8,12},{12,8},{9,1... | collective-permute-start | bytes 3145736 | tf_op jit(solution)/shard_map/ppermute | solution.py:147
  180.3 92.9 %collective-permute-start.10 = (bf16[160,2048]{1,0:T(8,128)(2,1)}, bf16[160,2048]{1,0:T(8,128)(2,1)S(1)}, u32[]{:S(2)}, u32[]{:S(2)}) collective-permute-start(bf16[160,2048]{1,0:T(8,128)(2,1)} %get-tuple-element.342), channel_id=1, source_target_pairs={{0,3},{1,0},{2,1},{3,2},{4,7},{5,4},{6,5},{7,6},{8,11},{9,8},{10,9... | collective-permute-start | bytes 1966088 | tf_op jit(solution)/shard_map/ppermute | solution.py:128
  180.9 95.2 %collective-permute-start.9 = (bf16[160,2048]{1,0:T(8,128)(2,1)}, bf16[160,2048]{1,0:T(8,128)(2,1)}, u32[]{:S(2)}, u32[]{:S(2)}) collective-permute-start(bf16[160,2048]{1,0:T(8,128)(2,1)} %get-tuple-element.343), channel_id=1, source_target_pairs={{0,2},{1,3},{2,0},{3,1},{4,6},{5,7},{6,4},{7,5},{8,10},{9,11},{10,... | collective-permute-start | bytes 1966088 | tf_op jit(solution)/shard_map/ppermute | solution.py:128
  180.9 95.2 %collective-permute-start.8 = (bf16[160,2048]{1,0:T(8,128)(2,1)}, bf16[160,2048]{1,0:T(8,128)(2,1)}, u32[]{:S(2)}, u32[]{:S(2)}) collective-permute-start(bf16[160,2048]{1,0:T(8,128)(2,1)} %get-tuple-element.341), channel_id=1, source_target_pairs={{0,1},{1,2},{2,3},{3,0},{4,5},{5,6},{6,7},{7,4},{8,9},{9,10},{10,1... | collective-permute-start | bytes 1966088 | tf_op jit(solution)/shard_map/ppermute | solution.py:128
  182.4 85.5 %collective-permute-start.3 = (bf16[96,2048]{1,0:T(8,128)(2,1)}, bf16[96,2048]{1,0:T(8,128)(2,1)}, u32[]{:S(2)}, u32[]{:S(2)}) collective-permute-start(bf16[96,2048]{1,0:T(8,128)(2,1)} %get-tuple-element.366), channel_id=1, source_target_pairs={{0,2},{1,3},{2,0},{3,1},{4,6},{5,7},{6,4},{7,5},{8,10},{9,11},{10,... | collective-permute-start | bytes 1179656 | tf_op jit(solution)/shard_map/ppermute | solution.py:128
  187.8 80.1 %collective-permute-start.2 = (bf16[96,2048]{1,0:T(8,128)(2,1)}, bf16[96,2048]{1,0:T(8,128)(2,1)}, u32[]{:S(2)}, u32[]{:S(2)}) collective-permute-start(bf16[96,2048]{1,0:T(8,128)(2,1)} %get-tuple-element.364), channel_id=1, source_target_pairs={{0,1},{1,2},{2,3},{3,0},{4,5},{5,6},{6,7},{7,4},{8,9},{9,10},{10,1... | collective-permute-start | bytes 1179656 | tf_op jit(solution)/shard_map/ppermute | solution.py:128
  278.4 71.2 %collective-permute-start.12 = (bf16[160,2048]{1,0:T(8,128)(2,1)S(1)}, bf16[160,2048]{1,0:T(8,128)(2,1)S(1)}, u32[]{:S(2)}, u32[]{:S(2)}) collective-permute-start(bf16[160,2048]{1,0:T(8,128)(2,1)S(1)} %get-tuple-element.315), channel_id=1, source_target_pairs={{0,2},{1,3},{2,0},{3,1},{4,6},{5,7},{6,4},{7,5},{8,10},{9,11},{10,... | collective-permute-start | bytes 1966088 | tf_op jit(solution)/shard_map/ppermute | solution.py:134
  283.7 66.0 %collective-permute-start.13 = (bf16[160,2048]{1,0:T(8,128)(2,1)S(1)}, bf16[160,2048]{1,0:T(8,128)(2,1)S(1)}, u32[]{:S(2)}, u32[]{:S(2)}) collective-permute-start(bf16[160,2048]{1,0:T(8,128)(2,1)S(1)} %get-tuple-element.315), channel_id=1, source_target_pairs={{0,3},{1,0},{2,1},{3,2},{4,7},{5,4},{6,5},{7,6},{8,11},{9,8},{10,9... | collective-permute-start | bytes 1966088 | tf_op jit(solution)/shard_map/ppermute | solution.py:134
  444.6 134.4 %collective-permute-start.22 = (bf16[160,2048]{1,0:T(8,128)(2,1)}, bf16[160,2048]{1,0:T(8,128)(2,1)}, u32[]{:S(2)}, u32[]{:S(2)}) collective-permute-start(bf16[160,2048]{1,0:T(8,128)(2,1)} %get-tuple-element.339), channel_id=1, source_target_pairs={{0,3},{1,0},{2,1},{3,2},{4,7},{5,4},{6,5},{7,6},{8,11},{9,8},{10,9... | collective-permute-start | bytes 1966088 | tf_op jit(solution)/shard_map/ppermute | solution.py:128
  461.8 120.9 %collective-permute-start.21 = (bf16[160,2048]{1,0:T(8,128)(2,1)}, bf16[160,2048]{1,0:T(8,128)(2,1)}, u32[]{:S(2)}, u32[]{:S(2)}) collective-permute-start(bf16[160,2048]{1,0:T(8,128)(2,1)} %get-tuple-element.340), channel_id=1, source_target_pairs={{0,2},{1,3},{2,0},{3,1},{4,6},{5,7},{6,4},{7,5},{8,10},{9,11},{10,... | collective-permute-start | bytes 1966088 | tf_op jit(solution)/shard_map/ppermute | solution.py:128
  516.8 60.4 %collective-permute-start.15 = (bf16[96,2048]{1,0:T(8,128)(2,1)}, bf16[96,2048]{1,0:T(8,128)(2,1)}, u32[]{:S(2)}, u32[]{:S(2)}) collective-permute-start(bf16[96,2048]{1,0:T(8,128)(2,1)} %get-tuple-element.363), channel_id=1, source_target_pairs={{0,2},{1,3},{2,0},{3,1},{4,6},{5,7},{6,4},{7,5},{8,10},{9,11},{10,... | collective-permute-start | bytes 1179656 | tf_op jit(solution)/shard_map/ppermute | solution.py:128
  519.6 57.6 %collective-permute-start.14 = (bf16[96,2048]{1,0:T(8,128)(2,1)S(1)}, bf16[96,2048]{1,0:T(8,128)(2,1)}, u32[]{:S(2)}, u32[]{:S(2)}) collective-permute-start(bf16[96,2048]{1,0:T(8,128)(2,1)S(1)} %get-tuple-element.361), channel_id=1, source_target_pairs={{0,1},{1,2},{2,3},{3,0},{4,5},{5,6},{6,7},{7,4},{8,9},{9,10},{10,1... | collective-permute-start | bytes 1179656 | tf_op jit(solution)/shard_map/ppermute | solution.py:128
  586.8 59.0 %collective-permute-start.24 = (bf16[160,2048]{1,0:T(8,128)(2,1)}, bf16[160,2048]{1,0:T(8,128)(2,1)}, u32[]{:S(2)}, u32[]{:S(2)}) collective-permute-start(bf16[160,2048]{1,0:T(8,128)(2,1)} %get-tuple-element.307), channel_id=1, source_target_pairs={{0,2},{1,3},{2,0},{3,1},{4,6},{5,7},{6,4},{7,5},{8,10},{9,11},{10,... | collective-permute-start | bytes 1966088 | tf_op jit(solution)/shard_map/ppermute | solution.py:134
  842.0 442.3 %reduce-scatter.6.cloned.1.call-start = ((), (), s32[]{:S(2)}) async-start(), calls=%async_computation.10 | async-start | bytes 7077888 | tf_op jit(solution)/shard_map/reduce_scatter | solution.py:163
  888.4 400.2 %reduce-scatter.10.cloned.1.call-start = ((), (), s32[]{:S(2)}) async-start(), calls=%async_computation.12 | async-start | bytes 9437184 | tf_op jit(solution)/shard_map/reduce_scatter | solution.py:163
  889.1 402.2 %reduce-scatter.12.cloned.1.call-start = ((), (), s32[]{:S(2)}) async-start(), calls=%async_computation.13 | async-start | bytes 9437184 | tf_op jit(solution)/shard_map/reduce_scatter | solution.py:163
  889.9 404.3 %reduce-scatter.14.cloned.1.call-start = ((), (), s32[]{:S(2)}) async-start(), calls=%async_computation.14 | async-start | bytes 9437184 | tf_op jit(solution)/shard_map/reduce_scatter | solution.py:163
  906.6 89.6 %collective-permute-start.27 = (bf16[256,2048]{1,0:T(8,128)(2,1)}, bf16[256,2048]{1,0:T(8,128)(2,1)}, u32[]{:S(2)}, u32[]{:S(2)}) collective-permute-start(bf16[256,2048]{1,0:T(8,128)(2,1)} %get-tuple-element.334), channel_id=1, source_target_pairs={{0,2},{1,3},{2,0},{3,1},{4,6},{5,7},{6,4},{7,5},{8,10},{9,11},{10,... | collective-permute-start | bytes 3145736 | tf_op jit(solution)/shard_map/ppermute | solution.py:128
  906.6 89.6 %collective-permute-start.26 = (bf16[256,2048]{1,0:T(8,128)(2,1)}, bf16[256,2048]{1,0:T(8,128)(2,1)}, u32[]{:S(2)}, u32[]{:S(2)}) collective-permute-start(bf16[256,2048]{1,0:T(8,128)(2,1)} %get-tuple-element.332), channel_id=1, source_target_pairs={{0,1},{1,2},{2,3},{3,0},{4,5},{5,6},{6,7},{7,4},{8,9},{9,10},{10,1... | collective-permute-start | bytes 3145736 | tf_op jit(solution)/shard_map/ppermute | solution.py:128
  1002.6 100.7 %collective-permute-start.30 = (bf16[256,2048]{1,0:T(8,128)(2,1)}, bf16[256,2048]{1,0:T(8,128)(2,1)}, u32[]{:S(2)}, u32[]{:S(2)}) collective-permute-start(bf16[256,2048]{1,0:T(8,128)(2,1)} %get-tuple-element.303), channel_id=1, source_target_pairs={{0,2},{1,3},{2,0},{3,1},{4,6},{5,7},{6,4},{7,5},{8,10},{9,11},{10,... | collective-permute-start | bytes 3145736 | tf_op jit(solution)/shard_map/ppermute | solution.py:134
  1004.4 124.5 %collective-permute-start.31 = (bf16[256,2048]{1,0:T(8,128)(2,1)}, bf16[256,2048]{1,0:T(8,128)(2,1)}, u32[]{:S(2)}, u32[]{:S(2)}) collective-permute-start(bf16[256,2048]{1,0:T(8,128)(2,1)} %get-tuple-element.303), channel_id=1, source_target_pairs={{0,3},{1,0},{2,1},{3,2},{4,7},{5,4},{6,5},{7,6},{8,11},{9,8},{10,9... | collective-permute-start | bytes 3145736 | tf_op jit(solution)/shard_map/ppermute | solution.py:134
  1013.1 177.6 %collective-permute-start.42 = (bf16[160,2048]{1,0:T(8,128)(2,1)}, bf16[160,2048]{1,0:T(8,128)(2,1)S(1)}, u32[]{:S(2)}, u32[]{:S(2)}) collective-permute-start(bf16[160,2048]{1,0:T(8,128)(2,1)} %get-tuple-element.336), channel_id=1, source_target_pairs={{0,3},{1,0},{2,1},{3,2},{4,7},{5,4},{6,5},{7,6},{8,11},{9,8},{10,9... | collective-permute-start | bytes 1966088 | tf_op jit(solution)/shard_map/ppermute | solution.py:128
  1013.3 180.0 %collective-permute-start.41 = (bf16[160,2048]{1,0:T(8,128)(2,1)S(1)}, bf16[160,2048]{1,0:T(8,128)(2,1)S(1)}, u32[]{:S(2)}, u32[]{:S(2)}) collective-permute-start(bf16[160,2048]{1,0:T(8,128)(2,1)S(1)} %get-tuple-element.337), channel_id=1, source_target_pairs={{0,2},{1,3},{2,0},{3,1},{4,6},{5,7},{6,4},{7,5},{8,10},{9,11},{10,... | collective-permute-start | bytes 1966088 | tf_op jit(solution)/shard_map/ppermute | solution.py:128
  1029.4 164.8 %collective-permute-start.40 = (bf16[160,2048]{1,0:T(8,128)(2,1)S(1)}, bf16[160,2048]{1,0:T(8,128)(2,1)}, u32[]{:S(2)}, u32[]{:S(2)}) collective-permute-start(bf16[160,2048]{1,0:T(8,128)(2,1)S(1)} %get-tuple-element.335), channel_id=1, source_target_pairs={{0,1},{1,2},{2,3},{3,0},{4,5},{5,6},{6,7},{7,4},{8,9},{9,10},{10,1... | collective-permute-start | bytes 1966088 | tf_op jit(solution)/shard_map/ppermute | solution.py:128
  1128.9 56.1 %collective-permute-start.35 = (bf16[96,2048]{1,0:T(8,128)(2,1)S(1)}, bf16[96,2048]{1,0:T(8,128)(2,1)}, u32[]{:S(2)}, u32[]{:S(2)}) collective-permute-start(bf16[96,2048]{1,0:T(8,128)(2,1)S(1)} %get-tuple-element.360), channel_id=1, source_target_pairs={{0,2},{1,3},{2,0},{3,1},{4,6},{5,7},{6,4},{7,5},{8,10},{9,11},{10,... | collective-permute-start | bytes 1179656 | tf_op jit(solution)/shard_map/ppermute | solution.py:128
  1197.3 70.5 %collective-permute-start.44 = (bf16[160,2048]{1,0:T(8,128)(2,1)}, bf16[160,2048]{1,0:T(8,128)(2,1)}, u32[]{:S(2)}, u32[]{:S(2)}) collective-permute-start(bf16[160,2048]{1,0:T(8,128)(2,1)} %get-tuple-element.301), channel_id=1, source_target_pairs={{0,2},{1,3},{2,0},{3,1},{4,6},{5,7},{6,4},{7,5},{8,10},{9,11},{10,... | collective-permute-start | bytes 1966088 | tf_op jit(solution)/shard_map/ppermute | solution.py:134
  1202.1 67.9 %collective-permute-start.45 = (bf16[160,2048]{1,0:T(8,128)(2,1)}, bf16[160,2048]{1,0:T(8,128)(2,1)}, u32[]{:S(2)}, u32[]{:S(2)}) collective-permute-start(bf16[160,2048]{1,0:T(8,128)(2,1)} %get-tuple-element.301), channel_id=1, source_target_pairs={{0,3},{1,0},{2,1},{3,2},{4,7},{5,4},{6,5},{7,6},{8,11},{9,8},{10,9... | collective-permute-start | bytes 1966088 | tf_op jit(solution)/shard_map/ppermute | solution.py:134
  (129 other events, 2139.0 us)
Sparse Core Ops, SparseCore 0:
  10.6 39.2 all-gather.7
  52.4 37.3 all-gather.5
  91.6 54.2 all-gather.11
  147.7 55.8 all-gather.13
  205.3 54.2 all-gather.9
  842.2 50.7 reduce-scatter.7
  896.4 63.4 reduce-scatter.5
  963.3 71.4 reduce-scatter.9
  1038.3 71.5 reduce-scatter.11
  1113.2 71.2 reduce-scatter.13

commit v8 on v7

--- a/solution.py
+++ b/solution.py
@@ -138,17 +138,6 @@
     return gathered
 
 
-def exchange_gather(piece, axis, count):
-    me = lax.axis_index(axis)
-    gathered = jnp.zeros((count,) + piece.shape, piece.dtype)
-    gathered = lax.dynamic_update_index_in_dim(gathered, piece, me, 0)
-    for shift in range(1, count):
-        pairs = [(i, (i + shift) % count) for i in range(count)]
-        got = lax.ppermute(piece, axis, pairs)
-        gathered = lax.dynamic_update_index_in_dim(gathered, got, (me + count - shift) % count, 0)
-    return gathered
-
-
 def exchange_scatter(blocks, axis, count):
     me = lax.axis_index(axis)
     total = lax.dynamic_index_in_dim(blocks, me, 0, keepdims=False)
@@ -252,12 +241,8 @@
     keys_rot = rotate(key_pre, cosine, sine_table).astype(bf_type)
     values_low = value_pre.astype(bf_type)
     keys_all, values_all = (
-        jnp.swapaxes(exchange_gather(keys_rot, CTX, ctx_count), 0, 1).reshape(
-            (seq_count, ctx_count * half_len, head_count, HEAD_DIM)
-        ),
-        jnp.swapaxes(exchange_gather(values_low, CTX, ctx_count), 0, 1).reshape(
-            (seq_count, ctx_count * half_len, head_count, HEAD_DIM)
-        ),
+        lax.all_gather(keys_rot, CTX, axis=1, tiled=True),
+        lax.all_gather(values_low, CTX, axis=1, tiled=True),
     )
     seq_index = 0
     attended, log_totals = attend_forward(

time: 1320 us -> 1310 us (level)
  local copies, waits for them, and re-layouts: 140 us -> 121 us
    all_gather x1, waiting for transfers between devices: 9.23 us -> 26.1 us  [block(): lax.all_gather(jnp.concatenate([attn_low[1], attn_low[2]], axis=1), (SHAR...]
    all_gather x1, waiting for transfers between devices: 16.4 us -> 1.57 us  [block(): lax.all_gather(jnp.concatenate([attn_low[0], attn_low[3].T], axis=1), (SH...]
    unnamed x188 -> x176, local copies, waits for them, and re-layouts: 31.3 us -> 28.8 us
  transfers between devices with their start and end apart: 56 -> 56, of which waited for: 23 -> 24; matrix products, arithmetic and copies ran while one was open for 31% -> 30% of each run, Pallas kernels for 0% -> 0%
where the time goes in v8:
time: 1310 us; the launch traced here: 1290 us
  waiting for transfers between devices  414 us (32%)
  matrix products  335 us (26%)
  starting transfers between devices  213 us (16%)
  other arithmetic  187 us (14%)
  local copies, waits for them, and re-layouts  121 us (9%)
  between operations  17.1 us (1%)
    ppermute x21, waiting for transfers between devices, tp_psum(): total = total + lax.ppermute(piece, TP, pairs).astype(jnp.float32)  197 us
    ppermute x21, waiting for transfers between devices, tp_psum(): got = lax.ppermute(reduced, TP, pairs)  187 us
    ppermute x21, starting transfers between devices, tp_psum(): total = total + lax.ppermute(piece, TP, pairs).astype(jnp.float32)  183 us
    dot_general x11, matrix products, matmul_low(): return jnp.dot(left, right, preferred_element_type=jnp.float32)  77.5 us
    convert_element_type x2, other arithmetic, one_block(): grad_scores = (probability * (grad_prob - inner_sum)).astype(jnp.bfloat16)  29.7 us
    ppermute x21, starting transfers between devices, tp_psum(): got = lax.ppermute(reduced, TP, pairs)  29.1 us
    unnamed x176, local copies, waits for them, and re-layouts  28.8 us
    dot_general x4, matrix products, score_block(): jnp.einsum('qhd,khd->hqk', query_rows, keys_seq, preferred_element_type=j...  27.9 us
  transfers between devices with their start and end apart: 56, of which 24 were waited for; matrix products, arithmetic and copies ran while one was open for 30% of the time, Pallas kernels for 0%

profile of v8, /device:TPU:0, one launch (start us, length us, event | category | flops | bytes accessed | tf_op | source)
XLA Modules:
  0.0 1290.3 jit_solution(8373454630894718752)
XLA Ops:
  23.7 26.1 %all-gather.11.cloned.1.call-done = bf16[2048,1024]{1,0:T(8,128)(2,1)} async-done(((bf16[256,1024]{1,0:T(8,128)(2,1)}), bf16[2048,1024]{1,0:T(8,128)(2,1)}) %all-gather.11.cloned.1.call-update) | async-done | bytes 4194320 | tf_op jit(solution)/shard_map/all_gather | solution.py:218
  115.0 37.7 %while.27 = (s32[]{:T(128)}, bf16[2,512,4,128]{3,2,1,0:T(4,128)(2,1)}, f32[2,4,512]{2,1,0:T(4,128)S(1)}, s32[2]{0:T(128)S(1)}, s32[]{:T(128)}, /*index=5*/s32[]{...) while((s32[]{:T(128)}, ...), condition=%wide.region_5.6_spmd, body=%wide.region_2.5_spmd.sunk | while | flops 2195980800 | bytes 77668600 | solution.py:77
  184.2 68.8 %collective-permute-done.1 = bf16[96,2048]{1,0:T(8,128)(2,1)} collective-permute-done((bf16[96,2048]{1,0:T(8,128)(2,1)}, bf16[96,2048]{1,0:T(8,128)(2,1)}, u32[]{:S(2)}, u32[]{:S(2)}) %collective-permute-start.1) | collective-permute-done | bytes 393248 | tf_op jit(solution)/shard_map/ppermute | solution.py:128
  269.9 15.8 %collective-permute-done.4 = bf16[96,2048]{1,0:T(8,128)(2,1)S(1)} collective-permute-done((bf16[96,2048]{1,0:T(8,128)(2,1)S(1)}, bf16[96,2048]{1,0:T(8,128)(2,1)S(1)}, u32[]{:S(2)}, u32[]{:S(2)}) %collective-permute-start.4) | collective-permute-done | bytes 393248 | tf_op jit(solution)/shard_map/ppermute | solution.py:134
  287.8 11.9 collective-permute-done.9
  299.8 34.9 %collective-permute-done.10 = bf16[160,2048]{1,0:T(8,128)(2,1)S(1)} collective-permute-done((bf16[160,2048]{1,0:T(8,128)(2,1)S(1)}, bf16[160,2048]{1,0:T(8,128)(2,1)S(1)}, u32[]{:S(2)}, u32[]{:S(2)}) %collective-permute-start.10) | collective-permute-done | bytes 655392 | tf_op jit(solution)/shard_map/ppermute | solution.py:134
  340.5 11.0 fusion.179
  351.6 11.1 fusion.130
  362.7 14.1 %multiply_convert_fusion.2 = (bf16[640,2048]{1,0:T(8,128)(2,1)S(1)}, bf16[640,2048]{1,0:T(8,128)(2,1)S(1)}, bf16[640,2048]{1,0:T(8,128)(2,1)S(1)}) fusion(f32[640,2048]{1,0:T(8,128)} %fusion.130, f32[640,2048]{1,0:T(8,128)} %fusion.179, bf16[640,2048]{1,0:T(8,128)(2,1)} %fusion.54, bf16[2048,2048]{1,0:T(8,128)(2,1)} %all-gather.15.cloned.1.call-done), kind=kOutput, calls=%fused_computation.85 | convolution fusion | flops 5389680640 | bytes 29360128 | tf_op jit(solution)/shard_map/dot_general | solution.py:159
  387.2 10.8 fusion.183
  429.7 17.1 %collective-permute-start.20 = (bf16[160,2048]{1,0:T(8,128)(2,1)}, bf16[160,2048]{1,0:T(8,128)(2,1)}, u32[]{:S(2)}, u32[]{:S(2)}) collective-permute-start(bf16[160,2048]{1,0:T(8,128)(2,1)} %get-tuple-element.339), channel_id=1, source_target_pairs={{0,3},{1,0},{2,1},{3,2},{4,7},{5,4},{6,5},{7,6},{8,11},{9,8},{10,9... | collective-permute-start | bytes 1966088 | tf_op jit(solution)/shard_map/ppermute | solution.py:128
  476.3 10.6 convolution_add_fusion.1
  506.4 11.0 convolution_add_fusion
  536.2 25.7 %collective-permute-done.13 = bf16[96,2048]{1,0:T(8,128)(2,1)} collective-permute-done((bf16[96,2048]{1,0:T(8,128)(2,1)}, bf16[96,2048]{1,0:T(8,128)(2,1)}, u32[]{:S(2)}, u32[]{:S(2)}) %collective-permute-start.13) | collective-permute-done | bytes 393248 | tf_op jit(solution)/shard_map/ppermute | solution.py:128
  578.5 15.4 %collective-permute-done.16 = bf16[96,2048]{1,0:T(8,128)(2,1)S(1)} collective-permute-done((bf16[96,2048]{1,0:T(8,128)(2,1)S(1)}, bf16[96,2048]{1,0:T(8,128)(2,1)S(1)}, u32[]{:S(2)}, u32[]{:S(2)}) %collective-permute-start.16) | collective-permute-done | bytes 393248 | tf_op jit(solution)/shard_map/ppermute | solution.py:134
  605.0 25.5 %collective-permute-done.22 = bf16[160,2048]{1,0:T(8,128)(2,1)} collective-permute-done((bf16[160,2048]{1,0:T(8,128)(2,1)}, bf16[160,2048]{1,0:T(8,128)(2,1)}, u32[]{:S(2)}, u32[]{:S(2)}) %collective-permute-start.22) | collective-permute-done | bytes 655392 | tf_op jit(solution)/shard_map/ppermute | solution.py:134
  646.9 129.9 %while.28 = (s32[]{:T(128)}, f32[2048,4,128]{0,2,1:T(8,128)}, f32[2048,4,128]{0,2,1:T(8,128)}, f32[2,512,4,128]{3,1,0,2:T(8,128)}, bf16[2,512,4,128]{3,1,2,0:T(8...) while((s32[]{:T(128)}, f32[2048,4,128]{0,2,1:T(8,128)}, ...), condition=%wide.region_16.17_spmd.clone, body=%wide.region_14.16_spmd.clone.sunk | while | flops 5439226368 | bytes 198246768 | solution.py:113
  659.0 12.9 %multiply_reduce_fusion.5 = (f32[4,512]{1,0:T(4,128)S(1)}, f32[4,512,2048]{2,1,0:T(8,128)}) fusion(f32[4,512,2048]{2,1,0:T(8,128)} %fusion.267, f32[4,512]{1,0:T(4,128)S(1)} %dynamic-slice_bitcast_fusion.23, pred[512,2048]{1,0:T(8,128)(4,1)S(1)} %fusion.268, bf16[2048,4,128]{2,0,1:T(8,128)(2,1)} %get-tuple-element.594, ...), kind=kOutput, calls=%fused_computation.22.clone.1 | convolution fusion | flops 1094711296 | bytes 37240836 | tf_op jit(solution)/shard_map/while/body/eval_jaxpr/qhd,khd->hqk/dot_general | solution.py:94
  671.9 14.8 %multiply_convert_fusion.9 = bf16[4,512,2048]{2,1,0:T(8,128)(2,1)} fusion(f32[4,512,2048]{2,1,0:T(8,128)} %get-tuple-element.518, f32[4,512,2048]{2,1,0:T(8,128)} %fusion.267, f32[4,512]{1,0:T(4,128)S(1)} %get-tuple-element.519, f32[4,512]{1,0:T(4,128)S(1)} %dynamic-slice_bitcast_fusion.23, pred[512,2048]{1,0:T(8,128)(4,1)S(1)} %fusion.268), kind=kLoop, calls=%fused_computation.21.clone.1 | loop fusion | flops 25165824 | bytes 43008000 | tf_op jit(solution)/shard_map/while/body/eval_jaxpr/convert_element_type | solution.py:98
  694.1 12.8 bitcast_add_fusion.7
  722.5 12.9 %multiply_reduce_fusion.5 = (f32[4,512]{1,0:T(4,128)S(1)}, f32[4,512,2048]{2,1,0:T(8,128)}) fusion(f32[4,512,2048]{2,1,0:T(8,128)} %fusion.267, f32[4,512]{1,0:T(4,128)S(1)} %dynamic-slice_bitcast_fusion.23, pred[512,2048]{1,0:T(8,128)(4,1)S(1)} %fusion.268, bf16[2048,4,128]{2,0,1:T(8,128)(2,1)} %get-tuple-element.594, ...), kind=kOutput, calls=%fused_computation.22.clone.1 | convolution fusion | flops 1094711296 | bytes 37240836 | tf_op jit(solution)/shard_map/while/body/eval_jaxpr/qhd,khd->hqk/dot_general | solution.py:94
  735.4 14.8 %multiply_convert_fusion.9 = bf16[4,512,2048]{2,1,0:T(8,128)(2,1)} fusion(f32[4,512,2048]{2,1,0:T(8,128)} %get-tuple-element.518, f32[4,512,2048]{2,1,0:T(8,128)} %fusion.267, f32[4,512]{1,0:T(4,128)S(1)} %get-tuple-element.519, f32[4,512]{1,0:T(4,128)S(1)} %dynamic-slice_bitcast_fusion.23, pred[512,2048]{1,0:T(8,128)(4,1)S(1)} %fusion.268), kind=kLoop, calls=%fused_computation.21.clone.1 | loop fusion | flops 25165824 | bytes 43008000 | tf_op jit(solution)/shard_map/while/body/eval_jaxpr/convert_element_type | solution.py:98
  758.8 14.0 %bitcast_add_fusion.7 = f32[2048,4,128]{0,2,1:T(8,128)} fusion(f32[2048,4,128]{0,2,1:T(8,128)} %get-tuple-element.570, f32[4,512,2048]{2,1,0:T(8,128)} %fusion.267, f32[4,512]{1,0:T(4,128)S(1)} %dynamic-slice_bitcast_fusion.23, pred[512,2048]{1,0:T(8,128)(4,1)S(1)} %fusion.268, pred[]{:T(512)S(6)} %compare.10, ...), kind=kOutput, calls=%fused_computation.27.clone.1 | convolution fusion | flops 1092616192 | bytes 26746884 | tf_op jit(solution)/shard_map/while/body/eval_jaxpr/hqk,qhd->khd/dot_general | solution.py:107
  862.2 11.5 pad_maximum_fusion.1
  878.8 12.8 collective-permute-start.26
  892.3 23.3 %collective-permute-done.26 = bf16[256,2048]{1,0:T(8,128)(2,1)} collective-permute-done((bf16[256,2048]{1,0:T(8,128)(2,1)}, bf16[256,2048]{1,0:T(8,128)(2,1)}, u32[]{:S(2)}, u32[]{:S(2)}) %collective-permute-start.26) | collective-permute-done | bytes 1048608 | tf_op jit(solution)/shard_map/ppermute | solution.py:128
  915.6 66.3 %collective-permute-done.25 = bf16[256,2048]{1,0:T(8,128)(2,1)} collective-permute-done((bf16[256,2048]{1,0:T(8,128)(2,1)}, bf16[256,2048]{1,0:T(8,128)(2,1)}, u32[]{:S(2)}, u32[]{:S(2)}) %collective-permute-start.25) | collective-permute-done | bytes 1048608 | tf_op jit(solution)/shard_map/ppermute | solution.py:128
  1015.0 72.4 %collective-permute-start.38 = (bf16[160,2048]{1,0:T(8,128)(2,1)S(1)}, bf16[160,2048]{1,0:T(8,128)(2,1)}, u32[]{:S(2)}, u32[]{:S(2)}) collective-permute-start(bf16[160,2048]{1,0:T(8,128)(2,1)S(1)} %get-tuple-element.335), channel_id=1, source_target_pairs={{0,1},{1,2},{2,3},{3,0},{4,5},{5,6},{6,7},{7,4},{8,9},{9,10},{10,1... | collective-permute-start | bytes 1966088 | tf_op jit(solution)/shard_map/ppermute | solution.py:128
  1088.9 23.9 %collective-permute-start.34 = (bf16[96,2048]{1,0:T(8,128)(2,1)S(1)}, bf16[96,2048]{1,0:T(8,128)(2,1)S(1)}, u32[]{:S(2)}, u32[]{:S(2)}) collective-permute-start(bf16[96,2048]{1,0:T(8,128)(2,1)S(1)} %get-tuple-element.357), channel_id=1, source_target_pairs={{0,3},{1,0},{2,1},{3,2},{4,7},{5,4},{6,5},{7,6},{8,11},{9,8},{10,9... | collective-permute-start | bytes 1179656 | tf_op jit(solution)/shard_map/ppermute | solution.py:128
  1123.1 40.9 %collective-permute-start.32 = (bf16[96,2048]{1,0:T(8,128)(2,1)S(1)}, bf16[96,2048]{1,0:T(8,128)(2,1)}, u32[]{:S(2)}, u32[]{:S(2)}) collective-permute-start(bf16[96,2048]{1,0:T(8,128)(2,1)S(1)} %get-tuple-element.356), channel_id=1, source_target_pairs={{0,1},{1,2},{2,3},{3,0},{4,5},{5,6},{6,7},{7,4},{8,9},{9,10},{10,1... | collective-permute-start | bytes 1179656 | tf_op jit(solution)/shard_map/ppermute | solution.py:128
  1188.3 16.8 %collective-permute-done.36 = bf16[96,2048]{1,0:T(8,128)(2,1)S(1)} collective-permute-done((bf16[96,2048]{1,0:T(8,128)(2,1)S(1)}, bf16[96,2048]{1,0:T(8,128)(2,1)S(1)}, u32[]{:S(2)}, u32[]{:S(2)}) %collective-permute-start.36) | collective-permute-done | bytes 393248 | tf_op jit(solution)/shard_map/ppermute | solution.py:134
  1221.2 32.7 %collective-permute-done.42 = bf16[160,2048]{1,0:T(8,128)(2,1)} collective-permute-done((bf16[160,2048]{1,0:T(8,128)(2,1)}, bf16[160,2048]{1,0:T(8,128)(2,1)}, u32[]{:S(2)}, u32[]{:S(2)}) %collective-permute-start.42) | collective-permute-done | bytes 655392 | tf_op jit(solution)/shard_map/ppermute | solution.py:134
  (527 shorter events, 576.3 us)
Async XLA Ops:
  10.4 79.3 %all-gather.9.cloned.1.call-start = ((), (), s32[]{:S(2)}) async-start(), calls=%async_computation.5 | async-start | bytes 4718592 | tf_op jit(solution)/shard_map/all_gather | solution.py:221
  11.5 102.8 %all-gather.13.cloned.1.call-start = ((), (), s32[]{:S(2)}) async-start(), calls=%async_computation.7 | async-start | bytes 3145728 | tf_op jit(solution)/shard_map/all_gather | solution.py:244
  71.5 269.0 %all-gather.17.cloned.1.call-start = ((), (), s32[]{:S(2)}) async-start(), calls=%async_computation.9 | async-start | bytes 9437184 | tf_op jit(solution)/shard_map/all_gather | solution.py:229
  72.8 278.8 %all-gather.19.cloned.1.call-start = ((), (), s32[]{:S(2)}) async-start(), calls=%async_computation.10 | async-start | bytes 9437184 | tf_op jit(solution)/shard_map/all_gather | solution.py:230
  76.1 286.6 %all-gather.15.cloned.1.call-start = ((), (), s32[]{:S(2)}) async-start(), calls=%async_computation.8 | async-start | bytes 9437184 | tf_op jit(solution)/shard_map/all_gather | solution.py:228
  77.3 1131.1 %reduce-scatter.8.cloned.1.call-start = ((), (), s32[]{:S(2)}) async-start(), calls=%async_computation.12 | async-start | bytes 2359296 | tf_op jit(solution)/shard_map/reduce_scatter | solution.py:152
  165.4 92.9 %collective-permute-start.8 = (bf16[160,2048]{1,0:T(8,128)(2,1)}, bf16[160,2048]{1,0:T(8,128)(2,1)S(1)}, u32[]{:S(2)}, u32[]{:S(2)}) collective-permute-start(bf16[160,2048]{1,0:T(8,128)(2,1)} %get-tuple-element.342), channel_id=1, source_target_pairs={{0,3},{1,0},{2,1},{3,2},{4,7},{5,4},{6,5},{7,6},{8,11},{9,8},{10,9... | collective-permute-start | bytes 1966088 | tf_op jit(solution)/shard_map/ppermute | solution.py:128
  166.0 95.2 %collective-permute-start.7 = (bf16[160,2048]{1,0:T(8,128)(2,1)}, bf16[160,2048]{1,0:T(8,128)(2,1)}, u32[]{:S(2)}, u32[]{:S(2)}) collective-permute-start(bf16[160,2048]{1,0:T(8,128)(2,1)} %get-tuple-element.343), channel_id=1, source_target_pairs={{0,2},{1,3},{2,0},{3,1},{4,6},{5,7},{6,4},{7,5},{8,10},{9,11},{10,... | collective-permute-start | bytes 1966088 | tf_op jit(solution)/shard_map/ppermute | solution.py:128
  166.0 95.2 %collective-permute-start.6 = (bf16[160,2048]{1,0:T(8,128)(2,1)}, bf16[160,2048]{1,0:T(8,128)(2,1)}, u32[]{:S(2)}, u32[]{:S(2)}) collective-permute-start(bf16[160,2048]{1,0:T(8,128)(2,1)} %get-tuple-element.341), channel_id=1, source_target_pairs={{0,1},{1,2},{2,3},{3,0},{4,5},{5,6},{6,7},{7,4},{8,9},{9,10},{10,1... | collective-permute-start | bytes 1966088 | tf_op jit(solution)/shard_map/ppermute | solution.py:128
  167.5 85.5 %collective-permute-start.1 = (bf16[96,2048]{1,0:T(8,128)(2,1)}, bf16[96,2048]{1,0:T(8,128)(2,1)}, u32[]{:S(2)}, u32[]{:S(2)}) collective-permute-start(bf16[96,2048]{1,0:T(8,128)(2,1)} %get-tuple-element.364), channel_id=1, source_target_pairs={{0,2},{1,3},{2,0},{3,1},{4,6},{5,7},{6,4},{7,5},{8,10},{9,11},{10,... | collective-permute-start | bytes 1179656 | tf_op jit(solution)/shard_map/ppermute | solution.py:128
  172.9 80.1 %collective-permute-start = (bf16[96,2048]{1,0:T(8,128)(2,1)}, bf16[96,2048]{1,0:T(8,128)(2,1)}, u32[]{:S(2)}, u32[]{:S(2)}) collective-permute-start(bf16[96,2048]{1,0:T(8,128)(2,1)} %get-tuple-element.362), channel_id=1, source_target_pairs={{0,1},{1,2},{2,3},{3,0},{4,5},{5,6},{6,7},{7,4},{8,9},{9,10},{10,1... | collective-permute-start | bytes 1179656 | tf_op jit(solution)/shard_map/ppermute | solution.py:128
  263.5 71.3 %collective-permute-start.10 = (bf16[160,2048]{1,0:T(8,128)(2,1)S(1)}, bf16[160,2048]{1,0:T(8,128)(2,1)S(1)}, u32[]{:S(2)}, u32[]{:S(2)}) collective-permute-start(bf16[160,2048]{1,0:T(8,128)(2,1)S(1)} %get-tuple-element.315), channel_id=1, source_target_pairs={{0,2},{1,3},{2,0},{3,1},{4,6},{5,7},{6,4},{7,5},{8,10},{9,11},{10,... | collective-permute-start | bytes 1966088 | tf_op jit(solution)/shard_map/ppermute | solution.py:134
  268.8 66.0 %collective-permute-start.11 = (bf16[160,2048]{1,0:T(8,128)(2,1)S(1)}, bf16[160,2048]{1,0:T(8,128)(2,1)S(1)}, u32[]{:S(2)}, u32[]{:S(2)}) collective-permute-start(bf16[160,2048]{1,0:T(8,128)(2,1)S(1)} %get-tuple-element.315), channel_id=1, source_target_pairs={{0,3},{1,0},{2,1},{3,2},{4,7},{5,4},{6,5},{7,6},{8,11},{9,8},{10,9... | collective-permute-start | bytes 1966088 | tf_op jit(solution)/shard_map/ppermute | solution.py:134
  429.7 134.1 %collective-permute-start.20 = (bf16[160,2048]{1,0:T(8,128)(2,1)}, bf16[160,2048]{1,0:T(8,128)(2,1)}, u32[]{:S(2)}, u32[]{:S(2)}) collective-permute-start(bf16[160,2048]{1,0:T(8,128)(2,1)} %get-tuple-element.339), channel_id=1, source_target_pairs={{0,3},{1,0},{2,1},{3,2},{4,7},{5,4},{6,5},{7,6},{8,11},{9,8},{10,9... | collective-permute-start | bytes 1966088 | tf_op jit(solution)/shard_map/ppermute | solution.py:128
  446.8 120.7 %collective-permute-start.19 = (bf16[160,2048]{1,0:T(8,128)(2,1)}, bf16[160,2048]{1,0:T(8,128)(2,1)}, u32[]{:S(2)}, u32[]{:S(2)}) collective-permute-start(bf16[160,2048]{1,0:T(8,128)(2,1)} %get-tuple-element.340), channel_id=1, source_target_pairs={{0,2},{1,3},{2,0},{3,1},{4,6},{5,7},{6,4},{7,5},{8,10},{9,11},{10,... | collective-permute-start | bytes 1966088 | tf_op jit(solution)/shard_map/ppermute | solution.py:128
  501.6 60.4 %collective-permute-start.13 = (bf16[96,2048]{1,0:T(8,128)(2,1)}, bf16[96,2048]{1,0:T(8,128)(2,1)}, u32[]{:S(2)}, u32[]{:S(2)}) collective-permute-start(bf16[96,2048]{1,0:T(8,128)(2,1)} %get-tuple-element.361), channel_id=1, source_target_pairs={{0,2},{1,3},{2,0},{3,1},{4,6},{5,7},{6,4},{7,5},{8,10},{9,11},{10,... | collective-permute-start | bytes 1179656 | tf_op jit(solution)/shard_map/ppermute | solution.py:128
  504.4 57.6 %collective-permute-start.12 = (bf16[96,2048]{1,0:T(8,128)(2,1)S(1)}, bf16[96,2048]{1,0:T(8,128)(2,1)}, u32[]{:S(2)}, u32[]{:S(2)}) collective-permute-start(bf16[96,2048]{1,0:T(8,128)(2,1)S(1)} %get-tuple-element.359), channel_id=1, source_target_pairs={{0,1},{1,2},{2,3},{3,0},{4,5},{5,6},{6,7},{7,4},{8,9},{9,10},{10,1... | collective-permute-start | bytes 1179656 | tf_op jit(solution)/shard_map/ppermute | solution.py:128
  571.8 58.8 %collective-permute-start.22 = (bf16[160,2048]{1,0:T(8,128)(2,1)}, bf16[160,2048]{1,0:T(8,128)(2,1)}, u32[]{:S(2)}, u32[]{:S(2)}) collective-permute-start(bf16[160,2048]{1,0:T(8,128)(2,1)} %get-tuple-element.307), channel_id=1, source_target_pairs={{0,2},{1,3},{2,0},{3,1},{4,6},{5,7},{6,4},{7,5},{8,10},{9,11},{10,... | collective-permute-start | bytes 1966088 | tf_op jit(solution)/shard_map/ppermute | solution.py:134
  827.7 442.8 %reduce-scatter.6.cloned.1.call-start = ((), (), s32[]{:S(2)}) async-start(), calls=%async_computation.11 | async-start | bytes 7077888 | tf_op jit(solution)/shard_map/reduce_scatter | solution.py:152
  873.8 400.9 %reduce-scatter.10.cloned.1.call-start = ((), (), s32[]{:S(2)}) async-start(), calls=%async_computation.13 | async-start | bytes 9437184 | tf_op jit(solution)/shard_map/reduce_scatter | solution.py:152
  874.4 403.1 %reduce-scatter.12.cloned.1.call-start = ((), (), s32[]{:S(2)}) async-start(), calls=%async_computation.14 | async-start | bytes 9437184 | tf_op jit(solution)/shard_map/reduce_scatter | solution.py:152
  875.1 405.2 %reduce-scatter.14.cloned.1.call-start = ((), (), s32[]{:S(2)}) async-start(), calls=%async_computation.15 | async-start | bytes 9437184 | tf_op jit(solution)/shard_map/reduce_scatter | solution.py:152
  891.6 90.3 %collective-permute-start.25 = (bf16[256,2048]{1,0:T(8,128)(2,1)}, bf16[256,2048]{1,0:T(8,128)(2,1)}, u32[]{:S(2)}, u32[]{:S(2)}) collective-permute-start(bf16[256,2048]{1,0:T(8,128)(2,1)} %get-tuple-element.334), channel_id=1, source_target_pairs={{0,2},{1,3},{2,0},{3,1},{4,6},{5,7},{6,4},{7,5},{8,10},{9,11},{10,... | collective-permute-start | bytes 3145736 | tf_op jit(solution)/shard_map/ppermute | solution.py:128
  891.6 90.3 %collective-permute-start.24 = (bf16[256,2048]{1,0:T(8,128)(2,1)}, bf16[256,2048]{1,0:T(8,128)(2,1)}, u32[]{:S(2)}, u32[]{:S(2)}) collective-permute-start(bf16[256,2048]{1,0:T(8,128)(2,1)} %get-tuple-element.332), channel_id=1, source_target_pairs={{0,1},{1,2},{2,3},{3,0},{4,5},{5,6},{6,7},{7,4},{8,9},{9,10},{10,1... | collective-permute-start | bytes 3145736 | tf_op jit(solution)/shard_map/ppermute | solution.py:128
  987.8 101.1 %collective-permute-start.28 = (bf16[256,2048]{1,0:T(8,128)(2,1)}, bf16[256,2048]{1,0:T(8,128)(2,1)}, u32[]{:S(2)}, u32[]{:S(2)}) collective-permute-start(bf16[256,2048]{1,0:T(8,128)(2,1)} %get-tuple-element.303), channel_id=1, source_target_pairs={{0,2},{1,3},{2,0},{3,1},{4,6},{5,7},{6,4},{7,5},{8,10},{9,11},{10,... | collective-permute-start | bytes 3145736 | tf_op jit(solution)/shard_map/ppermute | solution.py:134
  990.1 124.4 %collective-permute-start.29 = (bf16[256,2048]{1,0:T(8,128)(2,1)}, bf16[256,2048]{1,0:T(8,128)(2,1)}, u32[]{:S(2)}, u32[]{:S(2)}) collective-permute-start(bf16[256,2048]{1,0:T(8,128)(2,1)} %get-tuple-element.303), channel_id=1, source_target_pairs={{0,3},{1,0},{2,1},{3,2},{4,7},{5,4},{6,5},{7,6},{8,11},{9,8},{10,9... | collective-permute-start | bytes 3145736 | tf_op jit(solution)/shard_map/ppermute | solution.py:134
  998.8 178.1 %collective-permute-start.40 = (bf16[160,2048]{1,0:T(8,128)(2,1)}, bf16[160,2048]{1,0:T(8,128)(2,1)S(1)}, u32[]{:S(2)}, u32[]{:S(2)}) collective-permute-start(bf16[160,2048]{1,0:T(8,128)(2,1)} %get-tuple-element.336), channel_id=1, source_target_pairs={{0,3},{1,0},{2,1},{3,2},{4,7},{5,4},{6,5},{7,6},{8,11},{9,8},{10,9... | collective-permute-start | bytes 1966088 | tf_op jit(solution)/shard_map/ppermute | solution.py:128
  999.0 180.5 %collective-permute-start.39 = (bf16[160,2048]{1,0:T(8,128)(2,1)S(1)}, bf16[160,2048]{1,0:T(8,128)(2,1)S(1)}, u32[]{:S(2)}, u32[]{:S(2)}) collective-permute-start(bf16[160,2048]{1,0:T(8,128)(2,1)S(1)} %get-tuple-element.337), channel_id=1, source_target_pairs={{0,2},{1,3},{2,0},{3,1},{4,6},{5,7},{6,4},{7,5},{8,10},{9,11},{10,... | collective-permute-start | bytes 1966088 | tf_op jit(solution)/shard_map/ppermute | solution.py:128
  1015.0 165.4 %collective-permute-start.38 = (bf16[160,2048]{1,0:T(8,128)(2,1)S(1)}, bf16[160,2048]{1,0:T(8,128)(2,1)}, u32[]{:S(2)}, u32[]{:S(2)}) collective-permute-start(bf16[160,2048]{1,0:T(8,128)(2,1)S(1)} %get-tuple-element.335), channel_id=1, source_target_pairs={{0,1},{1,2},{2,3},{3,0},{4,5},{5,6},{6,7},{7,4},{8,9},{9,10},{10,1... | collective-permute-start | bytes 1966088 | tf_op jit(solution)/shard_map/ppermute | solution.py:128
  1114.5 56.6 %collective-permute-start.33 = (bf16[96,2048]{1,0:T(8,128)(2,1)S(1)}, bf16[96,2048]{1,0:T(8,128)(2,1)}, u32[]{:S(2)}, u32[]{:S(2)}) collective-permute-start(bf16[96,2048]{1,0:T(8,128)(2,1)S(1)} %get-tuple-element.358), channel_id=1, source_target_pairs={{0,2},{1,3},{2,0},{3,1},{4,6},{5,7},{6,4},{7,5},{8,10},{9,11},{10,... | collective-permute-start | bytes 1179656 | tf_op jit(solution)/shard_map/ppermute | solution.py:128
  1183.5 70.5 %collective-permute-start.42 = (bf16[160,2048]{1,0:T(8,128)(2,1)}, bf16[160,2048]{1,0:T(8,128)(2,1)}, u32[]{:S(2)}, u32[]{:S(2)}) collective-permute-start(bf16[160,2048]{1,0:T(8,128)(2,1)} %get-tuple-element.301), channel_id=1, source_target_pairs={{0,2},{1,3},{2,0},{3,1},{4,6},{5,7},{6,4},{7,5},{8,10},{9,11},{10,... | collective-permute-start | bytes 1966088 | tf_op jit(solution)/shard_map/ppermute | solution.py:134
  1188.2 67.9 %collective-permute-start.43 = (bf16[160,2048]{1,0:T(8,128)(2,1)}, bf16[160,2048]{1,0:T(8,128)(2,1)}, u32[]{:S(2)}, u32[]{:S(2)}) collective-permute-start(bf16[160,2048]{1,0:T(8,128)(2,1)} %get-tuple-element.301), channel_id=1, source_target_pairs={{0,3},{1,0},{2,1},{3,2},{4,7},{5,4},{6,5},{7,6},{8,11},{9,8},{10,9... | collective-permute-start | bytes 1966088 | tf_op jit(solution)/shard_map/ppermute | solution.py:134
  (123 other events, 2211.6 us)
Sparse Core Ops, SparseCore 0:
  10.5 39.2 all-gather.10
  52.3 37.3 all-gather.8
  91.2 10.5 all-gather.12
  103.2 11.7 all-gather.20
  116.7 55.4 all-gather.16
  174.5 55.8 all-gather.18
  232.3 54.2 all-gather.14
  827.8 51.7 reduce-scatter.7
  883.0 63.1 reduce-scatter.5
  949.5 71.4 reduce-scatter.9
  1024.5 71.4 reduce-scatter.11
  1099.3 71.2 reduce-scatter.13

commit v9 on v8

--- a/solution.py
+++ b/solution.py
@@ -162,7 +162,7 @@
 MID_SPLIT = (3, 5)
 
 
-def middle_rows(attn_rows, tokens_rows, grad_final, output_full, gate_full, up_full, down_full, tp_count):
+def middle_rows(attn_rows, tokens_rows, grad_final, output_full, gate_full, up_full, down_full, tp_count, before):
     bf_type = jnp.bfloat16
     resid = tokens_rows + tp_psum(matmul_low(attn_rows, output_full), tp_count).astype(jnp.float32)
     normed_two, scale_two = normalize(resid)
@@ -188,7 +188,9 @@
         "rd,rf->df", input_two, grad_gate_act, preferred_element_type=jnp.float32
     )
     grad_up = jnp.einsum("rd,rf->df", input_two, grad_up_act, preferred_element_type=jnp.float32)
-    grad_input_two = tp_psum(grad_input_two, tp_count)
+    if before is not None:
+        grad_input_two, _ = lax.optimization_barrier((grad_input_two, before))
+    grad_input_two = lax.psum(grad_input_two.astype(bf_type), TP)
     return [
         resid, branch_two, normed_two, scale_two, grad_final, grad_input_two,
         grad_gate, grad_up, grad_down,
@@ -265,6 +267,7 @@
             middle_rows(
                 attn_out[rows], tokens_wide[rows], grad_final[rows],
                 output_full, gate_full, up_full, down_full, tp_count,
+                pieces[-1][5] if pieces else None,
             )
         )
     grad_gate = sum(piece[6] for piece in pieces)
@@ -297,7 +300,7 @@
     grad_resid = jnp.concatenate(grad_resid_parts, axis=0)
     grad_attn = jnp.concatenate(grad_attn_parts, axis=0).astype(bf_type).reshape(split_heads)
     branch_two_part, grad_attn = lax.optimization_barrier((branch_two_part, grad_attn))
-    final_sum = resid + tp_psum(branch_two_part, tp_count).astype(jnp.float32)
+    final_sum = resid + lax.psum(branch_two_part.astype(bf_type), TP).astype(jnp.float32)
     seq_index = 0
     grad_queries, grad_keys_seq, grad_values_seq = attend_backward(
         queries[seq_index],

time: 1310 us -> 1370 us (1.046)
  waiting for transfers between devices: 414 us -> 662 us
  starting transfers between devices: 213 us -> 66.5 us
  local copies, waits for them, and re-layouts: 121 us -> 107 us
    reduce_scatter x5, waiting for transfers between devices: 0.01 us -> 207 us  [scatter_low(): lax.psum_scatter(grad.astype(jnp.bfloat16), (SHARD, CTX), scatter_dimensi...]
    ppermute x21 -> x12, starting transfers between devices: 183 us -> 49.3 us  [tp_psum(): total = total + lax.ppermute(piece, TP, pairs).astype(jnp.float32)]
    ppermute x21 -> x12, waiting for transfers between devices: 187 us -> 94.1 us  [tp_psum(): got = lax.ppermute(reduced, TP, pairs)]
    psum x0 -> x3, waiting for transfers between devices: none -> 85.3 us  [the longest x2 85.3 us: middle_rows(): grad_input_two = lax.psum(grad_input_two.astype(bf_type), TP)]
    ppermute x21 -> x12, waiting for transfers between devices: 197 us -> 243 us  [tp_psum(): total = total + lax.ppermute(piece, TP, pairs).astype(jnp.float32)]
    ppermute x21 -> x12, starting transfers between devices: 29.1 us -> 16.1 us  [tp_psum(): got = lax.ppermute(reduced, TP, pairs)]
    unnamed x176 -> x164, local copies, waits for them, and re-layouts: 28.8 us -> 32.3 us
  transfers between devices with their start and end apart: 56 -> 41, of which waited for: 24 -> 19; matrix products, arithmetic and copies ran while one was open for 30% -> 40% of each run, Pallas kernels for 0% -> 0%
where the time goes in v9:
time: 1370 us; the launch traced here: 1360 us
  waiting for transfers between devices  662 us (48%)
  matrix products  330 us (24%)
  other arithmetic  177 us (13%)
  local copies, waits for them, and re-layouts  107 us (8%)
  starting transfers between devices  66.5 us (5%)
  between operations  16.2 us (1%)
    ppermute x12, waiting for transfers between devices, tp_psum(): total = total + lax.ppermute(piece, TP, pairs).astype(jnp.float32)  243 us
    reduce_scatter x5, waiting for transfers between devices, scatter_low(): lax.psum_scatter(grad.astype(jnp.bfloat16), (SHARD, CTX), scatter_dimensi...  207 us
    ppermute x12, waiting for transfers between devices, tp_psum(): got = lax.ppermute(reduced, TP, pairs)  94.1 us
    psum x2, waiting for transfers between devices, middle_rows(): grad_input_two = lax.psum(grad_input_two.astype(bf_type), TP)  85.3 us
    dot_general x11, matrix products, matmul_low(): return jnp.dot(left, right, preferred_element_type=jnp.float32)  78.7 us
    ppermute x12, starting transfers between devices, tp_psum(): total = total + lax.ppermute(piece, TP, pairs).astype(jnp.float32)  49.3 us
    unnamed x164, local copies, waits for them, and re-layouts  32.3 us
    all_gather x1, waiting for transfers between devices, block(): lax.all_gather(jnp.concatenate([attn_low[1], attn_low[2]], axis=1), (SHAR...  31.4 us
  transfers between devices with their start and end apart: 41, of which 19 were waited for; matrix products, arithmetic and copies ran while one was open for 40% of the time, Pallas kernels for 0%

profile of v9, /device:TPU:0, one launch (start us, length us, event | category | flops | bytes accessed | tf_op | source)
XLA Modules:
  0.0 1363.2 jit_solution(15081265718942105346)
XLA Ops:
  18.5 31.4 %all-gather.11.cloned.1.call-done = bf16[2048,1024]{1,0:T(8,128)(2,1)} async-done(((bf16[256,1024]{1,0:T(8,128)(2,1)}), bf16[2048,1024]{1,0:T(8,128)(2,1)}) %all-gather.11.cloned.1.call-update) | async-done | bytes 4194320 | tf_op jit(solution)/shard_map/all_gather | solution.py:220
  116.5 37.5 %while.27 = (s32[]{:T(128)}, bf16[2,512,4,128]{3,2,1,0:T(4,128)(2,1)}, f32[2,4,512]{2,1,0:T(4,128)S(1)}, s32[2]{0:T(128)S(1)}, s32[]{:T(128)}, /*index=5*/s32[]{...) while((s32[]{:T(128)}, ...), condition=%wide.region_5.6_spmd, body=%wide.region_2.5_spmd.sunk | while | flops 2195980800 | bytes 77668600 | solution.py:77
  174.5 17.4 %collective-permute-start.7 = (bf16[160,2048]{1,0:T(8,128)(2,1)}, bf16[160,2048]{1,0:T(8,128)(2,1)}, u32[]{:S(2)}, u32[]{:S(2)}) collective-permute-start(bf16[160,2048]{1,0:T(8,128)(2,1)} %get-tuple-element.333), channel_id=1, source_target_pairs={{0,2},{1,3},{2,0},{3,1},{4,6},{5,7},{6,4},{7,5},{8,10},{9,11},{10,... | collective-permute-start | bytes 1966088 | tf_op jit(solution)/shard_map/ppermute | solution.py:128
  218.3 53.3 %collective-permute-done.7 = bf16[160,2048]{1,0:T(8,128)(2,1)} collective-permute-done((bf16[160,2048]{1,0:T(8,128)(2,1)}, bf16[160,2048]{1,0:T(8,128)(2,1)}, u32[]{:S(2)}, u32[]{:S(2)}) %collective-permute-start.7) | collective-permute-done | bytes 655392 | tf_op jit(solution)/shard_map/ppermute | solution.py:128
  278.3 29.7 %collective-permute-done.4 = bf16[96,2048]{1,0:T(8,128)(2,1)S(1)} collective-permute-done((bf16[96,2048]{1,0:T(8,128)(2,1)S(1)}, bf16[96,2048]{1,0:T(8,128)(2,1)S(1)}, u32[]{:S(2)}, u32[]{:S(2)}) %collective-permute-start.4) | collective-permute-done | bytes 393248 | tf_op jit(solution)/shard_map/ppermute | solution.py:134
  310.3 20.3 %collective-permute-done.10 = bf16[160,2048]{1,0:T(8,128)(2,1)S(1)} collective-permute-done((bf16[160,2048]{1,0:T(8,128)(2,1)S(1)}, bf16[160,2048]{1,0:T(8,128)(2,1)S(1)}, u32[]{:S(2)}, u32[]{:S(2)}) %collective-permute-start.10) | collective-permute-done | bytes 655392 | tf_op jit(solution)/shard_map/ppermute | solution.py:134
  383.0 11.5 fusion.123
  402.5 13.9 %multiply_convert_fusion.2 = (bf16[640,2048]{1,0:T(8,128)(2,1)S(1)}, bf16[640,2048]{1,0:T(8,128)(2,1)}, bf16[640,2048]{1,0:T(8,128)(2,1)}) fusion(f32[640,2048]{1,0:T(8,128)} %fusion.123, f32[640,2048]{1,0:T(8,128)S(1)} %fusion.164, bf16[640,2048]{1,0:T(8,128)(2,1)S(1)} %copy-done.44, bf16[2048,2048]{1,0:T(8,128)(2,1)} %all-gather.15.cloned.1.call-done), kind=kOutput, calls=%fused_computation.84 | convolution fusion | flops 5389680640 | bytes 29360128 | tf_op jit(solution)/shard_map/dot_general | solution.py:159
  416.4 10.4 fusion.168
  426.8 10.8 convolution_add_fusion.1
  437.6 12.6 fusion.167
  450.2 10.2 convolution_add_fusion.2
  460.4 13.2 fusion.122
  473.6 11.4 convolution_add_fusion
  485.1 10.8 fusion.165
  539.1 85.3 %all-reduce.6.cloned.1.call-done = bf16[640,2048]{1,0:T(8,128)(2,1)} async-done(((bf16[640,2048]{1,0:T(8,128)(2,1)}), bf16[640,2048]{1,0:T(8,128)(2,1)}) %all-reduce.6.cloned.1.call-update) | async-done | bytes 2621456 | tf_op jit(solution)/shard_map/psum | solution.py:193
  651.1 109.9 %while.28 = (s32[]{:T(128)}, f32[2048,4,128]{0,2,1:T(8,128)}, f32[2048,4,128]{0,2,1:T(8,128)}, f32[2,512,4,128]{3,1,0,2:T(8,128)}, bf16[2,512,4,128]{3,1,2,0:T(8...) while((s32[]{:T(128)}, f32[2048,4,128]{0,2,1:T(8,128)}, ...), condition=%wide.region_19.20_spmd.clone, body=%wide.region_17.19_spmd.clone.sunk | while | flops 5439226368 | bytes 219218320 | solution.py:113
  662.5 11.3 bitcast_add_fusion.7
  673.7 12.6 multiply_reduce_fusion.5
  686.3 12.2 multiply_convert_fusion.9
  716.6 12.4 bitcast_add_fusion.7
  729.0 12.4 multiply_reduce_fusion.5
  741.4 12.2 multiply_convert_fusion.9
  838.3 11.7 pad_maximum_fusion.1
  880.5 15.7 %collective-permute-start.21 = (bf16[160,2048]{1,0:T(8,128)(2,1)S(1)}, bf16[160,2048]{1,0:T(8,128)(2,1)S(1)}, u32[]{:S(2)}, u32[]{:S(2)}) collective-permute-start(bf16[160,2048]{1,0:T(8,128)(2,1)S(1)} %get-tuple-element.330), channel_id=1, source_target_pairs={{0,2},{1,3},{2,0},{3,1},{4,6},{5,7},{6,4},{7,5},{8,10},{9,11},{10,... | collective-permute-start | bytes 1966088 | tf_op jit(solution)/shard_map/ppermute | solution.py:128
  896.2 45.8 %collective-permute-done.15 = bf16[96,2048]{1,0:T(8,128)(2,1)S(1)} collective-permute-done((bf16[96,2048]{1,0:T(8,128)(2,1)S(1)}, bf16[96,2048]{1,0:T(8,128)(2,1)S(1)}, u32[]{:S(2)}, u32[]{:S(2)}) %collective-permute-start.15) | collective-permute-done | bytes 393248 | tf_op jit(solution)/shard_map/ppermute | solution.py:128
  946.9 121.0 %collective-permute-done.21 = bf16[160,2048]{1,0:T(8,128)(2,1)S(1)} collective-permute-done((bf16[160,2048]{1,0:T(8,128)(2,1)S(1)}, bf16[160,2048]{1,0:T(8,128)(2,1)S(1)}, u32[]{:S(2)}, u32[]{:S(2)}) %collective-permute-start.21) | collective-permute-done | bytes 655392 | tf_op jit(solution)/shard_map/ppermute | solution.py:128
  1073.4 17.0 %collective-permute-done.18 = bf16[96,2048]{1,0:T(8,128)(2,1)S(1)} collective-permute-done((bf16[96,2048]{1,0:T(8,128)(2,1)S(1)}, bf16[96,2048]{1,0:T(8,128)(2,1)S(1)}, u32[]{:S(2)}, u32[]{:S(2)}) %collective-permute-start.18) | collective-permute-done | bytes 393248 | tf_op jit(solution)/shard_map/ppermute | solution.py:134
  1100.2 12.7 collective-permute-done.24
  1141.4 62.6 %reduce-scatter.14.cloned.1.call-done = bf16[2048,256]{1,0:T(8,128)(2,1)} async-done(((bf16[2048,2048]{1,0:T(8,128)(2,1)}), bf16[2048,256]{1,0:T(8,128)(2,1)}) %reduce-scatter.14.cloned.1.call-update) | async-done | bytes 1048592 | tf_op jit(solution)/shard_map/reduce_scatter | solution.py:152
  1206.7 72.1 %reduce-scatter.12.cloned.1.call-done = bf16[256,2048]{1,0:T(8,128)(2,1)} async-done(((bf16[2048,2048]{1,0:T(8,128)(2,1)}), bf16[256,2048]{1,0:T(8,128)(2,1)}) %reduce-scatter.12.cloned.1.call-update) | async-done | bytes 1048592 | tf_op jit(solution)/shard_map/reduce_scatter | solution.py:152
  1281.6 72.0 %reduce-scatter.10.cloned.1.call-done = bf16[256,2048]{1,0:T(8,128)(2,1)} async-done(((bf16[2048,2048]{1,0:T(8,128)(2,1)}), bf16[256,2048]{1,0:T(8,128)(2,1)}) %reduce-scatter.10.cloned.1.call-update) | async-done | bytes 1048592 | tf_op jit(solution)/shard_map/reduce_scatter | solution.py:152
  (473 shorter events, 497.1 us)
Async XLA Ops:
  10.4 81.8 %all-gather.9.cloned.1.call-start = ((), (), s32[]{:S(2)}) async-start(), calls=%async_computation.5 | async-start | bytes 4718592 | tf_op jit(solution)/shard_map/all_gather | solution.py:223
  11.5 104.9 %all-gather.21.cloned.1.call-start = ((), (), s32[]{:S(2)}) async-start(), calls=%async_computation.19 | async-start | bytes 3145728 | tf_op jit(solution)/shard_map/all_gather | solution.py:247
  60.2 56.2 %all-gather.13.cloned.1.call-start = ((), (), s32[]{:S(2)}) async-start(), calls=%async_computation.7 | async-start | bytes 3145728 | tf_op jit(solution)/shard_map/all_gather | solution.py:246
  74.3 267.5 %all-gather.17.cloned.1.call-start = ((), (), s32[]{:S(2)}) async-start(), calls=%async_computation.9 | async-start | bytes 9437184 | tf_op jit(solution)/shard_map/all_gather | solution.py:231
  77.4 272.9 %all-gather.19.cloned.1.call-start = ((), (), s32[]{:S(2)}) async-start(), calls=%async_computation.10 | async-start | bytes 9437184 | tf_op jit(solution)/shard_map/all_gather | solution.py:232
  78.5 281.2 %all-gather.15.cloned.1.call-start = ((), (), s32[]{:S(2)}) async-start(), calls=%async_computation.8 | async-start | bytes 9437184 | tf_op jit(solution)/shard_map/all_gather | solution.py:230
  81.4 433.1 %all-reduce.4.cloned.1.call-start = ((), (), s32[]{:S(2)}) async-start(), calls=%async_computation.11 | async-start | bytes 3145728 | tf_op jit(solution)/shard_map/psum | solution.py:193
  163.8 48.8 %collective-permute-start.1 = (bf16[96,2048]{1,0:T(8,128)(2,1)}, bf16[96,2048]{1,0:T(8,128)(2,1)}, u32[]{:S(2)}, u32[]{:S(2)}) collective-permute-start(bf16[96,2048]{1,0:T(8,128)(2,1)} %get-tuple-element.351), channel_id=1, source_target_pairs={{0,2},{1,3},{2,0},{3,1},{4,6},{5,7},{6,4},{7,5},{8,10},{9,11},{10,... | collective-permute-start | bytes 1179656 | tf_op jit(solution)/shard_map/ppermute | solution.py:128
  167.2 47.3 %collective-permute-start.6 = (bf16[160,2048]{1,0:T(8,128)(2,1)}, bf16[160,2048]{1,0:T(8,128)(2,1)S(1)}, u32[]{:S(2)}, u32[]{:S(2)}) collective-permute-start(bf16[160,2048]{1,0:T(8,128)(2,1)} %get-tuple-element.331), channel_id=1, source_target_pairs={{0,1},{1,2},{2,3},{3,0},{4,5},{5,6},{6,7},{7,4},{8,9},{9,10},{10,1... | collective-permute-start | bytes 1966088 | tf_op jit(solution)/shard_map/ppermute | solution.py:128
  168.7 49.6 %collective-permute-start.8 = (bf16[160,2048]{1,0:T(8,128)(2,1)}, bf16[160,2048]{1,0:T(8,128)(2,1)}, u32[]{:S(2)}, u32[]{:S(2)}) collective-permute-start(bf16[160,2048]{1,0:T(8,128)(2,1)} %get-tuple-element.332), channel_id=1, source_target_pairs={{0,3},{1,0},{2,1},{3,2},{4,7},{5,4},{6,5},{7,6},{8,11},{9,8},{10,9... | collective-permute-start | bytes 1966088 | tf_op jit(solution)/shard_map/ppermute | solution.py:128
  174.5 97.1 %collective-permute-start.7 = (bf16[160,2048]{1,0:T(8,128)(2,1)}, bf16[160,2048]{1,0:T(8,128)(2,1)}, u32[]{:S(2)}, u32[]{:S(2)}) collective-permute-start(bf16[160,2048]{1,0:T(8,128)(2,1)} %get-tuple-element.333), channel_id=1, source_target_pairs={{0,2},{1,3},{2,0},{3,1},{4,6},{5,7},{6,4},{7,5},{8,10},{9,11},{10,... | collective-permute-start | bytes 1966088 | tf_op jit(solution)/shard_map/ppermute | solution.py:128
  214.4 93.7 %collective-permute-start.4 = (bf16[96,2048]{1,0:T(8,128)(2,1)S(1)}, bf16[96,2048]{1,0:T(8,128)(2,1)S(1)}, u32[]{:S(2)}, u32[]{:S(2)}) collective-permute-start(bf16[96,2048]{1,0:T(8,128)(2,1)S(1)} %get-tuple-element.307), channel_id=1, source_target_pairs={{0,2},{1,3},{2,0},{3,1},{4,6},{5,7},{6,4},{7,5},{8,10},{9,11},{10,... | collective-permute-start | bytes 1179656 | tf_op jit(solution)/shard_map/ppermute | solution.py:134
  214.5 62.1 %collective-permute-start.3 = (bf16[96,2048]{1,0:T(8,128)(2,1)S(1)}, bf16[96,2048]{1,0:T(8,128)(2,1)S(1)}, u32[]{:S(2)}, u32[]{:S(2)}) collective-permute-start(bf16[96,2048]{1,0:T(8,128)(2,1)S(1)} %get-tuple-element.307), channel_id=1, source_target_pairs={{0,1},{1,2},{2,3},{3,0},{4,5},{5,6},{6,7},{7,4},{8,9},{9,10},{10,1... | collective-permute-start | bytes 1179656 | tf_op jit(solution)/shard_map/ppermute | solution.py:134
  214.5 93.6 %collective-permute-start.5 = (bf16[96,2048]{1,0:T(8,128)(2,1)S(1)}, bf16[96,2048]{1,0:T(8,128)(2,1)S(1)}, u32[]{:S(2)}, u32[]{:S(2)}) collective-permute-start(bf16[96,2048]{1,0:T(8,128)(2,1)S(1)} %get-tuple-element.307), channel_id=1, source_target_pairs={{0,3},{1,0},{2,1},{3,2},{4,7},{5,4},{6,5},{7,6},{8,11},{9,8},{10,9... | collective-permute-start | bytes 1179656 | tf_op jit(solution)/shard_map/ppermute | solution.py:134
  273.9 56.7 %collective-permute-start.10 = (bf16[160,2048]{1,0:T(8,128)(2,1)S(1)}, bf16[160,2048]{1,0:T(8,128)(2,1)S(1)}, u32[]{:S(2)}, u32[]{:S(2)}) collective-permute-start(bf16[160,2048]{1,0:T(8,128)(2,1)S(1)} %get-tuple-element.311), channel_id=1, source_target_pairs={{0,2},{1,3},{2,0},{3,1},{4,6},{5,7},{6,4},{7,5},{8,10},{9,11},{10,... | collective-permute-start | bytes 1966088 | tf_op jit(solution)/shard_map/ppermute | solution.py:134
  276.5 59.5 %collective-permute-start.11 = (bf16[160,2048]{1,0:T(8,128)(2,1)S(1)}, bf16[160,2048]{1,0:T(8,128)(2,1)S(1)}, u32[]{:S(2)}, u32[]{:S(2)}) collective-permute-start(bf16[160,2048]{1,0:T(8,128)(2,1)S(1)} %get-tuple-element.311), channel_id=1, source_target_pairs={{0,3},{1,0},{2,1},{3,2},{4,7},{5,4},{6,5},{7,6},{8,11},{9,8},{10,9... | collective-permute-start | bytes 1966088 | tf_op jit(solution)/shard_map/ppermute | solution.py:134
  382.9 241.5 %all-reduce.6.cloned.1.call-start = ((), (), s32[]{:S(2)}) async-start(), calls=%async_computation.12 | async-start | bytes 5242880 | tf_op jit(solution)/shard_map/psum | solution.py:193
  514.5 579.3 %reduce-scatter.8.cloned.1.call-start = ((), (), s32[]{:S(2)}) async-start(), calls=%async_computation.15 | async-start | bytes 2359296 | tf_op jit(solution)/shard_map/reduce_scatter | solution.py:152
  640.7 490.5 %all-reduce.8.cloned.1.call-start = ((), (), s32[]{:S(2)}) async-start(), calls=%async_computation.13 | async-start | bytes 8388608 | tf_op jit(solution)/shard_map/psum | solution.py:303
  804.2 332.9 %reduce-scatter.6.cloned.1.call-start = ((), (), s32[]{:S(2)}) async-start(), calls=%async_computation.14 | async-start | bytes 7077888 | tf_op jit(solution)/shard_map/reduce_scatter | solution.py:152
  850.0 354.1 %reduce-scatter.14.cloned.1.call-start = ((), (), s32[]{:S(2)}) async-start(), calls=%async_computation.18 | async-start | bytes 9437184 | tf_op jit(solution)/shard_map/reduce_scatter | solution.py:152
  850.7 428.2 %reduce-scatter.12.cloned.1.call-start = ((), (), s32[]{:S(2)}) async-start(), calls=%async_computation.17 | async-start | bytes 9437184 | tf_op jit(solution)/shard_map/reduce_scatter | solution.py:152
  851.3 502.4 %reduce-scatter.10.cloned.1.call-start = ((), (), s32[]{:S(2)}) async-start(), calls=%async_computation.16 | async-start | bytes 9437184 | tf_op jit(solution)/shard_map/reduce_scatter | solution.py:152
  862.1 80.0 %collective-permute-start.15 = (bf16[96,2048]{1,0:T(8,128)(2,1)S(1)}, bf16[96,2048]{1,0:T(8,128)(2,1)S(1)}, u32[]{:S(2)}, u32[]{:S(2)}) collective-permute-start(bf16[96,2048]{1,0:T(8,128)(2,1)S(1)} %get-tuple-element.348), channel_id=1, source_target_pairs={{0,2},{1,3},{2,0},{3,1},{4,6},{5,7},{6,4},{7,5},{8,10},{9,11},{10,... | collective-permute-start | bytes 1179656 | tf_op jit(solution)/shard_map/ppermute | solution.py:128
  867.2 75.5 %collective-permute-start.20 = (bf16[160,2048]{1,0:T(8,128)(2,1)S(1)}, bf16[160,2048]{1,0:T(8,128)(2,1)S(1)}, u32[]{:S(2)}, u32[]{:S(2)}) collective-permute-start(bf16[160,2048]{1,0:T(8,128)(2,1)S(1)} %get-tuple-element.328), channel_id=1, source_target_pairs={{0,1},{1,2},{2,3},{3,0},{4,5},{5,6},{6,7},{7,4},{8,9},{9,10},{10,1... | collective-permute-start | bytes 1966088 | tf_op jit(solution)/shard_map/ppermute | solution.py:128
  867.8 79.1 %collective-permute-start.22 = (bf16[160,2048]{1,0:T(8,128)(2,1)S(1)}, bf16[160,2048]{1,0:T(8,128)(2,1)S(1)}, u32[]{:S(2)}, u32[]{:S(2)}) collective-permute-start(bf16[160,2048]{1,0:T(8,128)(2,1)S(1)} %get-tuple-element.329), channel_id=1, source_target_pairs={{0,3},{1,0},{2,1},{3,2},{4,7},{5,4},{6,5},{7,6},{8,11},{9,8},{10,9... | collective-permute-start | bytes 1966088 | tf_op jit(solution)/shard_map/ppermute | solution.py:128
  880.5 187.4 %collective-permute-start.21 = (bf16[160,2048]{1,0:T(8,128)(2,1)S(1)}, bf16[160,2048]{1,0:T(8,128)(2,1)S(1)}, u32[]{:S(2)}, u32[]{:S(2)}) collective-permute-start(bf16[160,2048]{1,0:T(8,128)(2,1)S(1)} %get-tuple-element.330), channel_id=1, source_target_pairs={{0,2},{1,3},{2,0},{3,1},{4,6},{5,7},{6,4},{7,5},{8,10},{9,11},{10,... | collective-permute-start | bytes 1966088 | tf_op jit(solution)/shard_map/ppermute | solution.py:128
  942.6 147.8 %collective-permute-start.18 = (bf16[96,2048]{1,0:T(8,128)(2,1)S(1)}, bf16[96,2048]{1,0:T(8,128)(2,1)S(1)}, u32[]{:S(2)}, u32[]{:S(2)}) collective-permute-start(bf16[96,2048]{1,0:T(8,128)(2,1)S(1)} %get-tuple-element.301), channel_id=1, source_target_pairs={{0,2},{1,3},{2,0},{3,1},{4,6},{5,7},{6,4},{7,5},{8,10},{9,11},{10,... | collective-permute-start | bytes 1179656 | tf_op jit(solution)/shard_map/ppermute | solution.py:134
  942.7 126.9 %collective-permute-start.17 = (bf16[96,2048]{1,0:T(8,128)(2,1)S(1)}, bf16[96,2048]{1,0:T(8,128)(2,1)S(1)}, u32[]{:S(2)}, u32[]{:S(2)}) collective-permute-start(bf16[96,2048]{1,0:T(8,128)(2,1)S(1)} %get-tuple-element.301), channel_id=1, source_target_pairs={{0,1},{1,2},{2,3},{3,0},{4,5},{5,6},{6,7},{7,4},{8,9},{9,10},{10,1... | collective-permute-start | bytes 1179656 | tf_op jit(solution)/shard_map/ppermute | solution.py:134
  942.7 147.7 %collective-permute-start.19 = (bf16[96,2048]{1,0:T(8,128)(2,1)S(1)}, bf16[96,2048]{1,0:T(8,128)(2,1)S(1)}, u32[]{:S(2)}, u32[]{:S(2)}) collective-permute-start(bf16[96,2048]{1,0:T(8,128)(2,1)S(1)} %get-tuple-element.301), channel_id=1, source_target_pairs={{0,3},{1,0},{2,1},{3,2},{4,7},{5,4},{6,5},{7,6},{8,11},{9,8},{10,9... | collective-permute-start | bytes 1179656 | tf_op jit(solution)/shard_map/ppermute | solution.py:134
  1069.5 43.4 %collective-permute-start.24 = (bf16[160,2048]{1,0:T(8,128)(2,1)}, bf16[160,2048]{1,0:T(8,128)(2,1)S(1)}, u32[]{:S(2)}, u32[]{:S(2)}) collective-permute-start(bf16[160,2048]{1,0:T(8,128)(2,1)} %get-tuple-element.303), channel_id=1, source_target_pairs={{0,2},{1,3},{2,0},{3,1},{4,6},{5,7},{6,4},{7,5},{8,10},{9,11},{10,... | collective-permute-start | bytes 1966088 | tf_op jit(solution)/shard_map/ppermute | solution.py:134
  1069.5 48.9 %collective-permute-start.25 = (bf16[160,2048]{1,0:T(8,128)(2,1)}, bf16[160,2048]{1,0:T(8,128)(2,1)}, u32[]{:S(2)}, u32[]{:S(2)}) collective-permute-start(bf16[160,2048]{1,0:T(8,128)(2,1)} %get-tuple-element.303), channel_id=1, source_target_pairs={{0,3},{1,0},{2,1},{3,2},{4,7},{5,4},{6,5},{7,6},{8,11},{9,8},{10,9... | collective-permute-start | bytes 1966088 | tf_op jit(solution)/shard_map/ppermute | solution.py:134
  (106 other events, 1562.2 us)
Sparse Core Ops, SparseCore 0:
  10.5 39.2 all-gather.10
  52.3 37.3 all-gather.8
  91.2 10.5 all-gather.20
  103.2 11.7 all-gather.12
  116.7 55.4 all-gather.16
  174.5 55.8 all-gather.18
  232.3 54.2 all-gather.14
  383.0 75.0 all-reduce.3
  514.6 109.7 all-reduce.5
  640.8 40.1 reduce-scatter.7
  804.3 261.8 all-reduce.7
  1069.5 59.7 reduce-scatter.5
  1132.7 71.2 reduce-scatter.13
  1207.3 71.4 reduce-scatter.11
  1282.2 71.4 reduce-scatter.9

commit v10 on v9

--- a/solution.py
+++ b/solution.py
@@ -183,7 +183,7 @@
         "rf,df->rd", grad_gate_act, gate_full, preferred_element_type=jnp.float32
     ) + jnp.einsum("rf,df->rd", grad_up_act, up_full, preferred_element_type=jnp.float32)
     branch_two = matmul_low(hidden, down_full)
-    grad_down = jnp.einsum("rf,rd->fd", hidden, grad_branch, preferred_element_type=jnp.float32)
+    grad_down = jnp.einsum("rd,rf->df", grad_branch, hidden, preferred_element_type=jnp.float32)
     grad_gate = jnp.einsum(
         "rd,rf->df", input_two, grad_gate_act, preferred_element_type=jnp.float32
     )
@@ -281,7 +281,6 @@
     mlp_grads = (
         scatter_low(grad_gate, 0),
         scatter_low(grad_up, 0),
-        scatter_low(grad_down, 1),
     )
     resid = jnp.concatenate([piece[0] for piece in pieces], axis=0)
     branch_two_part = jnp.concatenate([piece[1] for piece in pieces], axis=0)
@@ -352,9 +351,10 @@
     grad_wq = jnp.einsum("rd,rc->dc", input_one, grad_q_pre, preferred_element_type=jnp.float32)
     grad_wk = jnp.einsum("rd,rc->dc", input_one, grad_k_pre, preferred_element_type=jnp.float32)
     grad_wv = jnp.einsum("rd,rc->dc", input_one, grad_v_pre, preferred_element_type=jnp.float32)
-    qkv_grads = jnp.split(
-        scatter_low(jnp.concatenate([grad_wq, grad_wk, grad_wv], axis=1), 0), 3, axis=1
-    )
+    down_cols = grad_down.shape[1]
+    joined = scatter_low(jnp.concatenate([grad_down, grad_wq, grad_wk, grad_wv], axis=1), 0)
+    mlp_grads = mlp_grads + (joined[:, :down_cols].T,)
+    qkv_grads = jnp.split(joined[:, down_cols:], 3, axis=1)
     attn_grads = (qkv_grads[0], qkv_grads[1], qkv_grads[2], scatter_low(grad_wout, 1))
     grad_tokens = jnp.concatenate(token_parts, axis=0)
     output = final_sum.astype(bf_type).reshape(seq_count, half_len, model_width)

time: 1370 us -> 1110 us (0.81)
  waiting for transfers between devices: 662 us -> 395 us
    reduce_scatter x5 -> x4, waiting for transfers between devices: 207 us -> 19.8 us  [scatter_low(): lax.psum_scatter(grad.astype(jnp.bfloat16), (SHARD, CTX), scatter_dimensi...]
    ppermute x12, waiting for transfers between devices: 243 us -> 144 us  [tp_psum(): total = total + lax.ppermute(piece, TP, pairs).astype(jnp.float32)]
    ppermute x12, waiting for transfers between devices: 94.1 us -> 108 us  [tp_psum(): got = lax.ppermute(reduced, TP, pairs)]
    unnamed x164 -> x166, local copies, waits for them, and re-layouts: 32.3 us -> 31.3 us
  transfers between devices with their start and end apart: 41 -> 40, of which waited for: 19 -> 15; matrix products, arithmetic and copies ran while one was open for 40% -> 50% of each run, Pallas kernels for 0% -> 0%
where the time goes in v10:
time: 1110 us; the launch traced here: 1100 us
  waiting for transfers between devices  395 us (36%)
  matrix products  336 us (30%)
  other arithmetic  176 us (16%)
  local copies, waits for them, and re-layouts  106 us (10%)
  starting transfers between devices  66.9 us (6%)
  between operations  16.5 us (1%)
    ppermute x12, waiting for transfers between devices, tp_psum(): total = total + lax.ppermute(piece, TP, pairs).astype(jnp.float32)  144 us
    ppermute x12, waiting for transfers between devices, tp_psum(): got = lax.ppermute(reduced, TP, pairs)  108 us
    psum x2, waiting for transfers between devices, middle_rows(): grad_input_two = lax.psum(grad_input_two.astype(bf_type), TP)  91.2 us
    dot_general x11, matrix products, matmul_low(): return jnp.dot(left, right, preferred_element_type=jnp.float32)  78.8 us
    ppermute x12, starting transfers between devices, tp_psum(): total = total + lax.ppermute(piece, TP, pairs).astype(jnp.float32)  49.6 us
    all_gather x1, waiting for transfers between devices, block(): lax.all_gather(jnp.concatenate([attn_low[1], attn_low[2]], axis=1), (SHAR...  31.4 us
    unnamed x166, local copies, waits for them, and re-layouts  31.3 us
    dot_general x4, matrix products, score_block(): jnp.einsum('qhd,khd->hqk', query_rows, keys_seq, preferred_element_type=j...  25.9 us
  transfers between devices with their start and end apart: 40, of which 15 were waited for; matrix products, arithmetic and copies ran while one was open for 50% of the time, Pallas kernels for 0%

profile of v10, /device:TPU:0, one launch (start us, length us, event | category | flops | bytes accessed | tf_op | source)
XLA Modules:
  0.0 1100.5 jit_solution(4864326119857446754)
XLA Ops:
  18.5 31.4 %all-gather.11.cloned.1.call-done = bf16[2048,1024]{1,0:T(8,128)(2,1)} async-done(((bf16[256,1024]{1,0:T(8,128)(2,1)}), bf16[2048,1024]{1,0:T(8,128)(2,1)}) %all-gather.11.cloned.1.call-update) | async-done | bytes 4194320 | tf_op jit(solution)/shard_map/all_gather | solution.py:220
  116.5 37.7 %while.27 = (s32[]{:T(128)}, bf16[2,512,4,128]{3,2,1,0:T(4,128)(2,1)}, f32[2,4,512]{2,1,0:T(4,128)S(1)}, s32[2]{0:T(128)S(1)}, s32[]{:T(128)}, /*index=5*/s32[]{...) while((s32[]{:T(128)}, ...), condition=%wide.region_5.6_spmd, body=%wide.region_2.5_spmd.sunk | while | flops 2195980800 | bytes 77668600 | solution.py:77
  174.8 17.4 %collective-permute-start.7 = (bf16[160,2048]{1,0:T(8,128)(2,1)}, bf16[160,2048]{1,0:T(8,128)(2,1)}, u32[]{:S(2)}, u32[]{:S(2)}) collective-permute-start(bf16[160,2048]{1,0:T(8,128)(2,1)} %get-tuple-element.333), channel_id=1, source_target_pairs={{0,2},{1,3},{2,0},{3,1},{4,6},{5,7},{6,4},{7,5},{8,10},{9,11},{10,... | collective-permute-start | bytes 1966088 | tf_op jit(solution)/shard_map/ppermute | solution.py:128
  218.6 53.3 %collective-permute-done.7 = bf16[160,2048]{1,0:T(8,128)(2,1)} collective-permute-done((bf16[160,2048]{1,0:T(8,128)(2,1)}, bf16[160,2048]{1,0:T(8,128)(2,1)}, u32[]{:S(2)}, u32[]{:S(2)}) %collective-permute-start.7) | collective-permute-done | bytes 655392 | tf_op jit(solution)/shard_map/ppermute | solution.py:128
  278.3 30.0 %collective-permute-done.4 = bf16[96,2048]{1,0:T(8,128)(2,1)S(1)} collective-permute-done((bf16[96,2048]{1,0:T(8,128)(2,1)S(1)}, bf16[96,2048]{1,0:T(8,128)(2,1)S(1)}, u32[]{:S(2)}, u32[]{:S(2)}) %collective-permute-start.4) | collective-permute-done | bytes 393248 | tf_op jit(solution)/shard_map/ppermute | solution.py:134
  310.5 20.3 %collective-permute-done.10 = bf16[160,2048]{1,0:T(8,128)(2,1)S(1)} collective-permute-done((bf16[160,2048]{1,0:T(8,128)(2,1)S(1)}, bf16[160,2048]{1,0:T(8,128)(2,1)S(1)}, u32[]{:S(2)}, u32[]{:S(2)}) %collective-permute-start.10) | collective-permute-done | bytes 655392 | tf_op jit(solution)/shard_map/ppermute | solution.py:134
  360.1 10.3 multiply_convert_fusion.5
  373.9 10.2 add_convert_fusion.3
  384.1 11.8 %fusion.123 = f32[640,2048]{1,0:T(8,128)} fusion(bf16[2048,2048]{1,0:T(8,128)(2,1)} %all-gather.19.cloned.1.call-done, f32[1024,2048]{1,0:T(8,128)} %convert_multiply_fusion), kind=kOutput, calls=%fused_computation.201 | convolution fusion | flops 5368709120 | bytes 16252928 | tf_op jit(solution)/shard_map/rd,fd->rf/dot_general | solution.py:175
  404.0 13.9 %multiply_convert_fusion.2 = (bf16[640,2048]{1,0:T(8,128)(2,1)S(1)}, bf16[640,2048]{1,0:T(8,128)(2,1)}, bf16[640,2048]{1,0:T(8,128)(2,1)}) fusion(f32[640,2048]{1,0:T(8,128)} %fusion.123, f32[640,2048]{1,0:T(8,128)S(1)} %fusion.164, bf16[640,2048]{1,0:T(8,128)(2,1)S(1)} %copy-done.45, bf16[2048,2048]{1,0:T(8,128)(2,1)} %all-gather.15.cloned.1.call-done), kind=kOutput, calls=%fused_computation.84 | convolution fusion | flops 5389680640 | bytes 29360128 | tf_op jit(solution)/shard_map/dot_general | solution.py:159
  417.9 10.4 fusion.168
  428.3 10.8 convolution_add_fusion.1
  439.0 12.4 %fusion.167 = f32[2048,2048]{1,0:T(8,128)} fusion(bf16[640,2048]{1,0:T(8,128)(2,1)} %fusion.54, bf16[640,2048]{1,0:T(8,128)(2,1)} %get-tuple-element.317), kind=kOutput, calls=%fused_computation.303 | convolution fusion | flops 5368709120 | bytes 22020096 | tf_op jit(solution)/shard_map/rd,rf->df/dot_general | solution.py:187
  451.5 10.2 convolution_add_fusion.2
  461.7 13.3 %fusion.122 = f32[2048,2048]{1,0:T(8,128)} fusion(bf16[640,2048]{1,0:T(8,128)(2,1)} %get-tuple-element.318, f32[1024,2048]{1,0:T(8,128)} %convert_multiply_fusion), kind=kOutput, calls=%fused_computation.200 | convolution fusion | flops 5368709120 | bytes 22020096 | tf_op jit(solution)/shard_map/rd,rf->df/dot_general | solution.py:186
  475.0 11.5 %convolution_add_fusion = bf16[2048,2048]{1,0:T(8,128)(2,1)} fusion(f32[2048,2048]{1,0:T(8,128)} %fusion.122, bf16[384,2048]{1,0:T(8,128)(2,1)S(1)} %copy-done.54, f32[1024,2048]{1,0:T(8,128)} %convert_multiply_fusion), kind=kOutput, calls=%fused_computation.62 | convolution fusion | flops 3229614080 | bytes 28311552 | tf_op jit(solution)/shard_map/rd,rf->df/dot_general | solution.py:186
  486.4 11.3 %fusion.169 = f32[640,2048]{1,0:T(8,128)} fusion(bf16[640,2048]{1,0:T(8,128)(2,1)} %get-tuple-element.317, bf16[2048,2048]{1,0:T(8,128)(2,1)} %all-gather.15.cloned.1.call-done), kind=kOutput, calls=%fused_computation.305 | convolution fusion | flops 5368709120 | bytes 16252928 | tf_op jit(solution)/shard_map/rf,df->rd/dot_general | solution.py:182
  525.4 91.2 %all-reduce.6.cloned.1.call-done = bf16[640,2048]{1,0:T(8,128)(2,1)} async-done(((bf16[640,2048]{1,0:T(8,128)(2,1)}), bf16[640,2048]{1,0:T(8,128)(2,1)}) %all-reduce.6.cloned.1.call-update) | async-done | bytes 2621456 | tf_op jit(solution)/shard_map/psum | solution.py:193
  656.3 110.8 %while.28 = (s32[]{:T(128)}, f32[2048,4,128]{0,2,1:T(8,128)}, f32[2048,4,128]{0,2,1:T(8,128)}, f32[2,512,4,128]{3,1,0,2:T(8,128)}, bf16[2,512,4,128]{3,1,2,0:T(8...) while((s32[]{:T(128)}, f32[2048,4,128]{0,2,1:T(8,128)}, ...), condition=%wide.region_19.20_spmd.clone, body=%wide.region_17.19_spmd.clone.sunk | while | flops 5439226368 | bytes 219218320 | solution.py:113
  667.4 11.2 %bitcast_add_fusion.7 = f32[2048,4,128]{0,2,1:T(8,128)} fusion(f32[2048,4,128]{0,2,1:T(8,128)} %get-tuple-element.557, f32[4,512,2048]{2,1,0:T(8,128)} %fusion.252, f32[4,512]{1,0:T(4,128)S(1)} %dynamic-slice_bitcast_fusion.14, pred[512,2048]{1,0:T(8,128)(4,1)S(1)} %fusion.253, pred[]{:T(512)S(6)} %compare.10, ...), kind=kOutput, calls=%fused_computation.27.clone.1 | convolution fusion | flops 1092616192 | bytes 26746884 | tf_op jit(solution)/shard_map/while/body/eval_jaxpr/hqk,qhd->khd/dot_general | solution.py:107
  678.6 13.2 %multiply_reduce_fusion.5 = (f32[4,512]{1,0:T(4,128)S(1)}, f32[4,512,2048]{2,1,0:T(8,128)}) fusion(f32[4,512,2048]{2,1,0:T(8,128)} %fusion.252, f32[4,512]{1,0:T(4,128)S(1)} %dynamic-slice_bitcast_fusion.14, pred[512,2048]{1,0:T(8,128)(4,1)S(1)} %fusion.253, bf16[2048,4,128]{2,0,1:T(8,128)(2,1)S(1)} %copy-done.11, ...), kind=kOutput, calls=%fused_computation.22.clone.1 | convolution fusion | flops 1094711296 | bytes 37240836 | tf_op jit(solution)/shard_map/while/body/eval_jaxpr/qhd,khd->hqk/dot_general | solution.py:94
  691.8 12.3 %multiply_convert_fusion.9 = bf16[4,512,2048]{2,1,0:T(8,128)(2,1)S(1)} fusion(f32[4,512,2048]{2,1,0:T(8,128)} %get-tuple-element.505, f32[4,512,2048]{2,1,0:T(8,128)} %fusion.252, f32[4,512]{1,0:T(4,128)S(1)} %get-tuple-element.506, f32[4,512]{1,0:T(4,128)S(1)} %dynamic-slice_bitcast_fusion.14, pred[512,2048]{1,0:T(8,128)(4,1)S(1)} %fusion.253), kind=kLoop, calls=%fused_computation.21.clone.1 | loop fusion | flops 25165824 | bytes 43008000 | tf_op jit(solution)/shard_map/while/body/eval_jaxpr/convert_element_type | solution.py:98
  722.1 12.4 %bitcast_add_fusion.7 = f32[2048,4,128]{0,2,1:T(8,128)} fusion(f32[2048,4,128]{0,2,1:T(8,128)} %get-tuple-element.557, f32[4,512,2048]{2,1,0:T(8,128)} %fusion.252, f32[4,512]{1,0:T(4,128)S(1)} %dynamic-slice_bitcast_fusion.14, pred[512,2048]{1,0:T(8,128)(4,1)S(1)} %fusion.253, pred[]{:T(512)S(6)} %compare.10, ...), kind=kOutput, calls=%fused_computation.27.clone.1 | convolution fusion | flops 1092616192 | bytes 26746884 | tf_op jit(solution)/shard_map/while/body/eval_jaxpr/hqk,qhd->khd/dot_general | solution.py:107
  734.5 12.5 %multiply_reduce_fusion.5 = (f32[4,512]{1,0:T(4,128)S(1)}, f32[4,512,2048]{2,1,0:T(8,128)}) fusion(f32[4,512,2048]{2,1,0:T(8,128)} %fusion.252, f32[4,512]{1,0:T(4,128)S(1)} %dynamic-slice_bitcast_fusion.14, pred[512,2048]{1,0:T(8,128)(4,1)S(1)} %fusion.253, bf16[2048,4,128]{2,0,1:T(8,128)(2,1)S(1)} %copy-done.11, ...), kind=kOutput, calls=%fused_computation.22.clone.1 | convolution fusion | flops 1094711296 | bytes 37240836 | tf_op jit(solution)/shard_map/while/body/eval_jaxpr/qhd,khd->hqk/dot_general | solution.py:94
  747.1 12.4 %multiply_convert_fusion.9 = bf16[4,512,2048]{2,1,0:T(8,128)(2,1)S(1)} fusion(f32[4,512,2048]{2,1,0:T(8,128)} %get-tuple-element.505, f32[4,512,2048]{2,1,0:T(8,128)} %fusion.252, f32[4,512]{1,0:T(4,128)S(1)} %get-tuple-element.506, f32[4,512]{1,0:T(4,128)S(1)} %dynamic-slice_bitcast_fusion.14, pred[512,2048]{1,0:T(8,128)(4,1)S(1)} %fusion.253), kind=kLoop, calls=%fused_computation.21.clone.1 | loop fusion | flops 25165824 | bytes 43008000 | tf_op jit(solution)/shard_map/while/body/eval_jaxpr/convert_element_type | solution.py:98
  846.7 13.5 %pad_maximum_fusion = bf16[2048,3584]{1,0:T(8,128)(2,1)} fusion(bf16[2048,512]{1,0:T(8,128)(2,1)} %convolution_convert_fusion.1, bf16[2048,512]{1,0:T(8,128)(2,1)} %convolution_convert_fusion.2, bf16[2048,512]{1,0:T(8,128)(2,1)} %convolution_convert_fusion.3, bf16[2048,2048]{1,0:T(8,128)(2,1)S(1)} %bitcast.269), kind=kLoop, calls=%fused_computation.53 | loop fusion | flops 58720256 | bytes 29360128 | tf_op jit(solution)/shard_map/concatenate | solution.py:355
  880.7 16.2 %collective-permute-start.21 = (bf16[160,2048]{1,0:T(8,128)(2,1)S(1)}, bf16[160,2048]{1,0:T(8,128)(2,1)S(1)}, u32[]{:S(2)}, u32[]{:S(2)}) collective-permute-start(bf16[160,2048]{1,0:T(8,128)(2,1)S(1)} %get-tuple-element.330), channel_id=1, source_target_pairs={{0,2},{1,3},{2,0},{3,1},{4,6},{5,7},{6,4},{7,5},{8,10},{9,11},{10,... | collective-permute-start | bytes 1966088 | tf_op jit(solution)/shard_map/ppermute | solution.py:128
  896.9 22.5 %collective-permute-done.15 = bf16[96,2048]{1,0:T(8,128)(2,1)S(1)} collective-permute-done((bf16[96,2048]{1,0:T(8,128)(2,1)S(1)}, bf16[96,2048]{1,0:T(8,128)(2,1)S(1)}, u32[]{:S(2)}, u32[]{:S(2)}) %collective-permute-start.15) | collective-permute-done | bytes 393248 | tf_op jit(solution)/shard_map/ppermute | solution.py:128
  923.9 54.6 %collective-permute-done.21 = bf16[160,2048]{1,0:T(8,128)(2,1)S(1)} collective-permute-done((bf16[160,2048]{1,0:T(8,128)(2,1)S(1)}, bf16[160,2048]{1,0:T(8,128)(2,1)S(1)}, u32[]{:S(2)}, u32[]{:S(2)}) %collective-permute-start.21) | collective-permute-done | bytes 655392 | tf_op jit(solution)/shard_map/ppermute | solution.py:128
  984.2 30.7 %collective-permute-done.18 = bf16[96,2048]{1,0:T(8,128)(2,1)S(1)} collective-permute-done((bf16[96,2048]{1,0:T(8,128)(2,1)S(1)}, bf16[96,2048]{1,0:T(8,128)(2,1)S(1)}, u32[]{:S(2)}, u32[]{:S(2)}) %collective-permute-start.18) | collective-permute-done | bytes 393248 | tf_op jit(solution)/shard_map/ppermute | solution.py:134
  1021.3 16.2 %collective-permute-done.24 = bf16[160,2048]{1,0:T(8,128)(2,1)S(1)} collective-permute-done((bf16[160,2048]{1,0:T(8,128)(2,1)}, bf16[160,2048]{1,0:T(8,128)(2,1)S(1)}, u32[]{:S(2)}, u32[]{:S(2)}) %collective-permute-start.24) | collective-permute-done | bytes 655392 | tf_op jit(solution)/shard_map/ppermute | solution.py:134
  1067.5 19.8 %reduce-scatter.5.cloned.1.call-done = bf16[256,3584]{1,0:T(8,128)(2,1)} async-done(((bf16[2048,3584]{1,0:T(8,128)(2,1)}), bf16[256,3584]{1,0:T(8,128)(2,1)}) %reduce-scatter.5.cloned.1.call-update) | async-done | bytes 1835024 | tf_op jit(solution)/shard_map/reduce_scatter | solution.py:152
  (474 shorter events, 462.7 us)
Async XLA Ops:
  7.2 42.6 %all-gather.11.cloned.1.call-start = ((), (), s32[]{:S(2)}) async-start(), calls=%async_computation.5 | async-start | bytes 4718592 | tf_op jit(solution)/shard_map/all_gather | solution.py:220
  10.4 81.8 %all-gather.9.cloned.1.call-start = ((), (), s32[]{:S(2)}) async-start(), calls=%async_computation.4 | async-start | bytes 4718592 | tf_op jit(solution)/shard_map/all_gather | solution.py:223
  11.5 105.0 %all-gather.21.cloned.1.call-start = ((), (), s32[]{:S(2)}) async-start(), calls=%async_computation.17 | async-start | bytes 3145728 | tf_op jit(solution)/shard_map/all_gather | solution.py:247
  60.2 56.2 %all-gather.13.cloned.1.call-start = ((), (), s32[]{:S(2)}) async-start(), calls=%async_computation.6 | async-start | bytes 3145728 | tf_op jit(solution)/shard_map/all_gather | solution.py:246
  74.3 267.7 %all-gather.17.cloned.1.call-start = ((), (), s32[]{:S(2)}) async-start(), calls=%async_computation.8 | async-start | bytes 9437184 | tf_op jit(solution)/shard_map/all_gather | solution.py:231
  77.4 273.2 %all-gather.19.cloned.1.call-start = ((), (), s32[]{:S(2)}) async-start(), calls=%async_computation.9 | async-start | bytes 9437184 | tf_op jit(solution)/shard_map/all_gather | solution.py:232
  78.5 281.5 %all-gather.15.cloned.1.call-start = ((), (), s32[]{:S(2)}) async-start(), calls=%async_computation.7 | async-start | bytes 9437184 | tf_op jit(solution)/shard_map/all_gather | solution.py:230
  81.4 425.1 %all-reduce.4.cloned.1.call-start = ((), (), s32[]{:S(2)}) async-start(), calls=%async_computation.10 | async-start | bytes 3145728 | tf_op jit(solution)/shard_map/psum | solution.py:193
  164.0 48.8 %collective-permute-start.1 = (bf16[96,2048]{1,0:T(8,128)(2,1)}, bf16[96,2048]{1,0:T(8,128)(2,1)}, u32[]{:S(2)}, u32[]{:S(2)}) collective-permute-start(bf16[96,2048]{1,0:T(8,128)(2,1)} %get-tuple-element.354), channel_id=1, source_target_pairs={{0,2},{1,3},{2,0},{3,1},{4,6},{5,7},{6,4},{7,5},{8,10},{9,11},{10,... | collective-permute-start | bytes 1179656 | tf_op jit(solution)/shard_map/ppermute | solution.py:128
  167.5 47.2 %collective-permute-start.6 = (bf16[160,2048]{1,0:T(8,128)(2,1)}, bf16[160,2048]{1,0:T(8,128)(2,1)S(1)}, u32[]{:S(2)}, u32[]{:S(2)}) collective-permute-start(bf16[160,2048]{1,0:T(8,128)(2,1)} %get-tuple-element.331), channel_id=1, source_target_pairs={{0,1},{1,2},{2,3},{3,0},{4,5},{5,6},{6,7},{7,4},{8,9},{9,10},{10,1... | collective-permute-start | bytes 1966088 | tf_op jit(solution)/shard_map/ppermute | solution.py:128
  169.0 49.6 %collective-permute-start.8 = (bf16[160,2048]{1,0:T(8,128)(2,1)}, bf16[160,2048]{1,0:T(8,128)(2,1)}, u32[]{:S(2)}, u32[]{:S(2)}) collective-permute-start(bf16[160,2048]{1,0:T(8,128)(2,1)} %get-tuple-element.332), channel_id=1, source_target_pairs={{0,3},{1,0},{2,1},{3,2},{4,7},{5,4},{6,5},{7,6},{8,11},{9,8},{10,9... | collective-permute-start | bytes 1966088 | tf_op jit(solution)/shard_map/ppermute | solution.py:128
  174.8 97.1 %collective-permute-start.7 = (bf16[160,2048]{1,0:T(8,128)(2,1)}, bf16[160,2048]{1,0:T(8,128)(2,1)}, u32[]{:S(2)}, u32[]{:S(2)}) collective-permute-start(bf16[160,2048]{1,0:T(8,128)(2,1)} %get-tuple-element.333), channel_id=1, source_target_pairs={{0,2},{1,3},{2,0},{3,1},{4,6},{5,7},{6,4},{7,5},{8,10},{9,11},{10,... | collective-permute-start | bytes 1966088 | tf_op jit(solution)/shard_map/ppermute | solution.py:128
  214.6 93.7 %collective-permute-start.4 = (bf16[96,2048]{1,0:T(8,128)(2,1)S(1)}, bf16[96,2048]{1,0:T(8,128)(2,1)S(1)}, u32[]{:S(2)}, u32[]{:S(2)}) collective-permute-start(bf16[96,2048]{1,0:T(8,128)(2,1)S(1)} %get-tuple-element.307), channel_id=1, source_target_pairs={{0,2},{1,3},{2,0},{3,1},{4,6},{5,7},{6,4},{7,5},{8,10},{9,11},{10,... | collective-permute-start | bytes 1179656 | tf_op jit(solution)/shard_map/ppermute | solution.py:134
  214.7 62.1 %collective-permute-start.3 = (bf16[96,2048]{1,0:T(8,128)(2,1)S(1)}, bf16[96,2048]{1,0:T(8,128)(2,1)S(1)}, u32[]{:S(2)}, u32[]{:S(2)}) collective-permute-start(bf16[96,2048]{1,0:T(8,128)(2,1)S(1)} %get-tuple-element.307), channel_id=1, source_target_pairs={{0,1},{1,2},{2,3},{3,0},{4,5},{5,6},{6,7},{7,4},{8,9},{9,10},{10,1... | collective-permute-start | bytes 1179656 | tf_op jit(solution)/shard_map/ppermute | solution.py:134
  214.8 93.6 %collective-permute-start.5 = (bf16[96,2048]{1,0:T(8,128)(2,1)S(1)}, bf16[96,2048]{1,0:T(8,128)(2,1)S(1)}, u32[]{:S(2)}, u32[]{:S(2)}) collective-permute-start(bf16[96,2048]{1,0:T(8,128)(2,1)S(1)} %get-tuple-element.307), channel_id=1, source_target_pairs={{0,3},{1,0},{2,1},{3,2},{4,7},{5,4},{6,5},{7,6},{8,11},{9,8},{10,9... | collective-permute-start | bytes 1179656 | tf_op jit(solution)/shard_map/ppermute | solution.py:134
  274.1 56.7 %collective-permute-start.10 = (bf16[160,2048]{1,0:T(8,128)(2,1)S(1)}, bf16[160,2048]{1,0:T(8,128)(2,1)S(1)}, u32[]{:S(2)}, u32[]{:S(2)}) collective-permute-start(bf16[160,2048]{1,0:T(8,128)(2,1)S(1)} %get-tuple-element.311), channel_id=1, source_target_pairs={{0,2},{1,3},{2,0},{3,1},{4,6},{5,7},{6,4},{7,5},{8,10},{9,11},{10,... | collective-permute-start | bytes 1966088 | tf_op jit(solution)/shard_map/ppermute | solution.py:134
  276.8 59.4 %collective-permute-start.11 = (bf16[160,2048]{1,0:T(8,128)(2,1)S(1)}, bf16[160,2048]{1,0:T(8,128)(2,1)S(1)}, u32[]{:S(2)}, u32[]{:S(2)}) collective-permute-start(bf16[160,2048]{1,0:T(8,128)(2,1)S(1)} %get-tuple-element.311), channel_id=1, source_target_pairs={{0,3},{1,0},{2,1},{3,2},{4,7},{5,4},{6,5},{7,6},{8,11},{9,8},{10,9... | collective-permute-start | bytes 1966088 | tf_op jit(solution)/shard_map/ppermute | solution.py:134
  384.1 232.5 %all-reduce.6.cloned.1.call-start = ((), (), s32[]{:S(2)}) async-start(), calls=%async_computation.11 | async-start | bytes 5242880 | tf_op jit(solution)/shard_map/psum | solution.py:193
  506.6 511.8 %reduce-scatter.7.cloned.1.call-start = ((), (), s32[]{:S(2)}) async-start(), calls=%async_computation.14 | async-start | bytes 2359296 | tf_op jit(solution)/shard_map/reduce_scatter | solution.py:152
  632.9 422.7 %all-reduce.8.cloned.1.call-start = ((), (), s32[]{:S(2)}) async-start(), calls=%async_computation.12 | async-start | bytes 8388608 | tf_op jit(solution)/shard_map/psum | solution.py:302
  653.8 407.8 %reduce-scatter.11.cloned.1.call-start = ((), (), s32[]{:S(2)}) async-start(), calls=%async_computation.16 | async-start | bytes 9437184 | tf_op jit(solution)/shard_map/reduce_scatter | solution.py:152
  654.4 410.1 %reduce-scatter.9.cloned.1.call-start = ((), (), s32[]{:S(2)}) async-start(), calls=%async_computation.15 | async-start | bytes 9437184 | tf_op jit(solution)/shard_map/reduce_scatter | solution.py:152
  655.1 432.2 %reduce-scatter.5.cloned.1.call-start = ((), (), s32[]{:S(2)}) async-start(), calls=%async_computation.13 | async-start | bytes 16515072 | tf_op jit(solution)/shard_map/reduce_scatter | solution.py:152
  870.7 48.7 %collective-permute-start.15 = (bf16[96,2048]{1,0:T(8,128)(2,1)S(1)}, bf16[96,2048]{1,0:T(8,128)(2,1)S(1)}, u32[]{:S(2)}, u32[]{:S(2)}) collective-permute-start(bf16[96,2048]{1,0:T(8,128)(2,1)S(1)} %get-tuple-element.351), channel_id=1, source_target_pairs={{0,2},{1,3},{2,0},{3,1},{4,6},{5,7},{6,4},{7,5},{8,10},{9,11},{10,... | collective-permute-start | bytes 1179656 | tf_op jit(solution)/shard_map/ppermute | solution.py:128
  875.8 44.2 %collective-permute-start.20 = (bf16[160,2048]{1,0:T(8,128)(2,1)S(1)}, bf16[160,2048]{1,0:T(8,128)(2,1)S(1)}, u32[]{:S(2)}, u32[]{:S(2)}) collective-permute-start(bf16[160,2048]{1,0:T(8,128)(2,1)S(1)} %get-tuple-element.328), channel_id=1, source_target_pairs={{0,1},{1,2},{2,3},{3,0},{4,5},{5,6},{6,7},{7,4},{8,9},{9,10},{10,1... | collective-permute-start | bytes 1966088 | tf_op jit(solution)/shard_map/ppermute | solution.py:128
  876.4 47.5 %collective-permute-start.22 = (bf16[160,2048]{1,0:T(8,128)(2,1)S(1)}, bf16[160,2048]{1,0:T(8,128)(2,1)S(1)}, u32[]{:S(2)}, u32[]{:S(2)}) collective-permute-start(bf16[160,2048]{1,0:T(8,128)(2,1)S(1)} %get-tuple-element.329), channel_id=1, source_target_pairs={{0,3},{1,0},{2,1},{3,2},{4,7},{5,4},{6,5},{7,6},{8,11},{9,8},{10,9... | collective-permute-start | bytes 1966088 | tf_op jit(solution)/shard_map/ppermute | solution.py:128
  880.7 97.8 %collective-permute-start.21 = (bf16[160,2048]{1,0:T(8,128)(2,1)S(1)}, bf16[160,2048]{1,0:T(8,128)(2,1)S(1)}, u32[]{:S(2)}, u32[]{:S(2)}) collective-permute-start(bf16[160,2048]{1,0:T(8,128)(2,1)S(1)} %get-tuple-element.330), channel_id=1, source_target_pairs={{0,2},{1,3},{2,0},{3,1},{4,6},{5,7},{6,4},{7,5},{8,10},{9,11},{10,... | collective-permute-start | bytes 1966088 | tf_op jit(solution)/shard_map/ppermute | solution.py:128
  919.9 95.1 %collective-permute-start.18 = (bf16[96,2048]{1,0:T(8,128)(2,1)S(1)}, bf16[96,2048]{1,0:T(8,128)(2,1)S(1)}, u32[]{:S(2)}, u32[]{:S(2)}) collective-permute-start(bf16[96,2048]{1,0:T(8,128)(2,1)S(1)} %get-tuple-element.301), channel_id=1, source_target_pairs={{0,2},{1,3},{2,0},{3,1},{4,6},{5,7},{6,4},{7,5},{8,10},{9,11},{10,... | collective-permute-start | bytes 1179656 | tf_op jit(solution)/shard_map/ppermute | solution.py:134
  920.0 61.6 %collective-permute-start.17 = (bf16[96,2048]{1,0:T(8,128)(2,1)S(1)}, bf16[96,2048]{1,0:T(8,128)(2,1)S(1)}, u32[]{:S(2)}, u32[]{:S(2)}) collective-permute-start(bf16[96,2048]{1,0:T(8,128)(2,1)S(1)} %get-tuple-element.301), channel_id=1, source_target_pairs={{0,1},{1,2},{2,3},{3,0},{4,5},{5,6},{6,7},{7,4},{8,9},{9,10},{10,1... | collective-permute-start | bytes 1179656 | tf_op jit(solution)/shard_map/ppermute | solution.py:134
  920.1 95.0 %collective-permute-start.19 = (bf16[96,2048]{1,0:T(8,128)(2,1)S(1)}, bf16[96,2048]{1,0:T(8,128)(2,1)S(1)}, u32[]{:S(2)}, u32[]{:S(2)}) collective-permute-start(bf16[96,2048]{1,0:T(8,128)(2,1)S(1)} %get-tuple-element.301), channel_id=1, source_target_pairs={{0,3},{1,0},{2,1},{3,2},{4,7},{5,4},{6,5},{7,6},{8,11},{9,8},{10,9... | collective-permute-start | bytes 1179656 | tf_op jit(solution)/shard_map/ppermute | solution.py:134
  980.1 57.4 %collective-permute-start.24 = (bf16[160,2048]{1,0:T(8,128)(2,1)}, bf16[160,2048]{1,0:T(8,128)(2,1)S(1)}, u32[]{:S(2)}, u32[]{:S(2)}) collective-permute-start(bf16[160,2048]{1,0:T(8,128)(2,1)} %get-tuple-element.303), channel_id=1, source_target_pairs={{0,2},{1,3},{2,0},{3,1},{4,6},{5,7},{6,4},{7,5},{8,10},{9,11},{10,... | collective-permute-start | bytes 1966088 | tf_op jit(solution)/shard_map/ppermute | solution.py:134
  981.5 61.2 %collective-permute-start.25 = (bf16[160,2048]{1,0:T(8,128)(2,1)}, bf16[160,2048]{1,0:T(8,128)(2,1)}, u32[]{:S(2)}, u32[]{:S(2)}) collective-permute-start(bf16[160,2048]{1,0:T(8,128)(2,1)} %get-tuple-element.303), channel_id=1, source_target_pairs={{0,3},{1,0},{2,1},{3,2},{4,7},{5,4},{6,5},{7,6},{8,11},{9,8},{10,9... | collective-permute-start | bytes 1966088 | tf_op jit(solution)/shard_map/ppermute | solution.py:134
  (107 other events, 1445.9 us)
Sparse Core Ops, SparseCore 0:
  10.5 39.2 all-gather.10
  52.3 37.3 all-gather.8
  91.2 10.5 all-gather.20
  103.2 11.7 all-gather.12
  116.7 55.4 all-gather.16
  174.5 55.8 all-gather.18
  232.3 54.2 all-gather.14
  384.2 75.1 all-reduce.3
  506.7 109.8 all-reduce.5
  633.0 40.1 reduce-scatter.6
  675.5 154.9 all-reduce.7
  833.8 70.4 reduce-scatter.10
  907.8 71.4 reduce-scatter.8
  982.7 104.6 reduce-scatter.4

commit v11 on v10

--- a/solution.py
+++ b/solution.py
@@ -278,10 +278,6 @@
         ((grad_gate, grad_up, grad_down), last_sum)
     )
     pieces[-1][5] = last_sum
-    mlp_grads = (
-        scatter_low(grad_gate, 0),
-        scatter_low(grad_up, 0),
-    )
     resid = jnp.concatenate([piece[0] for piece in pieces], axis=0)
     branch_two_part = jnp.concatenate([piece[1] for piece in pieces], axis=0)
     grad_resid_parts, grad_attn_parts, grad_wout = [], [], 0.0
@@ -289,7 +285,7 @@
         grad_resid_part = piece[4] + norm_back(piece[2], piece[3], piece[5].astype(jnp.float32))
         resid_low = grad_resid_part.astype(bf_type)
         grad_wout = grad_wout + jnp.einsum(
-            "rc,rd->cd", attn_out[bounds[index]:bounds[index + 1]], resid_low,
+            "rd,rc->dc", resid_low, attn_out[bounds[index]:bounds[index + 1]],
             preferred_element_type=jnp.float32,
         )
         grad_attn_parts.append(
@@ -297,6 +293,10 @@
         )
         grad_resid_parts.append(grad_resid_part)
     grad_resid = jnp.concatenate(grad_resid_parts, axis=0)
+    gate_cols = grad_gate.shape[1]
+    front = scatter_low(jnp.concatenate([grad_gate, grad_up, grad_wout], axis=1), 0)
+    mlp_grads = (front[:, :gate_cols], front[:, gate_cols:2 * gate_cols])
+    wout_grad = front[:, 2 * gate_cols:].T
     grad_attn = jnp.concatenate(grad_attn_parts, axis=0).astype(bf_type).reshape(split_heads)
     branch_two_part, grad_attn = lax.optimization_barrier((branch_two_part, grad_attn))
     final_sum = resid + lax.psum(branch_two_part.astype(bf_type), TP).astype(jnp.float32)
@@ -355,7 +355,7 @@
     joined = scatter_low(jnp.concatenate([grad_down, grad_wq, grad_wk, grad_wv], axis=1), 0)
     mlp_grads = mlp_grads + (joined[:, :down_cols].T,)
     qkv_grads = jnp.split(joined[:, down_cols:], 3, axis=1)
-    attn_grads = (qkv_grads[0], qkv_grads[1], qkv_grads[2], scatter_low(grad_wout, 1))
+    attn_grads = (qkv_grads[0], qkv_grads[1], qkv_grads[2], wout_grad)
     grad_tokens = jnp.concatenate(token_parts, axis=0)
     output = final_sum.astype(bf_type).reshape(seq_count, half_len, model_width)
     grad_tokens = grad_tokens.reshape(seq_count, half_len, model_width)

time: 1110 us -> 1320 us (1.19)
  waiting for transfers between devices: 395 us -> 496 us
  starting transfers between devices: 66.9 us -> 152 us
    reduce_scatter x4 -> x2, waiting for transfers between devices: 19.8 us -> 146 us  [scatter_low(): lax.psum_scatter(grad.astype(jnp.bfloat16), (SHARD, CTX), scatter_dimensi...]
    ppermute x12, starting transfers between devices: 16 us -> 130 us  [tp_psum(): got = lax.ppermute(reduced, TP, pairs)]
    ppermute x12, starting transfers between devices: 49.6 us -> 20.1 us  [tp_psum(): total = total + lax.ppermute(piece, TP, pairs).astype(jnp.float32)]
    ppermute x12, waiting for transfers between devices: 144 us -> 123 us  [tp_psum(): total = total + lax.ppermute(piece, TP, pairs).astype(jnp.float32)]
    concatenate x0 -> x1, other arithmetic: none -> 16.6 us  [block(): jnp.concatenate([grad_gate, grad_up, grad_wout], axis=1)]
    unnamed x166 -> x171, local copies, waits for them, and re-layouts: 31.3 us -> 30.4 us
  transfers between devices with their start and end apart: 40 -> 38, of which waited for: 15 -> 16; matrix products, arithmetic and copies ran while one was open for 50% -> 33% of each run, Pallas kernels for 0% -> 0%
where the time goes in v11:
time: 1320 us; the launch traced here: 1310 us
  waiting for transfers between devices  496 us (38%)
  matrix products  348 us (26%)
  other arithmetic  183 us (14%)
  starting transfers between devices  152 us (12%)
  local copies, waits for them, and re-layouts  109 us (8%)
  between operations  16.7 us (1%)
    reduce_scatter x2, waiting for transfers between devices, scatter_low(): lax.psum_scatter(grad.astype(jnp.bfloat16), (SHARD, CTX), scatter_dimensi...  146 us
    ppermute x12, starting transfers between devices, tp_psum(): got = lax.ppermute(reduced, TP, pairs)  130 us
    ppermute x12, waiting for transfers between devices, tp_psum(): total = total + lax.ppermute(piece, TP, pairs).astype(jnp.float32)  123 us
    ppermute x12, waiting for transfers between devices, tp_psum(): got = lax.ppermute(reduced, TP, pairs)  104 us
    psum x2, waiting for transfers between devices, middle_rows(): grad_input_two = lax.psum(grad_input_two.astype(bf_type), TP)  94.8 us
    dot_general x11, matrix products, matmul_low(): return jnp.dot(left, right, preferred_element_type=jnp.float32)  81.6 us
    unnamed x171, local copies, waits for them, and re-layouts  30.4 us
    convert_element_type x2, other arithmetic, one_block(): grad_scores = (probability * (grad_prob - inner_sum)).astype(jnp.bfloat16)  29.7 us
  transfers between devices with their start and end apart: 38, of which 16 were waited for; matrix products, arithmetic and copies ran while one was open for 33% of the time, Pallas kernels for 0%

profile of v11, /device:TPU:0, one launch (start us, length us, event | category | flops | bytes accessed | tf_op | source)
XLA Modules:
  0.0 1308.5 jit_solution(12256841351445740341)
XLA Ops:
  23.7 26.1 %all-gather.11.cloned.1.call-done = bf16[2048,1024]{1,0:T(8,128)(2,1)} async-done(((bf16[256,1024]{1,0:T(8,128)(2,1)}), bf16[2048,1024]{1,0:T(8,128)(2,1)}) %all-gather.11.cloned.1.call-update) | async-done | bytes 4194320 | tf_op jit(solution)/shard_map/all_gather | solution.py:220
  115.3 37.4 %while.27 = (s32[]{:T(128)}, bf16[2,512,4,128]{3,2,1,0:T(4,128)(2,1)}, f32[2,4,512]{2,1,0:T(4,128)S(1)}, s32[2]{0:T(128)S(1)}, s32[]{:T(128)}, /*index=5*/s32[]{...) while((s32[]{:T(128)}, ...), condition=%wide.region_5.6_spmd, body=%wide.region_2.5_spmd.sunk | while | flops 2195980800 | bytes 77669096 | solution.py:77
  191.0 36.4 %collective-permute-start.3 = (bf16[96,2048]{1,0:T(8,128)(2,1)S(1)}, bf16[96,2048]{1,0:T(8,128)(2,1)S(1)}, u32[]{:S(2)}, u32[]{:S(2)}) collective-permute-start(bf16[96,2048]{1,0:T(8,128)(2,1)S(1)} %get-tuple-element.307), channel_id=1, source_target_pairs={{0,1},{1,2},{2,3},{3,0},{4,5},{5,6},{6,7},{7,4},{8,9},{9,10},{10,1... | collective-permute-start | bytes 1179656 | tf_op jit(solution)/shard_map/ppermute | solution.py:134
  229.9 26.0 %collective-permute-done.7 = bf16[160,2048]{1,0:T(8,128)(2,1)} collective-permute-done((bf16[160,2048]{1,0:T(8,128)(2,1)}, bf16[160,2048]{1,0:T(8,128)(2,1)}, u32[]{:S(2)}, u32[]{:S(2)}) %collective-permute-start.7) | collective-permute-done | bytes 655392 | tf_op jit(solution)/shard_map/ppermute | solution.py:128
  258.1 14.7 %collective-permute-start.9 = (bf16[160,2048]{1,0:T(8,128)(2,1)S(1)}, bf16[160,2048]{1,0:T(8,128)(2,1)S(1)}, u32[]{:S(2)}, u32[]{:S(2)}) collective-permute-start(bf16[160,2048]{1,0:T(8,128)(2,1)S(1)} %get-tuple-element.311), channel_id=1, source_target_pairs={{0,1},{1,2},{2,3},{3,0},{4,5},{5,6},{6,7},{7,4},{8,9},{9,10},{10,1... | collective-permute-start | bytes 1966088 | tf_op jit(solution)/shard_map/ppermute | solution.py:134
  275.4 31.0 %collective-permute-done.4 = bf16[96,2048]{1,0:T(8,128)(2,1)S(1)} collective-permute-done((bf16[96,2048]{1,0:T(8,128)(2,1)S(1)}, bf16[96,2048]{1,0:T(8,128)(2,1)S(1)}, u32[]{:S(2)}, u32[]{:S(2)}) %collective-permute-start.4) | collective-permute-done | bytes 393248 | tf_op jit(solution)/shard_map/ppermute | solution.py:134
  308.7 20.2 %collective-permute-done.10 = bf16[160,2048]{1,0:T(8,128)(2,1)S(1)} collective-permute-done((bf16[160,2048]{1,0:T(8,128)(2,1)S(1)}, bf16[160,2048]{1,0:T(8,128)(2,1)S(1)}, u32[]{:S(2)}, u32[]{:S(2)}) %collective-permute-start.10) | collective-permute-done | bytes 655392 | tf_op jit(solution)/shard_map/ppermute | solution.py:134
  376.5 11.7 fusion.123
  397.8 14.2 %multiply_convert_fusion.2 = (bf16[640,2048]{1,0:T(8,128)(2,1)S(1)}, bf16[640,2048]{1,0:T(8,128)(2,1)}, bf16[640,2048]{1,0:T(8,128)(2,1)S(1)}) fusion(f32[640,2048]{1,0:T(8,128)} %fusion.123, f32[640,2048]{1,0:T(8,128)} %fusion.165, bf16[640,2048]{1,0:T(8,128)(2,1)S(1)} %copy-done.43, bf16[2048,2048]{1,0:T(8,128)(2,1)} %all-gather.15.cloned.1.call-done), kind=kOutput, calls=%fused_computation.85 | convolution fusion | flops 5389680640 | bytes 29360128 | tf_op jit(solution)/shard_map/dot_general | solution.py:159
  443.2 11.2 convolution_add_fusion
  480.5 10.8 convolution_add_fusion.3
  491.3 12.0 fusion.168
  503.9 14.8 %convolution_add_fusion.2 = bf16[2048,2048]{1,0:T(8,128)(2,1)} fusion(f32[2048,2048]{1,0:T(8,128)} %fusion.168, bf16[384,2048]{1,0:T(8,128)(2,1)} %copy-done.12, bf16[384,2048]{1,0:T(8,128)(2,1)} %copy-done.48), kind=kOutput, calls=%fused_computation.65 | convolution fusion | flops 3229614080 | bytes 28311552 | tf_op jit(solution)/shard_map/rd,rf->df/dot_general | solution.py:187
  525.8 94.8 %all-reduce.6.cloned.1.call-done = bf16[640,2048]{1,0:T(8,128)(2,1)} async-done(((bf16[640,2048]{1,0:T(8,128)(2,1)}), bf16[640,2048]{1,0:T(8,128)(2,1)}) %all-reduce.6.cloned.1.call-update) | async-done | bytes 2621456 | tf_op jit(solution)/shard_map/psum | solution.py:193
  636.7 126.1 %while.28 = (s32[]{:T(128)}, f32[2048,4,128]{0,2,1:T(8,128)}, f32[2048,4,128]{0,2,1:T(8,128)}, f32[2,512,4,128]{3,1,0,2:T(8,128)}, bf16[2,512,4,128]{3,1,2,0:T(8...) while((s32[]{:T(128)}, f32[2048,4,128]{0,2,1:T(8,128)}, ...), condition=%wide.region_19.20_spmd.clone, body=%wide.region_17.19_spmd.clone.sunk | while | flops 5439226368 | bytes 210831184 | solution.py:113
  648.7 12.9 multiply_reduce_fusion.5
  661.6 14.8 %multiply_convert_fusion.9 = bf16[4,512,2048]{2,1,0:T(8,128)(2,1)} fusion(f32[4,512,2048]{2,1,0:T(8,128)} %get-tuple-element.507, f32[4,512,2048]{2,1,0:T(8,128)} %fusion.253, f32[4,512]{1,0:T(4,128)S(1)} %get-tuple-element.508, f32[4,512]{1,0:T(4,128)S(1)} %dynamic-slice_bitcast_fusion.14, pred[512,2048]{1,0:T(8,128)(4,1)S(1)} %fusion.254), kind=kLoop, calls=%fused_computation.21.clone.1 | loop fusion | flops 25165824 | bytes 43008000 | tf_op jit(solution)/shard_map/while/body/eval_jaxpr/convert_element_type | solution.py:98
  687.6 10.9 bitcast_add_fusion.7
  710.3 12.9 multiply_reduce_fusion.5
  723.2 14.8 %multiply_convert_fusion.9 = bf16[4,512,2048]{2,1,0:T(8,128)(2,1)} fusion(f32[4,512,2048]{2,1,0:T(8,128)} %get-tuple-element.507, f32[4,512,2048]{2,1,0:T(8,128)} %fusion.253, f32[4,512]{1,0:T(4,128)S(1)} %get-tuple-element.508, f32[4,512]{1,0:T(4,128)S(1)} %dynamic-slice_bitcast_fusion.14, pred[512,2048]{1,0:T(8,128)(4,1)S(1)} %fusion.254), kind=kLoop, calls=%fused_computation.21.clone.1 | loop fusion | flops 25165824 | bytes 43008000 | tf_op jit(solution)/shard_map/while/body/eval_jaxpr/convert_element_type | solution.py:98
  750.3 12.1 bitcast_add_fusion.7
  846.6 12.7 pad_maximum_fusion.1
  869.4 16.6 %pad_maximum_fusion = bf16[2048,4608]{1,0:T(8,128)(2,1)} fusion(bf16[2048,512]{1,0:T(8,128)(2,1)} %add_convert_fusion.1, bf16[2048,2048]{1,0:T(8,128)(2,1)} %convolution_add_fusion.1, bf16[2048,2048]{1,0:T(8,128)(2,1)} %convolution_add_fusion.2), kind=kLoop, calls=%fused_computation.53 | loop fusion | flops 56623104 | bytes 37748736 | tf_op jit(solution)/shard_map/concatenate | solution.py:297
  903.9 11.0 collective-permute-done.14
  920.6 21.4 %collective-permute-done.15 = bf16[96,2048]{1,0:T(8,128)(2,1)S(1)} collective-permute-done((bf16[96,2048]{1,0:T(8,128)(2,1)S(1)}, bf16[96,2048]{1,0:T(8,128)(2,1)S(1)}, u32[]{:S(2)}, u32[]{:S(2)}) %collective-permute-start.15) | collective-permute-done | bytes 393248 | tf_op jit(solution)/shard_map/ppermute | solution.py:128
  944.8 52.5 %collective-permute-start.17 = (bf16[96,2048]{1,0:T(8,128)(2,1)S(1)}, bf16[96,2048]{1,0:T(8,128)(2,1)S(1)}, u32[]{:S(2)}, u32[]{:S(2)}) collective-permute-start(bf16[96,2048]{1,0:T(8,128)(2,1)S(1)} %get-tuple-element.301), channel_id=1, source_target_pairs={{0,1},{1,2},{2,3},{3,0},{4,5},{5,6},{6,7},{7,4},{8,9},{9,10},{10,1... | collective-permute-start | bytes 1179656 | tf_op jit(solution)/shard_map/ppermute | solution.py:134
  999.7 53.6 %collective-permute-done.21 = bf16[160,2048]{1,0:T(8,128)(2,1)S(1)} collective-permute-done((bf16[160,2048]{1,0:T(8,128)(2,1)S(1)}, bf16[160,2048]{1,0:T(8,128)(2,1)S(1)}, u32[]{:S(2)}, u32[]{:S(2)}) %collective-permute-start.21) | collective-permute-done | bytes 655392 | tf_op jit(solution)/shard_map/ppermute | solution.py:128
  1054.1 16.7 %collective-permute-start.23 = (bf16[160,2048]{1,0:T(8,128)(2,1)S(1)}, bf16[160,2048]{1,0:T(8,128)(2,1)S(1)}, u32[]{:S(2)}, u32[]{:S(2)}) collective-permute-start(bf16[160,2048]{1,0:T(8,128)(2,1)S(1)} %get-tuple-element.303), channel_id=1, source_target_pairs={{0,1},{1,2},{2,3},{3,0},{4,5},{5,6},{6,7},{7,4},{8,9},{9,10},{10,1... | collective-permute-start | bytes 1966088 | tf_op jit(solution)/shard_map/ppermute | solution.py:134
  1073.5 32.4 %collective-permute-done.18 = bf16[96,2048]{1,0:T(8,128)(2,1)S(1)} collective-permute-done((bf16[96,2048]{1,0:T(8,128)(2,1)S(1)}, bf16[96,2048]{1,0:T(8,128)(2,1)S(1)}, u32[]{:S(2)}, u32[]{:S(2)}) %collective-permute-start.18) | collective-permute-done | bytes 393248 | tf_op jit(solution)/shard_map/ppermute | solution.py:134
  1107.8 20.6 %collective-permute-done.24 = bf16[160,2048]{1,0:T(8,128)(2,1)S(1)} collective-permute-done((bf16[160,2048]{1,0:T(8,128)(2,1)S(1)}, bf16[160,2048]{1,0:T(8,128)(2,1)S(1)}, u32[]{:S(2)}, u32[]{:S(2)}) %collective-permute-start.24) | collective-permute-done | bytes 655392 | tf_op jit(solution)/shard_map/ppermute | solution.py:134
  1142.7 22.6 %reduce-scatter.3.cloned.1.call-done = bf16[256,3584]{1,0:T(8,128)(2,1)} async-done(((bf16[2048,3584]{1,0:T(8,128)(2,1)}), bf16[256,3584]{1,0:T(8,128)(2,1)}) %reduce-scatter.3.cloned.1.call-update) | async-done | bytes 1835024 | tf_op jit(solution)/shard_map/reduce_scatter | solution.py:152
  1171.5 123.7 %reduce-scatter.5.cloned.1.call-done = bf16[256,4608]{1,0:T(8,128)(2,1)} async-done(((bf16[2048,4608]{1,0:T(8,128)(2,1)}), bf16[256,4608]{1,0:T(8,128)(2,1)}) %reduce-scatter.5.cloned.1.call-update) | async-done | bytes 2359312 | tf_op jit(solution)/shard_map/reduce_scatter | solution.py:152
  (466 shorter events, 502.0 us)
Async XLA Ops:
  7.2 42.6 %all-gather.11.cloned.1.call-start = ((), (), s32[]{:S(2)}) async-start(), calls=%async_computation.3 | async-start | bytes 4718592 | tf_op jit(solution)/shard_map/all_gather | solution.py:220
  10.4 79.3 %all-gather.9.cloned.1.call-start = ((), (), s32[]{:S(2)}) async-start(), calls=%async_computation.2 | async-start | bytes 4718592 | tf_op jit(solution)/shard_map/all_gather | solution.py:223
  11.5 103.8 %all-gather.13.cloned.1.call-start = ((), (), s32[]{:S(2)}) async-start(), calls=%async_computation.4 | async-start | bytes 3145728 | tf_op jit(solution)/shard_map/all_gather | solution.py:246
  60.8 54.4 %all-gather.21.cloned.1.call-start = ((), (), s32[]{:S(2)}) async-start(), calls=%async_computation.13 | async-start | bytes 3145728 | tf_op jit(solution)/shard_map/all_gather | solution.py:247
  71.5 263.1 %all-gather.17.cloned.1.call-start = ((), (), s32[]{:S(2)}) async-start(), calls=%async_computation.6 | async-start | bytes 9437184 | tf_op jit(solution)/shard_map/all_gather | solution.py:231
  72.7 270.3 %all-gather.19.cloned.1.call-start = ((), (), s32[]{:S(2)}) async-start(), calls=%async_computation.7 | async-start | bytes 9437184 | tf_op jit(solution)/shard_map/all_gather | solution.py:232
  76.1 276.4 %all-gather.15.cloned.1.call-start = ((), (), s32[]{:S(2)}) async-start(), calls=%async_computation.5 | async-start | bytes 9437184 | tf_op jit(solution)/shard_map/all_gather | solution.py:230
  77.2 426.1 %all-reduce.4.cloned.1.call-start = ((), (), s32[]{:S(2)}) async-start(), calls=%async_computation.8 | async-start | bytes 3145728 | tf_op jit(solution)/shard_map/psum | solution.py:193
  166.5 60.9 %collective-permute-start.6 = (bf16[160,2048]{1,0:T(8,128)(2,1)}, bf16[160,2048]{1,0:T(8,128)(2,1)S(1)}, u32[]{:S(2)}, u32[]{:S(2)}) collective-permute-start(bf16[160,2048]{1,0:T(8,128)(2,1)} %get-tuple-element.331), channel_id=1, source_target_pairs={{0,1},{1,2},{2,3},{3,0},{4,5},{5,6},{6,7},{7,4},{8,9},{9,10},{10,1... | collective-permute-start | bytes 1966088 | tf_op jit(solution)/shard_map/ppermute | solution.py:128
  167.1 88.8 %collective-permute-start.7 = (bf16[160,2048]{1,0:T(8,128)(2,1)}, bf16[160,2048]{1,0:T(8,128)(2,1)}, u32[]{:S(2)}, u32[]{:S(2)}) collective-permute-start(bf16[160,2048]{1,0:T(8,128)(2,1)} %get-tuple-element.333), channel_id=1, source_target_pairs={{0,2},{1,3},{2,0},{3,1},{4,6},{5,7},{6,4},{7,5},{8,10},{9,11},{10,... | collective-permute-start | bytes 1966088 | tf_op jit(solution)/shard_map/ppermute | solution.py:128
  173.0 82.9 %collective-permute-start.8 = (bf16[160,2048]{1,0:T(8,128)(2,1)}, bf16[160,2048]{1,0:T(8,128)(2,1)}, u32[]{:S(2)}, u32[]{:S(2)}) collective-permute-start(bf16[160,2048]{1,0:T(8,128)(2,1)} %get-tuple-element.332), channel_id=1, source_target_pairs={{0,3},{1,0},{2,1},{3,2},{4,7},{5,4},{6,5},{7,6},{8,11},{9,8},{10,9... | collective-permute-start | bytes 1966088 | tf_op jit(solution)/shard_map/ppermute | solution.py:128
  191.0 83.8 %collective-permute-start.3 = (bf16[96,2048]{1,0:T(8,128)(2,1)S(1)}, bf16[96,2048]{1,0:T(8,128)(2,1)S(1)}, u32[]{:S(2)}, u32[]{:S(2)}) collective-permute-start(bf16[96,2048]{1,0:T(8,128)(2,1)S(1)} %get-tuple-element.307), channel_id=1, source_target_pairs={{0,1},{1,2},{2,3},{3,0},{4,5},{5,6},{6,7},{7,4},{8,9},{9,10},{10,1... | collective-permute-start | bytes 1179656 | tf_op jit(solution)/shard_map/ppermute | solution.py:134
  227.4 79.0 %collective-permute-start.4 = (bf16[96,2048]{1,0:T(8,128)(2,1)S(1)}, bf16[96,2048]{1,0:T(8,128)(2,1)S(1)}, u32[]{:S(2)}, u32[]{:S(2)}) collective-permute-start(bf16[96,2048]{1,0:T(8,128)(2,1)S(1)} %get-tuple-element.307), channel_id=1, source_target_pairs={{0,2},{1,3},{2,0},{3,1},{4,6},{5,7},{6,4},{7,5},{8,10},{9,11},{10,... | collective-permute-start | bytes 1179656 | tf_op jit(solution)/shard_map/ppermute | solution.py:134
  227.4 79.0 %collective-permute-start.5 = (bf16[96,2048]{1,0:T(8,128)(2,1)S(1)}, bf16[96,2048]{1,0:T(8,128)(2,1)S(1)}, u32[]{:S(2)}, u32[]{:S(2)}) collective-permute-start(bf16[96,2048]{1,0:T(8,128)(2,1)S(1)} %get-tuple-element.307), channel_id=1, source_target_pairs={{0,3},{1,0},{2,1},{3,2},{4,7},{5,4},{6,5},{7,6},{8,11},{9,8},{10,9... | collective-permute-start | bytes 1179656 | tf_op jit(solution)/shard_map/ppermute | solution.py:134
  258.1 50.5 %collective-permute-start.9 = (bf16[160,2048]{1,0:T(8,128)(2,1)S(1)}, bf16[160,2048]{1,0:T(8,128)(2,1)S(1)}, u32[]{:S(2)}, u32[]{:S(2)}) collective-permute-start(bf16[160,2048]{1,0:T(8,128)(2,1)S(1)} %get-tuple-element.311), channel_id=1, source_target_pairs={{0,1},{1,2},{2,3},{3,0},{4,5},{5,6},{6,7},{7,4},{8,9},{9,10},{10,1... | collective-permute-start | bytes 1966088 | tf_op jit(solution)/shard_map/ppermute | solution.py:134
  272.8 56.1 %collective-permute-start.10 = (bf16[160,2048]{1,0:T(8,128)(2,1)S(1)}, bf16[160,2048]{1,0:T(8,128)(2,1)S(1)}, u32[]{:S(2)}, u32[]{:S(2)}) collective-permute-start(bf16[160,2048]{1,0:T(8,128)(2,1)S(1)} %get-tuple-element.311), channel_id=1, source_target_pairs={{0,2},{1,3},{2,0},{3,1},{4,6},{5,7},{6,4},{7,5},{8,10},{9,11},{10,... | collective-permute-start | bytes 1966088 | tf_op jit(solution)/shard_map/ppermute | solution.py:134
  274.9 54.1 %collective-permute-start.11 = (bf16[160,2048]{1,0:T(8,128)(2,1)S(1)}, bf16[160,2048]{1,0:T(8,128)(2,1)S(1)}, u32[]{:S(2)}, u32[]{:S(2)}) collective-permute-start(bf16[160,2048]{1,0:T(8,128)(2,1)S(1)} %get-tuple-element.311), channel_id=1, source_target_pairs={{0,3},{1,0},{2,1},{3,2},{4,7},{5,4},{6,5},{7,6},{8,11},{9,8},{10,9... | collective-permute-start | bytes 1966088 | tf_op jit(solution)/shard_map/ppermute | solution.py:134
  376.4 244.3 %all-reduce.6.cloned.1.call-start = ((), (), s32[]{:S(2)}) async-start(), calls=%async_computation.9 | async-start | bytes 5242880 | tf_op jit(solution)/shard_map/psum | solution.py:193
  503.4 633.3 %all-reduce.8.cloned.1.call-start = ((), (), s32[]{:S(2)}) async-start(), calls=%async_computation.10 | async-start | bytes 8388608 | tf_op jit(solution)/shard_map/psum | solution.py:302
  809.2 356.0 %reduce-scatter.3.cloned.1.call-start = ((), (), s32[]{:S(2)}) async-start(), calls=%async_computation.11 | async-start | bytes 16515072 | tf_op jit(solution)/shard_map/reduce_scatter | solution.py:152
  859.3 435.9 %reduce-scatter.5.cloned.1.call-start = ((), (), s32[]{:S(2)}) async-start(), calls=%async_computation.12 | async-start | bytes 21233664 | tf_op jit(solution)/shard_map/reduce_scatter | solution.py:152
  892.7 49.3 %collective-permute-start.15 = (bf16[96,2048]{1,0:T(8,128)(2,1)S(1)}, bf16[96,2048]{1,0:T(8,128)(2,1)S(1)}, u32[]{:S(2)}, u32[]{:S(2)}) collective-permute-start(bf16[96,2048]{1,0:T(8,128)(2,1)S(1)} %get-tuple-element.353), channel_id=1, source_target_pairs={{0,2},{1,3},{2,0},{3,1},{4,6},{5,7},{6,4},{7,5},{8,10},{9,11},{10,... | collective-permute-start | bytes 1179656 | tf_op jit(solution)/shard_map/ppermute | solution.py:128
  893.9 50.4 %collective-permute-start.16 = (bf16[96,2048]{1,0:T(8,128)(2,1)S(1)}, bf16[96,2048]{1,0:T(8,128)(2,1)S(1)}, u32[]{:S(2)}, u32[]{:S(2)}) collective-permute-start(bf16[96,2048]{1,0:T(8,128)(2,1)S(1)} %get-tuple-element.352), channel_id=1, source_target_pairs={{0,3},{1,0},{2,1},{3,2},{4,7},{5,4},{6,5},{7,6},{8,11},{9,8},{10,9... | collective-permute-start | bytes 1179656 | tf_op jit(solution)/shard_map/ppermute | solution.py:128
  901.8 95.5 %collective-permute-start.20 = (bf16[160,2048]{1,0:T(8,128)(2,1)S(1)}, bf16[160,2048]{1,0:T(8,128)(2,1)S(1)}, u32[]{:S(2)}, u32[]{:S(2)}) collective-permute-start(bf16[160,2048]{1,0:T(8,128)(2,1)S(1)} %get-tuple-element.328), channel_id=1, source_target_pairs={{0,1},{1,2},{2,3},{3,0},{4,5},{5,6},{6,7},{7,4},{8,9},{9,10},{10,1... | collective-permute-start | bytes 1966088 | tf_op jit(solution)/shard_map/ppermute | solution.py:128
  902.4 150.9 %collective-permute-start.21 = (bf16[160,2048]{1,0:T(8,128)(2,1)S(1)}, bf16[160,2048]{1,0:T(8,128)(2,1)S(1)}, u32[]{:S(2)}, u32[]{:S(2)}) collective-permute-start(bf16[160,2048]{1,0:T(8,128)(2,1)S(1)} %get-tuple-element.330), channel_id=1, source_target_pairs={{0,2},{1,3},{2,0},{3,1},{4,6},{5,7},{6,4},{7,5},{8,10},{9,11},{10,... | collective-permute-start | bytes 1966088 | tf_op jit(solution)/shard_map/ppermute | solution.py:128
  914.9 138.4 %collective-permute-start.22 = (bf16[160,2048]{1,0:T(8,128)(2,1)S(1)}, bf16[160,2048]{1,0:T(8,128)(2,1)S(1)}, u32[]{:S(2)}, u32[]{:S(2)}) collective-permute-start(bf16[160,2048]{1,0:T(8,128)(2,1)S(1)} %get-tuple-element.329), channel_id=1, source_target_pairs={{0,3},{1,0},{2,1},{3,2},{4,7},{5,4},{6,5},{7,6},{8,11},{9,8},{10,9... | collective-permute-start | bytes 1966088 | tf_op jit(solution)/shard_map/ppermute | solution.py:128
  944.8 127.1 %collective-permute-start.17 = (bf16[96,2048]{1,0:T(8,128)(2,1)S(1)}, bf16[96,2048]{1,0:T(8,128)(2,1)S(1)}, u32[]{:S(2)}, u32[]{:S(2)}) collective-permute-start(bf16[96,2048]{1,0:T(8,128)(2,1)S(1)} %get-tuple-element.301), channel_id=1, source_target_pairs={{0,1},{1,2},{2,3},{3,0},{4,5},{5,6},{6,7},{7,4},{8,9},{9,10},{10,1... | collective-permute-start | bytes 1179656 | tf_op jit(solution)/shard_map/ppermute | solution.py:134
  997.2 108.7 %collective-permute-start.18 = (bf16[96,2048]{1,0:T(8,128)(2,1)S(1)}, bf16[96,2048]{1,0:T(8,128)(2,1)S(1)}, u32[]{:S(2)}, u32[]{:S(2)}) collective-permute-start(bf16[96,2048]{1,0:T(8,128)(2,1)S(1)} %get-tuple-element.301), channel_id=1, source_target_pairs={{0,2},{1,3},{2,0},{3,1},{4,6},{5,7},{6,4},{7,5},{8,10},{9,11},{10,... | collective-permute-start | bytes 1179656 | tf_op jit(solution)/shard_map/ppermute | solution.py:134
  997.2 108.7 %collective-permute-start.19 = (bf16[96,2048]{1,0:T(8,128)(2,1)S(1)}, bf16[96,2048]{1,0:T(8,128)(2,1)S(1)}, u32[]{:S(2)}, u32[]{:S(2)}) collective-permute-start(bf16[96,2048]{1,0:T(8,128)(2,1)S(1)} %get-tuple-element.301), channel_id=1, source_target_pairs={{0,3},{1,0},{2,1},{3,2},{4,7},{5,4},{6,5},{7,6},{8,11},{9,8},{10,9... | collective-permute-start | bytes 1179656 | tf_op jit(solution)/shard_map/ppermute | solution.py:134
  1054.1 53.7 %collective-permute-start.23 = (bf16[160,2048]{1,0:T(8,128)(2,1)S(1)}, bf16[160,2048]{1,0:T(8,128)(2,1)S(1)}, u32[]{:S(2)}, u32[]{:S(2)}) collective-permute-start(bf16[160,2048]{1,0:T(8,128)(2,1)S(1)} %get-tuple-element.303), channel_id=1, source_target_pairs={{0,1},{1,2},{2,3},{3,0},{4,5},{5,6},{6,7},{7,4},{8,9},{9,10},{10,1... | collective-permute-start | bytes 1966088 | tf_op jit(solution)/shard_map/ppermute | solution.py:134
  1070.8 57.6 %collective-permute-start.24 = (bf16[160,2048]{1,0:T(8,128)(2,1)S(1)}, bf16[160,2048]{1,0:T(8,128)(2,1)S(1)}, u32[]{:S(2)}, u32[]{:S(2)}) collective-permute-start(bf16[160,2048]{1,0:T(8,128)(2,1)S(1)} %get-tuple-element.303), channel_id=1, source_target_pairs={{0,2},{1,3},{2,0},{3,1},{4,6},{5,7},{6,4},{7,5},{8,10},{9,11},{10,... | collective-permute-start | bytes 1966088 | tf_op jit(solution)/shard_map/ppermute | solution.py:134
  1071.9 56.6 %collective-permute-start.25 = (bf16[160,2048]{1,0:T(8,128)(2,1)S(1)}, bf16[160,2048]{1,0:T(8,128)(2,1)S(1)}, u32[]{:S(2)}, u32[]{:S(2)}) collective-permute-start(bf16[160,2048]{1,0:T(8,128)(2,1)S(1)} %get-tuple-element.303), channel_id=1, source_target_pairs={{0,3},{1,0},{2,1},{3,2},{4,7},{5,4},{6,5},{7,6},{8,11},{9,8},{10,9... | collective-permute-start | bytes 1966088 | tf_op jit(solution)/shard_map/ppermute | solution.py:134
  (103 other events, 1524.7 us)
Sparse Core Ops, SparseCore 0:
  10.5 39.2 all-gather.10
  52.3 37.3 all-gather.8
  91.2 10.5 all-gather.12
  103.2 11.7 all-gather.20
  116.7 55.4 all-gather.16
  174.5 55.8 all-gather.18
  232.3 54.2 all-gather.14
  376.5 82.0 all-reduce.3
  503.5 117.1 all-reduce.5
  809.4 248.6 all-reduce.7
  1061.6 103.6 reduce-scatter.2
  1168.8 126.4 reduce-scatter.4
